TPU v7x, 256 devices: a 8x8x2 block of a 8x8x16 slice. The times are simulated.
256 devices in a mesh: groups: 2 (over z), attn: 16 (over y, core), expert: 8 (over x).
Axes of the slice: x: 8, y: 8, z: 2, core: 2. Of those that a mesh axis runs over, the one named last changes fastest.
The devices are a block of a 8x8x16 slice.
Arguments:
- tokens: bfloat16 [4096, 4096], P(('groups', 'attn'), 'expert'), parts along dimension 0, may hold values from -6 to 6
- expert_ids: int32 [4096, 8], P(('groups', 'attn')), parts along dimension 0, may hold values from 0 to 63, all different within a row; in each aligned block of 128 rows (0 to 127, 128 to 255, ...) at most 48 rows name the same one
- gate_weight: bfloat16 [4096, 8], P(('groups', 'attn')), parts along dimension 0, may hold values from 0.049804688 to 0.29882812
- w_gate: bfloat16 [64, 4096, 768], P('attn', 'expert'), may hold values from -0.09375 to 0.09375
- w_up: bfloat16 [64, 4096, 768], P('attn', 'expert'), may hold values from -0.09375 to 0.09375
- w_down: bfloat16 [64, 768, 4096], P('attn', None, 'expert'), may hold values from -0.21875 to 0.21875
- query: bfloat16 [512, 64, 128], P(('groups', 'attn', 'expert')), parts along dimension 0, may hold values from -100 to 100
- cache_k: bfloat16 [512, 768, 4, 128], P(('groups', 'attn', 'expert')), parts along dimension 0, may hold values from -6 to 6
- cache_v: bfloat16 [512, 768, 4, 128], P(('groups', 'attn', 'expert')), parts along dimension 0, may hold values from -6 to 6
- lengths: int32 [512], P(('groups', 'attn', 'expert')), parts along dimension 0, may hold values from 2 to 768, as said below
Outputs:
- moe_out: bfloat16 [4096, 4096], P(('groups', 'attn'), 'expert'), parts along dimension 0
- attn_out: bfloat16 [512, 8192], P(('groups', 'attn', 'expert')), parts along dimension 0
There are 2 independent parts, one for each index of `groups`. A program takes and returns all parts, laid end to end along the dimension named above; an argument that names none is the same for every part. Nothing has to cross between parts.
Inputs may be any that keep to these rules, and one draw needn't show every extreme that they name: `expert_ids`: each row names 8 different experts. In the rows of one index of attn (aligned blocks of 128 rows) no expert is named by more than 48 rows, and in some block some expert by exactly 48. `lengths`: some sequence has all 768 positions live.
All inputs are finite; a program needn't handle non-finite values.
Results may differ from a plain program's by a relative error of at most 0.025.
Values may be sent and summed in bfloat16 or wider, within the bound.
No kernel may reach another device: no remote copies, remote signals or barrier semaphores. Data moves between devices by JAX's collectives and lax.ppermute only.
A program may use at most 64 MiB of HBM per device.

v0:
```python
import functools

import jax
import jax.numpy as jnp
from jax import lax
from jax.experimental import pallas as pl
from jax.experimental.pallas import tpu as pltpu
from jax.sharding import PartitionSpec as P


F32 = jnp.float32
BF16 = jnp.bfloat16
META = 16
VMEM_SPEC = pl.BlockSpec(memory_space=pltpu.VMEM)
SMEM_SPEC = pl.BlockSpec(memory_space=pltpu.SMEM)
HBM_SPEC = pl.BlockSpec(memory_space=pltpu.HBM)


def sum_kernel(info, home, swapped, total, right, left):
    count, rows, _ = home.shape
    mid = rows // 2
    total[...] = (home[...].astype(F32) + swapped[...].astype(F32)).astype(BF16)
    right[0:rows, :] = total[info[2]]
    right[rows:, :] = total[info[4], 0:mid, :]
    left[0:rows, :] = total[info[count - 2]]
    left[rows:, :] = total[info[4], mid:, :]


def relay_kernel(info, total, right, left, far_right, far_left, near_right, near_left):
    count, rows, _ = total.shape
    mid = rows // 2
    here = total[info[3]]
    far_right[0:mid, :] = (here[0:mid].astype(F32) + right[rows:, :].astype(F32)).astype(BF16)
    far_right[mid:, :] = here[mid:]
    here = total[info[count - 3]]
    far_left[0:mid, :] = here[0:mid]
    far_left[mid:, :] = (here[mid:].astype(F32) + left[rows:, :].astype(F32)).astype(BF16)
    near_right[...] = (total[info[1]].astype(F32) + right[0:rows, :].astype(F32)).astype(BF16)
    near_left[...] = (total[info[count - 1]].astype(F32) + left[0:rows, :].astype(F32)).astype(BF16)


def finish_kernel(info, total, a, b, c, d, out):
    out[...] = (
        total[info[0]].astype(F32)
        + (a[...].astype(F32) + b[...].astype(F32))
        + (c[...].astype(F32) + d[...].astype(F32))
    ).astype(BF16)


def in_hbm(value):
    return pltpu.with_memory_space_constraint(value, pltpu.HBM)


def in_vmem(value):
    return pltpu.with_memory_space_constraint(value, pltpu.VMEM)


def attention_kernel(lengths, query, cache_k, cache_v, out):
    heads, size = query.shape[1:]
    spots, groups, _ = cache_k.shape[1:]
    columns = spots * groups
    keys = cache_k[0].reshape(columns, size)
    values = cache_v[0].reshape(columns, size)
    scores = lax.dot_general(
        query[0], keys, (((1,), (1,)), ((), ())), preferred_element_type=F32
    ) * size ** (-0.5)
    place = lax.broadcasted_iota(jnp.int32, (heads, columns), 1)
    head = lax.broadcasted_iota(jnp.int32, (heads, columns), 0)
    live = (place % groups == head // (heads // groups)) & (
        place < lengths[pl.program_id(0)] * groups
    )
    masked = jnp.where(live, scores, -jnp.inf)
    weighted = jnp.exp(masked - jnp.max(masked, axis=1, keepdims=True))
    prob = (weighted / jnp.sum(weighted, axis=1, keepdims=True)).astype(BF16)
    out[0] = jnp.dot(prob, values, preferred_element_type=F32).astype(BF16)


def grouped_attention(query, cache_k, cache_v, lengths):
    count, heads, size = query.shape
    _, spots, groups, _ = cache_k.shape
    cache = pl.BlockSpec((1, spots, groups, size), lambda i: (i, 0, 0, 0))
    row = pl.BlockSpec((1, heads, size), lambda i: (i, 0, 0))
    out = pl.pallas_call(
        attention_kernel,
        grid=(count,),
        out_shape=jax.ShapeDtypeStruct((count, heads, size), BF16),
        in_specs=[SMEM_SPEC, row, cache, cache],
        out_specs=row,
        compiler_params=pltpu.CompilerParams(vmem_limit_bytes=12 << 20),
        cost_estimate=pl.CostEstimate(
            flops=10**9, bytes_accessed=3 * 10**6, transcendentals=4 * 10**5
        ),
        name="attention",
    )(lengths, query, in_hbm(cache_k), in_hbm(cache_v))
    return out.reshape(count, heads * size)


def shift(value, axis, step):
    count = lax.axis_size(axis)
    return lax.ppermute(value, axis, [(i, (i + step) % count) for i in range(count)])


def swap_cores(value):
    return lax.ppermute(value, "attn", [(i, i ^ 1) for i in range(lax.axis_size("attn"))])


def expert_parts(j0, info, place, tok, wg_hbm, wu_hbm, wg, wu, sems, onehot, out, work):
    n_blocks = place.shape[0]
    rows = tok.shape[0] // n_blocks
    n_dest, here_count, dest_rows, ff2 = out.shape
    ff = ff2 // 2
    capacity = n_dest * dest_rows

    def fetch(j):
        return (
            pltpu.make_async_copy(wg_hbm.at[j0 + j], wg.at[j], sems.at[0, j]),
            pltpu.make_async_copy(wu_hbm.at[j0 + j], wu.at[j], sems.at[1, j]),
        )

    for j in range(here_count):
        for copy in fetch(j):
            copy.start()
    work()
    row_id = lax.broadcasted_iota(jnp.int32, (capacity, rows), 0).astype(F32)

    def expert(j, carry):
        for i in range(n_blocks):
            spot = place[info[1 + i], pl.ds(j0 + j, 1), :]
            onehot[:, i * rows : (i + 1) * rows] = jnp.where(row_id == spot, 1.0, 0.0).astype(BF16)
        packed = jnp.dot(onehot[...], tok[...], preferred_element_type=F32).astype(BF16)
        for copy in fetch(j):
            copy.wait()
        gate = jnp.dot(packed, wg[j], preferred_element_type=F32).astype(BF16)
        up = jnp.dot(packed, wu[j], preferred_element_type=F32).astype(BF16)
        out[:, j, :, 0:ff] = gate.reshape(n_dest, dest_rows, ff)
        out[:, j, :, ff:] = up.reshape(n_dest, dest_rows, ff)
        return carry

    lax.fori_loop(0, here_count, expert, 0)


def pack_kernel(plan, half, local, info, *refs):
    n_ops = 1 + max(op for p in plan for op, _ in p)
    ops = refs[:n_ops]
    wg_hbm, wu_hbm, out, route, tok, meta, mem, onehot, wg, wu, sems = refs[n_ops:]
    n_blocks = len(plan)
    rows = tok.shape[0] // n_blocks
    capacity = out.shape[0] * out.shape[2]

    def work():
        for i, p in enumerate(plan):
            at = info[1 + i]
            op, r0 = p[0]
            if len(p) == 1:
                tok[i * rows : (i + 1) * rows, :] = ops[op][r0 : r0 + rows, :]
                meta[at] = ops[op][r0 + rows : r0 + rows + META, 0:128].astype(F32)
            else:
                op1, r1 = p[1]
                tok[i * rows : i * rows + half, :] = ops[op][r0 : r0 + half, :]
                tok[i * rows + half : (i + 1) * rows, :] = ops[op1][r1 : r1 + rows - half, :]
                meta[at] = ops[op1][r1 + rows - half : r1 + half, 0:128].astype(F32)
        first = info[0]

        def members(b, carry):
            ids = meta[b, 0:8, :]
            gates = meta[b, 8:16, :]
            for j in range(local):
                hit = ids == (first + j).astype(F32)
                mem[b, j : j + 1, :] = jnp.sum(jnp.where(hit, 1.0, 0.0), axis=0, keepdims=True)
                route[b, 4 + j : 5 + j, :] = jnp.sum(
                    jnp.where(hit, gates, 0.0), axis=0, keepdims=True
                )
            mem[b, local:8, :] = jnp.zeros((8 - local, rows), F32)
            return carry

        lax.fori_loop(0, n_blocks, members, 0)
        size = n_blocks * 8
        member = mem[...].reshape(size, rows)
        r = lax.broadcasted_iota(jnp.int32, (rows, rows), 0)
        c = lax.broadcasted_iota(jnp.int32, (rows, rows), 1)
        upper = jnp.where(r < c, 1.0, 0.0).astype(BF16)
        rr = lax.broadcasted_iota(jnp.int32, (size, size), 0)
        cc = lax.broadcasted_iota(jnp.int32, (size, size), 1)
        earlier = jnp.where((rr % 8 == cc % 8) & (cc // 8 < rr // 8), 1.0, 0.0).astype(BF16)
        member_b = member.astype(BF16)
        before = jnp.dot(earlier, member_b, preferred_element_type=F32).astype(BF16)
        place = jnp.dot(member_b, upper, preferred_element_type=F32) + jnp.dot(
            before, jnp.ones((rows, rows), BF16), preferred_element_type=F32
        )
        place = jnp.where((member > 0.5) & (place < capacity), place, -1.0)
        mem[...] = place.reshape(n_blocks, 8, rows)
        route[:, 0:local, :] = mem[:, 0:local, :]

    expert_parts(0, info, route, tok, wg_hbm, wu_hbm, wg, wu, sems, onehot, out, work)


def pack_more_kernel(j0, info, tok, route, wg_hbm, wu_hbm, out, onehot, wg, wu, sems):
    expert_parts(
        j0, info, route, tok, wg_hbm, wu_hbm, wg, wu, sems, onehot, out, lambda: None
    )


def mix_rows(side, route, res, mix, ref):
    n_dest, rows, _ = ref.shape
    group = mix.shape[0] // rows
    local = 4
    capacity = res.shape[0] // local
    r = lax.broadcasted_iota(jnp.int32, (rows, rows), 0)
    c = lax.broadcasted_iota(jnp.int32, (rows, rows), 1)
    eye = jnp.where(r == c, 1.0, 0.0).astype(BF16)
    col_id = lax.broadcasted_iota(jnp.int32, (rows, capacity), 1).astype(F32)

    def some(g, carry):
        for d in range(group):
            b = 2 * (g * group + d) + side
            rt = lax.dot_general(
                eye, route[b].astype(BF16), (((1,), (1,)), ((), ())), preferred_element_type=F32
            )
            for j in range(local):
                mix[d * rows : (d + 1) * rows, j * capacity : (j + 1) * capacity] = jnp.where(
                    col_id == rt[:, j : j + 1], rt[:, 4 + j : 5 + j], 0.0
                ).astype(BF16)
        got = jnp.dot(mix[...], res[...], preferred_element_type=F32).astype(BF16)
        ref[pl.ds(g * group, group)] = got.reshape(group, rows, got.shape[1])
        return carry

    lax.fori_loop(0, n_dest // group, some, 0)


def down_kernel(plan, info, *refs):
    n_ops = len(plan)
    ops = refs[:n_ops]
    wd_hbm, route, away, res, hid, mix, wd, sems = refs[n_ops:]
    local = wd.shape[0]
    capacity = hid.shape[1]

    def fetch(j):
        return pltpu.make_async_copy(wd_hbm.at[j], wd.at[j], sems.at[j])

    for j in range(local):
        fetch(j).start()
    for op, (j0, slot) in zip(ops, plan):
        at = pl.multiple_of(info[slot], op.shape[1])
        for j in range(op.shape[0]):
            hid[j0 + j, pl.ds(at, op.shape[1]), :] = op[j]

    def expert(j, carry):
        fetch(j).wait()
        res[pl.ds(pl.multiple_of(j * capacity, capacity), capacity), :] = jnp.dot(
            hid[j], wd[j], preferred_element_type=F32
        ).astype(BF16)
        return carry

    lax.fori_loop(0, local, expert, 0)
    mix_rows(1 - info[0], route, res, mix, away)


def home_kernel(info, res, route, home, mix):
    mix_rows(info[0], route, res, mix, home)


def scatter_sum(pieces, axis, stride, at):
    count = len(at)
    half = count // 2
    legs = {}
    for way in (1, -1):
        for s in range(2):
            start = half if (way == 1) == (s == 0) else half - 1
            legs[(way, s)] = [start, pieces[s](at[way * start % count]).astype(BF16)]
    for hop in range(half, 0, -1):
        for way in (1, -1):
            for s in range(2):
                leg = legs[(way, s)]
                if leg[0] != hop:
                    continue
                got = shift(leg[1], axis, way * stride).astype(F32)
                if hop > 1:
                    mine = pieces[s](at[way * (hop - 1) % count]).astype(F32)
                    legs[(way, s)] = [hop - 1, (got + mine).astype(BF16)]
                else:
                    legs[(way, s)] = [0, got]
    return [pieces[s](at[0]).astype(F32) + legs[(1, s)][1] + legs[(-1, s)][1] for s in range(2)]


def step(tokens, expert_ids, gate_weight, w_gate, w_up, w_down, query, cache_k, cache_v, lengths):
    rows, feat = tokens.shape
    local, _, ff = w_gate.shape
    attn_count = lax.axis_size("attn")
    n_expert = lax.axis_size("expert")
    chips = attn_count // 2
    top = expert_ids.shape[1]
    capacity = rows * top // local
    me = lax.axis_index("attn")
    col = lax.axis_index("expert")
    y = me // 2
    core = me % 2
    far = chips // 2
    dest_rows = capacity // n_expert

    y_at = [lax.rem(y + k, chips) for k in range(chips)]
    x_at = [lax.rem(col + k, n_expert).astype(jnp.uint32) for k in range(n_expert)]
    offsets = [0, -1, 1, -3, 3, -2, 2, far]
    pack_info = [local * me]
    for flip in (0, 1):
        pack_info += [2 * y_at[off % chips] + (core ^ flip) for off in offsets]
    row_at = [core] + [x.astype(jnp.int32) * dest_rows for x in x_at]
    pack_info = jnp.stack(pack_info).astype(jnp.int32)
    row_at = jnp.stack(row_at).astype(jnp.int32)
    core_at = core.reshape(1).astype(jnp.int32)
    y_info = jnp.stack(y_at).astype(jnp.int32)
    tokens, pack_info, row_at, core_at, y_info, x_at = lax.optimization_barrier(
        (tokens, pack_info, row_at, core_at, y_info, x_at)
    )

    meta = jnp.concatenate([expert_ids.astype(BF16).T, gate_weight.T], axis=0)
    block = jnp.concatenate([tokens, jnp.pad(meta, ((0, 0), (0, feat - rows)))], axis=0)
    half = (rows + META) // 2
    attn_out = grouped_attention(query, cache_k, cache_v, lengths)
    near = [shift(block, "attn", 2), shift(block, "attn", -2)]
    away3 = [shift(block, "attn", 6), shift(block, "attn", -6)]
    *near, attn_out = lax.optimization_barrier((*near, attn_out))
    right = shift(jnp.concatenate([near[0], away3[0][:half]], axis=0), "attn", 2)
    left = shift(jnp.concatenate([near[1], away3[1][half:]], axis=0), "attn", -2)
    swap_first = swap_cores(jnp.concatenate([block, *near, *away3], axis=0))
    swap_last = swap_cores(jnp.concatenate([right, left], axis=0))
    operands = [block, *near, *away3, right, left, swap_first, swap_last]
    height = rows + META
    plan = [((i, 0),) for i in range(7)] + [((5, height), (6, height))]
    plan += [((7, i * height),) for i in range(5)]
    plan += [((8, 0),), ((8, height + half),), ((8, height), (8, 2 * height + half))]

    cut = local // 2
    pack_scratch = [
        pltpu.VMEM((capacity, attn_count * rows), BF16),
        pltpu.VMEM((cut, *w_gate.shape[1:]), BF16),
        pltpu.VMEM((cut, *w_up.shape[1:]), BF16),
        pltpu.SemaphoreType.DMA((2, cut)),
    ]
    part_shape = jax.ShapeDtypeStruct((n_expert, cut, dest_rows, 2 * ff), BF16)
    pack_cost = pl.CostEstimate(flops=2 * 10**9, bytes_accessed=6 * 10**6, transcendentals=0)
    parts_a, route, tok = pl.pallas_call(
        functools.partial(pack_kernel, plan, half, local),
        out_shape=(
            part_shape,
            jax.ShapeDtypeStruct((attn_count, 8, rows), F32),
            jax.ShapeDtypeStruct((attn_count * rows, feat), BF16),
        ),
        in_specs=[SMEM_SPEC] + [VMEM_SPEC] * len(operands) + [HBM_SPEC] * 2,
        out_specs=(VMEM_SPEC, VMEM_SPEC, VMEM_SPEC),
        scratch_shapes=[
            pltpu.VMEM((attn_count, META, rows), F32),
            pltpu.VMEM((attn_count, 8, rows), F32),
            *pack_scratch,
        ],
        compiler_params=pltpu.CompilerParams(vmem_limit_bytes=7 << 20),
        cost_estimate=pack_cost,
        name="pack",
    )(pack_info, *map(in_vmem, operands), in_hbm(w_gate), in_hbm(w_up))
    parts_b = pl.pallas_call(
        functools.partial(pack_more_kernel, cut),
        out_shape=part_shape,
        in_specs=[SMEM_SPEC, VMEM_SPEC, VMEM_SPEC, HBM_SPEC, HBM_SPEC],
        out_specs=VMEM_SPEC,
        scratch_shapes=pack_scratch,
        compiler_params=pltpu.CompilerParams(vmem_limit_bytes=7 << 20),
        cost_estimate=pack_cost,
        name="pack_more",
    )(pack_info, in_vmem(tok), in_vmem(route), in_hbm(w_gate), in_hbm(w_up))

    sums = scatter_sum(
        [lambda at, p=p: lax.dynamic_index_in_dim(p, at, 0, keepdims=False) for p in (parts_a, parts_b)],
        "expert",
        1,
        x_at,
    )
    hidden = jnp.concatenate(
        [(jax.nn.silu(t[..., :ff]) * t[..., ff:]).astype(BF16) for t in sums], axis=0
    )

    n_half = n_expert // 2
    pieces_in, where = [hidden], [(0, 1)]
    rightward = leftward = hidden
    for hop in range(1, n_half + 1):
        if hop == n_half:
            rightward, leftward = rightward[:cut], leftward[cut:]
        rightward, leftward = shift(rightward, "expert", 1), shift(leftward, "expert", -1)
        pieces_in += [rightward, leftward]
        where += [(0, 1 + n_expert - hop), (cut if hop == n_half else 0, 1 + hop)]

    away, res = pl.pallas_call(
        functools.partial(down_kernel, where),
        out_shape=(
            jax.ShapeDtypeStruct((chips, rows, feat), BF16),
            jax.ShapeDtypeStruct((local * capacity, feat), BF16),
        ),
        in_specs=[SMEM_SPEC] + [VMEM_SPEC] * len(pieces_in) + [HBM_SPEC, VMEM_SPEC],
        out_specs=(VMEM_SPEC, VMEM_SPEC),
        scratch_shapes=[
            pltpu.VMEM((local, capacity, ff), BF16),
            pltpu.VMEM((2 * rows, local * capacity), BF16),
            pltpu.VMEM(w_down.shape, BF16),
            pltpu.SemaphoreType.DMA((local,)),
        ],
        compiler_params=pltpu.CompilerParams(vmem_limit_bytes=(15 << 20) // 2),
        cost_estimate=pl.CostEstimate(flops=2 * 10**9, bytes_accessed=6 * 10**6, transcendentals=0),
        name="down",
    )(row_at, *map(in_vmem, pieces_in), in_hbm(w_down), in_vmem(route))
    swapped = swap_cores(away)
    home = pl.pallas_call(
        home_kernel,
        out_shape=jax.ShapeDtypeStruct((chips, rows, feat), BF16),
        in_specs=[SMEM_SPEC, VMEM_SPEC, VMEM_SPEC],
        out_specs=VMEM_SPEC,
        scratch_shapes=[pltpu.VMEM((2 * rows, local * capacity), BF16)],
        compiler_params=pltpu.CompilerParams(vmem_limit_bytes=(5 << 20) // 2),
        cost_estimate=pl.CostEstimate(flops=10**9, bytes_accessed=2 * 10**6, transcendentals=0),
        name="home",
    )(core_at, in_vmem(res), in_vmem(route))

    block_shape = jax.ShapeDtypeStruct((rows, feat), BF16)
    long_shape = jax.ShapeDtypeStruct((rows + rows // 2, feat), BF16)
    small = {"compiler_params": pltpu.CompilerParams(vmem_limit_bytes=2 << 20)}
    total, right, left = pl.pallas_call(
        sum_kernel,
        out_shape=(jax.ShapeDtypeStruct(home.shape, BF16), long_shape, long_shape),
        in_specs=[SMEM_SPEC, VMEM_SPEC, VMEM_SPEC],
        out_specs=(VMEM_SPEC,) * 3,
        name="sum",
        **small,
    )(y_info, in_vmem(home), in_vmem(swapped))
    right, left = shift(right, "attn", 2), shift(left, "attn", -2)
    far_right, far_left, near_right, near_left = pl.pallas_call(
        relay_kernel,
        out_shape=(block_shape,) * 4,
        in_specs=[SMEM_SPEC] + [VMEM_SPEC] * 3,
        out_specs=(VMEM_SPEC,) * 4,
        name="relay",
        **small,
    )(y_info, in_vmem(total), in_vmem(right), in_vmem(left))
    last = [
        shift(far_right, "attn", 6),
        shift(far_left, "attn", -6),
        shift(near_right, "attn", 2),
        shift(near_left, "attn", -2),
    ]
    moe_out = pl.pallas_call(
        finish_kernel,
        out_shape=block_shape,
        in_specs=[SMEM_SPEC] + [VMEM_SPEC] * 5,
        out_specs=VMEM_SPEC,
        name="finish",
        **small,
    )(y_info, in_vmem(total), *map(in_vmem, last))
    return (moe_out, attn_out)


def solution(mesh):
    return jax.shard_map(
        step,
        mesh=mesh,
        in_specs=(
            P(("groups", "attn"), "expert"),
            P(("groups", "attn"), None),
            P(("groups", "attn"), None),
            P("attn", "expert", None),
            P("attn", "expert", None),
            P("attn", None, "expert"),
            P(("groups", "attn", "expert"), None, None),
            P(("groups", "attn", "expert"), None, None, None),
            P(("groups", "attn", "expert"), None, None, None),
            P(("groups", "attn", "expert")),
        ),
        out_specs=(P(("groups", "attn"), "expert"), P(("groups", "attn", "expert"), None)),
        check_vma=False,
    )
```

profile of v0, /device:TPU:513, one launch (start us, length us, event | category | flops | bytes accessed | tf_op | source)
XLA Modules:
  0.0 161.5 jit_solution(7835487983977655743)
XLA Ops:
  1.0 0.7 convert_bitcast_fusion
  1.7 0.9 constant_dynamic-update-slice_fusion.5
  2.6 0.7 constant_dynamic-update-slice_fusion.4
  3.3 0.9 pad_maximum_fusion.4.refs_0_
  4.2 12.5 %collective-permute-start.1 = (bf16[144,512]{1,0:T(8,128)(2,1)S(1)}, bf16[144,512]{1,0:T(8,128)(2,1)S(1)}, u32[]{:S(2)}, u32[]{:S(2)}) collective-permute-start(bf16[144,512]{1,0:T(8,128)(2,1)S(1)} %pad_maximum_fusion.4.refs_0_), channel_id=1, source_target_pairs={{0,112},{8,120},{16,0},{24,8},{32,16},{40,24},{48,32},{56,40},{64,... | collective-permute-start | bytes 442376 | tf_op jit(solution)/shard_map/ppermute | solution.py:100
  16.8 0.9 collective-permute-start.3
  17.7 2.4 %collective-permute-start.2 = (bf16[144,512]{1,0:T(8,128)(2,1)S(1)}, bf16[144,512]{1,0:T(8,128)(2,1)S(1)}, u32[]{:S(2)}, u32[]{:S(2)}) collective-permute-start(bf16[144,512]{1,0:T(8,128)(2,1)S(1)} %pad_maximum_fusion.4.refs_0_), channel_id=1, source_target_pairs={{0,48},{8,56},{16,64},{24,72},{32,80},{40,88},{48,96},{56,104},{64... | collective-permute-start | bytes 442376 | tf_op jit(solution)/shard_map/ppermute | solution.py:100
  20.0 0.8 copy-done
  20.8 0.7 copy-done.1
  21.4 3.4 %attention.1 = bf16[2,64,128]{2,1,0:T(8,128)(2,1)S(1)} custom-call(s32[2]{0:T(128)S(1)} %copy-done.1, bf16[2,64,128]{2,1,0:T(8,128)(2,1)S(1)} %copy-done, bf16[2,768,4,128]{3,2,1,0:T(4,128)(2,1)} %cache_k.1, bf16[2,768,4,128]{3,2,1,0:T(4,128)(2,1)} %cache_v.1), custom_call_target="tpu_custom_call" | custom-call | flops 1000000000 | bytes 3000000 | tf_op jit(solution)/shard_map/attention/pallas_call | solution.py:83
  24.8 0.6 copy.14
  25.5 2.4 %collective-permute-done.2.refs_3_ = bf16[144,512]{1,0:T(8,128)(2,1)S(1)} collective-permute-done((bf16[144,512]{1,0:T(8,128)(2,1)S(1)}, bf16[144,512]{1,0:T(8,128)(2,1)S(1)}, u32[]{:S(2)}, u32[]{:S(2)}) %collective-permute-start.2) | collective-permute-done | bytes 147488 | tf_op jit(solution)/shard_map/ppermute | solution.py:100
  28.0 1.6 collective-permute-start.5
  29.6 12.2 %collective-permute-start.6 = (bf16[720,512]{1,0:T(8,128)(2,1)S(1)}, bf16[720,512]{1,0:T(8,128)(2,1)S(1)}, u32[]{:S(2)}, u32[]{:S(2)}) collective-permute-start(bf16[720,512]{1,0:T(8,128)(2,1)S(1)} %constant_dynamic-update-slice_fusion), channel_id=1, source_target_pairs={{0,8},{8,0},{16,24},{24,16},{32,40},{40,32},{48,56},{56,48},{64,72... | collective-permute-start | bytes 2211848 | tf_op jit(solution)/shard_map/ppermute | solution.py:104
  41.9 6.4 %collective-permute-start.7 = (bf16[432,512]{1,0:T(8,128)(2,1)S(1)}, bf16[432,512]{1,0:T(8,128)(2,1)S(1)}, u32[]{:S(2)}, u32[]{:S(2)}) collective-permute-start(bf16[432,512]{1,0:T(8,128)(2,1)S(1)} %pad_maximum_fusion), channel_id=1, source_target_pairs={{0,8},{8,0},{16,24},{24,16},{32,40},{40,32},{48,56},{56,48},{64,72... | collective-permute-start | bytes 1327112 | tf_op jit(solution)/shard_map/ppermute | solution.py:104
  48.3 1.4 collective-permute-done.7.refs_8_
  49.7 3.9 %pack.1 = (bf16[8,2,32,1536]{3,2,1,0:T(8,128)(2,1)S(1)}, f32[16,8,128]{2,1,0:T(8,128)S(1)}, bf16[2048,512]{1,0:T(8,128)(2,1)S(1)}) custom-call(s32[17]{0:T(128)S(1)} %stack.128.info, bf16[144,512]{1,0:T(8,128)(2,1)S(1)} %pad_maximum_fusion.4.refs_0_, bf16[144,512]{1,0:T(8,128)(2,1)S(1)} %collective-permute-done.refs_1_, ...), custom_call_target="tpu_custom_call" | custom-call | flops 2000000000 | bytes 6000000 | tf_op jit(solution)/shard_map/pack/pallas_call | solution.py:341
  53.6 3.9 %pack_more.1 = bf16[8,2,32,1536]{3,2,1,0:T(8,128)(2,1)S(1)} custom-call(s32[17]{0:T(128)S(1)} %stack.128.info, bf16[2048,512]{1,0:T(8,128)(2,1)S(1)} %get-tuple-element.46.tok, f32[16,8,128]{2,1,0:T(8,128)S(1)} %get-tuple-element.47.route.refs_10_, bf16[4,512,768]{2,1,0:T(8,128)(2,1)} %wg_hbm.1, bf16[4,512,768]{2,1,0:T(8,128)(2,1)} %wu_hbm.1), custom_call_target="tpu_custom_call" | custom-call | flops 2000000000 | bytes 6000000 | tf_op jit(solution)/shard_map/pack_more/pallas_call | solution.py:359
  57.5 0.1 collective-permute-start.15
  57.6 2.6 %collective-permute-start.18 = (bf16[2,32,1536]{2,1,0:T(8,128)(2,1)S(1)}, bf16[2,32,1536]{2,1,0:T(8,128)(2,1)S(1)}, u32[]{:S(2)}, u32[]{:S(2)}) collective-permute-start(bf16[2,32,1536]{2,1,0:T(8,128)(2,1)S(1)} %get-tuple-element.69), channel_id=1, source_target_pairs={{0,7},{1,0},{2,1},{3,2},{4,3},{5,4},{6,5},{7,6},{8,15},{9,8},{10,9... | collective-permute-start | bytes 589832 | tf_op jit(solution)/shard_map/ppermute | solution.py:100
  60.3 0.3 collective-permute-start.8
  60.6 2.6 %collective-permute-start.12 = (bf16[2,32,1536]{2,1,0:T(8,128)(2,1)S(1)}, bf16[2,32,1536]{2,1,0:T(8,128)(2,1)S(1)}, u32[]{:S(2)}, u32[]{:S(2)}) collective-permute-start(bf16[2,32,1536]{2,1,0:T(8,128)(2,1)S(1)} %get-tuple-element.63), channel_id=1, source_target_pairs={{0,7},{1,0},{2,1},{3,2},{4,3},{5,4},{6,5},{7,6},{8,15},{9,8},{10,9... | collective-permute-start | bytes 589832 | tf_op jit(solution)/shard_map/ppermute | solution.py:100
  63.3 0.6 collective-permute-done.18
  63.9 3.5 %collective-permute-start.19 = (bf16[2,32,1536]{2,1,0:T(8,128)(2,1)S(1)}, bf16[2,32,1536]{2,1,0:T(8,128)(2,1)S(1)}, u32[]{:S(2)}, u32[]{:S(2)}) collective-permute-start(bf16[2,32,1536]{2,1,0:T(8,128)(2,1)S(1)} %fusion.2), channel_id=1, source_target_pairs={{0,7},{1,0},{2,1},{3,2},{4,3},{5,4},{6,5},{7,6},{8,15},{9,8},{10,9... | collective-permute-start | bytes 589832 | tf_op jit(solution)/shard_map/ppermute | solution.py:100
  67.5 1.7 %collective-permute-done.8 = bf16[2,32,1536]{2,1,0:T(8,128)(2,1)S(1)} collective-permute-done((bf16[2,32,1536]{2,1,0:T(8,128)(2,1)S(1)}, bf16[2,32,1536]{2,1,0:T(8,128)(2,1)S(1)}, u32[]{:S(2)}, u32[]{:S(2)}) %collective-permute-start.8) | collective-permute-done | bytes 196640 | tf_op jit(solution)/shard_map/ppermute | solution.py:100
  69.2 0.1 collective-permute-start.9
  69.3 2.8 %collective-permute-done.19 = bf16[2,32,1536]{2,1,0:T(8,128)(2,1)S(1)} collective-permute-done((bf16[2,32,1536]{2,1,0:T(8,128)(2,1)S(1)}, bf16[2,32,1536]{2,1,0:T(8,128)(2,1)S(1)}, u32[]{:S(2)}, u32[]{:S(2)}) %collective-permute-start.19) | collective-permute-done | bytes 196640 | tf_op jit(solution)/shard_map/ppermute | solution.py:100
  72.2 0.1 collective-permute-start.16
  72.4 3.0 %collective-permute-start.20 = (bf16[2,32,1536]{2,1,0:T(8,128)(2,1)S(1)}, bf16[2,32,1536]{2,1,0:T(8,128)(2,1)S(1)}, u32[]{:S(2)}, u32[]{:S(2)}) collective-permute-start(bf16[2,32,1536]{2,1,0:T(8,128)(2,1)S(1)} %get-tuple-element.67), channel_id=1, source_target_pairs={{0,7},{1,0},{2,1},{3,2},{4,3},{5,4},{6,5},{7,6},{8,15},{9,8},{10,9... | collective-permute-start | bytes 589832 | tf_op jit(solution)/shard_map/ppermute | solution.py:100
  75.3 0.3 collective-permute-done.9
  75.8 0.1 collective-permute-start.10
  75.9 2.6 %collective-permute-start.13 = (bf16[2,32,1536]{2,1,0:T(8,128)(2,1)S(1)}, bf16[2,32,1536]{2,1,0:T(8,128)(2,1)S(1)}, u32[]{:S(2)}, u32[]{:S(2)}) collective-permute-start(bf16[2,32,1536]{2,1,0:T(8,128)(2,1)S(1)} %get-tuple-element.61), channel_id=1, source_target_pairs={{0,7},{1,0},{2,1},{3,2},{4,3},{5,4},{6,5},{7,6},{8,15},{9,8},{10,9... | collective-permute-start | bytes 589832 | tf_op jit(solution)/shard_map/ppermute | solution.py:100
  78.6 1.6 collective-permute-done.16
  80.2 0.1 collective-permute-start.17
  80.4 2.6 %collective-permute-start.21 = (bf16[2,32,1536]{2,1,0:T(8,128)(2,1)S(1)}, bf16[2,32,1536]{2,1,0:T(8,128)(2,1)S(1)}, u32[]{:S(2)}, u32[]{:S(2)}) collective-permute-start(bf16[2,32,1536]{2,1,0:T(8,128)(2,1)S(1)} %get-tuple-element.65), channel_id=1, source_target_pairs={{0,7},{1,0},{2,1},{3,2},{4,3},{5,4},{6,5},{7,6},{8,15},{9,8},{10,9... | collective-permute-start | bytes 589832 | tf_op jit(solution)/shard_map/ppermute | solution.py:100
  83.0 1.1 collective-permute-done.10
  84.2 0.1 collective-permute-start.11
  84.4 2.6 %collective-permute-start.14 = (bf16[2,32,1536]{2,1,0:T(8,128)(2,1)S(1)}, bf16[2,32,1536]{2,1,0:T(8,128)(2,1)S(1)}, u32[]{:S(2)}, u32[]{:S(2)}) collective-permute-start(bf16[2,32,1536]{2,1,0:T(8,128)(2,1)S(1)} %get-tuple-element.59), channel_id=1, source_target_pairs={{0,7},{1,0},{2,1},{3,2},{4,3},{5,4},{6,5},{7,6},{8,15},{9,8},{10,9... | collective-permute-start | bytes 589832 | tf_op jit(solution)/shard_map/ppermute | solution.py:100
  87.0 0.6 collective-permute-done.17
  87.8 4.3 %collective-permute-done.11 = bf16[2,32,1536]{2,1,0:T(8,128)(2,1)S(1)} collective-permute-done((bf16[2,32,1536]{2,1,0:T(8,128)(2,1)S(1)}, bf16[2,32,1536]{2,1,0:T(8,128)(2,1)S(1)}, u32[]{:S(2)}, u32[]{:S(2)}) %collective-permute-start.11) | collective-permute-done | bytes 196640 | tf_op jit(solution)/shard_map/ppermute | solution.py:100
  92.3 3.0 %collective-permute-start.23 = (bf16[4,32,768]{2,1,0:T(8,128)(2,1)S(1)}, bf16[4,32,768]{2,1,0:T(8,128)(2,1)S(1)}, u32[]{:S(2)}, u32[]{:S(2)}) collective-permute-start(bf16[4,32,768]{2,1,0:T(8,128)(2,1)S(1)} %pad_maximum_fusion.3.refs_0_), channel_id=1, source_target_pairs={{0,7},{1,0},{2,1},{3,2},{4,3},{5,4},{6,5},{7,6},{8,15},{9,8},{10,9... | collective-permute-start | bytes 589832 | tf_op jit(solution)/shard_map/ppermute | solution.py:100
  95.3 2.6 %collective-permute-done.23.refs_2_ = bf16[4,32,768]{2,1,0:T(8,128)(2,1)S(1)} collective-permute-done((bf16[4,32,768]{2,1,0:T(8,128)(2,1)S(1)}, bf16[4,32,768]{2,1,0:T(8,128)(2,1)S(1)}, u32[]{:S(2)}, u32[]{:S(2)}) %collective-permute-start.23) | collective-permute-done | bytes 196640 | tf_op jit(solution)/shard_map/ppermute | solution.py:100
  97.9 3.1 %collective-permute-start.25 = (bf16[4,32,768]{2,1,0:T(8,128)(2,1)S(1)}, bf16[4,32,768]{2,1,0:T(8,128)(2,1)S(1)}, u32[]{:S(2)}, u32[]{:S(2)}) collective-permute-start(bf16[4,32,768]{2,1,0:T(8,128)(2,1)S(1)} %collective-permute-done.23.refs_2_), channel_id=1, source_target_pairs={{0,7},{1,0},{2,1},{3,2},{4,3},{5,4},{6,5},{7,6},{8,15},{9,8},{10,9... | collective-permute-start | bytes 589832 | tf_op jit(solution)/shard_map/ppermute | solution.py:100
  101.0 2.6 %collective-permute-done.25.refs_4_ = bf16[4,32,768]{2,1,0:T(8,128)(2,1)S(1)} collective-permute-done((bf16[4,32,768]{2,1,0:T(8,128)(2,1)S(1)}, bf16[4,32,768]{2,1,0:T(8,128)(2,1)S(1)}, u32[]{:S(2)}, u32[]{:S(2)}) %collective-permute-start.25) | collective-permute-done | bytes 196640 | tf_op jit(solution)/shard_map/ppermute | solution.py:100
  103.7 3.1 %collective-permute-start.27 = (bf16[4,32,768]{2,1,0:T(8,128)(2,1)S(1)}, bf16[4,32,768]{2,1,0:T(8,128)(2,1)S(1)}, u32[]{:S(2)}, u32[]{:S(2)}) collective-permute-start(bf16[4,32,768]{2,1,0:T(8,128)(2,1)S(1)} %collective-permute-done.25.refs_4_), channel_id=1, source_target_pairs={{0,7},{1,0},{2,1},{3,2},{4,3},{5,4},{6,5},{7,6},{8,15},{9,8},{10,9... | collective-permute-start | bytes 589832 | tf_op jit(solution)/shard_map/ppermute | solution.py:100
  106.8 3.4 %collective-permute-done.27.refs_6_ = bf16[4,32,768]{2,1,0:T(8,128)(2,1)S(1)} collective-permute-done((bf16[4,32,768]{2,1,0:T(8,128)(2,1)S(1)}, bf16[4,32,768]{2,1,0:T(8,128)(2,1)S(1)}, u32[]{:S(2)}, u32[]{:S(2)}) %collective-permute-start.27) | collective-permute-done | bytes 196640 | tf_op jit(solution)/shard_map/ppermute | solution.py:100
  110.2 3.2 %collective-permute-start.29 = (bf16[2,32,768]{2,1,0:T(8,128)(2,1)S(1)}, bf16[2,32,768]{2,1,0:T(8,128)(2,1)S(1)}, u32[]{:S(2)}, u32[]{:S(2)}) collective-permute-start(bf16[2,32,768]{2,1,0:T(8,128)(2,1)S(1)} %slice.39), channel_id=1, source_target_pairs={{0,7},{1,0},{2,1},{3,2},{4,3},{5,4},{6,5},{7,6},{8,15},{9,8},{10,9... | collective-permute-start | bytes 294920 | tf_op jit(solution)/shard_map/ppermute | solution.py:100
  113.4 0.2 collective-permute-done.26.refs_5_
  113.7 2.3 %collective-permute-done.29.refs_8_ = bf16[2,32,768]{2,1,0:T(8,128)(2,1)S(1)} collective-permute-done((bf16[2,32,768]{2,1,0:T(8,128)(2,1)S(1)}, bf16[2,32,768]{2,1,0:T(8,128)(2,1)S(1)}, u32[]{:S(2)}, u32[]{:S(2)}) %collective-permute-start.29) | collective-permute-done | bytes 98336 | tf_op jit(solution)/shard_map/ppermute | solution.py:100
  116.0 3.7 %collective-permute-done.28.refs_7_ = bf16[2,32,768]{2,1,0:T(8,128)(2,1)S(1)} collective-permute-done((bf16[2,32,768]{2,1,0:T(8,128)(2,1)S(1)}, bf16[2,32,768]{2,1,0:T(8,128)(2,1)S(1)}, u32[]{:S(2)}, u32[]{:S(2)}) %collective-permute-start.28) | collective-permute-done | bytes 98336 | tf_op jit(solution)/shard_map/ppermute | solution.py:100
  119.7 5.8 %down.1 = (bf16[8,128,512]{2,1,0:T(8,128)(2,1)S(1)}, bf16[1024,512]{1,0:T(8,128)(2,1)S(1)}) custom-call(s32[9]{0:T(128)S(1)} %stack.138.info, bf16[4,32,768]{2,1,0:T(8,128)(2,1)S(1)} %pad_maximum_fusion.3.refs_0_, bf16[4,32,768]{2,1,0:T(8,128)(2,1)S(1)} %collective-permute-done.22.refs_1_, bf16[4,32,768]{2,1,0:T(8,128)(2,1)S(1)} %collective-permute-done.23.refs_2_, ...), custom_call_target="tpu_custom_call" | custom-call | flops 2000000000 | bytes 6000000 | tf_op jit(solution)/shard_map/down/pallas_call | solution.py:390
  125.6 7.5 %collective-permute-start.30 = (bf16[8,128,512]{2,1,0:T(8,128)(2,1)S(1)}, bf16[8,128,512]{2,1,0:T(8,128)(2,1)S(1)}, u32[]{:S(2)}, u32[]{:S(2)}) collective-permute-start(bf16[8,128,512]{2,1,0:T(8,128)(2,1)S(1)} %get-tuple-element.49), channel_id=1, source_target_pairs={{0,8},{8,0},{16,24},{24,16},{32,40},{40,32},{48,56},{56,48},{64,72... | collective-permute-start | bytes 3145736 | tf_op jit(solution)/shard_map/ppermute | solution.py:104
  133.1 2.7 %home.1 = bf16[8,128,512]{2,1,0:T(8,128)(2,1)S(1)} custom-call(s32[1]{0:T(128)} %bitcast.17.info, bf16[1024,512]{1,0:T(8,128)(2,1)S(1)} %get-tuple-element.48.res, f32[16,8,128]{2,1,0:T(8,128)S(1)} %get-tuple-element.47.route.refs_10_), custom_call_target="tpu_custom_call" | custom-call | flops 1000000000 | bytes 2000000 | tf_op jit(solution)/shard_map/home/pallas_call | solution.py:409
  135.8 1.1 sum.1
  136.9 0.1 collective-permute-start.31
  137.0 2.6 %collective-permute-start.32 = (bf16[192,512]{1,0:T(8,128)(2,1)S(1)}, bf16[192,512]{1,0:T(8,128)(2,1)S(1)}, u32[]{:S(2)}, u32[]{:S(2)}) collective-permute-start(bf16[192,512]{1,0:T(8,128)(2,1)S(1)} %get-tuple-element.52), channel_id=1, source_target_pairs={{0,112},{8,120},{16,0},{24,8},{32,16},{40,24},{48,32},{56,40},{64,... | collective-permute-start | bytes 589832 | tf_op jit(solution)/shard_map/ppermute | solution.py:100
  139.7 5.0 %collective-permute-done.31.right = bf16[192,512]{1,0:T(8,128)(2,1)S(1)} collective-permute-done((bf16[192,512]{1,0:T(8,128)(2,1)S(1)}, bf16[192,512]{1,0:T(8,128)(2,1)S(1)}, u32[]{:S(2)}, u32[]{:S(2)}) %collective-permute-start.31) | collective-permute-done | bytes 196640 | tf_op jit(solution)/shard_map/ppermute | solution.py:100
  144.6 0.6 relay.1
  145.3 2.9 %collective-permute-start.33 = (bf16[128,512]{1,0:T(8,128)(2,1)S(1)}, bf16[128,512]{1,0:T(8,128)(2,1)S(1)}, u32[]{:S(2)}, u32[]{:S(2)}) collective-permute-start(bf16[128,512]{1,0:T(8,128)(2,1)S(1)} %get-tuple-element.53), channel_id=1, source_target_pairs={{0,48},{8,56},{16,64},{24,72},{32,80},{40,88},{48,96},{56,104},{64... | collective-permute-start | bytes 393224 | tf_op jit(solution)/shard_map/ppermute | solution.py:100
  148.2 1.7 %collective-permute-start.34 = (bf16[128,512]{1,0:T(8,128)(2,1)S(1)}, bf16[128,512]{1,0:T(8,128)(2,1)S(1)}, u32[]{:S(2)}, u32[]{:S(2)}) collective-permute-start(bf16[128,512]{1,0:T(8,128)(2,1)S(1)} %get-tuple-element.54), channel_id=1, source_target_pairs={{0,80},{8,88},{16,96},{24,104},{32,112},{40,120},{48,0},{56,8},{64... | collective-permute-start | bytes 393224 | tf_op jit(solution)/shard_map/ppermute | solution.py:100
  149.9 2.7 %collective-permute-start.36 = (bf16[128,512]{1,0:T(8,128)(2,1)S(1)}, bf16[128,512]{1,0:T(8,128)(2,1)S(1)}, u32[]{:S(2)}, u32[]{:S(2)}) collective-permute-start(bf16[128,512]{1,0:T(8,128)(2,1)S(1)} %get-tuple-element.56), channel_id=1, source_target_pairs={{0,112},{8,120},{16,0},{24,8},{32,16},{40,24},{48,32},{56,40},{64,... | collective-permute-start | bytes 393224 | tf_op jit(solution)/shard_map/ppermute | solution.py:100
  152.5 0.6 collective-permute-done.33.a
  153.2 7.0 %collective-permute-done.34.b = bf16[128,512]{1,0:T(8,128)(2,1)S(1)} collective-permute-done((bf16[128,512]{1,0:T(8,128)(2,1)S(1)}, bf16[128,512]{1,0:T(8,128)(2,1)S(1)}, u32[]{:S(2)}, u32[]{:S(2)}) %collective-permute-start.34) | collective-permute-done | bytes 131104 | tf_op jit(solution)/shard_map/ppermute | solution.py:100
  160.2 1.3 finish.1
  (54 shorter events, 1.4 us)
Async XLA Ops:
  4.2 21.2 %collective-permute-start.1 = (bf16[144,512]{1,0:T(8,128)(2,1)S(1)}, bf16[144,512]{1,0:T(8,128)(2,1)S(1)}, u32[]{:S(2)}, u32[]{:S(2)}) collective-permute-start(bf16[144,512]{1,0:T(8,128)(2,1)S(1)} %pad_maximum_fusion.4.refs_0_), channel_id=1, source_target_pairs={{0,112},{8,120},{16,0},{24,8},{32,16},{40,24},{48,32},{56,40},{64,... | collective-permute-start | bytes 442376 | tf_op jit(solution)/shard_map/ppermute | solution.py:100
  16.8 8.7 %collective-permute-start = (bf16[144,512]{1,0:T(8,128)(2,1)S(1)}, bf16[144,512]{1,0:T(8,128)(2,1)S(1)}, u32[]{:S(2)}, u32[]{:S(2)}) collective-permute-start(bf16[144,512]{1,0:T(8,128)(2,1)S(1)} %pad_maximum_fusion.4.refs_0_), channel_id=1, source_target_pairs={{0,16},{8,24},{16,32},{24,40},{32,48},{40,56},{48,64},{56,72},{64,... | collective-permute-start | bytes 442376 | tf_op jit(solution)/shard_map/ppermute | solution.py:100
  16.8 11.2 %collective-permute-start.3 = (bf16[144,512]{1,0:T(8,128)(2,1)S(1)}, bf16[144,512]{1,0:T(8,128)(2,1)S(1)}, u32[]{:S(2)}, u32[]{:S(2)}) collective-permute-start(bf16[144,512]{1,0:T(8,128)(2,1)S(1)} %pad_maximum_fusion.4.refs_0_), channel_id=1, source_target_pairs={{0,80},{8,88},{16,96},{24,104},{32,112},{40,120},{48,0},{56,8},{64... | collective-permute-start | bytes 442376 | tf_op jit(solution)/shard_map/ppermute | solution.py:100
  17.7 10.3 %collective-permute-start.2 = (bf16[144,512]{1,0:T(8,128)(2,1)S(1)}, bf16[144,512]{1,0:T(8,128)(2,1)S(1)}, u32[]{:S(2)}, u32[]{:S(2)}) collective-permute-start(bf16[144,512]{1,0:T(8,128)(2,1)S(1)} %pad_maximum_fusion.4.refs_0_), channel_id=1, source_target_pairs={{0,48},{8,56},{16,64},{24,72},{32,80},{40,88},{48,96},{56,104},{64... | collective-permute-start | bytes 442376 | tf_op jit(solution)/shard_map/ppermute | solution.py:100
  20.0 0.8 copy-start
  20.8 0.7 copy-start.1
  28.0 13.8 %collective-permute-start.5 = (bf16[216,512]{1,0:T(8,128)(2,1)S(1)}, bf16[216,512]{1,0:T(8,128)(2,1)S(1)}, u32[]{:S(2)}, u32[]{:S(2)}) collective-permute-start(bf16[216,512]{1,0:T(8,128)(2,1)S(1)} %pad_maximum_fusion.2), channel_id=1, source_target_pairs={{0,112},{8,120},{16,0},{24,8},{32,16},{40,24},{48,32},{56,40},{64,... | collective-permute-start | bytes 663560 | tf_op jit(solution)/shard_map/ppermute | solution.py:100
  29.6 12.3 %collective-permute-start.4 = (bf16[216,512]{1,0:T(8,128)(2,1)S(1)}, bf16[216,512]{1,0:T(8,128)(2,1)S(1)}, u32[]{:S(2)}, u32[]{:S(2)}) collective-permute-start(bf16[216,512]{1,0:T(8,128)(2,1)S(1)} %pad_maximum_fusion.1), channel_id=1, source_target_pairs={{0,16},{8,24},{16,32},{24,40},{32,48},{40,56},{48,64},{56,72},{64,... | collective-permute-start | bytes 663560 | tf_op jit(solution)/shard_map/ppermute | solution.py:100
  29.6 20.0 %collective-permute-start.6 = (bf16[720,512]{1,0:T(8,128)(2,1)S(1)}, bf16[720,512]{1,0:T(8,128)(2,1)S(1)}, u32[]{:S(2)}, u32[]{:S(2)}) collective-permute-start(bf16[720,512]{1,0:T(8,128)(2,1)S(1)} %constant_dynamic-update-slice_fusion), channel_id=1, source_target_pairs={{0,8},{8,0},{16,24},{24,16},{32,40},{40,32},{48,56},{56,48},{64,72... | collective-permute-start | bytes 2211848 | tf_op jit(solution)/shard_map/ppermute | solution.py:104
  41.9 7.8 %collective-permute-start.7 = (bf16[432,512]{1,0:T(8,128)(2,1)S(1)}, bf16[432,512]{1,0:T(8,128)(2,1)S(1)}, u32[]{:S(2)}, u32[]{:S(2)}) collective-permute-start(bf16[432,512]{1,0:T(8,128)(2,1)S(1)} %pad_maximum_fusion), channel_id=1, source_target_pairs={{0,8},{8,0},{16,24},{24,16},{32,40},{40,32},{48,56},{56,48},{64,72... | collective-permute-start | bytes 1327112 | tf_op jit(solution)/shard_map/ppermute | solution.py:104
  57.5 11.8 %collective-permute-start.15 = (bf16[2,32,1536]{2,1,0:T(8,128)(2,1)S(1)}, bf16[2,32,1536]{2,1,0:T(8,128)(2,1)S(1)}, u32[]{:S(2)}, u32[]{:S(2)}) collective-permute-start(bf16[2,32,1536]{2,1,0:T(8,128)(2,1)S(1)} %get-tuple-element.68), channel_id=1, source_target_pairs={{0,1},{1,2},{2,3},{3,4},{4,5},{5,6},{6,7},{7,0},{8,9},{9,10},{10,1... | collective-permute-start | bytes 589832 | tf_op jit(solution)/shard_map/ppermute | solution.py:100
  57.6 6.3 %collective-permute-start.18 = (bf16[2,32,1536]{2,1,0:T(8,128)(2,1)S(1)}, bf16[2,32,1536]{2,1,0:T(8,128)(2,1)S(1)}, u32[]{:S(2)}, u32[]{:S(2)}) collective-permute-start(bf16[2,32,1536]{2,1,0:T(8,128)(2,1)S(1)} %get-tuple-element.69), channel_id=1, source_target_pairs={{0,7},{1,0},{2,1},{3,2},{4,3},{5,4},{6,5},{7,6},{8,15},{9,8},{10,9... | collective-permute-start | bytes 589832 | tf_op jit(solution)/shard_map/ppermute | solution.py:100
  60.3 8.8 %collective-permute-start.8 = (bf16[2,32,1536]{2,1,0:T(8,128)(2,1)S(1)}, bf16[2,32,1536]{2,1,0:T(8,128)(2,1)S(1)}, u32[]{:S(2)}, u32[]{:S(2)}) collective-permute-start(bf16[2,32,1536]{2,1,0:T(8,128)(2,1)S(1)} %get-tuple-element.62), channel_id=1, source_target_pairs={{0,1},{1,2},{2,3},{3,4},{4,5},{5,6},{6,7},{7,0},{8,9},{9,10},{10,1... | collective-permute-start | bytes 589832 | tf_op jit(solution)/shard_map/ppermute | solution.py:100
  60.6 14.7 %collective-permute-start.12 = (bf16[2,32,1536]{2,1,0:T(8,128)(2,1)S(1)}, bf16[2,32,1536]{2,1,0:T(8,128)(2,1)S(1)}, u32[]{:S(2)}, u32[]{:S(2)}) collective-permute-start(bf16[2,32,1536]{2,1,0:T(8,128)(2,1)S(1)} %get-tuple-element.63), channel_id=1, source_target_pairs={{0,7},{1,0},{2,1},{3,2},{4,3},{5,4},{6,5},{7,6},{8,15},{9,8},{10,9... | collective-permute-start | bytes 589832 | tf_op jit(solution)/shard_map/ppermute | solution.py:100
  63.9 8.2 %collective-permute-start.19 = (bf16[2,32,1536]{2,1,0:T(8,128)(2,1)S(1)}, bf16[2,32,1536]{2,1,0:T(8,128)(2,1)S(1)}, u32[]{:S(2)}, u32[]{:S(2)}) collective-permute-start(bf16[2,32,1536]{2,1,0:T(8,128)(2,1)S(1)} %fusion.2), channel_id=1, source_target_pairs={{0,7},{1,0},{2,1},{3,2},{4,3},{5,4},{6,5},{7,6},{8,15},{9,8},{10,9... | collective-permute-start | bytes 589832 | tf_op jit(solution)/shard_map/ppermute | solution.py:100
  69.2 6.5 %collective-permute-start.9 = (bf16[2,32,1536]{2,1,0:T(8,128)(2,1)S(1)}, bf16[2,32,1536]{2,1,0:T(8,128)(2,1)S(1)}, u32[]{:S(2)}, u32[]{:S(2)}) collective-permute-start(bf16[2,32,1536]{2,1,0:T(8,128)(2,1)S(1)} %fusion.10), channel_id=1, source_target_pairs={{0,1},{1,2},{2,3},{3,4},{4,5},{5,6},{6,7},{7,0},{8,9},{9,10},{10,1... | collective-permute-start | bytes 589832 | tf_op jit(solution)/shard_map/ppermute | solution.py:100
  72.2 7.9 %collective-permute-start.16 = (bf16[2,32,1536]{2,1,0:T(8,128)(2,1)S(1)}, bf16[2,32,1536]{2,1,0:T(8,128)(2,1)S(1)}, u32[]{:S(2)}, u32[]{:S(2)}) collective-permute-start(bf16[2,32,1536]{2,1,0:T(8,128)(2,1)S(1)} %get-tuple-element.66), channel_id=1, source_target_pairs={{0,1},{1,2},{2,3},{3,4},{4,5},{5,6},{6,7},{7,0},{8,9},{9,10},{10,1... | collective-permute-start | bytes 589832 | tf_op jit(solution)/shard_map/ppermute | solution.py:100
  72.4 7.8 %collective-permute-start.20 = (bf16[2,32,1536]{2,1,0:T(8,128)(2,1)S(1)}, bf16[2,32,1536]{2,1,0:T(8,128)(2,1)S(1)}, u32[]{:S(2)}, u32[]{:S(2)}) collective-permute-start(bf16[2,32,1536]{2,1,0:T(8,128)(2,1)S(1)} %get-tuple-element.67), channel_id=1, source_target_pairs={{0,7},{1,0},{2,1},{3,2},{4,3},{5,4},{6,5},{7,6},{8,15},{9,8},{10,9... | collective-permute-start | bytes 589832 | tf_op jit(solution)/shard_map/ppermute | solution.py:100
  75.8 8.3 %collective-permute-start.10 = (bf16[2,32,1536]{2,1,0:T(8,128)(2,1)S(1)}, bf16[2,32,1536]{2,1,0:T(8,128)(2,1)S(1)}, u32[]{:S(2)}, u32[]{:S(2)}) collective-permute-start(bf16[2,32,1536]{2,1,0:T(8,128)(2,1)S(1)} %get-tuple-element.60), channel_id=1, source_target_pairs={{0,1},{1,2},{2,3},{3,4},{4,5},{5,6},{6,7},{7,0},{8,9},{9,10},{10,1... | collective-permute-start | bytes 589832 | tf_op jit(solution)/shard_map/ppermute | solution.py:100
  75.9 8.2 %collective-permute-start.13 = (bf16[2,32,1536]{2,1,0:T(8,128)(2,1)S(1)}, bf16[2,32,1536]{2,1,0:T(8,128)(2,1)S(1)}, u32[]{:S(2)}, u32[]{:S(2)}) collective-permute-start(bf16[2,32,1536]{2,1,0:T(8,128)(2,1)S(1)} %get-tuple-element.61), channel_id=1, source_target_pairs={{0,7},{1,0},{2,1},{3,2},{4,3},{5,4},{6,5},{7,6},{8,15},{9,8},{10,9... | collective-permute-start | bytes 589832 | tf_op jit(solution)/shard_map/ppermute | solution.py:100
  80.2 7.4 %collective-permute-start.17 = (bf16[2,32,1536]{2,1,0:T(8,128)(2,1)S(1)}, bf16[2,32,1536]{2,1,0:T(8,128)(2,1)S(1)}, u32[]{:S(2)}, u32[]{:S(2)}) collective-permute-start(bf16[2,32,1536]{2,1,0:T(8,128)(2,1)S(1)} %get-tuple-element.64), channel_id=1, source_target_pairs={{0,1},{1,2},{2,3},{3,4},{4,5},{5,6},{6,7},{7,0},{8,9},{9,10},{10,1... | collective-permute-start | bytes 589832 | tf_op jit(solution)/shard_map/ppermute | solution.py:100
  80.4 7.3 %collective-permute-start.21 = (bf16[2,32,1536]{2,1,0:T(8,128)(2,1)S(1)}, bf16[2,32,1536]{2,1,0:T(8,128)(2,1)S(1)}, u32[]{:S(2)}, u32[]{:S(2)}) collective-permute-start(bf16[2,32,1536]{2,1,0:T(8,128)(2,1)S(1)} %get-tuple-element.65), channel_id=1, source_target_pairs={{0,7},{1,0},{2,1},{3,2},{4,3},{5,4},{6,5},{7,6},{8,15},{9,8},{10,9... | collective-permute-start | bytes 589832 | tf_op jit(solution)/shard_map/ppermute | solution.py:100
  84.2 7.9 %collective-permute-start.11 = (bf16[2,32,1536]{2,1,0:T(8,128)(2,1)S(1)}, bf16[2,32,1536]{2,1,0:T(8,128)(2,1)S(1)}, u32[]{:S(2)}, u32[]{:S(2)}) collective-permute-start(bf16[2,32,1536]{2,1,0:T(8,128)(2,1)S(1)} %get-tuple-element.58), channel_id=1, source_target_pairs={{0,1},{1,2},{2,3},{3,4},{4,5},{5,6},{6,7},{7,0},{8,9},{9,10},{10,1... | collective-permute-start | bytes 589832 | tf_op jit(solution)/shard_map/ppermute | solution.py:100
  84.4 7.8 %collective-permute-start.14 = (bf16[2,32,1536]{2,1,0:T(8,128)(2,1)S(1)}, bf16[2,32,1536]{2,1,0:T(8,128)(2,1)S(1)}, u32[]{:S(2)}, u32[]{:S(2)}) collective-permute-start(bf16[2,32,1536]{2,1,0:T(8,128)(2,1)S(1)} %get-tuple-element.59), channel_id=1, source_target_pairs={{0,7},{1,0},{2,1},{3,2},{4,3},{5,4},{6,5},{7,6},{8,15},{9,8},{10,9... | collective-permute-start | bytes 589832 | tf_op jit(solution)/shard_map/ppermute | solution.py:100
  92.3 5.6 %collective-permute-start.23 = (bf16[4,32,768]{2,1,0:T(8,128)(2,1)S(1)}, bf16[4,32,768]{2,1,0:T(8,128)(2,1)S(1)}, u32[]{:S(2)}, u32[]{:S(2)}) collective-permute-start(bf16[4,32,768]{2,1,0:T(8,128)(2,1)S(1)} %pad_maximum_fusion.3.refs_0_), channel_id=1, source_target_pairs={{0,7},{1,0},{2,1},{3,2},{4,3},{5,4},{6,5},{7,6},{8,15},{9,8},{10,9... | collective-permute-start | bytes 589832 | tf_op jit(solution)/shard_map/ppermute | solution.py:100
  95.3 5.7 %collective-permute-start.22 = (bf16[4,32,768]{2,1,0:T(8,128)(2,1)S(1)}, bf16[4,32,768]{2,1,0:T(8,128)(2,1)S(1)}, u32[]{:S(2)}, u32[]{:S(2)}) collective-permute-start(bf16[4,32,768]{2,1,0:T(8,128)(2,1)S(1)} %pad_maximum_fusion.3.refs_0_), channel_id=1, source_target_pairs={{0,1},{1,2},{2,3},{3,4},{4,5},{5,6},{6,7},{7,0},{8,9},{9,10},{10,1... | collective-permute-start | bytes 589832 | tf_op jit(solution)/shard_map/ppermute | solution.py:100
  97.9 5.7 %collective-permute-start.25 = (bf16[4,32,768]{2,1,0:T(8,128)(2,1)S(1)}, bf16[4,32,768]{2,1,0:T(8,128)(2,1)S(1)}, u32[]{:S(2)}, u32[]{:S(2)}) collective-permute-start(bf16[4,32,768]{2,1,0:T(8,128)(2,1)S(1)} %collective-permute-done.23.refs_2_), channel_id=1, source_target_pairs={{0,7},{1,0},{2,1},{3,2},{4,3},{5,4},{6,5},{7,6},{8,15},{9,8},{10,9... | collective-permute-start | bytes 589832 | tf_op jit(solution)/shard_map/ppermute | solution.py:100
  101.0 5.7 %collective-permute-start.24 = (bf16[4,32,768]{2,1,0:T(8,128)(2,1)S(1)}, bf16[4,32,768]{2,1,0:T(8,128)(2,1)S(1)}, u32[]{:S(2)}, u32[]{:S(2)}) collective-permute-start(bf16[4,32,768]{2,1,0:T(8,128)(2,1)S(1)} %collective-permute-done.22.refs_1_), channel_id=1, source_target_pairs={{0,1},{1,2},{2,3},{3,4},{4,5},{5,6},{6,7},{7,0},{8,9},{9,10},{10,1... | collective-permute-start | bytes 589832 | tf_op jit(solution)/shard_map/ppermute | solution.py:100
  103.7 6.5 %collective-permute-start.27 = (bf16[4,32,768]{2,1,0:T(8,128)(2,1)S(1)}, bf16[4,32,768]{2,1,0:T(8,128)(2,1)S(1)}, u32[]{:S(2)}, u32[]{:S(2)}) collective-permute-start(bf16[4,32,768]{2,1,0:T(8,128)(2,1)S(1)} %collective-permute-done.25.refs_4_), channel_id=1, source_target_pairs={{0,7},{1,0},{2,1},{3,2},{4,3},{5,4},{6,5},{7,6},{8,15},{9,8},{10,9... | collective-permute-start | bytes 589832 | tf_op jit(solution)/shard_map/ppermute | solution.py:100
  106.8 6.8 %collective-permute-start.26 = (bf16[4,32,768]{2,1,0:T(8,128)(2,1)S(1)}, bf16[4,32,768]{2,1,0:T(8,128)(2,1)S(1)}, u32[]{:S(2)}, u32[]{:S(2)}) collective-permute-start(bf16[4,32,768]{2,1,0:T(8,128)(2,1)S(1)} %collective-permute-done.24.refs_3_), channel_id=1, source_target_pairs={{0,1},{1,2},{2,3},{3,4},{4,5},{5,6},{6,7},{7,0},{8,9},{9,10},{10,1... | collective-permute-start | bytes 589832 | tf_op jit(solution)/shard_map/ppermute | solution.py:100
  110.2 5.8 %collective-permute-start.29 = (bf16[2,32,768]{2,1,0:T(8,128)(2,1)S(1)}, bf16[2,32,768]{2,1,0:T(8,128)(2,1)S(1)}, u32[]{:S(2)}, u32[]{:S(2)}) collective-permute-start(bf16[2,32,768]{2,1,0:T(8,128)(2,1)S(1)} %slice.39), channel_id=1, source_target_pairs={{0,7},{1,0},{2,1},{3,2},{4,3},{5,4},{6,5},{7,6},{8,15},{9,8},{10,9... | collective-permute-start | bytes 294920 | tf_op jit(solution)/shard_map/ppermute | solution.py:100
  113.6 6.1 %collective-permute-start.28 = (bf16[2,32,768]{2,1,0:T(8,128)(2,1)S(1)}, bf16[2,32,768]{2,1,0:T(8,128)(2,1)S(1)}, u32[]{:S(2)}, u32[]{:S(2)}) collective-permute-start(bf16[2,32,768]{2,1,0:T(8,128)(2,1)S(1)} %slice.38), channel_id=1, source_target_pairs={{0,1},{1,2},{2,3},{3,4},{4,5},{5,6},{6,7},{7,0},{8,9},{9,10},{10,1... | collective-permute-start | bytes 294920 | tf_op jit(solution)/shard_map/ppermute | solution.py:100
  125.6 10.2 %collective-permute-start.30 = (bf16[8,128,512]{2,1,0:T(8,128)(2,1)S(1)}, bf16[8,128,512]{2,1,0:T(8,128)(2,1)S(1)}, u32[]{:S(2)}, u32[]{:S(2)}) collective-permute-start(bf16[8,128,512]{2,1,0:T(8,128)(2,1)S(1)} %get-tuple-element.49), channel_id=1, source_target_pairs={{0,8},{8,0},{16,24},{24,16},{32,40},{40,32},{48,56},{56,48},{64,72... | collective-permute-start | bytes 3145736 | tf_op jit(solution)/shard_map/ppermute | solution.py:104
  136.9 7.8 %collective-permute-start.31 = (bf16[192,512]{1,0:T(8,128)(2,1)S(1)}, bf16[192,512]{1,0:T(8,128)(2,1)S(1)}, u32[]{:S(2)}, u32[]{:S(2)}) collective-permute-start(bf16[192,512]{1,0:T(8,128)(2,1)S(1)} %get-tuple-element.51), channel_id=1, source_target_pairs={{0,16},{8,24},{16,32},{24,40},{32,48},{40,56},{48,64},{56,72},{64,... | collective-permute-start | bytes 589832 | tf_op jit(solution)/shard_map/ppermute | solution.py:100
  137.0 7.6 %collective-permute-start.32 = (bf16[192,512]{1,0:T(8,128)(2,1)S(1)}, bf16[192,512]{1,0:T(8,128)(2,1)S(1)}, u32[]{:S(2)}, u32[]{:S(2)}) collective-permute-start(bf16[192,512]{1,0:T(8,128)(2,1)S(1)} %get-tuple-element.52), channel_id=1, source_target_pairs={{0,112},{8,120},{16,0},{24,8},{32,16},{40,24},{48,32},{56,40},{64,... | collective-permute-start | bytes 589832 | tf_op jit(solution)/shard_map/ppermute | solution.py:100
  145.3 7.9 %collective-permute-start.33 = (bf16[128,512]{1,0:T(8,128)(2,1)S(1)}, bf16[128,512]{1,0:T(8,128)(2,1)S(1)}, u32[]{:S(2)}, u32[]{:S(2)}) collective-permute-start(bf16[128,512]{1,0:T(8,128)(2,1)S(1)} %get-tuple-element.53), channel_id=1, source_target_pairs={{0,48},{8,56},{16,64},{24,72},{32,80},{40,88},{48,96},{56,104},{64... | collective-permute-start | bytes 393224 | tf_op jit(solution)/shard_map/ppermute | solution.py:100
  148.2 12.0 %collective-permute-start.34 = (bf16[128,512]{1,0:T(8,128)(2,1)S(1)}, bf16[128,512]{1,0:T(8,128)(2,1)S(1)}, u32[]{:S(2)}, u32[]{:S(2)}) collective-permute-start(bf16[128,512]{1,0:T(8,128)(2,1)S(1)} %get-tuple-element.54), channel_id=1, source_target_pairs={{0,80},{8,88},{16,96},{24,104},{32,112},{40,120},{48,0},{56,8},{64... | collective-permute-start | bytes 393224 | tf_op jit(solution)/shard_map/ppermute | solution.py:100
  149.9 10.3 %collective-permute-start.35 = (bf16[128,512]{1,0:T(8,128)(2,1)S(1)}, bf16[128,512]{1,0:T(8,128)(2,1)S(1)}, u32[]{:S(2)}, u32[]{:S(2)}) collective-permute-start(bf16[128,512]{1,0:T(8,128)(2,1)S(1)} %get-tuple-element.55), channel_id=1, source_target_pairs={{0,16},{8,24},{16,32},{24,40},{32,48},{40,56},{48,64},{56,72},{64,... | collective-permute-start | bytes 393224 | tf_op jit(solution)/shard_map/ppermute | solution.py:100
  149.9 10.3 %collective-permute-start.36 = (bf16[128,512]{1,0:T(8,128)(2,1)S(1)}, bf16[128,512]{1,0:T(8,128)(2,1)S(1)}, u32[]{:S(2)}, u32[]{:S(2)}) collective-permute-start(bf16[128,512]{1,0:T(8,128)(2,1)S(1)} %get-tuple-element.56), channel_id=1, source_target_pairs={{0,112},{8,120},{16,0},{24,8},{32,16},{40,24},{48,32},{56,40},{64,... | collective-permute-start | bytes 393224 | tf_op jit(solution)/shard_map/ppermute | solution.py:100
where the time goes:
time: 162 us; the launch traced here: 161 us
  starting transfers between devices  87 us (54%)
  waiting for transfers between devices  44.3 us (27%)
  Pallas kernels  22.6 us (14%)
  local copies, waits for them, and re-layouts  3.38 us (2%)
  other arithmetic  3.1 us (2%)
    ppermute x34, starting transfers between devices, shift(): lax.ppermute(value, axis, [(i, (i + step) % count) for i in range(count)])  60.9 us
    ppermute x34, waiting for transfers between devices, shift(): lax.ppermute(value, axis, [(i, (i + step) % count) for i in range(count)])  42.9 us
    ppermute x3, starting transfers between devices, swap_cores(): lax.ppermute(value, 'attn', [(i, i ^ 1) for i in range(lax.axis_size('att...  26.1 us
    pallas_call x1, Pallas kernels, step(): pl.pallas_call(functools.partial(down_kernel, where), out_shape=(jax.Shap...  5.84 us
    pallas_call x1, Pallas kernels, step(): pl.pallas_call(functools.partial(pack_kernel, plan, half, local), out_sha...  3.88 us
    pallas_call x1, Pallas kernels, step(): pl.pallas_call(functools.partial(pack_more_kernel, cut), out_shape=part_s...  3.85 us
    pallas_call x1, Pallas kernels, grouped_attention(): pl.pallas_call(attention_kernel, grid=(count,), out_shape=jax.ShapeDtypeS...  3.36 us
  transfers between devices with their start and end apart: 37, of which 19 were waited for; matrix products, arithmetic and copies ran while one was open for 1% of the time, Pallas kernels for 4%

commit v1 on v0

v1 whole, which is shorter than its diff:
```python
import functools

import jax
import jax.numpy as jnp
from jax import lax
from jax.experimental import pallas as pl
from jax.experimental.pallas import tpu as pltpu
from jax.sharding import PartitionSpec as P


F32 = jnp.float32
BF16 = jnp.bfloat16
META = 8
VMEM_SPEC = pl.BlockSpec(memory_space=pltpu.VMEM)
SMEM_SPEC = pl.BlockSpec(memory_space=pltpu.SMEM)
HBM_SPEC = pl.BlockSpec(memory_space=pltpu.HBM)
SMALL = {"compiler_params": pltpu.CompilerParams(vmem_limit_bytes=2 << 20)}


def both_cores(home, swapped, at):
    return home[at].astype(F32) + swapped[at].astype(F32)


def first_kernel(info, home, swapped, right, left):
    count, rows, _ = home.shape
    mid = rows // 2
    right[0:rows, :] = both_cores(home, swapped, info[2]).astype(BF16)
    left[0:rows, :] = both_cores(home, swapped, info[count - 2]).astype(BF16)
    across = both_cores(home, swapped, info[count // 2]).astype(BF16)
    right[rows:, :] = across[0:mid]
    left[rows:, :] = across[mid:]


def rest_kernel(info, home, swapped, total):
    count = home.shape[0]
    for i, k in enumerate((0, 1, count - 1, 3, count - 3)):
        total[i] = both_cores(home, swapped, info[k]).astype(BF16)


def relay_kernel(total, right, left, far_right, far_left, near_right, near_left):
    _, rows, _ = total.shape
    mid = rows // 2
    far_right[0:mid, :] = (total[3, 0:mid].astype(F32) + right[rows:, :].astype(F32)).astype(BF16)
    far_right[mid:, :] = total[3, mid:]
    far_left[0:mid, :] = total[4, 0:mid]
    far_left[mid:, :] = (total[4, mid:].astype(F32) + left[rows:, :].astype(F32)).astype(BF16)
    near_right[...] = (total[1].astype(F32) + right[0:rows, :].astype(F32)).astype(BF16)
    near_left[...] = (total[2].astype(F32) + left[0:rows, :].astype(F32)).astype(BF16)


def finish_kernel(total, a, b, c, d, out):
    out[...] = (
        total[0].astype(F32)
        + (a[...].astype(F32) + b[...].astype(F32))
        + (c[...].astype(F32) + d[...].astype(F32))
    ).astype(BF16)


def in_hbm(value):
    return pltpu.with_memory_space_constraint(value, pltpu.HBM)


def in_vmem(value):
    return pltpu.with_memory_space_constraint(value, pltpu.VMEM)


def attention_kernel(lengths, query, cache_k, cache_v, out):
    heads, size = query.shape[1:]
    spots, groups, _ = cache_k.shape[1:]
    columns = spots * groups
    keys = cache_k[0].reshape(columns, size)
    values = cache_v[0].reshape(columns, size)
    scores = lax.dot_general(
        query[0], keys, (((1,), (1,)), ((), ())), preferred_element_type=F32
    ) * size ** (-0.5)
    place = lax.broadcasted_iota(jnp.int32, (heads, columns), 1)
    head = lax.broadcasted_iota(jnp.int32, (heads, columns), 0)
    live = (place % groups == head // (heads // groups)) & (
        place < lengths[pl.program_id(0)] * groups
    )
    masked = jnp.where(live, scores, -jnp.inf)
    weighted = jnp.exp(masked - jnp.max(masked, axis=1, keepdims=True))
    prob = (weighted / jnp.sum(weighted, axis=1, keepdims=True)).astype(BF16)
    out[0] = jnp.dot(prob, values, preferred_element_type=F32).astype(BF16)


def grouped_attention(query, cache_k, cache_v, lengths):
    count, heads, size = query.shape
    _, spots, groups, _ = cache_k.shape
    cache = pl.BlockSpec((1, spots, groups, size), lambda i: (i, 0, 0, 0))
    row = pl.BlockSpec((1, heads, size), lambda i: (i, 0, 0))
    out = pl.pallas_call(
        attention_kernel,
        grid=(count,),
        out_shape=jax.ShapeDtypeStruct((count, heads, size), BF16),
        in_specs=[SMEM_SPEC, row, cache, cache],
        out_specs=row,
        compiler_params=pltpu.CompilerParams(vmem_limit_bytes=12 << 20),
        cost_estimate=pl.CostEstimate(
            flops=10**9, bytes_accessed=3 * 10**6, transcendentals=4 * 10**5
        ),
        name="attention",
    )(lengths, query, in_hbm(cache_k), in_hbm(cache_v))
    return out.reshape(count, heads * size)


def shift(value, axis, step):
    count = lax.axis_size(axis)
    return lax.ppermute(value, axis, [(i, (i + step) % count) for i in range(count)])


def swap_cores(value):
    return lax.ppermute(value, "attn", [(i, i ^ 1) for i in range(lax.axis_size("attn"))])


def prepare_kernel(tokens, ids, gates, block, ids_v, gates_v, sems):
    rows = tokens.shape[0]
    copies = (
        pltpu.make_async_copy(tokens, block.at[0:rows], sems.at[0]),
        pltpu.make_async_copy(ids, ids_v, sems.at[1]),
        pltpu.make_async_copy(gates, gates_v, sems.at[2]),
    )
    for copy in copies:
        copy.start()
    block[rows:, 2 * rows :] = jnp.zeros((META, block.shape[1] - 2 * rows), BF16)
    for copy in copies[1:]:
        copy.wait()
    block[rows:, 0:rows] = ids_v[...].astype(F32).astype(BF16)
    block[rows:, rows : 2 * rows] = gates_v[...]
    copies[0].wait()


def bundle_kernel(*refs):
    out = refs[-1]
    height = refs[0].shape[0]
    for i, ref in enumerate(refs[:-1]):
        out[i * height : (i + 1) * height, :] = ref[...]


def expert_parts(j0, info, place, tok, wg_hbm, wu_hbm, wg, wu, sems, onehot, out, work):
    n_blocks = place.shape[0]
    rows = tok.shape[0] // n_blocks
    n_dest = len(out)
    here_count, dest_rows, ff2 = out[0].shape
    ff = ff2 // 2
    capacity = n_dest * dest_rows

    def fetch(j):
        return (
            pltpu.make_async_copy(wg_hbm.at[j0 + j], wg.at[j], sems.at[0, j]),
            pltpu.make_async_copy(wu_hbm.at[j0 + j], wu.at[j], sems.at[1, j]),
        )

    for j in range(here_count):
        for copy in fetch(j):
            copy.start()
    work()
    row_id = lax.broadcasted_iota(jnp.int32, (capacity, rows), 0) + info[1 + n_blocks]
    row_id = jnp.where(row_id < capacity, row_id, row_id - capacity).astype(F32)

    def expert(j, carry):
        for i in range(n_blocks):
            spot = place[info[1 + i], pl.ds(j0 + j, 1), :]
            onehot[:, i * rows : (i + 1) * rows] = jnp.where(row_id == spot, 1.0, 0.0).astype(BF16)
        packed = jnp.dot(onehot[...], tok[...], preferred_element_type=F32).astype(BF16)
        for copy in fetch(j):
            copy.wait()
        gate = jnp.dot(packed, wg[j], preferred_element_type=F32).astype(BF16)
        up = jnp.dot(packed, wu[j], preferred_element_type=F32).astype(BF16)
        for d in range(n_dest):
            out[d][j, :, 0:ff] = gate[d * dest_rows : (d + 1) * dest_rows]
            out[d][j, :, ff:] = up[d * dest_rows : (d + 1) * dest_rows]
        return carry

    lax.fori_loop(0, here_count, expert, 0)


def pack_kernel(plan, half, local, n_dest, info, *refs):
    n_ops = 1 + max(op for p in plan for op, _ in p)
    ops = refs[:n_ops]
    wg_hbm, wu_hbm = refs[n_ops : n_ops + 2]
    out = refs[n_ops + 2 : n_ops + 2 + n_dest]
    route, tok, meta, onehot, wg, wu, sems = refs[n_ops + 2 + n_dest :]
    n_blocks = len(plan)
    rows = tok.shape[0] // n_blocks
    capacity = n_dest * out[0].shape[1]

    def work():
        for i, p in enumerate(plan):
            at = pl.ds(pl.multiple_of(info[1 + i] * rows, rows), rows)
            op, r0 = p[0]
            if len(p) == 1:
                tok[i * rows : (i + 1) * rows, :] = ops[op][r0 : r0 + rows, :]
                low = r0 + rows
            else:
                tok[i * rows : i * rows + half, :] = ops[op][r0 : r0 + half, :]
                op, r0 = p[1]
                low = r0 + rows - half
                tok[i * rows + half : (i + 1) * rows, :] = ops[op][r0:low, :]
            meta[0:8, at] = ops[op][low : low + META, 0:rows].astype(F32)
            meta[8:16, at] = ops[op][low : low + META, rows : 2 * rows].astype(F32)
        ids = meta[0:8, :]
        gates = meta[8:16, :]
        hits = [ids == (info[0] + j).astype(F32) for j in range(local)]
        stack = jnp.concatenate(
            [jnp.where(h, 1.0, 0.0) for h in hits] + [jnp.where(h, gates, 0.0) for h in hits], axis=0
        ).astype(BF16)
        one = lax.broadcasted_iota(jnp.int32, (8, 64), 0)
        two = lax.broadcasted_iota(jnp.int32, (8, 64), 1)
        pick = jnp.where(one == two // 8, 1.0, 0.0).astype(BF16)
        both = jnp.dot(pick, stack, preferred_element_type=F32)
        member = jnp.concatenate(
            [both[:, b * rows : (b + 1) * rows] for b in range(n_blocks)], axis=0
        )
        size = n_blocks * 8
        r = lax.broadcasted_iota(jnp.int32, (rows, rows), 0)
        c = lax.broadcasted_iota(jnp.int32, (rows, rows), 1)
        upper = jnp.where(r < c, 1.0, 0.0).astype(BF16)
        rr = lax.broadcasted_iota(jnp.int32, (size, size), 0)
        cc = lax.broadcasted_iota(jnp.int32, (size, size), 1)
        earlier = jnp.where((rr % 8 == cc % 8) & (cc // 8 < rr // 8), 1.0, 0.0).astype(BF16)
        member_b = member.astype(BF16)
        before = jnp.dot(earlier, member_b, preferred_element_type=F32).astype(BF16)
        place = jnp.dot(member_b, upper, preferred_element_type=F32) + jnp.dot(
            before, jnp.ones((rows, rows), BF16), preferred_element_type=F32
        )
        place = jnp.where((member > 0.5) & (place < capacity), place, -1.0)
        row = lax.broadcasted_iota(jnp.int32, (size, rows), 0)
        route[...] = jnp.where(row % 8 < local, place, member).reshape(n_blocks, 8, rows)

    expert_parts(0, info, route, tok, wg_hbm, wu_hbm, wg, wu, sems, onehot, out, work)


def pack_more_kernel(j0, info, tok, route, wg_hbm, wu_hbm, *refs):
    *out, onehot, wg, wu, sems = refs
    expert_parts(
        j0, info, route, tok, wg_hbm, wu_hbm, wg, wu, sems, onehot, out, lambda: None
    )


def hidden_kernel(*refs):
    *terms, out = refs
    ways = 3
    row = 0
    for s in range(len(terms) // ways):
        a, b, c = (t[...].astype(F32) for t in terms[s * ways : (s + 1) * ways])
        total = a + (b + c)
        ff = total.shape[-1] // 2
        v = total[..., :ff]
        out[row : row + total.shape[0]] = (v / (1.0 + jnp.exp(-v)) * total[..., ff:]).astype(BF16)
        row += total.shape[0]


def mix_kernel(info, route, wd_hbm, away, home, wd, sem):
    copy = pltpu.make_async_copy(wd_hbm, wd, sem)
    copy.start()
    n_blocks, _, rows = route.shape
    local = wd.shape[0]
    capacity = away.shape[1] // local
    r = lax.broadcasted_iota(jnp.int32, (rows, rows), 0)
    c = lax.broadcasted_iota(jnp.int32, (rows, rows), 1)
    eye = jnp.where(r == c, 1.0, 0.0).astype(BF16)
    col_id = lax.broadcasted_iota(jnp.int32, (rows, capacity), 1).astype(F32)

    def block(d, carry):
        at = pl.ds(pl.multiple_of(d * rows, rows), rows)
        for side, ref in ((1 - info[0], away), (info[0], home)):
            rt = lax.dot_general(
                eye,
                route[2 * d + side].astype(BF16),
                (((1,), (1,)), ((), ())),
                preferred_element_type=F32,
            )
            for j in range(local):
                ref[at, j * capacity : (j + 1) * capacity] = jnp.where(
                    col_id == rt[:, j : j + 1], rt[:, local + j : local + j + 1], 0.0
                ).astype(BF16)
        return carry

    lax.fori_loop(0, n_blocks // 2, block, 0)
    copy.wait()


def mix_rows(mix, res, ref):
    n_dest, rows, feat = ref.shape
    group = 2

    def some(g, carry):
        at = pl.ds(pl.multiple_of(g * group * rows, group * rows), group * rows)
        got = jnp.dot(mix[at, :], res[...], preferred_element_type=F32).astype(BF16)
        ref[pl.ds(g * group, group)] = got.reshape(group, rows, feat)
        return carry

    lax.fori_loop(0, n_dest // group, some, 0)


def down_kernel(plan, info, *refs):
    n_ops = len(plan)
    ops = refs[:n_ops]
    wd, mix, away, res, hid = refs[n_ops:]
    local = wd.shape[0]
    capacity = hid.shape[1]
    for op, (j0, slot) in zip(ops, plan):
        at = pl.multiple_of(info[slot], op.shape[1])
        for j in range(op.shape[0]):
            hid[j0 + j, pl.ds(at, op.shape[1]), :] = op[j]

    def expert(j, carry):
        res[pl.ds(pl.multiple_of(j * capacity, capacity), capacity), :] = jnp.dot(
            hid[j], wd[j], preferred_element_type=F32
        ).astype(BF16)
        return carry

    lax.fori_loop(0, local, expert, 0)
    mix_rows(mix, res, away)


def home_kernel(mix, res, home):
    mix_rows(mix, res, home)


def scatter_sum(pieces, axis):
    count = len(pieces[0])
    half = count // 2
    legs = {}
    for way in (1, -1):
        for s in range(2):
            start = half if (way == 1) == (s == 0) else half - 1
            legs[(way, s)] = [start, pieces[s][way * start % count]]
    for hop in range(half, 0, -1):
        for way in (1, -1):
            for s in range(2):
                leg = legs[(way, s)]
                if leg[0] != hop:
                    continue
                got = shift(leg[1], axis, way)
                if hop > 1:
                    mine = pieces[s][way * (hop - 1) % count]
                    got = (got.astype(F32) + mine.astype(F32)).astype(BF16)
                legs[(way, s)] = [hop - 1, got]
    return [(pieces[s][0], legs[(1, s)][1], legs[(-1, s)][1]) for s in range(2)]


def step(tokens, expert_ids, gate_weight, w_gate, w_up, w_down, query, cache_k, cache_v, lengths):
    rows, feat = tokens.shape
    local, _, ff = w_gate.shape
    attn_count = lax.axis_size("attn")
    n_expert = lax.axis_size("expert")
    chips = attn_count // 2
    top = expert_ids.shape[1]
    capacity = rows * top // local
    me = lax.axis_index("attn")
    col = lax.axis_index("expert")
    y = me // 2
    core = me % 2
    far = chips // 2
    dest_rows = capacity // n_expert

    y_at = [lax.rem(y + k, chips) for k in range(chips)]
    x_at = [lax.rem(col + k, n_expert) for k in range(n_expert)]
    offsets = [0, -1, 1, -3, 3, -2, 2, far]
    pack_info = [local * me]
    for flip in (0, 1):
        pack_info += [2 * y_at[off % chips] + (core ^ flip) for off in offsets]
    row_at = [core] + [x * dest_rows for x in x_at]
    pack_info.append(col * dest_rows)
    pack_info = jnp.stack(pack_info).astype(jnp.int32)
    row_at = jnp.stack(row_at).astype(jnp.int32)
    core_at = core.reshape(1).astype(jnp.int32)
    y_info = jnp.stack(y_at).astype(jnp.int32)
    tokens, pack_info, row_at, core_at, y_info = lax.optimization_barrier(
        (tokens, pack_info, row_at, core_at, y_info)
    )

    height = rows + META
    half = rows // 2
    block = pl.pallas_call(
        prepare_kernel,
        out_shape=jax.ShapeDtypeStruct((height, feat), BF16),
        in_specs=[HBM_SPEC] * 3,
        out_specs=VMEM_SPEC,
        scratch_shapes=[
            pltpu.VMEM((top, rows), jnp.int32),
            pltpu.VMEM((top, rows), BF16),
            pltpu.SemaphoreType.DMA((3,)),
        ],
        name="prepare",
        **SMALL,
    )(in_hbm(tokens), in_hbm(expert_ids.T), in_hbm(gate_weight.T))
    attn_out = grouped_attention(query, cache_k, cache_v, lengths)

    away3 = [shift(block, "attn", 6), shift(block, "attn", -6)]
    near = [shift(block, "attn", 2), shift(block, "attn", -2)]
    *near, attn_out = lax.optimization_barrier((*near, attn_out))
    right = shift(jnp.concatenate([near[0], away3[0][:half]], axis=0), "attn", 2)
    left = shift(jnp.concatenate([near[1], away3[1][half:]], axis=0), "attn", -2)
    bundle = pl.pallas_call(
        bundle_kernel,
        out_shape=jax.ShapeDtypeStruct((5 * height, feat), BF16),
        in_specs=[VMEM_SPEC] * 5,
        out_specs=VMEM_SPEC,
        name="bundle",
        **SMALL,
    )(*map(in_vmem, (block, *near, *away3)))
    swap_first = swap_cores(bundle)
    swap_last = swap_cores(jnp.concatenate([right, left], axis=0))
    operands = [block, *near, *away3, right, left, swap_first, swap_last]
    plan = [((i, 0),) for i in range(7)] + [((5, height), (6, height))]
    plan += [((7, i * height),) for i in range(5)]
    second = height + half
    plan += [((8, 0),), ((8, second),), ((8, height), (8, second + height))]

    cut = local // 2
    pack_scratch = [
        pltpu.VMEM((capacity, attn_count * rows), BF16),
        pltpu.VMEM((cut, *w_gate.shape[1:]), BF16),
        pltpu.VMEM((cut, *w_up.shape[1:]), BF16),
        pltpu.SemaphoreType.DMA((2, cut)),
    ]
    part_shapes = (jax.ShapeDtypeStruct((cut, dest_rows, 2 * ff), BF16),) * n_expert
    pack_cost = pl.CostEstimate(flops=2 * 10**9, bytes_accessed=6 * 10**6, transcendentals=0)
    *parts_a, route, tok = pl.pallas_call(
        functools.partial(pack_kernel, plan, half, local, n_expert),
        out_shape=(
            *part_shapes,
            jax.ShapeDtypeStruct((attn_count, 8, rows), F32),
            jax.ShapeDtypeStruct((attn_count * rows, feat), BF16),
        ),
        in_specs=[SMEM_SPEC] + [VMEM_SPEC] * len(operands) + [HBM_SPEC] * 2,
        out_specs=(VMEM_SPEC,) * (n_expert + 2),
        scratch_shapes=[
            pltpu.VMEM((2 * META, attn_count * rows), F32),
            *pack_scratch,
        ],
        compiler_params=pltpu.CompilerParams(vmem_limit_bytes=7 << 20),
        cost_estimate=pack_cost,
        name="pack",
    )(pack_info, *map(in_vmem, operands), in_hbm(w_gate), in_hbm(w_up))
    parts_b = pl.pallas_call(
        functools.partial(pack_more_kernel, cut),
        out_shape=part_shapes,
        in_specs=[SMEM_SPEC, VMEM_SPEC, VMEM_SPEC, HBM_SPEC, HBM_SPEC],
        out_specs=(VMEM_SPEC,) * n_expert,
        scratch_shapes=pack_scratch,
        compiler_params=pltpu.CompilerParams(vmem_limit_bytes=7 << 20),
        cost_estimate=pack_cost,
        name="pack_more",
    )(pack_info, in_vmem(tok), in_vmem(route), in_hbm(w_gate), in_hbm(w_up))

    terms = sum(scatter_sum([parts_a, parts_b], "expert"), ())
    hidden = pl.pallas_call(
        hidden_kernel,
        out_shape=jax.ShapeDtypeStruct((local, dest_rows, ff), BF16),
        in_specs=[VMEM_SPEC] * len(terms),
        out_specs=VMEM_SPEC,
        name="hidden",
        **SMALL,
    )(*map(in_vmem, terms))

    r2, l2 = shift(hidden, "expert", 2), shift(hidden, "expert", -2)
    r1, l1 = shift(hidden, "expert", 1), shift(hidden, "expert", -1)
    r4, l4 = shift(r2[:cut], "expert", 2), shift(l2[cut:], "expert", -2)
    r3, l3 = shift(r2, "expert", 1), shift(l2, "expert", -1)
    pieces_in = [hidden, r1, l1, r2, l2, r3, l3, r4, l4]
    where = [(0, 1 + k % n_expert) for k in (0, -1, 1, -2, 2, -3, 3, -4)] + [(cut, 1 + 4)]

    mix_shape = jax.ShapeDtypeStruct((chips * rows, local * capacity), BF16)
    mix_away, mix_home, wd = pl.pallas_call(
        mix_kernel,
        out_shape=(mix_shape, mix_shape, jax.ShapeDtypeStruct(w_down.shape, BF16)),
        in_specs=[SMEM_SPEC, VMEM_SPEC, HBM_SPEC],
        out_specs=(VMEM_SPEC,) * 3,
        scratch_shapes=[pltpu.SemaphoreType.DMA],
        name="mix",
        **SMALL,
    )(core_at, in_vmem(route), in_hbm(w_down))
    away, res = pl.pallas_call(
        functools.partial(down_kernel, where),
        out_shape=(
            jax.ShapeDtypeStruct((chips, rows, feat), BF16),
            jax.ShapeDtypeStruct((local * capacity, feat), BF16),
        ),
        in_specs=[SMEM_SPEC] + [VMEM_SPEC] * (len(pieces_in) + 2),
        out_specs=(VMEM_SPEC, VMEM_SPEC),
        scratch_shapes=[pltpu.VMEM((local, capacity, ff), BF16)],
        compiler_params=pltpu.CompilerParams(vmem_limit_bytes=4 << 20),
        cost_estimate=pl.CostEstimate(flops=2 * 10**9, bytes_accessed=6 * 10**6, transcendentals=0),
        name="down",
    )(row_at, *map(in_vmem, pieces_in), in_vmem(wd), in_vmem(mix_away))
    swapped = swap_cores(away)
    home = pl.pallas_call(
        home_kernel,
        out_shape=jax.ShapeDtypeStruct((chips, rows, feat), BF16),
        in_specs=[VMEM_SPEC, VMEM_SPEC],
        out_specs=VMEM_SPEC,
        cost_estimate=pl.CostEstimate(flops=10**9, bytes_accessed=2 * 10**6, transcendentals=0),
        name="home",
        **SMALL,
    )(in_vmem(mix_home), in_vmem(res))

    block_shape = jax.ShapeDtypeStruct((rows, feat), BF16)
    long_shape = jax.ShapeDtypeStruct((rows + rows // 2, feat), BF16)
    right, left = pl.pallas_call(
        first_kernel,
        out_shape=(long_shape, long_shape),
        in_specs=[SMEM_SPEC, VMEM_SPEC, VMEM_SPEC],
        out_specs=(VMEM_SPEC,) * 2,
        name="first",
        **SMALL,
    )(y_info, in_vmem(home), in_vmem(swapped))
    right, left = shift(right, "attn", 2), shift(left, "attn", -2)
    total = pl.pallas_call(
        rest_kernel,
        out_shape=jax.ShapeDtypeStruct((5, rows, feat), BF16),
        in_specs=[SMEM_SPEC, VMEM_SPEC, VMEM_SPEC],
        out_specs=VMEM_SPEC,
        name="rest",
        **SMALL,
    )(y_info, in_vmem(home), in_vmem(swapped))
    far_right, far_left, near_right, near_left = pl.pallas_call(
        relay_kernel,
        out_shape=(block_shape,) * 4,
        in_specs=[VMEM_SPEC] * 3,
        out_specs=(VMEM_SPEC,) * 4,
        name="relay",
        **SMALL,
    )(in_vmem(total), in_vmem(right), in_vmem(left))
    last = [
        shift(far_right, "attn", 6),
        shift(far_left, "attn", -6),
        shift(near_right, "attn", 2),
        shift(near_left, "attn", -2),
    ]
    moe_out = pl.pallas_call(
        finish_kernel,
        out_shape=block_shape,
        in_specs=[VMEM_SPEC] * 5,
        out_specs=VMEM_SPEC,
        name="finish",
        **SMALL,
    )(in_vmem(total), *map(in_vmem, last))
    return (moe_out, attn_out)


def solution(mesh):
    return jax.shard_map(
        step,
        mesh=mesh,
        in_specs=(
            P(("groups", "attn"), "expert"),
            P(("groups", "attn"), None),
            P(("groups", "attn"), None),
            P("attn", "expert", None),
            P("attn", "expert", None),
            P("attn", None, "expert"),
            P(("groups", "attn", "expert"), None, None),
            P(("groups", "attn", "expert"), None, None, None),
            P(("groups", "attn", "expert"), None, None, None),
            P(("groups", "attn", "expert")),
        ),
        out_specs=(P(("groups", "attn"), "expert"), P(("groups", "attn", "expert"), None)),
        check_vma=False,
    )
```

time: 162 us -> 147 us (0.907)
  waiting for transfers between devices: 44.3 us -> 28.9 us
  other arithmetic: 3.1 us -> 0.55 us
    ppermute x34, waiting for transfers between devices: 42.9 us -> 27 us  [shift(): lax.ppermute(value, axis, [(i, (i + step) % count) for i in range(count)])]
    ppermute x34, starting transfers between devices: 60.9 us -> 66.1 us  [shift(): lax.ppermute(value, axis, [(i, (i + step) % count) for i in range(count)])]
    pallas_call x4 -> x9, Pallas kernels: 6.91 us -> 11 us  [the longest x1 3.97 us: step(): pl.pallas_call(functools.partial(pack_kernel, plan, half, local, n_expert...]
    ppermute x3, starting transfers between devices: 26.1 us -> 22.4 us  [swap_cores(): lax.ppermute(value, 'attn', [(i, i ^ 1) for i in range(lax.axis_size('att...]
    pallas_call x1, Pallas kernels: 5.84 us -> 3.88 us  [step(): pl.pallas_call(functools.partial(down_kernel, where), out_shape=(jax.Shap...]
  transfers between devices with their start and end apart: 37 -> 37, of which waited for: 19 -> 15; matrix products, arithmetic and copies ran while one was open for 1% -> 1% of each run, Pallas kernels for 4% -> 9%
where the time goes in v1:
time: 147 us; the launch traced here: 145 us
  starting transfers between devices  88.5 us (60%)
  waiting for transfers between devices  28.9 us (20%)
  Pallas kernels  23.9 us (16%)
  local copies, waits for them, and re-layouts  2.36 us (2%)
    ppermute x34, starting transfers between devices, shift(): lax.ppermute(value, axis, [(i, (i + step) % count) for i in range(count)])  66.1 us
    ppermute x34, waiting for transfers between devices, shift(): lax.ppermute(value, axis, [(i, (i + step) % count) for i in range(count)])  27 us
    ppermute x3, starting transfers between devices, swap_cores(): lax.ppermute(value, 'attn', [(i, i ^ 1) for i in range(lax.axis_size('att...  22.4 us
    pallas_call x1, Pallas kernels, step(): pl.pallas_call(functools.partial(pack_kernel, plan, half, local, n_expert...  3.97 us
    pallas_call x1, Pallas kernels, step(): pl.pallas_call(functools.partial(down_kernel, where), out_shape=(jax.Shap...  3.88 us
    pallas_call x1, Pallas kernels, step(): pl.pallas_call(functools.partial(pack_more_kernel, cut), out_shape=part_s...  3.86 us
    pallas_call x1, Pallas kernels, step(): pl.pallas_call(mix_kernel, out_shape=(mix_shape, mix_shape, jax.ShapeDtyp...  3.66 us
    pallas_call x1, Pallas kernels, grouped_attention(): pl.pallas_call(attention_kernel, grid=(count,), out_shape=jax.ShapeDtypeS...  3.36 us
  transfers between devices with their start and end apart: 37, of which 15 were waited for; matrix products, arithmetic and copies ran while one was open for 1% of the time, Pallas kernels for 9%

profile of v1, /device:TPU:513, one launch (start us, length us, event | category | flops | bytes accessed | tf_op | source)
XLA Modules:
  0.0 145.2 jit_solution(4659035958311015993)
XLA Ops:
  0.9 0.1 stack.132.info
  1.0 0.9 prepare.1.refs_0_
  2.0 12.5 %collective-permute-start.1 = (bf16[136,512]{1,0:T(8,128)(2,1)S(1)}, bf16[136,512]{1,0:T(8,128)(2,1)S(1)}, u32[]{:S(2)}, u32[]{:S(2)}) collective-permute-start(bf16[136,512]{1,0:T(8,128)(2,1)S(1)} %prepare.1.refs_0_), channel_id=1, source_target_pairs={{0,112},{8,120},{16,0},{24,8},{32,16},{40,24},{48,32},{56,40},{64,... | collective-permute-start | bytes 417800 | tf_op jit(solution)/shard_map/ppermute | solution.py:109
  14.5 0.9 collective-permute-start.3
  15.4 2.4 %collective-permute-start.2 = (bf16[136,512]{1,0:T(8,128)(2,1)S(1)}, bf16[136,512]{1,0:T(8,128)(2,1)S(1)}, u32[]{:S(2)}, u32[]{:S(2)}) collective-permute-start(bf16[136,512]{1,0:T(8,128)(2,1)S(1)} %prepare.1.refs_0_), channel_id=1, source_target_pairs={{0,48},{8,56},{16,64},{24,72},{32,80},{40,88},{48,96},{56,104},{64... | collective-permute-start | bytes 417800 | tf_op jit(solution)/shard_map/ppermute | solution.py:109
  17.8 0.8 copy-done
  18.5 0.7 copy-done.1
  19.2 3.4 %attention.1 = bf16[2,64,128]{2,1,0:T(8,128)(2,1)S(1)} custom-call(s32[2]{0:T(128)S(1)} %copy-done.1, bf16[2,64,128]{2,1,0:T(8,128)(2,1)S(1)} %copy-done, bf16[2,768,4,128]{3,2,1,0:T(4,128)(2,1)} %cache_k.1, bf16[2,768,4,128]{3,2,1,0:T(4,128)(2,1)} %cache_v.1), custom_call_target="tpu_custom_call" | custom-call | flops 1000000000 | bytes 3000000 | tf_op jit(solution)/shard_map/attention/pallas_call | solution.py:92
  22.5 0.6 copy.14
  23.2 4.0 %collective-permute-start.5 = (bf16[208,512]{1,0:T(8,128)(2,1)S(1)}, bf16[208,512]{1,0:T(8,128)(2,1)S(1)}, u32[]{:S(2)}, u32[]{:S(2)}) collective-permute-start(bf16[208,512]{1,0:T(8,128)(2,1)S(1)} %pad_maximum_fusion.1), channel_id=1, source_target_pairs={{0,112},{8,120},{16,0},{24,8},{32,16},{40,24},{48,32},{56,40},{64,... | collective-permute-start | bytes 638984 | tf_op jit(solution)/shard_map/ppermute | solution.py:109
  27.3 0.1 collective-permute-start.4
  27.5 10.0 %collective-permute-start.6 = (bf16[680,512]{1,0:T(8,128)(2,1)S(1)}, bf16[680,512]{1,0:T(8,128)(2,1)S(1)}, u32[]{:S(2)}, u32[]{:S(2)}) collective-permute-start(bf16[680,512]{1,0:T(8,128)(2,1)S(1)} %bundle.1), channel_id=1, source_target_pairs={{0,8},{8,0},{16,24},{24,16},{32,40},{40,32},{48,56},{56,48},{64,72... | collective-permute-start | bytes 2088968 | tf_op jit(solution)/shard_map/ppermute | solution.py:113
  37.5 6.9 %collective-permute-start.7 = (bf16[408,512]{1,0:T(8,128)(2,1)S(1)}, bf16[408,512]{1,0:T(8,128)(2,1)S(1)}, u32[]{:S(2)}, u32[]{:S(2)}) collective-permute-start(bf16[408,512]{1,0:T(8,128)(2,1)S(1)} %pad_maximum_fusion), channel_id=1, source_target_pairs={{0,8},{8,0},{16,24},{24,16},{32,40},{40,32},{48,56},{56,48},{64,72... | collective-permute-start | bytes 1253384 | tf_op jit(solution)/shard_map/ppermute | solution.py:113
  44.4 1.4 collective-permute-done.7.refs_8_
  45.8 4.0 %pack.1 = (bf16[2,32,1536]{2,1,0:T(8,128)(2,1)S(1)}, bf16[2,32,1536]{2,1,0:T(8,128)(2,1)S(1)}, bf16[2,32,1536]{2,1,0:T(8,128)(2,1)S(1)}, bf16[2,32,1536]{2,1,0:T...) custom-call(s32[18]{0:T(128)S(1)} %stack.132.info, ...), custom_call_target="tpu_custom_call" | custom-call | flops 2000000000 | bytes 6000000 | tf_op jit(solution)/shard_map/pack/pallas_call | solution.py:422
  49.8 0.1 collective-permute-start.8
  49.9 2.6 %collective-permute-start.12 = (bf16[2,32,1536]{2,1,0:T(8,128)(2,1)S(1)}, bf16[2,32,1536]{2,1,0:T(8,128)(2,1)S(1)}, u32[]{:S(2)}, u32[]{:S(2)}) collective-permute-start(bf16[2,32,1536]{2,1,0:T(8,128)(2,1)S(1)} %get-tuple-element.53), channel_id=1, source_target_pairs={{0,7},{1,0},{2,1},{3,2},{4,3},{5,4},{6,5},{7,6},{8,15},{9,8},{10,9... | collective-permute-start | bytes 589832 | tf_op jit(solution)/shard_map/ppermute | solution.py:109
  52.6 3.9 %pack_more.1 = (bf16[2,32,1536]{2,1,0:T(8,128)(2,1)S(1)}, bf16[2,32,1536]{2,1,0:T(8,128)(2,1)S(1)}, bf16[2,32,1536]{2,1,0:T(8,128)(2,1)S(1)}, bf16[2,32,1536]{2,...) custom-call(s32[18]{0:T(128)S(1)} %stack.132.info, ...), custom_call_target="tpu_custom_call" | custom-call | flops 2000000000 | bytes 6000000 | tf_op jit(solution)/shard_map/pack_more/pallas_call | solution.py:439
  56.4 0.3 collective-permute-start.15
  56.8 2.6 %collective-permute-start.18 = (bf16[2,32,1536]{2,1,0:T(8,128)(2,1)S(1)}, bf16[2,32,1536]{2,1,0:T(8,128)(2,1)S(1)}, u32[]{:S(2)}, u32[]{:S(2)}) collective-permute-start(bf16[2,32,1536]{2,1,0:T(8,128)(2,1)S(1)} %get-tuple-element.61), channel_id=1, source_target_pairs={{0,7},{1,0},{2,1},{3,2},{4,3},{5,4},{6,5},{7,6},{8,15},{9,8},{10,9... | collective-permute-start | bytes 589832 | tf_op jit(solution)/shard_map/ppermute | solution.py:109
  59.5 0.1 collective-permute-start.9
  59.7 2.8 %collective-permute-start.13 = (bf16[2,32,1536]{2,1,0:T(8,128)(2,1)S(1)}, bf16[2,32,1536]{2,1,0:T(8,128)(2,1)S(1)}, u32[]{:S(2)}, u32[]{:S(2)}) collective-permute-start(bf16[2,32,1536]{2,1,0:T(8,128)(2,1)S(1)} %add_convert_fusion.6), channel_id=1, source_target_pairs={{0,7},{1,0},{2,1},{3,2},{4,3},{5,4},{6,5},{7,6},{8,15},{9,8},{10,9... | collective-permute-start | bytes 589832 | tf_op jit(solution)/shard_map/ppermute | solution.py:109
  62.4 1.1 collective-permute-done.15
  63.5 0.1 collective-permute-start.16
  63.7 2.8 %collective-permute-start.19 = (bf16[2,32,1536]{2,1,0:T(8,128)(2,1)S(1)}, bf16[2,32,1536]{2,1,0:T(8,128)(2,1)S(1)}, u32[]{:S(2)}, u32[]{:S(2)}) collective-permute-start(bf16[2,32,1536]{2,1,0:T(8,128)(2,1)S(1)} %add_convert_fusion.2), channel_id=1, source_target_pairs={{0,7},{1,0},{2,1},{3,2},{4,3},{5,4},{6,5},{7,6},{8,15},{9,8},{10,9... | collective-permute-start | bytes 589832 | tf_op jit(solution)/shard_map/ppermute | solution.py:109
  66.5 1.2 collective-permute-done.9
  67.8 0.1 collective-permute-start.10
  68.0 2.8 %collective-permute-start.14 = (bf16[2,32,1536]{2,1,0:T(8,128)(2,1)S(1)}, bf16[2,32,1536]{2,1,0:T(8,128)(2,1)S(1)}, u32[]{:S(2)}, u32[]{:S(2)}) collective-permute-start(bf16[2,32,1536]{2,1,0:T(8,128)(2,1)S(1)} %add_convert_fusion.5), channel_id=1, source_target_pairs={{0,7},{1,0},{2,1},{3,2},{4,3},{5,4},{6,5},{7,6},{8,15},{9,8},{10,9... | collective-permute-start | bytes 589832 | tf_op jit(solution)/shard_map/ppermute | solution.py:109
  70.7 0.5 collective-permute-done.16
  71.2 0.1 collective-permute-start.17
  71.4 2.8 %collective-permute-start.20 = (bf16[2,32,1536]{2,1,0:T(8,128)(2,1)S(1)}, bf16[2,32,1536]{2,1,0:T(8,128)(2,1)S(1)}, u32[]{:S(2)}, u32[]{:S(2)}) collective-permute-start(bf16[2,32,1536]{2,1,0:T(8,128)(2,1)S(1)} %add_convert_fusion.1), channel_id=1, source_target_pairs={{0,7},{1,0},{2,1},{3,2},{4,3},{5,4},{6,5},{7,6},{8,15},{9,8},{10,9... | collective-permute-start | bytes 589832 | tf_op jit(solution)/shard_map/ppermute | solution.py:109
  74.2 1.2 collective-permute-done.10
  75.5 0.1 collective-permute-start.11
  75.6 3.7 %collective-permute-done.20 = bf16[2,32,1536]{2,1,0:T(8,128)(2,1)S(1)} collective-permute-done((bf16[2,32,1536]{2,1,0:T(8,128)(2,1)S(1)}, bf16[2,32,1536]{2,1,0:T(8,128)(2,1)S(1)}, u32[]{:S(2)}, u32[]{:S(2)}) %collective-permute-start.20) | collective-permute-done | bytes 196640 | tf_op jit(solution)/shard_map/ppermute | solution.py:109
  79.4 3.5 %collective-permute-start.21 = (bf16[2,32,1536]{2,1,0:T(8,128)(2,1)S(1)}, bf16[2,32,1536]{2,1,0:T(8,128)(2,1)S(1)}, u32[]{:S(2)}, u32[]{:S(2)}) collective-permute-start(bf16[2,32,1536]{2,1,0:T(8,128)(2,1)S(1)} %add_convert_fusion), channel_id=1, source_target_pairs={{0,7},{1,0},{2,1},{3,2},{4,3},{5,4},{6,5},{7,6},{8,15},{9,8},{10,9... | collective-permute-start | bytes 589832 | tf_op jit(solution)/shard_map/ppermute | solution.py:109
  82.9 0.8 collective-permute-done.11.refs_1_
  83.7 1.8 %collective-permute-done.21.refs_5_ = bf16[2,32,1536]{2,1,0:T(8,128)(2,1)S(1)} collective-permute-done((bf16[2,32,1536]{2,1,0:T(8,128)(2,1)S(1)}, bf16[2,32,1536]{2,1,0:T(8,128)(2,1)S(1)}, u32[]{:S(2)}, u32[]{:S(2)}) %collective-permute-start.21) | collective-permute-done | bytes 196640 | tf_op jit(solution)/shard_map/ppermute | solution.py:109
  85.5 0.2 hidden.1.refs_0_
  85.7 1.8 %collective-permute-start.25 = (bf16[4,32,768]{2,1,0:T(8,128)(2,1)S(1)}, bf16[4,32,768]{2,1,0:T(8,128)(2,1)S(1)}, u32[]{:S(2)}, u32[]{:S(2)}) collective-permute-start(bf16[4,32,768]{2,1,0:T(8,128)(2,1)S(1)} %hidden.1.refs_0_), channel_id=1, source_target_pairs={{0,6},{1,7},{2,0},{3,1},{4,2},{5,3},{6,4},{7,5},{8,14},{9,15},{10,... | collective-permute-start | bytes 589832 | tf_op jit(solution)/shard_map/ppermute | solution.py:109
  87.5 0.7 collective-permute-start.24
  88.2 4.3 %collective-permute-start.23 = (bf16[4,32,768]{2,1,0:T(8,128)(2,1)S(1)}, bf16[4,32,768]{2,1,0:T(8,128)(2,1)S(1)}, u32[]{:S(2)}, u32[]{:S(2)}) collective-permute-start(bf16[4,32,768]{2,1,0:T(8,128)(2,1)S(1)} %hidden.1.refs_0_), channel_id=1, source_target_pairs={{0,7},{1,0},{2,1},{3,2},{4,3},{5,4},{6,5},{7,6},{8,15},{9,8},{10,9... | collective-permute-start | bytes 589832 | tf_op jit(solution)/shard_map/ppermute | solution.py:109
  92.5 3.9 %collective-permute-start.27 = (bf16[4,32,768]{2,1,0:T(8,128)(2,1)S(1)}, bf16[4,32,768]{2,1,0:T(8,128)(2,1)S(1)}, u32[]{:S(2)}, u32[]{:S(2)}) collective-permute-start(bf16[4,32,768]{2,1,0:T(8,128)(2,1)S(1)} %collective-permute-done.25.refs_4_), channel_id=1, source_target_pairs={{0,7},{1,0},{2,1},{3,2},{4,3},{5,4},{6,5},{7,6},{8,15},{9,8},{10,9... | collective-permute-start | bytes 589832 | tf_op jit(solution)/shard_map/ppermute | solution.py:109
  96.5 1.9 %collective-permute-start.26 = (bf16[4,32,768]{2,1,0:T(8,128)(2,1)S(1)}, bf16[4,32,768]{2,1,0:T(8,128)(2,1)S(1)}, u32[]{:S(2)}, u32[]{:S(2)}) collective-permute-start(bf16[4,32,768]{2,1,0:T(8,128)(2,1)S(1)} %collective-permute-done.24.refs_3_), channel_id=1, source_target_pairs={{0,1},{1,2},{2,3},{3,4},{4,5},{5,6},{6,7},{7,0},{8,9},{9,10},{10,1... | collective-permute-start | bytes 589832 | tf_op jit(solution)/shard_map/ppermute | solution.py:109
  98.4 0.1 collective-permute-start.29
  98.5 2.4 %collective-permute-start.28 = (bf16[2,32,768]{2,1,0:T(8,128)(2,1)S(1)}, bf16[2,32,768]{2,1,0:T(8,128)(2,1)S(1)}, u32[]{:S(2)}, u32[]{:S(2)}) collective-permute-start(bf16[2,32,768]{2,1,0:T(8,128)(2,1)S(1)} %slice.18), channel_id=1, source_target_pairs={{0,2},{1,3},{2,4},{3,5},{4,6},{5,7},{6,0},{7,1},{8,10},{9,11},{10,... | collective-permute-start | bytes 294920 | tf_op jit(solution)/shard_map/ppermute | solution.py:109
  101.0 3.7 %mix.1 = (bf16[1024,1024]{1,0:T(8,128)(2,1)S(1)}, bf16[1024,1024]{1,0:T(8,128)(2,1)S(1)}, bf16[4,768,512]{2,1,0:T(8,128)(2,1)S(1)}) custom-call(s32[1]{0:T(128)} %bitcast.18.info, f32[16,8,128]{2,1,0:T(8,128)S(1)} %get-tuple-element.45.route, bf16[4,768,512]{2,1,0:T(8,128)(2,1)} %wd_hbm.1), custom_call_target="tpu_custom_call" | custom-call | tf_op jit(solution)/shard_map/mix/pallas_call | solution.py:468
  104.6 1.3 collective-permute-done.29.refs_8_
  105.9 3.8 %collective-permute-done.28.refs_7_ = bf16[2,32,768]{2,1,0:T(8,128)(2,1)S(1)} collective-permute-done((bf16[2,32,768]{2,1,0:T(8,128)(2,1)S(1)}, bf16[2,32,768]{2,1,0:T(8,128)(2,1)S(1)}, u32[]{:S(2)}, u32[]{:S(2)}) %collective-permute-start.28) | collective-permute-done | bytes 98336 | tf_op jit(solution)/shard_map/ppermute | solution.py:109
  109.7 3.9 %down.1 = (bf16[8,128,512]{2,1,0:T(8,128)(2,1)S(1)}, bf16[1024,512]{1,0:T(8,128)(2,1)S(1)}) custom-call(s32[9]{0:T(128)S(1)} %stack.142.info, bf16[4,32,768]{2,1,0:T(8,128)(2,1)S(1)} %hidden.1.refs_0_, bf16[4,32,768]{2,1,0:T(8,128)(2,1)S(1)} %collective-permute-done.22.refs_1_, bf16[4,32,768]{2,1,0:T(8,128)(2,1)S(1)} %collective-permute-done.23.refs_2_, ...), custom_call_target="tpu_custom_call" | custom-call | flops 2000000000 | bytes 6000000 | tf_op jit(solution)/shard_map/down/pallas_call | solution.py:477
  113.6 5.5 %collective-permute-start.30 = (bf16[8,128,512]{2,1,0:T(8,128)(2,1)S(1)}, bf16[8,128,512]{2,1,0:T(8,128)(2,1)S(1)}, u32[]{:S(2)}, u32[]{:S(2)}) collective-permute-start(bf16[8,128,512]{2,1,0:T(8,128)(2,1)S(1)} %get-tuple-element.68), channel_id=1, source_target_pairs={{0,8},{8,0},{16,24},{24,16},{32,40},{40,32},{48,56},{56,48},{64,72... | collective-permute-start | bytes 3145736 | tf_op jit(solution)/shard_map/ppermute | solution.py:113
  119.2 1.7 %home.1 = bf16[8,128,512]{2,1,0:T(8,128)(2,1)S(1)} custom-call(bf16[1024,1024]{1,0:T(8,128)(2,1)S(1)} %get-tuple-element.46.mix, bf16[1024,512]{1,0:T(8,128)(2,1)S(1)} %get-tuple-element.67.res), custom_call_target="tpu_custom_call" | custom-call | flops 1000000000 | bytes 2000000 | tf_op jit(solution)/shard_map/home/pallas_call | solution.py:491
  120.9 0.5 collective-permute-done.30.swapped
  121.4 0.6 first.1
  122.1 0.1 collective-permute-start.31
  122.2 2.6 %collective-permute-start.32 = (bf16[192,512]{1,0:T(8,128)(2,1)S(1)}, bf16[192,512]{1,0:T(8,128)(2,1)S(1)}, u32[]{:S(2)}, u32[]{:S(2)}) collective-permute-start(bf16[192,512]{1,0:T(8,128)(2,1)S(1)} %get-tuple-element.70), channel_id=1, source_target_pairs={{0,112},{8,120},{16,0},{24,8},{32,16},{40,24},{48,32},{56,40},{64,... | collective-permute-start | bytes 589832 | tf_op jit(solution)/shard_map/ppermute | solution.py:109
  124.9 0.7 rest.1.total
  125.6 3.9 %collective-permute-done.31.right = bf16[192,512]{1,0:T(8,128)(2,1)S(1)} collective-permute-done((bf16[192,512]{1,0:T(8,128)(2,1)S(1)}, bf16[192,512]{1,0:T(8,128)(2,1)S(1)}, u32[]{:S(2)}, u32[]{:S(2)}) %collective-permute-start.31) | collective-permute-done | bytes 196640 | tf_op jit(solution)/shard_map/ppermute | solution.py:109
  129.6 2.9 %collective-permute-start.33 = (bf16[128,512]{1,0:T(8,128)(2,1)S(1)}, bf16[128,512]{1,0:T(8,128)(2,1)S(1)}, u32[]{:S(2)}, u32[]{:S(2)}) collective-permute-start(bf16[128,512]{1,0:T(8,128)(2,1)S(1)} %get-tuple-element.71), channel_id=1, source_target_pairs={{0,48},{8,56},{16,64},{24,72},{32,80},{40,88},{48,96},{56,104},{64... | collective-permute-start | bytes 393224 | tf_op jit(solution)/shard_map/ppermute | solution.py:109
  132.5 1.6 %collective-permute-start.34 = (bf16[128,512]{1,0:T(8,128)(2,1)S(1)}, bf16[128,512]{1,0:T(8,128)(2,1)S(1)}, u32[]{:S(2)}, u32[]{:S(2)}) collective-permute-start(bf16[128,512]{1,0:T(8,128)(2,1)S(1)} %get-tuple-element.72), channel_id=1, source_target_pairs={{0,80},{8,88},{16,96},{24,104},{32,112},{40,120},{48,0},{56,8},{64... | collective-permute-start | bytes 393224 | tf_op jit(solution)/shard_map/ppermute | solution.py:109
  134.2 2.7 %collective-permute-start.36 = (bf16[128,512]{1,0:T(8,128)(2,1)S(1)}, bf16[128,512]{1,0:T(8,128)(2,1)S(1)}, u32[]{:S(2)}, u32[]{:S(2)}) collective-permute-start(bf16[128,512]{1,0:T(8,128)(2,1)S(1)} %get-tuple-element.74), channel_id=1, source_target_pairs={{0,112},{8,120},{16,0},{24,8},{32,16},{40,24},{48,32},{56,40},{64,... | collective-permute-start | bytes 393224 | tf_op jit(solution)/shard_map/ppermute | solution.py:109
  136.9 6.8 %collective-permute-done.34.b = bf16[128,512]{1,0:T(8,128)(2,1)S(1)} collective-permute-done((bf16[128,512]{1,0:T(8,128)(2,1)S(1)}, bf16[128,512]{1,0:T(8,128)(2,1)S(1)}, u32[]{:S(2)}, u32[]{:S(2)}) %collective-permute-start.34) | collective-permute-done | bytes 131104 | tf_op jit(solution)/shard_map/ppermute | solution.py:109
  143.6 0.7 collective-permute-done.35.c
  144.3 0.2 collective-permute-done.36.d
  144.5 0.7 finish.1
  (48 shorter events, 1.0 us)
Async XLA Ops:
  2.0 21.2 %collective-permute-start.1 = (bf16[136,512]{1,0:T(8,128)(2,1)S(1)}, bf16[136,512]{1,0:T(8,128)(2,1)S(1)}, u32[]{:S(2)}, u32[]{:S(2)}) collective-permute-start(bf16[136,512]{1,0:T(8,128)(2,1)S(1)} %prepare.1.refs_0_), channel_id=1, source_target_pairs={{0,112},{8,120},{16,0},{24,8},{32,16},{40,24},{48,32},{56,40},{64,... | collective-permute-start | bytes 417800 | tf_op jit(solution)/shard_map/ppermute | solution.py:109
  14.5 8.7 %collective-permute-start = (bf16[136,512]{1,0:T(8,128)(2,1)S(1)}, bf16[136,512]{1,0:T(8,128)(2,1)S(1)}, u32[]{:S(2)}, u32[]{:S(2)}) collective-permute-start(bf16[136,512]{1,0:T(8,128)(2,1)S(1)} %prepare.1.refs_0_), channel_id=1, source_target_pairs={{0,16},{8,24},{16,32},{24,40},{32,48},{40,56},{48,64},{56,72},{64,... | collective-permute-start | bytes 417800 | tf_op jit(solution)/shard_map/ppermute | solution.py:109
  14.5 8.7 %collective-permute-start.3 = (bf16[136,512]{1,0:T(8,128)(2,1)S(1)}, bf16[136,512]{1,0:T(8,128)(2,1)S(1)}, u32[]{:S(2)}, u32[]{:S(2)}) collective-permute-start(bf16[136,512]{1,0:T(8,128)(2,1)S(1)} %prepare.1.refs_0_), channel_id=1, source_target_pairs={{0,80},{8,88},{16,96},{24,104},{32,112},{40,120},{48,0},{56,8},{64... | collective-permute-start | bytes 417800 | tf_op jit(solution)/shard_map/ppermute | solution.py:109
  15.4 11.8 %collective-permute-start.2 = (bf16[136,512]{1,0:T(8,128)(2,1)S(1)}, bf16[136,512]{1,0:T(8,128)(2,1)S(1)}, u32[]{:S(2)}, u32[]{:S(2)}) collective-permute-start(bf16[136,512]{1,0:T(8,128)(2,1)S(1)} %prepare.1.refs_0_), channel_id=1, source_target_pairs={{0,48},{8,56},{16,64},{24,72},{32,80},{40,88},{48,96},{56,104},{64... | collective-permute-start | bytes 417800 | tf_op jit(solution)/shard_map/ppermute | solution.py:109
  17.8 0.8 copy-start
  18.5 0.7 copy-start.1
  23.2 14.2 %collective-permute-start.5 = (bf16[208,512]{1,0:T(8,128)(2,1)S(1)}, bf16[208,512]{1,0:T(8,128)(2,1)S(1)}, u32[]{:S(2)}, u32[]{:S(2)}) collective-permute-start(bf16[208,512]{1,0:T(8,128)(2,1)S(1)} %pad_maximum_fusion.1), channel_id=1, source_target_pairs={{0,112},{8,120},{16,0},{24,8},{32,16},{40,24},{48,32},{56,40},{64,... | collective-permute-start | bytes 638984 | tf_op jit(solution)/shard_map/ppermute | solution.py:109
  27.3 10.2 %collective-permute-start.4 = (bf16[200,512]{1,0:T(8,128)(2,1)S(1)}, bf16[200,512]{1,0:T(8,128)(2,1)S(1)}, u32[]{:S(2)}, u32[]{:S(2)}) collective-permute-start(bf16[200,512]{1,0:T(8,128)(2,1)S(1)} %pad_maximum_fusion.2), channel_id=1, source_target_pairs={{0,16},{8,24},{16,32},{24,40},{32,48},{40,56},{48,64},{56,72},{64,... | collective-permute-start | bytes 614408 | tf_op jit(solution)/shard_map/ppermute | solution.py:109
  27.5 18.3 %collective-permute-start.6 = (bf16[680,512]{1,0:T(8,128)(2,1)S(1)}, bf16[680,512]{1,0:T(8,128)(2,1)S(1)}, u32[]{:S(2)}, u32[]{:S(2)}) collective-permute-start(bf16[680,512]{1,0:T(8,128)(2,1)S(1)} %bundle.1), channel_id=1, source_target_pairs={{0,8},{8,0},{16,24},{24,16},{32,40},{40,32},{48,56},{56,48},{64,72... | collective-permute-start | bytes 2088968 | tf_op jit(solution)/shard_map/ppermute | solution.py:113
  37.5 8.3 %collective-permute-start.7 = (bf16[408,512]{1,0:T(8,128)(2,1)S(1)}, bf16[408,512]{1,0:T(8,128)(2,1)S(1)}, u32[]{:S(2)}, u32[]{:S(2)}) collective-permute-start(bf16[408,512]{1,0:T(8,128)(2,1)S(1)} %pad_maximum_fusion), channel_id=1, source_target_pairs={{0,8},{8,0},{16,24},{24,16},{32,40},{40,32},{48,56},{56,48},{64,72... | collective-permute-start | bytes 1253384 | tf_op jit(solution)/shard_map/ppermute | solution.py:113
  49.8 9.6 %collective-permute-start.8 = (bf16[2,32,1536]{2,1,0:T(8,128)(2,1)S(1)}, bf16[2,32,1536]{2,1,0:T(8,128)(2,1)S(1)}, u32[]{:S(2)}, u32[]{:S(2)}) collective-permute-start(bf16[2,32,1536]{2,1,0:T(8,128)(2,1)S(1)} %get-tuple-element.49), channel_id=1, source_target_pairs={{0,1},{1,2},{2,3},{3,4},{4,5},{5,6},{6,7},{7,0},{8,9},{9,10},{10,1... | collective-permute-start | bytes 589832 | tf_op jit(solution)/shard_map/ppermute | solution.py:109
  49.9 9.7 %collective-permute-start.12 = (bf16[2,32,1536]{2,1,0:T(8,128)(2,1)S(1)}, bf16[2,32,1536]{2,1,0:T(8,128)(2,1)S(1)}, u32[]{:S(2)}, u32[]{:S(2)}) collective-permute-start(bf16[2,32,1536]{2,1,0:T(8,128)(2,1)S(1)} %get-tuple-element.53), channel_id=1, source_target_pairs={{0,7},{1,0},{2,1},{3,2},{4,3},{5,4},{6,5},{7,6},{8,15},{9,8},{10,9... | collective-permute-start | bytes 589832 | tf_op jit(solution)/shard_map/ppermute | solution.py:109
  56.4 7.0 %collective-permute-start.15 = (bf16[2,32,1536]{2,1,0:T(8,128)(2,1)S(1)}, bf16[2,32,1536]{2,1,0:T(8,128)(2,1)S(1)}, u32[]{:S(2)}, u32[]{:S(2)}) collective-permute-start(bf16[2,32,1536]{2,1,0:T(8,128)(2,1)S(1)} %get-tuple-element.58), channel_id=1, source_target_pairs={{0,1},{1,2},{2,3},{3,4},{4,5},{5,6},{6,7},{7,0},{8,9},{9,10},{10,1... | collective-permute-start | bytes 589832 | tf_op jit(solution)/shard_map/ppermute | solution.py:109
  56.8 6.9 %collective-permute-start.18 = (bf16[2,32,1536]{2,1,0:T(8,128)(2,1)S(1)}, bf16[2,32,1536]{2,1,0:T(8,128)(2,1)S(1)}, u32[]{:S(2)}, u32[]{:S(2)}) collective-permute-start(bf16[2,32,1536]{2,1,0:T(8,128)(2,1)S(1)} %get-tuple-element.61), channel_id=1, source_target_pairs={{0,7},{1,0},{2,1},{3,2},{4,3},{5,4},{6,5},{7,6},{8,15},{9,8},{10,9... | collective-permute-start | bytes 589832 | tf_op jit(solution)/shard_map/ppermute | solution.py:109
  59.5 8.2 %collective-permute-start.9 = (bf16[2,32,1536]{2,1,0:T(8,128)(2,1)S(1)}, bf16[2,32,1536]{2,1,0:T(8,128)(2,1)S(1)}, u32[]{:S(2)}, u32[]{:S(2)}) collective-permute-start(bf16[2,32,1536]{2,1,0:T(8,128)(2,1)S(1)} %add_convert_fusion.9), channel_id=1, source_target_pairs={{0,1},{1,2},{2,3},{3,4},{4,5},{5,6},{6,7},{7,0},{8,9},{9,10},{10,1... | collective-permute-start | bytes 589832 | tf_op jit(solution)/shard_map/ppermute | solution.py:109
  59.7 8.2 %collective-permute-start.13 = (bf16[2,32,1536]{2,1,0:T(8,128)(2,1)S(1)}, bf16[2,32,1536]{2,1,0:T(8,128)(2,1)S(1)}, u32[]{:S(2)}, u32[]{:S(2)}) collective-permute-start(bf16[2,32,1536]{2,1,0:T(8,128)(2,1)S(1)} %add_convert_fusion.6), channel_id=1, source_target_pairs={{0,7},{1,0},{2,1},{3,2},{4,3},{5,4},{6,5},{7,6},{8,15},{9,8},{10,9... | collective-permute-start | bytes 589832 | tf_op jit(solution)/shard_map/ppermute | solution.py:109
  63.5 7.7 %collective-permute-start.16 = (bf16[2,32,1536]{2,1,0:T(8,128)(2,1)S(1)}, bf16[2,32,1536]{2,1,0:T(8,128)(2,1)S(1)}, u32[]{:S(2)}, u32[]{:S(2)}) collective-permute-start(bf16[2,32,1536]{2,1,0:T(8,128)(2,1)S(1)} %add_convert_fusion.4), channel_id=1, source_target_pairs={{0,1},{1,2},{2,3},{3,4},{4,5},{5,6},{6,7},{7,0},{8,9},{9,10},{10,1... | collective-permute-start | bytes 589832 | tf_op jit(solution)/shard_map/ppermute | solution.py:109
  63.7 7.6 %collective-permute-start.19 = (bf16[2,32,1536]{2,1,0:T(8,128)(2,1)S(1)}, bf16[2,32,1536]{2,1,0:T(8,128)(2,1)S(1)}, u32[]{:S(2)}, u32[]{:S(2)}) collective-permute-start(bf16[2,32,1536]{2,1,0:T(8,128)(2,1)S(1)} %add_convert_fusion.2), channel_id=1, source_target_pairs={{0,7},{1,0},{2,1},{3,2},{4,3},{5,4},{6,5},{7,6},{8,15},{9,8},{10,9... | collective-permute-start | bytes 589832 | tf_op jit(solution)/shard_map/ppermute | solution.py:109
  67.8 7.7 %collective-permute-start.10 = (bf16[2,32,1536]{2,1,0:T(8,128)(2,1)S(1)}, bf16[2,32,1536]{2,1,0:T(8,128)(2,1)S(1)}, u32[]{:S(2)}, u32[]{:S(2)}) collective-permute-start(bf16[2,32,1536]{2,1,0:T(8,128)(2,1)S(1)} %add_convert_fusion.8), channel_id=1, source_target_pairs={{0,1},{1,2},{2,3},{3,4},{4,5},{5,6},{6,7},{7,0},{8,9},{9,10},{10,1... | collective-permute-start | bytes 589832 | tf_op jit(solution)/shard_map/ppermute | solution.py:109
  68.0 14.9 %collective-permute-start.14 = (bf16[2,32,1536]{2,1,0:T(8,128)(2,1)S(1)}, bf16[2,32,1536]{2,1,0:T(8,128)(2,1)S(1)}, u32[]{:S(2)}, u32[]{:S(2)}) collective-permute-start(bf16[2,32,1536]{2,1,0:T(8,128)(2,1)S(1)} %add_convert_fusion.5), channel_id=1, source_target_pairs={{0,7},{1,0},{2,1},{3,2},{4,3},{5,4},{6,5},{7,6},{8,15},{9,8},{10,9... | collective-permute-start | bytes 589832 | tf_op jit(solution)/shard_map/ppermute | solution.py:109
  71.2 11.6 %collective-permute-start.17 = (bf16[2,32,1536]{2,1,0:T(8,128)(2,1)S(1)}, bf16[2,32,1536]{2,1,0:T(8,128)(2,1)S(1)}, u32[]{:S(2)}, u32[]{:S(2)}) collective-permute-start(bf16[2,32,1536]{2,1,0:T(8,128)(2,1)S(1)} %add_convert_fusion.3), channel_id=1, source_target_pairs={{0,1},{1,2},{2,3},{3,4},{4,5},{5,6},{6,7},{7,0},{8,9},{9,10},{10,1... | collective-permute-start | bytes 589832 | tf_op jit(solution)/shard_map/ppermute | solution.py:109
  71.4 7.9 %collective-permute-start.20 = (bf16[2,32,1536]{2,1,0:T(8,128)(2,1)S(1)}, bf16[2,32,1536]{2,1,0:T(8,128)(2,1)S(1)}, u32[]{:S(2)}, u32[]{:S(2)}) collective-permute-start(bf16[2,32,1536]{2,1,0:T(8,128)(2,1)S(1)} %add_convert_fusion.1), channel_id=1, source_target_pairs={{0,7},{1,0},{2,1},{3,2},{4,3},{5,4},{6,5},{7,6},{8,15},{9,8},{10,9... | collective-permute-start | bytes 589832 | tf_op jit(solution)/shard_map/ppermute | solution.py:109
  75.5 8.2 %collective-permute-start.11 = (bf16[2,32,1536]{2,1,0:T(8,128)(2,1)S(1)}, bf16[2,32,1536]{2,1,0:T(8,128)(2,1)S(1)}, u32[]{:S(2)}, u32[]{:S(2)}) collective-permute-start(bf16[2,32,1536]{2,1,0:T(8,128)(2,1)S(1)} %add_convert_fusion.7), channel_id=1, source_target_pairs={{0,1},{1,2},{2,3},{3,4},{4,5},{5,6},{6,7},{7,0},{8,9},{9,10},{10,1... | collective-permute-start | bytes 589832 | tf_op jit(solution)/shard_map/ppermute | solution.py:109
  79.4 6.1 %collective-permute-start.21 = (bf16[2,32,1536]{2,1,0:T(8,128)(2,1)S(1)}, bf16[2,32,1536]{2,1,0:T(8,128)(2,1)S(1)}, u32[]{:S(2)}, u32[]{:S(2)}) collective-permute-start(bf16[2,32,1536]{2,1,0:T(8,128)(2,1)S(1)} %add_convert_fusion), channel_id=1, source_target_pairs={{0,7},{1,0},{2,1},{3,2},{4,3},{5,4},{6,5},{7,6},{8,15},{9,8},{10,9... | collective-permute-start | bytes 589832 | tf_op jit(solution)/shard_map/ppermute | solution.py:109
  85.7 6.8 %collective-permute-start.25 = (bf16[4,32,768]{2,1,0:T(8,128)(2,1)S(1)}, bf16[4,32,768]{2,1,0:T(8,128)(2,1)S(1)}, u32[]{:S(2)}, u32[]{:S(2)}) collective-permute-start(bf16[4,32,768]{2,1,0:T(8,128)(2,1)S(1)} %hidden.1.refs_0_), channel_id=1, source_target_pairs={{0,6},{1,7},{2,0},{3,1},{4,2},{5,3},{6,4},{7,5},{8,14},{9,15},{10,... | collective-permute-start | bytes 589832 | tf_op jit(solution)/shard_map/ppermute | solution.py:109
  87.5 9.0 %collective-permute-start.24 = (bf16[4,32,768]{2,1,0:T(8,128)(2,1)S(1)}, bf16[4,32,768]{2,1,0:T(8,128)(2,1)S(1)}, u32[]{:S(2)}, u32[]{:S(2)}) collective-permute-start(bf16[4,32,768]{2,1,0:T(8,128)(2,1)S(1)} %hidden.1.refs_0_), channel_id=1, source_target_pairs={{0,2},{1,3},{2,4},{3,5},{4,6},{5,7},{6,0},{7,1},{8,10},{9,11},{10,... | collective-permute-start | bytes 589832 | tf_op jit(solution)/shard_map/ppermute | solution.py:109
  88.2 10.3 %collective-permute-start.23 = (bf16[4,32,768]{2,1,0:T(8,128)(2,1)S(1)}, bf16[4,32,768]{2,1,0:T(8,128)(2,1)S(1)}, u32[]{:S(2)}, u32[]{:S(2)}) collective-permute-start(bf16[4,32,768]{2,1,0:T(8,128)(2,1)S(1)} %hidden.1.refs_0_), channel_id=1, source_target_pairs={{0,7},{1,0},{2,1},{3,2},{4,3},{5,4},{6,5},{7,6},{8,15},{9,8},{10,9... | collective-permute-start | bytes 589832 | tf_op jit(solution)/shard_map/ppermute | solution.py:109
  92.5 12.1 %collective-permute-start.22 = (bf16[4,32,768]{2,1,0:T(8,128)(2,1)S(1)}, bf16[4,32,768]{2,1,0:T(8,128)(2,1)S(1)}, u32[]{:S(2)}, u32[]{:S(2)}) collective-permute-start(bf16[4,32,768]{2,1,0:T(8,128)(2,1)S(1)} %hidden.1.refs_0_), channel_id=1, source_target_pairs={{0,1},{1,2},{2,3},{3,4},{4,5},{5,6},{6,7},{7,0},{8,9},{9,10},{10,1... | collective-permute-start | bytes 589832 | tf_op jit(solution)/shard_map/ppermute | solution.py:109
  92.5 17.2 %collective-permute-start.27 = (bf16[4,32,768]{2,1,0:T(8,128)(2,1)S(1)}, bf16[4,32,768]{2,1,0:T(8,128)(2,1)S(1)}, u32[]{:S(2)}, u32[]{:S(2)}) collective-permute-start(bf16[4,32,768]{2,1,0:T(8,128)(2,1)S(1)} %collective-permute-done.25.refs_4_), channel_id=1, source_target_pairs={{0,7},{1,0},{2,1},{3,2},{4,3},{5,4},{6,5},{7,6},{8,15},{9,8},{10,9... | collective-permute-start | bytes 589832 | tf_op jit(solution)/shard_map/ppermute | solution.py:109
  96.5 13.3 %collective-permute-start.26 = (bf16[4,32,768]{2,1,0:T(8,128)(2,1)S(1)}, bf16[4,32,768]{2,1,0:T(8,128)(2,1)S(1)}, u32[]{:S(2)}, u32[]{:S(2)}) collective-permute-start(bf16[4,32,768]{2,1,0:T(8,128)(2,1)S(1)} %collective-permute-done.24.refs_3_), channel_id=1, source_target_pairs={{0,1},{1,2},{2,3},{3,4},{4,5},{5,6},{6,7},{7,0},{8,9},{9,10},{10,1... | collective-permute-start | bytes 589832 | tf_op jit(solution)/shard_map/ppermute | solution.py:109
  98.4 7.5 %collective-permute-start.29 = (bf16[2,32,768]{2,1,0:T(8,128)(2,1)S(1)}, bf16[2,32,768]{2,1,0:T(8,128)(2,1)S(1)}, u32[]{:S(2)}, u32[]{:S(2)}) collective-permute-start(bf16[2,32,768]{2,1,0:T(8,128)(2,1)S(1)} %slice.19), channel_id=1, source_target_pairs={{0,6},{1,7},{2,0},{3,1},{4,2},{5,3},{6,4},{7,5},{8,14},{9,15},{10,... | collective-permute-start | bytes 294920 | tf_op jit(solution)/shard_map/ppermute | solution.py:109
  98.5 11.2 %collective-permute-start.28 = (bf16[2,32,768]{2,1,0:T(8,128)(2,1)S(1)}, bf16[2,32,768]{2,1,0:T(8,128)(2,1)S(1)}, u32[]{:S(2)}, u32[]{:S(2)}) collective-permute-start(bf16[2,32,768]{2,1,0:T(8,128)(2,1)S(1)} %slice.18), channel_id=1, source_target_pairs={{0,2},{1,3},{2,4},{3,5},{4,6},{5,7},{6,0},{7,1},{8,10},{9,11},{10,... | collective-permute-start | bytes 294920 | tf_op jit(solution)/shard_map/ppermute | solution.py:109
  113.6 7.8 %collective-permute-start.30 = (bf16[8,128,512]{2,1,0:T(8,128)(2,1)S(1)}, bf16[8,128,512]{2,1,0:T(8,128)(2,1)S(1)}, u32[]{:S(2)}, u32[]{:S(2)}) collective-permute-start(bf16[8,128,512]{2,1,0:T(8,128)(2,1)S(1)} %get-tuple-element.68), channel_id=1, source_target_pairs={{0,8},{8,0},{16,24},{24,16},{32,40},{40,32},{48,56},{56,48},{64,72... | collective-permute-start | bytes 3145736 | tf_op jit(solution)/shard_map/ppermute | solution.py:113
  122.1 7.4 %collective-permute-start.31 = (bf16[192,512]{1,0:T(8,128)(2,1)S(1)}, bf16[192,512]{1,0:T(8,128)(2,1)S(1)}, u32[]{:S(2)}, u32[]{:S(2)}) collective-permute-start(bf16[192,512]{1,0:T(8,128)(2,1)S(1)} %get-tuple-element.69), channel_id=1, source_target_pairs={{0,16},{8,24},{16,32},{24,40},{32,48},{40,56},{48,64},{56,72},{64,... | collective-permute-start | bytes 589832 | tf_op jit(solution)/shard_map/ppermute | solution.py:109
  122.2 7.3 %collective-permute-start.32 = (bf16[192,512]{1,0:T(8,128)(2,1)S(1)}, bf16[192,512]{1,0:T(8,128)(2,1)S(1)}, u32[]{:S(2)}, u32[]{:S(2)}) collective-permute-start(bf16[192,512]{1,0:T(8,128)(2,1)S(1)} %get-tuple-element.70), channel_id=1, source_target_pairs={{0,112},{8,120},{16,0},{24,8},{32,16},{40,24},{48,32},{56,40},{64,... | collective-permute-start | bytes 589832 | tf_op jit(solution)/shard_map/ppermute | solution.py:109
  129.6 7.3 %collective-permute-start.33 = (bf16[128,512]{1,0:T(8,128)(2,1)S(1)}, bf16[128,512]{1,0:T(8,128)(2,1)S(1)}, u32[]{:S(2)}, u32[]{:S(2)}) collective-permute-start(bf16[128,512]{1,0:T(8,128)(2,1)S(1)} %get-tuple-element.71), channel_id=1, source_target_pairs={{0,48},{8,56},{16,64},{24,72},{32,80},{40,88},{48,96},{56,104},{64... | collective-permute-start | bytes 393224 | tf_op jit(solution)/shard_map/ppermute | solution.py:109
  132.5 11.1 %collective-permute-start.34 = (bf16[128,512]{1,0:T(8,128)(2,1)S(1)}, bf16[128,512]{1,0:T(8,128)(2,1)S(1)}, u32[]{:S(2)}, u32[]{:S(2)}) collective-permute-start(bf16[128,512]{1,0:T(8,128)(2,1)S(1)} %get-tuple-element.72), channel_id=1, source_target_pairs={{0,80},{8,88},{16,96},{24,104},{32,112},{40,120},{48,0},{56,8},{64... | collective-permute-start | bytes 393224 | tf_op jit(solution)/shard_map/ppermute | solution.py:109
  134.2 10.1 %collective-permute-start.35 = (bf16[128,512]{1,0:T(8,128)(2,1)S(1)}, bf16[128,512]{1,0:T(8,128)(2,1)S(1)}, u32[]{:S(2)}, u32[]{:S(2)}) collective-permute-start(bf16[128,512]{1,0:T(8,128)(2,1)S(1)} %get-tuple-element.73), channel_id=1, source_target_pairs={{0,16},{8,24},{16,32},{24,40},{32,48},{40,56},{48,64},{56,72},{64,... | collective-permute-start | bytes 393224 | tf_op jit(solution)/shard_map/ppermute | solution.py:109
  134.2 10.3 %collective-permute-start.36 = (bf16[128,512]{1,0:T(8,128)(2,1)S(1)}, bf16[128,512]{1,0:T(8,128)(2,1)S(1)}, u32[]{:S(2)}, u32[]{:S(2)}) collective-permute-start(bf16[128,512]{1,0:T(8,128)(2,1)S(1)} %get-tuple-element.74), channel_id=1, source_target_pairs={{0,112},{8,120},{16,0},{24,8},{32,16},{40,24},{48,32},{56,40},{64,... | collective-permute-start | bytes 393224 | tf_op jit(solution)/shard_map/ppermute | solution.py:109

commit v2 on v1

--- a/solution.py
+++ b/solution.py
@@ -137,36 +137,33 @@
         out[i * height : (i + 1) * height, :] = ref[...]
 
 
-def expert_parts(j0, info, place, tok, wg_hbm, wu_hbm, wg, wu, sems, onehot, out, work):
+def expert_parts(j0, info, place, tok, wg, wu, onehot, packed, out):
     n_blocks = place.shape[0]
     rows = tok.shape[0] // n_blocks
     n_dest = len(out)
     here_count, dest_rows, ff2 = out[0].shape
     ff = ff2 // 2
     capacity = n_dest * dest_rows
-
-    def fetch(j):
-        return (
-            pltpu.make_async_copy(wg_hbm.at[j0 + j], wg.at[j], sems.at[0, j]),
-            pltpu.make_async_copy(wu_hbm.at[j0 + j], wu.at[j], sems.at[1, j]),
-        )
-
-    for j in range(here_count):
-        for copy in fetch(j):
-            copy.start()
-    work()
     row_id = lax.broadcasted_iota(jnp.int32, (capacity, rows), 0) + info[1 + n_blocks]
     row_id = jnp.where(row_id < capacity, row_id, row_id - capacity).astype(F32)
 
+    def select(i, carry):
+        at = pl.ds(pl.multiple_of(i * rows, rows), rows)
+        block = info[1 + i]
+        for j in range(here_count):
+            spot = place[block, j0 + j : j0 + j + 1, :]
+            onehot[j * capacity : (j + 1) * capacity, at] = jnp.where(
+                row_id == spot, 1.0, 0.0
+            ).astype(BF16)
+        return carry
+
+    lax.fori_loop(0, n_blocks, select, 0, unroll=2)
+    packed[...] = jnp.dot(onehot[...], tok[...], preferred_element_type=F32).astype(BF16)
+
     def expert(j, carry):
-        for i in range(n_blocks):
-            spot = place[info[1 + i], pl.ds(j0 + j, 1), :]
-            onehot[:, i * rows : (i + 1) * rows] = jnp.where(row_id == spot, 1.0, 0.0).astype(BF16)
-        packed = jnp.dot(onehot[...], tok[...], preferred_element_type=F32).astype(BF16)
-        for copy in fetch(j):
-            copy.wait()
-        gate = jnp.dot(packed, wg[j], preferred_element_type=F32).astype(BF16)
-        up = jnp.dot(packed, wu[j], preferred_element_type=F32).astype(BF16)
+        mine = packed[pl.ds(pl.multiple_of(j * capacity, capacity), capacity), :]
+        gate = jnp.dot(mine, wg[j0 + j], preferred_element_type=F32).astype(BF16)
+        up = jnp.dot(mine, wu[j0 + j], preferred_element_type=F32).astype(BF16)
         for d in range(n_dest):
             out[d][j, :, 0:ff] = gate[d * dest_rows : (d + 1) * dest_rows]
             out[d][j, :, ff:] = up[d * dest_rows : (d + 1) * dest_rows]
@@ -175,67 +172,75 @@
     lax.fori_loop(0, here_count, expert, 0)
 
 
+def fetch_kernel(wg_hbm, wu_hbm, wg, wu, sems):
+    copies = (
+        pltpu.make_async_copy(wg_hbm, wg, sems.at[0]),
+        pltpu.make_async_copy(wu_hbm, wu, sems.at[1]),
+    )
+    for copy in copies:
+        copy.start()
+    for copy in copies:
+        copy.wait()
+
+
 def pack_kernel(plan, half, local, n_dest, info, *refs):
     n_ops = 1 + max(op for p in plan for op, _ in p)
     ops = refs[:n_ops]
-    wg_hbm, wu_hbm = refs[n_ops : n_ops + 2]
+    wg, wu = refs[n_ops : n_ops + 2]
     out = refs[n_ops + 2 : n_ops + 2 + n_dest]
-    route, tok, meta, onehot, wg, wu, sems = refs[n_ops + 2 + n_dest :]
+    route, tok, meta, onehot, packed = refs[n_ops + 2 + n_dest :]
     n_blocks = len(plan)
     rows = tok.shape[0] // n_blocks
     capacity = n_dest * out[0].shape[1]
 
-    def work():
-        for i, p in enumerate(plan):
-            at = pl.ds(pl.multiple_of(info[1 + i] * rows, rows), rows)
-            op, r0 = p[0]
-            if len(p) == 1:
-                tok[i * rows : (i + 1) * rows, :] = ops[op][r0 : r0 + rows, :]
-                low = r0 + rows
-            else:
-                tok[i * rows : i * rows + half, :] = ops[op][r0 : r0 + half, :]
-                op, r0 = p[1]
-                low = r0 + rows - half
-                tok[i * rows + half : (i + 1) * rows, :] = ops[op][r0:low, :]
-            meta[0:8, at] = ops[op][low : low + META, 0:rows].astype(F32)
-            meta[8:16, at] = ops[op][low : low + META, rows : 2 * rows].astype(F32)
-        ids = meta[0:8, :]
-        gates = meta[8:16, :]
-        hits = [ids == (info[0] + j).astype(F32) for j in range(local)]
-        stack = jnp.concatenate(
-            [jnp.where(h, 1.0, 0.0) for h in hits] + [jnp.where(h, gates, 0.0) for h in hits], axis=0
-        ).astype(BF16)
-        one = lax.broadcasted_iota(jnp.int32, (8, 64), 0)
-        two = lax.broadcasted_iota(jnp.int32, (8, 64), 1)
-        pick = jnp.where(one == two // 8, 1.0, 0.0).astype(BF16)
-        both = jnp.dot(pick, stack, preferred_element_type=F32)
-        member = jnp.concatenate(
-            [both[:, b * rows : (b + 1) * rows] for b in range(n_blocks)], axis=0
-        )
-        size = n_blocks * 8
-        r = lax.broadcasted_iota(jnp.int32, (rows, rows), 0)
-        c = lax.broadcasted_iota(jnp.int32, (rows, rows), 1)
-        upper = jnp.where(r < c, 1.0, 0.0).astype(BF16)
-        rr = lax.broadcasted_iota(jnp.int32, (size, size), 0)
-        cc = lax.broadcasted_iota(jnp.int32, (size, size), 1)
-        earlier = jnp.where((rr % 8 == cc % 8) & (cc // 8 < rr // 8), 1.0, 0.0).astype(BF16)
-        member_b = member.astype(BF16)
-        before = jnp.dot(earlier, member_b, preferred_element_type=F32).astype(BF16)
-        place = jnp.dot(member_b, upper, preferred_element_type=F32) + jnp.dot(
-            before, jnp.ones((rows, rows), BF16), preferred_element_type=F32
-        )
-        place = jnp.where((member > 0.5) & (place < capacity), place, -1.0)
-        row = lax.broadcasted_iota(jnp.int32, (size, rows), 0)
-        route[...] = jnp.where(row % 8 < local, place, member).reshape(n_blocks, 8, rows)
-
-    expert_parts(0, info, route, tok, wg_hbm, wu_hbm, wg, wu, sems, onehot, out, work)
-
-
-def pack_more_kernel(j0, info, tok, route, wg_hbm, wu_hbm, *refs):
-    *out, onehot, wg, wu, sems = refs
-    expert_parts(
-        j0, info, route, tok, wg_hbm, wu_hbm, wg, wu, sems, onehot, out, lambda: None
-    )
+    for i, p in enumerate(plan):
+        at = pl.ds(pl.multiple_of(info[1 + i] * rows, rows), rows)
+        op, r0 = p[0]
+        if len(p) == 1:
+            tok[i * rows : (i + 1) * rows, :] = ops[op][r0 : r0 + rows, :]
+            low = r0 + rows
+        else:
+            tok[i * rows : i * rows + half, :] = ops[op][r0 : r0 + half, :]
+            op, r0 = p[1]
+            low = r0 + rows - half
+            tok[i * rows + half : (i + 1) * rows, :] = ops[op][r0:low, :]
+        meta[0:8, at] = ops[op][low : low + META, 0:rows].astype(F32)
+        meta[8:16, at] = ops[op][low : low + META, rows : 2 * rows].astype(F32)
+    ids = meta[0:8, :]
+    gates = meta[8:16, :]
+    hits = [ids == (info[0] + j).astype(F32) for j in range(local)]
+    stack = jnp.concatenate(
+        [jnp.where(h, 1.0, 0.0) for h in hits] + [jnp.where(h, gates, 0.0) for h in hits], axis=0
+    ).astype(BF16)
+    one = lax.broadcasted_iota(jnp.int32, (8, 64), 0)
+    two = lax.broadcasted_iota(jnp.int32, (8, 64), 1)
+    pick = jnp.where(one == two // 8, 1.0, 0.0).astype(BF16)
+    both = jnp.dot(pick, stack, preferred_element_type=F32)
+    member = jnp.concatenate(
+        [both[:, b * rows : (b + 1) * rows] for b in range(n_blocks)], axis=0
+    )
+    size = n_blocks * 8
+    r = lax.broadcasted_iota(jnp.int32, (rows, rows), 0)
+    c = lax.broadcasted_iota(jnp.int32, (rows, rows), 1)
+    upper = jnp.where(r < c, 1.0, 0.0).astype(BF16)
+    rr = lax.broadcasted_iota(jnp.int32, (size, size), 0)
+    cc = lax.broadcasted_iota(jnp.int32, (size, size), 1)
+    earlier = jnp.where((rr % 8 == cc % 8) & (cc // 8 < rr // 8), 1.0, 0.0).astype(BF16)
+    member_b = member.astype(BF16)
+    before = jnp.dot(earlier, member_b, preferred_element_type=F32).astype(BF16)
+    place = jnp.dot(member_b, upper, preferred_element_type=F32) + jnp.dot(
+        before, jnp.ones((rows, rows), BF16), preferred_element_type=F32
+    )
+    place = jnp.where((member > 0.5) & (place < capacity), place, -1.0)
+    row = lax.broadcasted_iota(jnp.int32, (size, rows), 0)
+    route[...] = jnp.where(row % 8 < local, place, member).reshape(n_blocks, 8, rows)
+
+    expert_parts(0, info, route, tok, wg, wu, onehot, packed, out)
+
+
+def pack_more_kernel(j0, info, tok, route, wg, wu, *refs):
+    *out, onehot, packed = refs
+    expert_parts(j0, info, route, tok, wg, wu, onehot, packed, out)
 
 
 def hidden_kernel(*refs):
@@ -283,7 +288,7 @@
 
 def mix_rows(mix, res, ref):
     n_dest, rows, feat = ref.shape
-    group = 2
+    group = 4
 
     def some(g, carry):
         at = pl.ds(pl.multiple_of(g * group * rows, group * rows), group * rows)
@@ -412,11 +417,18 @@
 
     cut = local // 2
     pack_scratch = [
-        pltpu.VMEM((capacity, attn_count * rows), BF16),
-        pltpu.VMEM((cut, *w_gate.shape[1:]), BF16),
-        pltpu.VMEM((cut, *w_up.shape[1:]), BF16),
-        pltpu.SemaphoreType.DMA((2, cut)),
+        pltpu.VMEM((cut * capacity, attn_count * rows), BF16),
+        pltpu.VMEM((cut * capacity, feat), BF16),
     ]
+    wg, wu = pl.pallas_call(
+        fetch_kernel,
+        out_shape=tuple(jax.ShapeDtypeStruct(w.shape, BF16) for w in (w_gate, w_up)),
+        in_specs=[HBM_SPEC] * 2,
+        out_specs=(VMEM_SPEC,) * 2,
+        scratch_shapes=[pltpu.SemaphoreType.DMA((2,))],
+        name="weights",
+        **SMALL,
+    )(in_hbm(w_gate), in_hbm(w_up))
     part_shapes = (jax.ShapeDtypeStruct((cut, dest_rows, 2 * ff), BF16),) * n_expert
     pack_cost = pl.CostEstimate(flops=2 * 10**9, bytes_accessed=6 * 10**6, transcendentals=0)
     *parts_a, route, tok = pl.pallas_call(
@@ -426,7 +438,7 @@
             jax.ShapeDtypeStruct((attn_count, 8, rows), F32),
             jax.ShapeDtypeStruct((attn_count * rows, feat), BF16),
         ),
-        in_specs=[SMEM_SPEC] + [VMEM_SPEC] * len(operands) + [HBM_SPEC] * 2,
+        in_specs=[SMEM_SPEC] + [VMEM_SPEC] * (len(operands) + 2),
         out_specs=(VMEM_SPEC,) * (n_expert + 2),
         scratch_shapes=[
             pltpu.VMEM((2 * META, attn_count * rows), F32),
@@ -435,17 +447,17 @@
         compiler_params=pltpu.CompilerParams(vmem_limit_bytes=7 << 20),
         cost_estimate=pack_cost,
         name="pack",
-    )(pack_info, *map(in_vmem, operands), in_hbm(w_gate), in_hbm(w_up))
+    )(pack_info, *map(in_vmem, (*operands, wg, wu)))
     parts_b = pl.pallas_call(
         functools.partial(pack_more_kernel, cut),
         out_shape=part_shapes,
-        in_specs=[SMEM_SPEC, VMEM_SPEC, VMEM_SPEC, HBM_SPEC, HBM_SPEC],
+        in_specs=[SMEM_SPEC] + [VMEM_SPEC] * 4,
         out_specs=(VMEM_SPEC,) * n_expert,
         scratch_shapes=pack_scratch,
         compiler_params=pltpu.CompilerParams(vmem_limit_bytes=7 << 20),
         cost_estimate=pack_cost,
         name="pack_more",
-    )(pack_info, in_vmem(tok), in_vmem(route), in_hbm(w_gate), in_hbm(w_up))
+    )(pack_info, *map(in_vmem, (tok, route, wg, wu)))
 
     terms = sum(scatter_sum([parts_a, parts_b], "expert"), ())
     hidden = pl.pallas_call(

time: 147 us -> 147 us (level)
  Pallas kernels: 23.9 us -> 25.9 us
    pallas_call x0 -> x1, Pallas kernels: none -> 2.86 us  [step(): pl.pallas_call(fetch_kernel, out_shape=tuple((jax.ShapeDtypeStruct(w.shap...]
  transfers between devices with their start and end apart: 37 -> 37, of which waited for: 15 -> 15; matrix products, arithmetic and copies ran while one was open for 1% -> 1% of each run, Pallas kernels for 9% -> 11%
where the time goes in v2:
time: 147 us; the launch traced here: 145 us
  starting transfers between devices  87.8 us (60%)
  waiting for transfers between devices  27.7 us (19%)
  Pallas kernels  25.9 us (18%)
  local copies, waits for them, and re-layouts  2.36 us (2%)
    ppermute x34, starting transfers between devices, shift(): lax.ppermute(value, axis, [(i, (i + step) % count) for i in range(count)])  65.7 us
    ppermute x34, waiting for transfers between devices, shift(): lax.ppermute(value, axis, [(i, (i + step) % count) for i in range(count)])  26.8 us
    ppermute x3, starting transfers between devices, swap_cores(): lax.ppermute(value, 'attn', [(i, i ^ 1) for i in range(lax.axis_size('att...  22.1 us
    pallas_call x1, Pallas kernels, step(): pl.pallas_call(functools.partial(pack_kernel, plan, half, local, n_expert...  4.11 us
    pallas_call x1, Pallas kernels, step(): pl.pallas_call(mix_kernel, out_shape=(mix_shape, mix_shape, jax.ShapeDtyp...  3.66 us
    pallas_call x1, Pallas kernels, step(): pl.pallas_call(functools.partial(down_kernel, where), out_shape=(jax.Shap...  3.56 us
    pallas_call x1, Pallas kernels, step(): pl.pallas_call(functools.partial(pack_more_kernel, cut), out_shape=part_s...  3.53 us
    pallas_call x1, Pallas kernels, grouped_attention(): pl.pallas_call(attention_kernel, grid=(count,), out_shape=jax.ShapeDtypeS...  3.36 us
  transfers between devices with their start and end apart: 37, of which 15 were waited for; matrix products, arithmetic and copies ran while one was open for 1% of the time, Pallas kernels for 11%

profile of v2, /device:TPU:513, one launch (start us, length us, event | category | flops | bytes accessed | tf_op | source)
XLA Modules:
  0.0 145.4 jit_solution(16746070733603299432)
XLA Ops:
  1.0 0.9 prepare.1.refs_0_
  2.0 12.5 %collective-permute-start.1 = (bf16[136,512]{1,0:T(8,128)(2,1)S(1)}, bf16[136,512]{1,0:T(8,128)(2,1)S(1)}, u32[]{:S(2)}, u32[]{:S(2)}) collective-permute-start(bf16[136,512]{1,0:T(8,128)(2,1)S(1)} %prepare.1.refs_0_), channel_id=1, source_target_pairs={{0,112},{8,120},{16,0},{24,8},{32,16},{40,24},{48,32},{56,40},{64,... | collective-permute-start | bytes 417800 | tf_op jit(solution)/shard_map/ppermute | solution.py:109
  14.5 0.9 collective-permute-start.3
  15.4 2.4 %collective-permute-start.2 = (bf16[136,512]{1,0:T(8,128)(2,1)S(1)}, bf16[136,512]{1,0:T(8,128)(2,1)S(1)}, u32[]{:S(2)}, u32[]{:S(2)}) collective-permute-start(bf16[136,512]{1,0:T(8,128)(2,1)S(1)} %prepare.1.refs_0_), channel_id=1, source_target_pairs={{0,48},{8,56},{16,64},{24,72},{32,80},{40,88},{48,96},{56,104},{64... | collective-permute-start | bytes 417800 | tf_op jit(solution)/shard_map/ppermute | solution.py:109
  17.8 0.8 copy-done
  18.5 0.7 copy-done.1
  19.2 3.4 %attention.1 = bf16[2,64,128]{2,1,0:T(8,128)(2,1)S(1)} custom-call(s32[2]{0:T(128)S(1)} %copy-done.1, bf16[2,64,128]{2,1,0:T(8,128)(2,1)S(1)} %copy-done, bf16[2,768,4,128]{3,2,1,0:T(4,128)(2,1)} %cache_k.1, bf16[2,768,4,128]{3,2,1,0:T(4,128)(2,1)} %cache_v.1), custom_call_target="tpu_custom_call" | custom-call | flops 1000000000 | bytes 3000000 | tf_op jit(solution)/shard_map/attention/pallas_call | solution.py:92
  22.5 0.6 copy.14
  23.2 4.0 %collective-permute-start.5 = (bf16[208,512]{1,0:T(8,128)(2,1)S(1)}, bf16[208,512]{1,0:T(8,128)(2,1)S(1)}, u32[]{:S(2)}, u32[]{:S(2)}) collective-permute-start(bf16[208,512]{1,0:T(8,128)(2,1)S(1)} %pad_maximum_fusion.1), channel_id=1, source_target_pairs={{0,112},{8,120},{16,0},{24,8},{32,16},{40,24},{48,32},{56,40},{64,... | collective-permute-start | bytes 638984 | tf_op jit(solution)/shard_map/ppermute | solution.py:109
  27.3 0.1 collective-permute-start.4
  27.5 10.0 %collective-permute-start.6 = (bf16[680,512]{1,0:T(8,128)(2,1)S(1)}, bf16[680,512]{1,0:T(8,128)(2,1)S(1)}, u32[]{:S(2)}, u32[]{:S(2)}) collective-permute-start(bf16[680,512]{1,0:T(8,128)(2,1)S(1)} %bundle.1), channel_id=1, source_target_pairs={{0,8},{8,0},{16,24},{24,16},{32,40},{40,32},{48,56},{56,48},{64,72... | collective-permute-start | bytes 2088968 | tf_op jit(solution)/shard_map/ppermute | solution.py:113
  37.5 6.9 %collective-permute-start.7 = (bf16[408,512]{1,0:T(8,128)(2,1)S(1)}, bf16[408,512]{1,0:T(8,128)(2,1)S(1)}, u32[]{:S(2)}, u32[]{:S(2)}) collective-permute-start(bf16[408,512]{1,0:T(8,128)(2,1)S(1)} %pad_maximum_fusion), channel_id=1, source_target_pairs={{0,8},{8,0},{16,24},{24,16},{32,40},{40,32},{48,56},{56,48},{64,72... | collective-permute-start | bytes 1253384 | tf_op jit(solution)/shard_map/ppermute | solution.py:113
  44.4 2.9 %weights.1 = (bf16[4,512,768]{2,1,0:T(8,128)(2,1)S(1)}, bf16[4,512,768]{2,1,0:T(8,128)(2,1)S(1)}) custom-call(bf16[4,512,768]{2,1,0:T(8,128)(2,1)} %wg_hbm.1, bf16[4,512,768]{2,1,0:T(8,128)(2,1)} %wu_hbm.1), custom_call_target="tpu_custom_call" | custom-call | tf_op jit(solution)/shard_map/weights/pallas_call | solution.py:423
  47.3 4.1 %pack.1 = (bf16[2,32,1536]{2,1,0:T(8,128)(2,1)S(1)}, bf16[2,32,1536]{2,1,0:T(8,128)(2,1)S(1)}, bf16[2,32,1536]{2,1,0:T(8,128)(2,1)S(1)}, bf16[2,32,1536]{2,1,0:T...) custom-call(s32[18]{0:T(128)S(1)} %stack.132.info, ...), custom_call_target="tpu_custom_call" | custom-call | flops 2000000000 | bytes 6000000 | tf_op jit(solution)/shard_map/pack/pallas_call | solution.py:434
  51.4 0.1 collective-permute-start.8
  51.5 2.7 %collective-permute-start.12 = (bf16[2,32,1536]{2,1,0:T(8,128)(2,1)S(1)}, bf16[2,32,1536]{2,1,0:T(8,128)(2,1)S(1)}, u32[]{:S(2)}, u32[]{:S(2)}) collective-permute-start(bf16[2,32,1536]{2,1,0:T(8,128)(2,1)S(1)} %get-tuple-element.57), channel_id=1, source_target_pairs={{0,7},{1,0},{2,1},{3,2},{4,3},{5,4},{6,5},{7,6},{8,15},{9,8},{10,9... | collective-permute-start | bytes 589832 | tf_op jit(solution)/shard_map/ppermute | solution.py:109
  54.2 3.5 %pack_more.1 = (bf16[2,32,1536]{2,1,0:T(8,128)(2,1)S(1)}, bf16[2,32,1536]{2,1,0:T(8,128)(2,1)S(1)}, bf16[2,32,1536]{2,1,0:T(8,128)(2,1)S(1)}, bf16[2,32,1536]{2,...) custom-call(s32[18]{0:T(128)S(1)} %stack.132.info, ...), custom_call_target="tpu_custom_call" | custom-call | flops 2000000000 | bytes 6000000 | tf_op jit(solution)/shard_map/pack_more/pallas_call | solution.py:451
  57.7 0.1 collective-permute-start.15
  57.9 2.6 %collective-permute-start.18 = (bf16[2,32,1536]{2,1,0:T(8,128)(2,1)S(1)}, bf16[2,32,1536]{2,1,0:T(8,128)(2,1)S(1)}, u32[]{:S(2)}, u32[]{:S(2)}) collective-permute-start(bf16[2,32,1536]{2,1,0:T(8,128)(2,1)S(1)} %get-tuple-element.65), channel_id=1, source_target_pairs={{0,7},{1,0},{2,1},{3,2},{4,3},{5,4},{6,5},{7,6},{8,15},{9,8},{10,9... | collective-permute-start | bytes 589832 | tf_op jit(solution)/shard_map/ppermute | solution.py:109
  60.6 0.1 collective-permute-start.9
  60.8 2.8 %collective-permute-start.13 = (bf16[2,32,1536]{2,1,0:T(8,128)(2,1)S(1)}, bf16[2,32,1536]{2,1,0:T(8,128)(2,1)S(1)}, u32[]{:S(2)}, u32[]{:S(2)}) collective-permute-start(bf16[2,32,1536]{2,1,0:T(8,128)(2,1)S(1)} %add_convert_fusion.6), channel_id=1, source_target_pairs={{0,7},{1,0},{2,1},{3,2},{4,3},{5,4},{6,5},{7,6},{8,15},{9,8},{10,9... | collective-permute-start | bytes 589832 | tf_op jit(solution)/shard_map/ppermute | solution.py:109
  63.5 1.4 collective-permute-done.15
  65.0 0.1 collective-permute-start.16
  65.2 2.8 %collective-permute-start.19 = (bf16[2,32,1536]{2,1,0:T(8,128)(2,1)S(1)}, bf16[2,32,1536]{2,1,0:T(8,128)(2,1)S(1)}, u32[]{:S(2)}, u32[]{:S(2)}) collective-permute-start(bf16[2,32,1536]{2,1,0:T(8,128)(2,1)S(1)} %add_convert_fusion.2), channel_id=1, source_target_pairs={{0,7},{1,0},{2,1},{3,2},{4,3},{5,4},{6,5},{7,6},{8,15},{9,8},{10,9... | collective-permute-start | bytes 589832 | tf_op jit(solution)/shard_map/ppermute | solution.py:109
  67.9 1.2 collective-permute-done.9
  69.2 0.1 collective-permute-start.10
  69.4 2.8 %collective-permute-start.14 = (bf16[2,32,1536]{2,1,0:T(8,128)(2,1)S(1)}, bf16[2,32,1536]{2,1,0:T(8,128)(2,1)S(1)}, u32[]{:S(2)}, u32[]{:S(2)}) collective-permute-start(bf16[2,32,1536]{2,1,0:T(8,128)(2,1)S(1)} %add_convert_fusion.5), channel_id=1, source_target_pairs={{0,7},{1,0},{2,1},{3,2},{4,3},{5,4},{6,5},{7,6},{8,15},{9,8},{10,9... | collective-permute-start | bytes 589832 | tf_op jit(solution)/shard_map/ppermute | solution.py:109
  72.2 0.5 collective-permute-done.16
  72.7 0.1 collective-permute-start.17
  72.9 2.8 %collective-permute-start.20 = (bf16[2,32,1536]{2,1,0:T(8,128)(2,1)S(1)}, bf16[2,32,1536]{2,1,0:T(8,128)(2,1)S(1)}, u32[]{:S(2)}, u32[]{:S(2)}) collective-permute-start(bf16[2,32,1536]{2,1,0:T(8,128)(2,1)S(1)} %add_convert_fusion.1), channel_id=1, source_target_pairs={{0,7},{1,0},{2,1},{3,2},{4,3},{5,4},{6,5},{7,6},{8,15},{9,8},{10,9... | collective-permute-start | bytes 589832 | tf_op jit(solution)/shard_map/ppermute | solution.py:109
  75.6 1.2 collective-permute-done.10
  76.9 0.1 collective-permute-start.11
  77.0 3.1 %collective-permute-done.20 = bf16[2,32,1536]{2,1,0:T(8,128)(2,1)S(1)} collective-permute-done((bf16[2,32,1536]{2,1,0:T(8,128)(2,1)S(1)}, bf16[2,32,1536]{2,1,0:T(8,128)(2,1)S(1)}, u32[]{:S(2)}, u32[]{:S(2)}) %collective-permute-start.20) | collective-permute-done | bytes 196640 | tf_op jit(solution)/shard_map/ppermute | solution.py:109
  80.2 3.3 %collective-permute-start.21 = (bf16[2,32,1536]{2,1,0:T(8,128)(2,1)S(1)}, bf16[2,32,1536]{2,1,0:T(8,128)(2,1)S(1)}, u32[]{:S(2)}, u32[]{:S(2)}) collective-permute-start(bf16[2,32,1536]{2,1,0:T(8,128)(2,1)S(1)} %add_convert_fusion), channel_id=1, source_target_pairs={{0,7},{1,0},{2,1},{3,2},{4,3},{5,4},{6,5},{7,6},{8,15},{9,8},{10,9... | collective-permute-start | bytes 589832 | tf_op jit(solution)/shard_map/ppermute | solution.py:109
  83.4 1.3 collective-permute-done.11.refs_1_
  84.7 1.3 collective-permute-done.21.refs_5_
  86.1 0.2 hidden.1.refs_0_
  86.3 2.0 %collective-permute-start.25 = (bf16[4,32,768]{2,1,0:T(8,128)(2,1)S(1)}, bf16[4,32,768]{2,1,0:T(8,128)(2,1)S(1)}, u32[]{:S(2)}, u32[]{:S(2)}) collective-permute-start(bf16[4,32,768]{2,1,0:T(8,128)(2,1)S(1)} %hidden.1.refs_0_), channel_id=1, source_target_pairs={{0,6},{1,7},{2,0},{3,1},{4,2},{5,3},{6,4},{7,5},{8,14},{9,15},{10,... | collective-permute-start | bytes 589832 | tf_op jit(solution)/shard_map/ppermute | solution.py:109
  88.3 0.7 collective-permute-start.24
  89.0 4.3 %collective-permute-start.23 = (bf16[4,32,768]{2,1,0:T(8,128)(2,1)S(1)}, bf16[4,32,768]{2,1,0:T(8,128)(2,1)S(1)}, u32[]{:S(2)}, u32[]{:S(2)}) collective-permute-start(bf16[4,32,768]{2,1,0:T(8,128)(2,1)S(1)} %hidden.1.refs_0_), channel_id=1, source_target_pairs={{0,7},{1,0},{2,1},{3,2},{4,3},{5,4},{6,5},{7,6},{8,15},{9,8},{10,9... | collective-permute-start | bytes 589832 | tf_op jit(solution)/shard_map/ppermute | solution.py:109
  93.3 3.6 %collective-permute-start.27 = (bf16[4,32,768]{2,1,0:T(8,128)(2,1)S(1)}, bf16[4,32,768]{2,1,0:T(8,128)(2,1)S(1)}, u32[]{:S(2)}, u32[]{:S(2)}) collective-permute-start(bf16[4,32,768]{2,1,0:T(8,128)(2,1)S(1)} %collective-permute-done.25.refs_4_), channel_id=1, source_target_pairs={{0,7},{1,0},{2,1},{3,2},{4,3},{5,4},{6,5},{7,6},{8,15},{9,8},{10,9... | collective-permute-start | bytes 589832 | tf_op jit(solution)/shard_map/ppermute | solution.py:109
  96.9 0.2 collective-permute-done.24.refs_3_
  97.1 2.0 %collective-permute-start.26 = (bf16[4,32,768]{2,1,0:T(8,128)(2,1)S(1)}, bf16[4,32,768]{2,1,0:T(8,128)(2,1)S(1)}, u32[]{:S(2)}, u32[]{:S(2)}) collective-permute-start(bf16[4,32,768]{2,1,0:T(8,128)(2,1)S(1)} %collective-permute-done.24.refs_3_), channel_id=1, source_target_pairs={{0,1},{1,2},{2,3},{3,4},{4,5},{5,6},{6,7},{7,0},{8,9},{9,10},{10,1... | collective-permute-start | bytes 589832 | tf_op jit(solution)/shard_map/ppermute | solution.py:109
  99.2 0.1 collective-permute-start.29
  99.3 2.4 %collective-permute-start.28 = (bf16[2,32,768]{2,1,0:T(8,128)(2,1)S(1)}, bf16[2,32,768]{2,1,0:T(8,128)(2,1)S(1)}, u32[]{:S(2)}, u32[]{:S(2)}) collective-permute-start(bf16[2,32,768]{2,1,0:T(8,128)(2,1)S(1)} %slice.18), channel_id=1, source_target_pairs={{0,2},{1,3},{2,4},{3,5},{4,6},{5,7},{6,0},{7,1},{8,10},{9,11},{10,... | collective-permute-start | bytes 294920 | tf_op jit(solution)/shard_map/ppermute | solution.py:109
  101.8 3.7 %mix.1 = (bf16[1024,1024]{1,0:T(8,128)(2,1)S(1)}, bf16[1024,1024]{1,0:T(8,128)(2,1)S(1)}, bf16[4,768,512]{2,1,0:T(8,128)(2,1)S(1)}) custom-call(s32[1]{0:T(128)} %bitcast.18.info, f32[16,8,128]{2,1,0:T(8,128)S(1)} %get-tuple-element.49.route, bf16[4,768,512]{2,1,0:T(8,128)(2,1)} %wd_hbm.1), custom_call_target="tpu_custom_call" | custom-call | tf_op jit(solution)/shard_map/mix/pallas_call | solution.py:480
  105.4 0.9 collective-permute-done.29.refs_8_
  106.4 4.2 %collective-permute-done.28.refs_7_ = bf16[2,32,768]{2,1,0:T(8,128)(2,1)S(1)} collective-permute-done((bf16[2,32,768]{2,1,0:T(8,128)(2,1)S(1)}, bf16[2,32,768]{2,1,0:T(8,128)(2,1)S(1)}, u32[]{:S(2)}, u32[]{:S(2)}) %collective-permute-start.28) | collective-permute-done | bytes 98336 | tf_op jit(solution)/shard_map/ppermute | solution.py:109
  110.5 3.6 %down.1 = (bf16[8,128,512]{2,1,0:T(8,128)(2,1)S(1)}, bf16[1024,512]{1,0:T(8,128)(2,1)S(1)}) custom-call(s32[9]{0:T(128)S(1)} %stack.142.info, bf16[4,32,768]{2,1,0:T(8,128)(2,1)S(1)} %hidden.1.refs_0_, bf16[4,32,768]{2,1,0:T(8,128)(2,1)S(1)} %collective-permute-done.22.refs_1_, bf16[4,32,768]{2,1,0:T(8,128)(2,1)S(1)} %collective-permute-done.23.refs_2_, ...), custom_call_target="tpu_custom_call" | custom-call | flops 2000000000 | bytes 6000000 | tf_op jit(solution)/shard_map/down/pallas_call | solution.py:489
  114.1 5.2 %collective-permute-start.30 = (bf16[8,128,512]{2,1,0:T(8,128)(2,1)S(1)}, bf16[8,128,512]{2,1,0:T(8,128)(2,1)S(1)}, u32[]{:S(2)}, u32[]{:S(2)}) collective-permute-start(bf16[8,128,512]{2,1,0:T(8,128)(2,1)S(1)} %get-tuple-element.72), channel_id=1, source_target_pairs={{0,8},{8,0},{16,24},{24,16},{32,40},{40,32},{48,56},{56,48},{64,72... | collective-permute-start | bytes 3145736 | tf_op jit(solution)/shard_map/ppermute | solution.py:113
  119.3 1.4 home.1
  120.7 0.9 collective-permute-done.30.swapped
  121.6 0.6 first.1
  122.2 0.1 collective-permute-start.31
  122.4 2.6 %collective-permute-start.32 = (bf16[192,512]{1,0:T(8,128)(2,1)S(1)}, bf16[192,512]{1,0:T(8,128)(2,1)S(1)}, u32[]{:S(2)}, u32[]{:S(2)}) collective-permute-start(bf16[192,512]{1,0:T(8,128)(2,1)S(1)} %get-tuple-element.74), channel_id=1, source_target_pairs={{0,112},{8,120},{16,0},{24,8},{32,16},{40,24},{48,32},{56,40},{64,... | collective-permute-start | bytes 589832 | tf_op jit(solution)/shard_map/ppermute | solution.py:109
  125.0 0.7 rest.1.total
  125.7 3.9 %collective-permute-done.31.right = bf16[192,512]{1,0:T(8,128)(2,1)S(1)} collective-permute-done((bf16[192,512]{1,0:T(8,128)(2,1)S(1)}, bf16[192,512]{1,0:T(8,128)(2,1)S(1)}, u32[]{:S(2)}, u32[]{:S(2)}) %collective-permute-start.31) | collective-permute-done | bytes 196640 | tf_op jit(solution)/shard_map/ppermute | solution.py:109
  129.7 2.9 %collective-permute-start.33 = (bf16[128,512]{1,0:T(8,128)(2,1)S(1)}, bf16[128,512]{1,0:T(8,128)(2,1)S(1)}, u32[]{:S(2)}, u32[]{:S(2)}) collective-permute-start(bf16[128,512]{1,0:T(8,128)(2,1)S(1)} %get-tuple-element.75), channel_id=1, source_target_pairs={{0,48},{8,56},{16,64},{24,72},{32,80},{40,88},{48,96},{56,104},{64... | collective-permute-start | bytes 393224 | tf_op jit(solution)/shard_map/ppermute | solution.py:109
  132.7 1.7 %collective-permute-start.34 = (bf16[128,512]{1,0:T(8,128)(2,1)S(1)}, bf16[128,512]{1,0:T(8,128)(2,1)S(1)}, u32[]{:S(2)}, u32[]{:S(2)}) collective-permute-start(bf16[128,512]{1,0:T(8,128)(2,1)S(1)} %get-tuple-element.76), channel_id=1, source_target_pairs={{0,80},{8,88},{16,96},{24,104},{32,112},{40,120},{48,0},{56,8},{64... | collective-permute-start | bytes 393224 | tf_op jit(solution)/shard_map/ppermute | solution.py:109
  134.3 2.7 %collective-permute-start.36 = (bf16[128,512]{1,0:T(8,128)(2,1)S(1)}, bf16[128,512]{1,0:T(8,128)(2,1)S(1)}, u32[]{:S(2)}, u32[]{:S(2)}) collective-permute-start(bf16[128,512]{1,0:T(8,128)(2,1)S(1)} %get-tuple-element.78), channel_id=1, source_target_pairs={{0,112},{8,120},{16,0},{24,8},{32,16},{40,24},{48,32},{56,40},{64,... | collective-permute-start | bytes 393224 | tf_op jit(solution)/shard_map/ppermute | solution.py:109
  137.0 6.9 %collective-permute-done.34.b = bf16[128,512]{1,0:T(8,128)(2,1)S(1)} collective-permute-done((bf16[128,512]{1,0:T(8,128)(2,1)S(1)}, bf16[128,512]{1,0:T(8,128)(2,1)S(1)}, u32[]{:S(2)}, u32[]{:S(2)}) %collective-permute-start.34) | collective-permute-done | bytes 131104 | tf_op jit(solution)/shard_map/ppermute | solution.py:109
  143.9 0.4 collective-permute-done.35.c
  144.4 0.3 collective-permute-done.36.d
  144.6 0.7 finish.1
  (49 shorter events, 1.1 us)
Async XLA Ops:
  2.0 21.2 %collective-permute-start.1 = (bf16[136,512]{1,0:T(8,128)(2,1)S(1)}, bf16[136,512]{1,0:T(8,128)(2,1)S(1)}, u32[]{:S(2)}, u32[]{:S(2)}) collective-permute-start(bf16[136,512]{1,0:T(8,128)(2,1)S(1)} %prepare.1.refs_0_), channel_id=1, source_target_pairs={{0,112},{8,120},{16,0},{24,8},{32,16},{40,24},{48,32},{56,40},{64,... | collective-permute-start | bytes 417800 | tf_op jit(solution)/shard_map/ppermute | solution.py:109
  14.5 8.7 %collective-permute-start = (bf16[136,512]{1,0:T(8,128)(2,1)S(1)}, bf16[136,512]{1,0:T(8,128)(2,1)S(1)}, u32[]{:S(2)}, u32[]{:S(2)}) collective-permute-start(bf16[136,512]{1,0:T(8,128)(2,1)S(1)} %prepare.1.refs_0_), channel_id=1, source_target_pairs={{0,16},{8,24},{16,32},{24,40},{32,48},{40,56},{48,64},{56,72},{64,... | collective-permute-start | bytes 417800 | tf_op jit(solution)/shard_map/ppermute | solution.py:109
  14.5 8.7 %collective-permute-start.3 = (bf16[136,512]{1,0:T(8,128)(2,1)S(1)}, bf16[136,512]{1,0:T(8,128)(2,1)S(1)}, u32[]{:S(2)}, u32[]{:S(2)}) collective-permute-start(bf16[136,512]{1,0:T(8,128)(2,1)S(1)} %prepare.1.refs_0_), channel_id=1, source_target_pairs={{0,80},{8,88},{16,96},{24,104},{32,112},{40,120},{48,0},{56,8},{64... | collective-permute-start | bytes 417800 | tf_op jit(solution)/shard_map/ppermute | solution.py:109
  15.4 11.8 %collective-permute-start.2 = (bf16[136,512]{1,0:T(8,128)(2,1)S(1)}, bf16[136,512]{1,0:T(8,128)(2,1)S(1)}, u32[]{:S(2)}, u32[]{:S(2)}) collective-permute-start(bf16[136,512]{1,0:T(8,128)(2,1)S(1)} %prepare.1.refs_0_), channel_id=1, source_target_pairs={{0,48},{8,56},{16,64},{24,72},{32,80},{40,88},{48,96},{56,104},{64... | collective-permute-start | bytes 417800 | tf_op jit(solution)/shard_map/ppermute | solution.py:109
  17.8 0.8 copy-start
  18.5 0.7 copy-start.1
  23.2 14.2 %collective-permute-start.5 = (bf16[208,512]{1,0:T(8,128)(2,1)S(1)}, bf16[208,512]{1,0:T(8,128)(2,1)S(1)}, u32[]{:S(2)}, u32[]{:S(2)}) collective-permute-start(bf16[208,512]{1,0:T(8,128)(2,1)S(1)} %pad_maximum_fusion.1), channel_id=1, source_target_pairs={{0,112},{8,120},{16,0},{24,8},{32,16},{40,24},{48,32},{56,40},{64,... | collective-permute-start | bytes 638984 | tf_op jit(solution)/shard_map/ppermute | solution.py:109
  27.3 10.2 %collective-permute-start.4 = (bf16[200,512]{1,0:T(8,128)(2,1)S(1)}, bf16[200,512]{1,0:T(8,128)(2,1)S(1)}, u32[]{:S(2)}, u32[]{:S(2)}) collective-permute-start(bf16[200,512]{1,0:T(8,128)(2,1)S(1)} %pad_maximum_fusion.2), channel_id=1, source_target_pairs={{0,16},{8,24},{16,32},{24,40},{32,48},{40,56},{48,64},{56,72},{64,... | collective-permute-start | bytes 614408 | tf_op jit(solution)/shard_map/ppermute | solution.py:109
  27.5 19.8 %collective-permute-start.6 = (bf16[680,512]{1,0:T(8,128)(2,1)S(1)}, bf16[680,512]{1,0:T(8,128)(2,1)S(1)}, u32[]{:S(2)}, u32[]{:S(2)}) collective-permute-start(bf16[680,512]{1,0:T(8,128)(2,1)S(1)} %bundle.1), channel_id=1, source_target_pairs={{0,8},{8,0},{16,24},{24,16},{32,40},{40,32},{48,56},{56,48},{64,72... | collective-permute-start | bytes 2088968 | tf_op jit(solution)/shard_map/ppermute | solution.py:113
  37.5 9.8 %collective-permute-start.7 = (bf16[408,512]{1,0:T(8,128)(2,1)S(1)}, bf16[408,512]{1,0:T(8,128)(2,1)S(1)}, u32[]{:S(2)}, u32[]{:S(2)}) collective-permute-start(bf16[408,512]{1,0:T(8,128)(2,1)S(1)} %pad_maximum_fusion), channel_id=1, source_target_pairs={{0,8},{8,0},{16,24},{24,16},{32,40},{40,32},{48,56},{56,48},{64,72... | collective-permute-start | bytes 1253384 | tf_op jit(solution)/shard_map/ppermute | solution.py:113
  51.4 9.1 %collective-permute-start.8 = (bf16[2,32,1536]{2,1,0:T(8,128)(2,1)S(1)}, bf16[2,32,1536]{2,1,0:T(8,128)(2,1)S(1)}, u32[]{:S(2)}, u32[]{:S(2)}) collective-permute-start(bf16[2,32,1536]{2,1,0:T(8,128)(2,1)S(1)} %get-tuple-element.53), channel_id=1, source_target_pairs={{0,1},{1,2},{2,3},{3,4},{4,5},{5,6},{6,7},{7,0},{8,9},{9,10},{10,1... | collective-permute-start | bytes 589832 | tf_op jit(solution)/shard_map/ppermute | solution.py:109
  51.5 9.2 %collective-permute-start.12 = (bf16[2,32,1536]{2,1,0:T(8,128)(2,1)S(1)}, bf16[2,32,1536]{2,1,0:T(8,128)(2,1)S(1)}, u32[]{:S(2)}, u32[]{:S(2)}) collective-permute-start(bf16[2,32,1536]{2,1,0:T(8,128)(2,1)S(1)} %get-tuple-element.57), channel_id=1, source_target_pairs={{0,7},{1,0},{2,1},{3,2},{4,3},{5,4},{6,5},{7,6},{8,15},{9,8},{10,9... | collective-permute-start | bytes 589832 | tf_op jit(solution)/shard_map/ppermute | solution.py:109
  57.7 7.2 %collective-permute-start.15 = (bf16[2,32,1536]{2,1,0:T(8,128)(2,1)S(1)}, bf16[2,32,1536]{2,1,0:T(8,128)(2,1)S(1)}, u32[]{:S(2)}, u32[]{:S(2)}) collective-permute-start(bf16[2,32,1536]{2,1,0:T(8,128)(2,1)S(1)} %get-tuple-element.62), channel_id=1, source_target_pairs={{0,1},{1,2},{2,3},{3,4},{4,5},{5,6},{6,7},{7,0},{8,9},{9,10},{10,1... | collective-permute-start | bytes 589832 | tf_op jit(solution)/shard_map/ppermute | solution.py:109
  57.9 7.2 %collective-permute-start.18 = (bf16[2,32,1536]{2,1,0:T(8,128)(2,1)S(1)}, bf16[2,32,1536]{2,1,0:T(8,128)(2,1)S(1)}, u32[]{:S(2)}, u32[]{:S(2)}) collective-permute-start(bf16[2,32,1536]{2,1,0:T(8,128)(2,1)S(1)} %get-tuple-element.65), channel_id=1, source_target_pairs={{0,7},{1,0},{2,1},{3,2},{4,3},{5,4},{6,5},{7,6},{8,15},{9,8},{10,9... | collective-permute-start | bytes 589832 | tf_op jit(solution)/shard_map/ppermute | solution.py:109
  60.6 8.6 %collective-permute-start.9 = (bf16[2,32,1536]{2,1,0:T(8,128)(2,1)S(1)}, bf16[2,32,1536]{2,1,0:T(8,128)(2,1)S(1)}, u32[]{:S(2)}, u32[]{:S(2)}) collective-permute-start(bf16[2,32,1536]{2,1,0:T(8,128)(2,1)S(1)} %add_convert_fusion.9), channel_id=1, source_target_pairs={{0,1},{1,2},{2,3},{3,4},{4,5},{5,6},{6,7},{7,0},{8,9},{9,10},{10,1... | collective-permute-start | bytes 589832 | tf_op jit(solution)/shard_map/ppermute | solution.py:109
  60.8 8.5 %collective-permute-start.13 = (bf16[2,32,1536]{2,1,0:T(8,128)(2,1)S(1)}, bf16[2,32,1536]{2,1,0:T(8,128)(2,1)S(1)}, u32[]{:S(2)}, u32[]{:S(2)}) collective-permute-start(bf16[2,32,1536]{2,1,0:T(8,128)(2,1)S(1)} %add_convert_fusion.6), channel_id=1, source_target_pairs={{0,7},{1,0},{2,1},{3,2},{4,3},{5,4},{6,5},{7,6},{8,15},{9,8},{10,9... | collective-permute-start | bytes 589832 | tf_op jit(solution)/shard_map/ppermute | solution.py:109
  65.0 7.7 %collective-permute-start.16 = (bf16[2,32,1536]{2,1,0:T(8,128)(2,1)S(1)}, bf16[2,32,1536]{2,1,0:T(8,128)(2,1)S(1)}, u32[]{:S(2)}, u32[]{:S(2)}) collective-permute-start(bf16[2,32,1536]{2,1,0:T(8,128)(2,1)S(1)} %add_convert_fusion.4), channel_id=1, source_target_pairs={{0,1},{1,2},{2,3},{3,4},{4,5},{5,6},{6,7},{7,0},{8,9},{9,10},{10,1... | collective-permute-start | bytes 589832 | tf_op jit(solution)/shard_map/ppermute | solution.py:109
  65.2 7.6 %collective-permute-start.19 = (bf16[2,32,1536]{2,1,0:T(8,128)(2,1)S(1)}, bf16[2,32,1536]{2,1,0:T(8,128)(2,1)S(1)}, u32[]{:S(2)}, u32[]{:S(2)}) collective-permute-start(bf16[2,32,1536]{2,1,0:T(8,128)(2,1)S(1)} %add_convert_fusion.2), channel_id=1, source_target_pairs={{0,7},{1,0},{2,1},{3,2},{4,3},{5,4},{6,5},{7,6},{8,15},{9,8},{10,9... | collective-permute-start | bytes 589832 | tf_op jit(solution)/shard_map/ppermute | solution.py:109
  69.2 7.7 %collective-permute-start.10 = (bf16[2,32,1536]{2,1,0:T(8,128)(2,1)S(1)}, bf16[2,32,1536]{2,1,0:T(8,128)(2,1)S(1)}, u32[]{:S(2)}, u32[]{:S(2)}) collective-permute-start(bf16[2,32,1536]{2,1,0:T(8,128)(2,1)S(1)} %add_convert_fusion.8), channel_id=1, source_target_pairs={{0,1},{1,2},{2,3},{3,4},{4,5},{5,6},{6,7},{7,0},{8,9},{9,10},{10,1... | collective-permute-start | bytes 589832 | tf_op jit(solution)/shard_map/ppermute | solution.py:109
  69.4 14.0 %collective-permute-start.14 = (bf16[2,32,1536]{2,1,0:T(8,128)(2,1)S(1)}, bf16[2,32,1536]{2,1,0:T(8,128)(2,1)S(1)}, u32[]{:S(2)}, u32[]{:S(2)}) collective-permute-start(bf16[2,32,1536]{2,1,0:T(8,128)(2,1)S(1)} %add_convert_fusion.5), channel_id=1, source_target_pairs={{0,7},{1,0},{2,1},{3,2},{4,3},{5,4},{6,5},{7,6},{8,15},{9,8},{10,9... | collective-permute-start | bytes 589832 | tf_op jit(solution)/shard_map/ppermute | solution.py:109
  72.7 10.8 %collective-permute-start.17 = (bf16[2,32,1536]{2,1,0:T(8,128)(2,1)S(1)}, bf16[2,32,1536]{2,1,0:T(8,128)(2,1)S(1)}, u32[]{:S(2)}, u32[]{:S(2)}) collective-permute-start(bf16[2,32,1536]{2,1,0:T(8,128)(2,1)S(1)} %add_convert_fusion.3), channel_id=1, source_target_pairs={{0,1},{1,2},{2,3},{3,4},{4,5},{5,6},{6,7},{7,0},{8,9},{9,10},{10,1... | collective-permute-start | bytes 589832 | tf_op jit(solution)/shard_map/ppermute | solution.py:109
  72.9 7.2 %collective-permute-start.20 = (bf16[2,32,1536]{2,1,0:T(8,128)(2,1)S(1)}, bf16[2,32,1536]{2,1,0:T(8,128)(2,1)S(1)}, u32[]{:S(2)}, u32[]{:S(2)}) collective-permute-start(bf16[2,32,1536]{2,1,0:T(8,128)(2,1)S(1)} %add_convert_fusion.1), channel_id=1, source_target_pairs={{0,7},{1,0},{2,1},{3,2},{4,3},{5,4},{6,5},{7,6},{8,15},{9,8},{10,9... | collective-permute-start | bytes 589832 | tf_op jit(solution)/shard_map/ppermute | solution.py:109
  76.9 7.8 %collective-permute-start.11 = (bf16[2,32,1536]{2,1,0:T(8,128)(2,1)S(1)}, bf16[2,32,1536]{2,1,0:T(8,128)(2,1)S(1)}, u32[]{:S(2)}, u32[]{:S(2)}) collective-permute-start(bf16[2,32,1536]{2,1,0:T(8,128)(2,1)S(1)} %add_convert_fusion.7), channel_id=1, source_target_pairs={{0,1},{1,2},{2,3},{3,4},{4,5},{5,6},{6,7},{7,0},{8,9},{9,10},{10,1... | collective-permute-start | bytes 589832 | tf_op jit(solution)/shard_map/ppermute | solution.py:109
  80.2 5.9 %collective-permute-start.21 = (bf16[2,32,1536]{2,1,0:T(8,128)(2,1)S(1)}, bf16[2,32,1536]{2,1,0:T(8,128)(2,1)S(1)}, u32[]{:S(2)}, u32[]{:S(2)}) collective-permute-start(bf16[2,32,1536]{2,1,0:T(8,128)(2,1)S(1)} %add_convert_fusion), channel_id=1, source_target_pairs={{0,7},{1,0},{2,1},{3,2},{4,3},{5,4},{6,5},{7,6},{8,15},{9,8},{10,9... | collective-permute-start | bytes 589832 | tf_op jit(solution)/shard_map/ppermute | solution.py:109
  86.3 7.0 %collective-permute-start.25 = (bf16[4,32,768]{2,1,0:T(8,128)(2,1)S(1)}, bf16[4,32,768]{2,1,0:T(8,128)(2,1)S(1)}, u32[]{:S(2)}, u32[]{:S(2)}) collective-permute-start(bf16[4,32,768]{2,1,0:T(8,128)(2,1)S(1)} %hidden.1.refs_0_), channel_id=1, source_target_pairs={{0,6},{1,7},{2,0},{3,1},{4,2},{5,3},{6,4},{7,5},{8,14},{9,15},{10,... | collective-permute-start | bytes 589832 | tf_op jit(solution)/shard_map/ppermute | solution.py:109
  88.3 8.8 %collective-permute-start.24 = (bf16[4,32,768]{2,1,0:T(8,128)(2,1)S(1)}, bf16[4,32,768]{2,1,0:T(8,128)(2,1)S(1)}, u32[]{:S(2)}, u32[]{:S(2)}) collective-permute-start(bf16[4,32,768]{2,1,0:T(8,128)(2,1)S(1)} %hidden.1.refs_0_), channel_id=1, source_target_pairs={{0,2},{1,3},{2,4},{3,5},{4,6},{5,7},{6,0},{7,1},{8,10},{9,11},{10,... | collective-permute-start | bytes 589832 | tf_op jit(solution)/shard_map/ppermute | solution.py:109
  89.0 10.3 %collective-permute-start.23 = (bf16[4,32,768]{2,1,0:T(8,128)(2,1)S(1)}, bf16[4,32,768]{2,1,0:T(8,128)(2,1)S(1)}, u32[]{:S(2)}, u32[]{:S(2)}) collective-permute-start(bf16[4,32,768]{2,1,0:T(8,128)(2,1)S(1)} %hidden.1.refs_0_), channel_id=1, source_target_pairs={{0,7},{1,0},{2,1},{3,2},{4,3},{5,4},{6,5},{7,6},{8,15},{9,8},{10,9... | collective-permute-start | bytes 589832 | tf_op jit(solution)/shard_map/ppermute | solution.py:109
  93.3 12.1 %collective-permute-start.22 = (bf16[4,32,768]{2,1,0:T(8,128)(2,1)S(1)}, bf16[4,32,768]{2,1,0:T(8,128)(2,1)S(1)}, u32[]{:S(2)}, u32[]{:S(2)}) collective-permute-start(bf16[4,32,768]{2,1,0:T(8,128)(2,1)S(1)} %hidden.1.refs_0_), channel_id=1, source_target_pairs={{0,1},{1,2},{2,3},{3,4},{4,5},{5,6},{6,7},{7,0},{8,9},{9,10},{10,1... | collective-permute-start | bytes 589832 | tf_op jit(solution)/shard_map/ppermute | solution.py:109
  93.3 17.2 %collective-permute-start.27 = (bf16[4,32,768]{2,1,0:T(8,128)(2,1)S(1)}, bf16[4,32,768]{2,1,0:T(8,128)(2,1)S(1)}, u32[]{:S(2)}, u32[]{:S(2)}) collective-permute-start(bf16[4,32,768]{2,1,0:T(8,128)(2,1)S(1)} %collective-permute-done.25.refs_4_), channel_id=1, source_target_pairs={{0,7},{1,0},{2,1},{3,2},{4,3},{5,4},{6,5},{7,6},{8,15},{9,8},{10,9... | collective-permute-start | bytes 589832 | tf_op jit(solution)/shard_map/ppermute | solution.py:109
  97.1 13.4 %collective-permute-start.26 = (bf16[4,32,768]{2,1,0:T(8,128)(2,1)S(1)}, bf16[4,32,768]{2,1,0:T(8,128)(2,1)S(1)}, u32[]{:S(2)}, u32[]{:S(2)}) collective-permute-start(bf16[4,32,768]{2,1,0:T(8,128)(2,1)S(1)} %collective-permute-done.24.refs_3_), channel_id=1, source_target_pairs={{0,1},{1,2},{2,3},{3,4},{4,5},{5,6},{6,7},{7,0},{8,9},{9,10},{10,1... | collective-permute-start | bytes 589832 | tf_op jit(solution)/shard_map/ppermute | solution.py:109
  99.2 7.2 %collective-permute-start.29 = (bf16[2,32,768]{2,1,0:T(8,128)(2,1)S(1)}, bf16[2,32,768]{2,1,0:T(8,128)(2,1)S(1)}, u32[]{:S(2)}, u32[]{:S(2)}) collective-permute-start(bf16[2,32,768]{2,1,0:T(8,128)(2,1)S(1)} %slice.19), channel_id=1, source_target_pairs={{0,6},{1,7},{2,0},{3,1},{4,2},{5,3},{6,4},{7,5},{8,14},{9,15},{10,... | collective-permute-start | bytes 294920 | tf_op jit(solution)/shard_map/ppermute | solution.py:109
  99.3 11.2 %collective-permute-start.28 = (bf16[2,32,768]{2,1,0:T(8,128)(2,1)S(1)}, bf16[2,32,768]{2,1,0:T(8,128)(2,1)S(1)}, u32[]{:S(2)}, u32[]{:S(2)}) collective-permute-start(bf16[2,32,768]{2,1,0:T(8,128)(2,1)S(1)} %slice.18), channel_id=1, source_target_pairs={{0,2},{1,3},{2,4},{3,5},{4,6},{5,7},{6,0},{7,1},{8,10},{9,11},{10,... | collective-permute-start | bytes 294920 | tf_op jit(solution)/shard_map/ppermute | solution.py:109
  114.1 7.5 %collective-permute-start.30 = (bf16[8,128,512]{2,1,0:T(8,128)(2,1)S(1)}, bf16[8,128,512]{2,1,0:T(8,128)(2,1)S(1)}, u32[]{:S(2)}, u32[]{:S(2)}) collective-permute-start(bf16[8,128,512]{2,1,0:T(8,128)(2,1)S(1)} %get-tuple-element.72), channel_id=1, source_target_pairs={{0,8},{8,0},{16,24},{24,16},{32,40},{40,32},{48,56},{56,48},{64,72... | collective-permute-start | bytes 3145736 | tf_op jit(solution)/shard_map/ppermute | solution.py:113
  122.2 7.4 %collective-permute-start.31 = (bf16[192,512]{1,0:T(8,128)(2,1)S(1)}, bf16[192,512]{1,0:T(8,128)(2,1)S(1)}, u32[]{:S(2)}, u32[]{:S(2)}) collective-permute-start(bf16[192,512]{1,0:T(8,128)(2,1)S(1)} %get-tuple-element.73), channel_id=1, source_target_pairs={{0,16},{8,24},{16,32},{24,40},{32,48},{40,56},{48,64},{56,72},{64,... | collective-permute-start | bytes 589832 | tf_op jit(solution)/shard_map/ppermute | solution.py:109
  122.4 7.3 %collective-permute-start.32 = (bf16[192,512]{1,0:T(8,128)(2,1)S(1)}, bf16[192,512]{1,0:T(8,128)(2,1)S(1)}, u32[]{:S(2)}, u32[]{:S(2)}) collective-permute-start(bf16[192,512]{1,0:T(8,128)(2,1)S(1)} %get-tuple-element.74), channel_id=1, source_target_pairs={{0,112},{8,120},{16,0},{24,8},{32,16},{40,24},{48,32},{56,40},{64,... | collective-permute-start | bytes 589832 | tf_op jit(solution)/shard_map/ppermute | solution.py:109
  129.7 7.3 %collective-permute-start.33 = (bf16[128,512]{1,0:T(8,128)(2,1)S(1)}, bf16[128,512]{1,0:T(8,128)(2,1)S(1)}, u32[]{:S(2)}, u32[]{:S(2)}) collective-permute-start(bf16[128,512]{1,0:T(8,128)(2,1)S(1)} %get-tuple-element.75), channel_id=1, source_target_pairs={{0,48},{8,56},{16,64},{24,72},{32,80},{40,88},{48,96},{56,104},{64... | collective-permute-start | bytes 393224 | tf_op jit(solution)/shard_map/ppermute | solution.py:109
  132.7 11.2 %collective-permute-start.34 = (bf16[128,512]{1,0:T(8,128)(2,1)S(1)}, bf16[128,512]{1,0:T(8,128)(2,1)S(1)}, u32[]{:S(2)}, u32[]{:S(2)}) collective-permute-start(bf16[128,512]{1,0:T(8,128)(2,1)S(1)} %get-tuple-element.76), channel_id=1, source_target_pairs={{0,80},{8,88},{16,96},{24,104},{32,112},{40,120},{48,0},{56,8},{64... | collective-permute-start | bytes 393224 | tf_op jit(solution)/shard_map/ppermute | solution.py:109
  134.3 10.0 %collective-permute-start.35 = (bf16[128,512]{1,0:T(8,128)(2,1)S(1)}, bf16[128,512]{1,0:T(8,128)(2,1)S(1)}, u32[]{:S(2)}, u32[]{:S(2)}) collective-permute-start(bf16[128,512]{1,0:T(8,128)(2,1)S(1)} %get-tuple-element.77), channel_id=1, source_target_pairs={{0,16},{8,24},{16,32},{24,40},{32,48},{40,56},{48,64},{56,72},{64,... | collective-permute-start | bytes 393224 | tf_op jit(solution)/shard_map/ppermute | solution.py:109
  134.3 10.3 %collective-permute-start.36 = (bf16[128,512]{1,0:T(8,128)(2,1)S(1)}, bf16[128,512]{1,0:T(8,128)(2,1)S(1)}, u32[]{:S(2)}, u32[]{:S(2)}) collective-permute-start(bf16[128,512]{1,0:T(8,128)(2,1)S(1)} %get-tuple-element.78), channel_id=1, source_target_pairs={{0,112},{8,120},{16,0},{24,8},{32,16},{40,24},{48,32},{56,40},{64,... | collective-permute-start | bytes 393224 | tf_op jit(solution)/shard_map/ppermute | solution.py:109

commit v3 on v2

--- a/solution.py
+++ b/solution.py
@@ -17,43 +17,36 @@
 SMALL = {"compiler_params": pltpu.CompilerParams(vmem_limit_bytes=2 << 20)}
 
 
-def both_cores(home, swapped, at):
-    return home[at].astype(F32) + swapped[at].astype(F32)
-
-
-def first_kernel(info, home, swapped, right, left):
-    count, rows, _ = home.shape
-    mid = rows // 2
-    right[0:rows, :] = both_cores(home, swapped, info[2]).astype(BF16)
-    left[0:rows, :] = both_cores(home, swapped, info[count - 2]).astype(BF16)
-    across = both_cores(home, swapped, info[count // 2]).astype(BF16)
-    right[rows:, :] = across[0:mid]
-    left[rows:, :] = across[mid:]
-
-
-def rest_kernel(info, home, swapped, total):
-    count = home.shape[0]
-    for i, k in enumerate((0, 1, count - 1, 3, count - 3)):
-        total[i] = both_cores(home, swapped, info[k]).astype(BF16)
-
-
-def relay_kernel(total, right, left, far_right, far_left, near_right, near_left):
-    _, rows, _ = total.shape
-    mid = rows // 2
-    far_right[0:mid, :] = (total[3, 0:mid].astype(F32) + right[rows:, :].astype(F32)).astype(BF16)
-    far_right[mid:, :] = total[3, mid:]
-    far_left[0:mid, :] = total[4, 0:mid]
-    far_left[mid:, :] = (total[4, mid:].astype(F32) + left[rows:, :].astype(F32)).astype(BF16)
-    near_right[...] = (total[1].astype(F32) + right[0:rows, :].astype(F32)).astype(BF16)
-    near_left[...] = (total[2].astype(F32) + left[0:rows, :].astype(F32)).astype(BF16)
-
-
-def finish_kernel(total, a, b, c, d, out):
-    out[...] = (
-        total[0].astype(F32)
-        + (a[...].astype(F32) + b[...].astype(F32))
-        + (c[...].astype(F32) + d[...].astype(F32))
+def both_cores(home, swapped, i):
+    return home[i].astype(F32) + swapped[i].astype(F32)
+
+
+def first_kernel(home, swapped, three, four, one):
+    rows = home.shape[1]
+    four[...] = both_cores(home, swapped, 6).astype(BF16)
+    for c in range(2):
+        three[c * rows : (c + 1) * rows, :] = both_cores(home, swapped, 4 + c).astype(BF16)
+        one[c * rows : (c + 1) * rows, :] = both_cores(home, swapped, c).astype(BF16)
+
+
+def relay_kernel(home, swapped, three, four, two):
+    rows = home.shape[1]
+    came = three[...].astype(F32)
+    two[0:rows, :] = (
+        both_cores(home, swapped, 2) + (came[0:rows] + four[...].astype(F32))
     ).astype(BF16)
+    two[rows:, :] = (both_cores(home, swapped, 3) + came[rows:]).astype(BF16)
+
+
+def cross_kernel(home, swapped, one, two, own, other):
+    rows = home.shape[1]
+    total = one[...].astype(F32) + two[...].astype(F32)
+    other[...] = total[rows:].astype(BF16)
+    own[...] = total[0:rows] + both_cores(home, swapped, 7)
+
+
+def finish_kernel(own, came, out):
+    out[...] = (own[...] + came[...].astype(F32)).astype(BF16)
 
 
 def in_hbm(value):
@@ -100,13 +93,19 @@
             flops=10**9, bytes_accessed=3 * 10**6, transcendentals=4 * 10**5
         ),
         name="attention",
-    )(lengths, query, in_hbm(cache_k), in_hbm(cache_v))
+    )(lengths, in_hbm(query), in_hbm(cache_k), in_hbm(cache_v))
     return out.reshape(count, heads * size)
 
 
 def shift(value, axis, step):
     count = lax.axis_size(axis)
     return lax.ppermute(value, axis, [(i, (i + step) % count) for i in range(count)])
+
+
+def both_ways(value, places):
+    count = lax.axis_size("attn")
+    pairs = [(i, (i + (-2 if i % 2 else 2) * places) % count) for i in range(count)]
+    return lax.ppermute(value, "attn", pairs)
 
 
 def swap_cores(value):
@@ -183,8 +182,8 @@
         copy.wait()
 
 
-def pack_kernel(plan, half, local, n_dest, info, *refs):
-    n_ops = 1 + max(op for p in plan for op, _ in p)
+def pack_kernel(plan, local, n_dest, info, *refs):
+    n_ops = 1 + max(op for op, _ in plan)
     ops = refs[:n_ops]
     wg, wu = refs[n_ops : n_ops + 2]
     out = refs[n_ops + 2 : n_ops + 2 + n_dest]
@@ -193,17 +192,10 @@
     rows = tok.shape[0] // n_blocks
     capacity = n_dest * out[0].shape[1]
 
-    for i, p in enumerate(plan):
+    for i, (op, r0) in enumerate(plan):
         at = pl.ds(pl.multiple_of(info[1 + i] * rows, rows), rows)
-        op, r0 = p[0]
-        if len(p) == 1:
-            tok[i * rows : (i + 1) * rows, :] = ops[op][r0 : r0 + rows, :]
-            low = r0 + rows
-        else:
-            tok[i * rows : i * rows + half, :] = ops[op][r0 : r0 + half, :]
-            op, r0 = p[1]
-            low = r0 + rows - half
-            tok[i * rows + half : (i + 1) * rows, :] = ops[op][r0:low, :]
+        low = r0 + rows
+        tok[i * rows : (i + 1) * rows, :] = ops[op][r0:low, :]
         meta[0:8, at] = ops[op][low : low + META, 0:rows].astype(F32)
         meta[8:16, at] = ops[op][low : low + META, rows : 2 * rows].astype(F32)
     ids = meta[0:8, :]
@@ -256,42 +248,38 @@
         row += total.shape[0]
 
 
-def mix_kernel(info, route, wd_hbm, away, home, wd, sem):
+def mix_kernel(info, route, wd_hbm, mix, wd, sem):
     copy = pltpu.make_async_copy(wd_hbm, wd, sem)
     copy.start()
     n_blocks, _, rows = route.shape
     local = wd.shape[0]
-    capacity = away.shape[1] // local
+    capacity = mix.shape[1] // local
     r = lax.broadcasted_iota(jnp.int32, (rows, rows), 0)
     c = lax.broadcasted_iota(jnp.int32, (rows, rows), 1)
     eye = jnp.where(r == c, 1.0, 0.0).astype(BF16)
     col_id = lax.broadcasted_iota(jnp.int32, (rows, capacity), 1).astype(F32)
 
-    def block(d, carry):
-        at = pl.ds(pl.multiple_of(d * rows, rows), rows)
-        for side, ref in ((1 - info[0], away), (info[0], home)):
-            rt = lax.dot_general(
-                eye,
-                route[2 * d + side].astype(BF16),
-                (((1,), (1,)), ((), ())),
-                preferred_element_type=F32,
-            )
-            for j in range(local):
-                ref[at, j * capacity : (j + 1) * capacity] = jnp.where(
-                    col_id == rt[:, j : j + 1], rt[:, local + j : local + j + 1], 0.0
-                ).astype(BF16)
+    def block(i, carry):
+        at = pl.ds(pl.multiple_of(i * rows, rows), rows)
+        rt = lax.dot_general(
+            eye, route[info[i]].astype(BF16), (((1,), (1,)), ((), ())), preferred_element_type=F32
+        )
+        for j in range(local):
+            mix[at, j * capacity : (j + 1) * capacity] = jnp.where(
+                col_id == rt[:, j : j + 1], rt[:, local + j : local + j + 1], 0.0
+            ).astype(BF16)
         return carry
 
-    lax.fori_loop(0, n_blocks // 2, block, 0)
+    lax.fori_loop(0, n_blocks, block, 0, unroll=2)
     copy.wait()
 
 
-def mix_rows(mix, res, ref):
+def mix_rows(first, mix, res, ref):
     n_dest, rows, feat = ref.shape
     group = 4
 
     def some(g, carry):
-        at = pl.ds(pl.multiple_of(g * group * rows, group * rows), group * rows)
+        at = pl.ds(pl.multiple_of(first + g * group * rows, group * rows), group * rows)
         got = jnp.dot(mix[at, :], res[...], preferred_element_type=F32).astype(BF16)
         ref[pl.ds(g * group, group)] = got.reshape(group, rows, feat)
         return carry
@@ -317,11 +305,11 @@
         return carry
 
     lax.fori_loop(0, local, expert, 0)
-    mix_rows(mix, res, away)
+    mix_rows(0, mix, res, away)
 
 
 def home_kernel(mix, res, home):
-    mix_rows(mix, res, home)
+    mix_rows(mix.shape[0] // 2, mix, res, home)
 
 
 def scatter_sum(pieces, axis):
@@ -361,24 +349,29 @@
     far = chips // 2
     dest_rows = capacity // n_expert
 
-    y_at = [lax.rem(y + k, chips) for k in range(chips)]
     x_at = [lax.rem(col + k, n_expert) for k in range(n_expert)]
-    offsets = [0, -1, 1, -3, 3, -2, 2, far]
-    pack_info = [local * me]
-    for flip in (0, 1):
-        pack_info += [2 * y_at[off % chips] + (core ^ flip) for off in offsets]
-    row_at = [core] + [x * dest_rows for x in x_at]
+    ahead = jnp.where(core == 0, 1, -1)
+
+    def token_block(places, flip):
+        return 2 * lax.rem(y + places * ahead + chips, chips) + (core ^ flip)
+
+    order = [(0, 0), (0, 1)]
+    order += [(-k, flip) for k in (1, 2, 3) for flip in (0, 1)] + [(far, 0)]
+    order += [(k, flip) for k in (1, 2, 3) for flip in (1, 0)] + [(far, 1)]
+    pack_info = [local * me] + [token_block(*at) for at in order]
+    onward = [(k, flip) for k in (1, 2, 3) for flip in (0, 1)] + [(far, 0), (0, 0)]
+    mix_info = [token_block(-k, 1 - flip) for k, flip in onward]
+    mix_info += [token_block(k, flip) for k, flip in onward]
+    row_at = [x * dest_rows for x in x_at]
     pack_info.append(col * dest_rows)
     pack_info = jnp.stack(pack_info).astype(jnp.int32)
+    mix_info = jnp.stack(mix_info).astype(jnp.int32)
     row_at = jnp.stack(row_at).astype(jnp.int32)
-    core_at = core.reshape(1).astype(jnp.int32)
-    y_info = jnp.stack(y_at).astype(jnp.int32)
-    tokens, pack_info, row_at, core_at, y_info = lax.optimization_barrier(
-        (tokens, pack_info, row_at, core_at, y_info)
+    tokens, pack_info, mix_info, row_at = lax.optimization_barrier(
+        (tokens, pack_info, mix_info, row_at)
     )
 
     height = rows + META
-    half = rows // 2
     block = pl.pallas_call(
         prepare_kernel,
         out_shape=jax.ShapeDtypeStruct((height, feat), BF16),
@@ -394,26 +387,20 @@
     )(in_hbm(tokens), in_hbm(expert_ids.T), in_hbm(gate_weight.T))
     attn_out = grouped_attention(query, cache_k, cache_v, lengths)
 
-    away3 = [shift(block, "attn", 6), shift(block, "attn", -6)]
-    near = [shift(block, "attn", 2), shift(block, "attn", -2)]
-    *near, attn_out = lax.optimization_barrier((*near, attn_out))
-    right = shift(jnp.concatenate([near[0], away3[0][:half]], axis=0), "attn", 2)
-    left = shift(jnp.concatenate([near[1], away3[1][half:]], axis=0), "attn", -2)
-    bundle = pl.pallas_call(
+    pair = pl.pallas_call(
         bundle_kernel,
-        out_shape=jax.ShapeDtypeStruct((5 * height, feat), BF16),
-        in_specs=[VMEM_SPEC] * 5,
+        out_shape=jax.ShapeDtypeStruct((2 * height, feat), BF16),
+        in_specs=[VMEM_SPEC] * 2,
         out_specs=VMEM_SPEC,
-        name="bundle",
+        name="pair",
         **SMALL,
-    )(*map(in_vmem, (block, *near, *away3)))
-    swap_first = swap_cores(bundle)
-    swap_last = swap_cores(jnp.concatenate([right, left], axis=0))
-    operands = [block, *near, *away3, right, left, swap_first, swap_last]
-    plan = [((i, 0),) for i in range(7)] + [((5, height), (6, height))]
-    plan += [((7, i * height),) for i in range(5)]
-    second = height + half
-    plan += [((8, 0),), ((8, second),), ((8, height), (8, second + height))]
+    )(*map(in_vmem, (block, swap_cores(block))))
+    two, one = both_ways(pair, 2), both_ways(pair, 1)
+    four, three = both_ways(two[:height], 2), both_ways(two, 1)
+    operands = [pair, one, two, three, four]
+    operands += [swap_cores(one), swap_cores(two), swap_cores(three), swap_cores(four)]
+    pairs = [((i, 0), (i, height)) for i in range(8) if i != 4]
+    plan = [at for p in pairs[:4] for at in p] + [(4, 0)] + [at for p in pairs[4:] for at in p] + [(8, 0)]
 
     cut = local // 2
     pack_scratch = [
@@ -432,7 +419,7 @@
     part_shapes = (jax.ShapeDtypeStruct((cut, dest_rows, 2 * ff), BF16),) * n_expert
     pack_cost = pl.CostEstimate(flops=2 * 10**9, bytes_accessed=6 * 10**6, transcendentals=0)
     *parts_a, route, tok = pl.pallas_call(
-        functools.partial(pack_kernel, plan, half, local, n_expert),
+        functools.partial(pack_kernel, plan, local, n_expert),
         out_shape=(
             *part_shapes,
             jax.ShapeDtypeStruct((attn_count, 8, rows), F32),
@@ -474,18 +461,20 @@
     r4, l4 = shift(r2[:cut], "expert", 2), shift(l2[cut:], "expert", -2)
     r3, l3 = shift(r2, "expert", 1), shift(l2, "expert", -1)
     pieces_in = [hidden, r1, l1, r2, l2, r3, l3, r4, l4]
-    where = [(0, 1 + k % n_expert) for k in (0, -1, 1, -2, 2, -3, 3, -4)] + [(cut, 1 + 4)]
-
-    mix_shape = jax.ShapeDtypeStruct((chips * rows, local * capacity), BF16)
-    mix_away, mix_home, wd = pl.pallas_call(
+    where = [(0, k % n_expert) for k in (0, -1, 1, -2, 2, -3, 3, -4)] + [(cut, n_expert // 2)]
+
+    mix, wd = pl.pallas_call(
         mix_kernel,
-        out_shape=(mix_shape, mix_shape, jax.ShapeDtypeStruct(w_down.shape, BF16)),
+        out_shape=(
+            jax.ShapeDtypeStruct((attn_count * rows, local * capacity), BF16),
+            jax.ShapeDtypeStruct(w_down.shape, BF16),
+        ),
         in_specs=[SMEM_SPEC, VMEM_SPEC, HBM_SPEC],
-        out_specs=(VMEM_SPEC,) * 3,
+        out_specs=(VMEM_SPEC,) * 2,
         scratch_shapes=[pltpu.SemaphoreType.DMA],
         name="mix",
         **SMALL,
-    )(core_at, in_vmem(route), in_hbm(w_down))
+    )(mix_info, in_vmem(route), in_hbm(w_down))
     away, res = pl.pallas_call(
         functools.partial(down_kernel, where),
         out_shape=(
@@ -498,7 +487,7 @@
         compiler_params=pltpu.CompilerParams(vmem_limit_bytes=4 << 20),
         cost_estimate=pl.CostEstimate(flops=2 * 10**9, bytes_accessed=6 * 10**6, transcendentals=0),
         name="down",
-    )(row_at, *map(in_vmem, pieces_in), in_vmem(wd), in_vmem(mix_away))
+    )(row_at, *map(in_vmem, pieces_in), in_vmem(wd), in_vmem(mix))
     swapped = swap_cores(away)
     home = pl.pallas_call(
         home_kernel,
@@ -508,49 +497,26 @@
         cost_estimate=pl.CostEstimate(flops=10**9, bytes_accessed=2 * 10**6, transcendentals=0),
         name="home",
         **SMALL,
-    )(in_vmem(mix_home), in_vmem(res))
-
-    block_shape = jax.ShapeDtypeStruct((rows, feat), BF16)
-    long_shape = jax.ShapeDtypeStruct((rows + rows // 2, feat), BF16)
-    right, left = pl.pallas_call(
-        first_kernel,
-        out_shape=(long_shape, long_shape),
-        in_specs=[SMEM_SPEC, VMEM_SPEC, VMEM_SPEC],
-        out_specs=(VMEM_SPEC,) * 2,
-        name="first",
-        **SMALL,
-    )(y_info, in_vmem(home), in_vmem(swapped))
-    right, left = shift(right, "attn", 2), shift(left, "attn", -2)
-    total = pl.pallas_call(
-        rest_kernel,
-        out_shape=jax.ShapeDtypeStruct((5, rows, feat), BF16),
-        in_specs=[SMEM_SPEC, VMEM_SPEC, VMEM_SPEC],
-        out_specs=VMEM_SPEC,
-        name="rest",
-        **SMALL,
-    )(y_info, in_vmem(home), in_vmem(swapped))
-    far_right, far_left, near_right, near_left = pl.pallas_call(
-        relay_kernel,
-        out_shape=(block_shape,) * 4,
-        in_specs=[VMEM_SPEC] * 3,
-        out_specs=(VMEM_SPEC,) * 4,
-        name="relay",
-        **SMALL,
-    )(in_vmem(total), in_vmem(right), in_vmem(left))
-    last = [
-        shift(far_right, "attn", 6),
-        shift(far_left, "attn", -6),
-        shift(near_right, "attn", 2),
-        shift(near_left, "attn", -2),
-    ]
-    moe_out = pl.pallas_call(
-        finish_kernel,
-        out_shape=block_shape,
-        in_specs=[VMEM_SPEC] * 5,
-        out_specs=VMEM_SPEC,
-        name="finish",
-        **SMALL,
-    )(in_vmem(total), *map(in_vmem, last))
+    )(in_vmem(mix), in_vmem(res))
+
+    def small_call(kernel, shapes, *operands):
+        out = pl.pallas_call(
+            kernel,
+            out_shape=tuple(jax.ShapeDtypeStruct((r, feat), t) for r, t in shapes),
+            in_specs=[VMEM_SPEC] * len(operands),
+            out_specs=(VMEM_SPEC,) * len(shapes),
+            **SMALL,
+        )(*map(in_vmem, operands))
+        return out if len(shapes) > 1 else out[0]
+
+    twice = (2 * rows, BF16)
+    once = (rows, BF16)
+    three, four, one = small_call(first_kernel, (twice, once, twice), home, swapped)
+    four, three, one = both_ways(four, 2), both_ways(three, 1), both_ways(one, 1)
+    two = small_call(relay_kernel, (twice,), home, swapped, three, four)
+    two = both_ways(two, 2)
+    own, other = small_call(cross_kernel, ((rows, F32), once), home, swapped, one, two)
+    moe_out = small_call(finish_kernel, (once,), own, swap_cores(other))
     return (moe_out, attn_out)
 
 

time: 147 us -> 146 us (level); the launches traced: 145 us -> 146 us
  waiting for transfers between devices: 27.7 us -> 55.1 us
  starting transfers between devices: 87.8 us -> 63.4 us
    ppermute x34 -> x22, starting transfers between devices: 65.7 us -> 22.6 us  [shift(): lax.ppermute(value, axis, [(i, (i + step) % count) for i in range(count)])]
    ppermute x0 -> x8, waiting for transfers between devices: none -> 25.2 us  [both_ways(): return lax.ppermute(value, 'attn', pairs)]
    ppermute x3 -> x7, starting transfers between devices: 22.1 us -> 37.5 us  [swap_cores(): lax.ppermute(value, 'attn', [(i, i ^ 1) for i in range(lax.axis_size('att...]
    ppermute x0 -> x8, starting transfers between devices: none -> 3.2 us  [both_ways(): return lax.ppermute(value, 'attn', pairs)]
    ppermute x34 -> x22, waiting for transfers between devices: 26.8 us -> 28 us  [shift(): lax.ppermute(value, axis, [(i, (i + step) % count) for i in range(count)])]
  transfers between devices with their start and end apart: 37 -> 37, of which waited for: 15 -> 19; matrix products, arithmetic and copies ran while one was open for 1% -> 1% of each run, Pallas kernels for 11% -> 8%
where the time goes in v3:
time: 146 us
  starting transfers between devices  63.4 us (43%)
  waiting for transfers between devices  55.1 us (38%)
  Pallas kernels  25.3 us (17%)
    ppermute x7, starting transfers between devices, swap_cores(): lax.ppermute(value, 'attn', [(i, i ^ 1) for i in range(lax.axis_size('att...  37.5 us
    ppermute x22, waiting for transfers between devices, shift(): lax.ppermute(value, axis, [(i, (i + step) % count) for i in range(count)])  28 us
    ppermute x8, waiting for transfers between devices, both_ways(): return lax.ppermute(value, 'attn', pairs)  25.2 us
    ppermute x22, starting transfers between devices, shift(): lax.ppermute(value, axis, [(i, (i + step) % count) for i in range(count)])  22.6 us
    pallas_call x1, Pallas kernels, step(): pl.pallas_call(mix_kernel, out_shape=(jax.ShapeDtypeStruct((attn_count *...  4.25 us
    pallas_call x1, Pallas kernels, step(): pl.pallas_call(functools.partial(pack_kernel, plan, local, n_expert), out...  4.11 us
    pallas_call x1, Pallas kernels, step(): pl.pallas_call(functools.partial(down_kernel, where), out_shape=(jax.Shap...  3.54 us
    pallas_call x1, Pallas kernels, step(): pl.pallas_call(functools.partial(pack_more_kernel, cut), out_shape=part_s...  3.54 us
  transfers between devices with their start and end apart: 37, of which 19 were waited for; matrix products, arithmetic and copies ran while one was open for 1% of the time, Pallas kernels for 8%

profile of v3, /device:TPU:513, one launch (start us, length us, event | category | flops | bytes accessed | tf_op | source)
XLA Modules:
  0.0 146.3 jit_solution(5510444588223594120)
XLA Ops:
  1.1 0.9 prepare.1.refs_0_
  2.0 20.5 %collective-permute-start = (bf16[136,512]{1,0:T(8,128)(2,1)S(1)}, bf16[136,512]{1,0:T(8,128)(2,1)S(1)}, u32[]{:S(2)}, u32[]{:S(2)}) collective-permute-start(bf16[136,512]{1,0:T(8,128)(2,1)S(1)} %prepare.1.refs_0_), channel_id=1, source_target_pairs={{0,8},{8,0},{16,24},{24,16},{32,40},{40,32},{48,56},{56,48},{64,72... | collective-permute-start | bytes 417800 | tf_op jit(solution)/shard_map/ppermute | solution.py:112
  22.5 1.0 collective-permute-done.refs_1_
  23.6 0.1 collective-permute-start.2
  23.7 0.1 collective-permute-start.1
  23.8 6.5 %collective-permute-done.2.refs_2_ = bf16[272,512]{1,0:T(8,128)(2,1)S(1)} collective-permute-done((bf16[272,512]{1,0:T(8,128)(2,1)S(1)}, bf16[272,512]{1,0:T(8,128)(2,1)S(1)}, u32[]{:S(2)}, u32[]{:S(2)}) %collective-permute-start.2) | collective-permute-done | bytes 278560 | tf_op jit(solution)/shard_map/ppermute | solution.py:108
  30.3 1.0 collective-permute-start.4
  31.3 1.7 %collective-permute-start.6 = (bf16[272,512]{1,0:T(8,128)(2,1)S(1)}, bf16[272,512]{1,0:T(8,128)(2,1)S(1)}, u32[]{:S(2)}, u32[]{:S(2)}) collective-permute-start(bf16[272,512]{1,0:T(8,128)(2,1)S(1)} %collective-permute-done.2.refs_2_), channel_id=1, source_target_pairs={{0,8},{8,0},{16,24},{24,16},{32,40},{40,32},{48,56},{56,48},{64,72... | collective-permute-start | bytes 835592 | tf_op jit(solution)/shard_map/ppermute | solution.py:112
  33.1 1.8 %collective-permute-start.5 = (bf16[272,512]{1,0:T(8,128)(2,1)S(1)}, bf16[272,512]{1,0:T(8,128)(2,1)S(1)}, u32[]{:S(2)}, u32[]{:S(2)}) collective-permute-start(bf16[272,512]{1,0:T(8,128)(2,1)S(1)} %collective-permute-done.1.refs_1_), channel_id=1, source_target_pairs={{0,8},{8,0},{16,24},{24,16},{32,40},{40,32},{48,56},{56,48},{64,72... | collective-permute-start | bytes 835592 | tf_op jit(solution)/shard_map/ppermute | solution.py:112
  34.9 0.8 collective-permute-done.3.refs_3_
  35.7 6.3 %collective-permute-start.7 = (bf16[272,512]{1,0:T(8,128)(2,1)S(1)}, bf16[272,512]{1,0:T(8,128)(2,1)S(1)}, u32[]{:S(2)}, u32[]{:S(2)}) collective-permute-start(bf16[272,512]{1,0:T(8,128)(2,1)S(1)} %collective-permute-done.3.refs_3_), channel_id=1, source_target_pairs={{0,8},{8,0},{16,24},{24,16},{32,40},{40,32},{48,56},{56,48},{64,72... | collective-permute-start | bytes 835592 | tf_op jit(solution)/shard_map/ppermute | solution.py:112
  42.1 2.9 %weights.1 = (bf16[4,512,768]{2,1,0:T(8,128)(2,1)S(1)}, bf16[4,512,768]{2,1,0:T(8,128)(2,1)S(1)}) custom-call(bf16[4,512,768]{2,1,0:T(8,128)(2,1)} %wg_hbm.1, bf16[4,512,768]{2,1,0:T(8,128)(2,1)} %wu_hbm.1), custom_call_target="tpu_custom_call" | custom-call | tf_op jit(solution)/shard_map/weights/pallas_call | solution.py:410
  45.0 4.1 %pack.1 = (bf16[2,32,1536]{2,1,0:T(8,128)(2,1)S(1)}, bf16[2,32,1536]{2,1,0:T(8,128)(2,1)S(1)}, bf16[2,32,1536]{2,1,0:T(8,128)(2,1)S(1)}, bf16[2,32,1536]{2,1,0:T...) custom-call(s32[18]{0:T(128)S(1)} %stack.123.info, ...), custom_call_target="tpu_custom_call" | custom-call | flops 2000000000 | bytes 6000000 | tf_op jit(solution)/shard_map/pack/pallas_call | solution.py:421
  49.1 3.5 %pack_more.1 = (bf16[2,32,1536]{2,1,0:T(8,128)(2,1)S(1)}, bf16[2,32,1536]{2,1,0:T(8,128)(2,1)S(1)}, bf16[2,32,1536]{2,1,0:T(8,128)(2,1)S(1)}, bf16[2,32,1536]{2,...) custom-call(s32[18]{0:T(128)S(1)} %stack.123.info, ...), custom_call_target="tpu_custom_call" | custom-call | flops 2000000000 | bytes 6000000 | tf_op jit(solution)/shard_map/pack_more/pallas_call | solution.py:438
  52.6 0.1 collective-permute-start.19
  52.8 1.4 collective-permute-start.16
  54.2 1.4 collective-permute-start.13
  55.6 0.1 collective-permute-start.9
  55.7 3.0 %collective-permute-done.19 = bf16[2,32,1536]{2,1,0:T(8,128)(2,1)S(1)} collective-permute-done((bf16[2,32,1536]{2,1,0:T(8,128)(2,1)S(1)}, bf16[2,32,1536]{2,1,0:T(8,128)(2,1)S(1)}, u32[]{:S(2)}, u32[]{:S(2)}) %collective-permute-start.19) | collective-permute-done | bytes 196640 | tf_op jit(solution)/shard_map/ppermute | solution.py:102
  58.7 1.6 %collective-permute-start.20 = (bf16[2,32,1536]{2,1,0:T(8,128)(2,1)S(1)}, bf16[2,32,1536]{2,1,0:T(8,128)(2,1)S(1)}, u32[]{:S(2)}, u32[]{:S(2)}) collective-permute-start(bf16[2,32,1536]{2,1,0:T(8,128)(2,1)S(1)} %add_convert_fusion.2), channel_id=1, source_target_pairs={{0,7},{1,0},{2,1},{3,2},{4,3},{5,4},{6,5},{7,6},{8,15},{9,8},{10,9... | collective-permute-start | bytes 589832 | tf_op jit(solution)/shard_map/ppermute | solution.py:102
  60.4 0.1 collective-permute-start.17
  60.6 2.3 %collective-permute-done.13 = bf16[2,32,1536]{2,1,0:T(8,128)(2,1)S(1)} collective-permute-done((bf16[2,32,1536]{2,1,0:T(8,128)(2,1)S(1)}, bf16[2,32,1536]{2,1,0:T(8,128)(2,1)S(1)}, u32[]{:S(2)}, u32[]{:S(2)}) %collective-permute-start.13) | collective-permute-done | bytes 196640 | tf_op jit(solution)/shard_map/ppermute | solution.py:102
  63.0 1.6 %collective-permute-start.14 = (bf16[2,32,1536]{2,1,0:T(8,128)(2,1)S(1)}, bf16[2,32,1536]{2,1,0:T(8,128)(2,1)S(1)}, u32[]{:S(2)}, u32[]{:S(2)}) collective-permute-start(bf16[2,32,1536]{2,1,0:T(8,128)(2,1)S(1)} %add_convert_fusion.6), channel_id=1, source_target_pairs={{0,7},{1,0},{2,1},{3,2},{4,3},{5,4},{6,5},{7,6},{8,15},{9,8},{10,9... | collective-permute-start | bytes 589832 | tf_op jit(solution)/shard_map/ppermute | solution.py:102
  64.6 0.1 collective-permute-start.10
  64.8 2.3 %collective-permute-done.20 = bf16[2,32,1536]{2,1,0:T(8,128)(2,1)S(1)} collective-permute-done((bf16[2,32,1536]{2,1,0:T(8,128)(2,1)S(1)}, bf16[2,32,1536]{2,1,0:T(8,128)(2,1)S(1)}, u32[]{:S(2)}, u32[]{:S(2)}) %collective-permute-start.20) | collective-permute-done | bytes 196640 | tf_op jit(solution)/shard_map/ppermute | solution.py:102
  67.2 0.9 collective-permute-start.21
  68.1 0.8 collective-permute-start.18
  68.9 2.4 %collective-permute-done.14 = bf16[2,32,1536]{2,1,0:T(8,128)(2,1)S(1)} collective-permute-done((bf16[2,32,1536]{2,1,0:T(8,128)(2,1)S(1)}, bf16[2,32,1536]{2,1,0:T(8,128)(2,1)S(1)}, u32[]{:S(2)}, u32[]{:S(2)}) %collective-permute-start.14) | collective-permute-done | bytes 196640 | tf_op jit(solution)/shard_map/ppermute | solution.py:102
  71.4 0.9 collective-permute-start.15
  72.3 0.8 collective-permute-start.11
  73.1 2.4 %collective-permute-done.21 = bf16[2,32,1536]{2,1,0:T(8,128)(2,1)S(1)} collective-permute-done((bf16[2,32,1536]{2,1,0:T(8,128)(2,1)S(1)}, bf16[2,32,1536]{2,1,0:T(8,128)(2,1)S(1)}, u32[]{:S(2)}, u32[]{:S(2)}) %collective-permute-start.21) | collective-permute-done | bytes 196640 | tf_op jit(solution)/shard_map/ppermute | solution.py:102
  75.6 0.8 collective-permute-start.22
  76.4 3.3 %collective-permute-done.11 = bf16[2,32,1536]{2,1,0:T(8,128)(2,1)S(1)} collective-permute-done((bf16[2,32,1536]{2,1,0:T(8,128)(2,1)S(1)}, bf16[2,32,1536]{2,1,0:T(8,128)(2,1)S(1)}, u32[]{:S(2)}, u32[]{:S(2)}) %collective-permute-start.11) | collective-permute-done | bytes 196640 | tf_op jit(solution)/shard_map/ppermute | solution.py:102
  79.7 1.4 collective-permute-start.12
  81.1 2.9 %collective-permute-done.22.refs_5_ = bf16[2,32,1536]{2,1,0:T(8,128)(2,1)S(1)} collective-permute-done((bf16[2,32,1536]{2,1,0:T(8,128)(2,1)S(1)}, bf16[2,32,1536]{2,1,0:T(8,128)(2,1)S(1)}, u32[]{:S(2)}, u32[]{:S(2)}) %collective-permute-start.22) | collective-permute-done | bytes 196640 | tf_op jit(solution)/shard_map/ppermute | solution.py:102
  84.0 1.6 %collective-permute-done.12.refs_1_ = bf16[2,32,1536]{2,1,0:T(8,128)(2,1)S(1)} collective-permute-done((bf16[2,32,1536]{2,1,0:T(8,128)(2,1)S(1)}, bf16[2,32,1536]{2,1,0:T(8,128)(2,1)S(1)}, u32[]{:S(2)}, u32[]{:S(2)}) %collective-permute-start.12) | collective-permute-done | bytes 196640 | tf_op jit(solution)/shard_map/ppermute | solution.py:102
  85.6 0.2 hidden.1.refs_0_
  85.8 0.7 collective-permute-start.25
  86.6 2.9 %collective-permute-start.26 = (bf16[4,32,768]{2,1,0:T(8,128)(2,1)S(1)}, bf16[4,32,768]{2,1,0:T(8,128)(2,1)S(1)}, u32[]{:S(2)}, u32[]{:S(2)}) collective-permute-start(bf16[4,32,768]{2,1,0:T(8,128)(2,1)S(1)} %hidden.1.refs_0_), channel_id=1, source_target_pairs={{0,6},{1,7},{2,0},{3,1},{4,2},{5,3},{6,4},{7,5},{8,14},{9,15},{10,... | collective-permute-start | bytes 589832 | tf_op jit(solution)/shard_map/ppermute | solution.py:102
  89.6 2.6 %collective-permute-start.24 = (bf16[4,32,768]{2,1,0:T(8,128)(2,1)S(1)}, bf16[4,32,768]{2,1,0:T(8,128)(2,1)S(1)}, u32[]{:S(2)}, u32[]{:S(2)}) collective-permute-start(bf16[4,32,768]{2,1,0:T(8,128)(2,1)S(1)} %hidden.1.refs_0_), channel_id=1, source_target_pairs={{0,7},{1,0},{2,1},{3,2},{4,3},{5,4},{6,5},{7,6},{8,15},{9,8},{10,9... | collective-permute-start | bytes 589832 | tf_op jit(solution)/shard_map/ppermute | solution.py:102
  92.2 3.6 %collective-permute-done.25.refs_3_ = bf16[4,32,768]{2,1,0:T(8,128)(2,1)S(1)} collective-permute-done((bf16[4,32,768]{2,1,0:T(8,128)(2,1)S(1)}, bf16[4,32,768]{2,1,0:T(8,128)(2,1)S(1)}, u32[]{:S(2)}, u32[]{:S(2)}) %collective-permute-start.25) | collective-permute-done | bytes 196640 | tf_op jit(solution)/shard_map/ppermute | solution.py:102
  95.8 2.7 %collective-permute-start.28 = (bf16[4,32,768]{2,1,0:T(8,128)(2,1)S(1)}, bf16[4,32,768]{2,1,0:T(8,128)(2,1)S(1)}, u32[]{:S(2)}, u32[]{:S(2)}) collective-permute-start(bf16[4,32,768]{2,1,0:T(8,128)(2,1)S(1)} %collective-permute-done.26.refs_4_), channel_id=1, source_target_pairs={{0,7},{1,0},{2,1},{3,2},{4,3},{5,4},{6,5},{7,6},{8,15},{9,8},{10,9... | collective-permute-start | bytes 589832 | tf_op jit(solution)/shard_map/ppermute | solution.py:102
  98.5 0.1 collective-permute-start.29
  98.6 2.3 %collective-permute-done.23.refs_1_ = bf16[4,32,768]{2,1,0:T(8,128)(2,1)S(1)} collective-permute-done((bf16[4,32,768]{2,1,0:T(8,128)(2,1)S(1)}, bf16[4,32,768]{2,1,0:T(8,128)(2,1)S(1)}, u32[]{:S(2)}, u32[]{:S(2)}) %collective-permute-start.23) | collective-permute-done | bytes 196640 | tf_op jit(solution)/shard_map/ppermute | solution.py:102
  100.9 1.4 collective-permute-start.30
  102.3 4.3 %mix.1 = (bf16[2048,1024]{1,0:T(8,128)(2,1)S(1)}, bf16[4,768,512]{2,1,0:T(8,128)(2,1)S(1)}) custom-call(s32[16]{0:T(128)S(1)} %stack.125.info, f32[16,8,128]{2,1,0:T(8,128)S(1)} %get-tuple-element.40.route, bf16[4,768,512]{2,1,0:T(8,128)(2,1)} %wd_hbm.1), custom_call_target="tpu_custom_call" | custom-call | tf_op jit(solution)/shard_map/mix/pallas_call | solution.py:466
  106.5 1.6 %collective-permute-done.29.refs_7_ = bf16[2,32,768]{2,1,0:T(8,128)(2,1)S(1)} collective-permute-done((bf16[2,32,768]{2,1,0:T(8,128)(2,1)S(1)}, bf16[2,32,768]{2,1,0:T(8,128)(2,1)S(1)}, u32[]{:S(2)}, u32[]{:S(2)}) %collective-permute-start.29) | collective-permute-done | bytes 98336 | tf_op jit(solution)/shard_map/ppermute | solution.py:102
  108.1 0.3 collective-permute-done.30.refs_8_
  108.4 3.5 %down.1 = (bf16[8,128,512]{2,1,0:T(8,128)(2,1)S(1)}, bf16[1024,512]{1,0:T(8,128)(2,1)S(1)}) custom-call(s32[8]{0:T(128)S(1)} %stack.134.info, bf16[4,32,768]{2,1,0:T(8,128)(2,1)S(1)} %hidden.1.refs_0_, bf16[4,32,768]{2,1,0:T(8,128)(2,1)S(1)} %collective-permute-done.23.refs_1_, bf16[4,32,768]{2,1,0:T(8,128)(2,1)S(1)} %collective-permute-done.24.refs_2_, ...), custom_call_target="tpu_custom_call" | custom-call | flops 2000000000 | bytes 6000000 | tf_op jit(solution)/shard_map/down/pallas_call | solution.py:478
  112.0 4.9 %collective-permute-start.31 = (bf16[8,128,512]{2,1,0:T(8,128)(2,1)S(1)}, bf16[8,128,512]{2,1,0:T(8,128)(2,1)S(1)}, u32[]{:S(2)}, u32[]{:S(2)}) collective-permute-start(bf16[8,128,512]{2,1,0:T(8,128)(2,1)S(1)} %get-tuple-element.62), channel_id=1, source_target_pairs={{0,8},{8,0},{16,24},{24,16},{32,40},{40,32},{48,56},{56,48},{64,72... | collective-permute-start | bytes 3145736 | tf_op jit(solution)/shard_map/ppermute | solution.py:112
  116.9 1.4 home.1
  118.3 0.9 collective-permute-done.31.swapped
  119.2 0.2 shard_map.113
  119.4 1.5 %collective-permute-start.33 = (bf16[256,512]{1,0:T(8,128)(2,1)S(1)}, bf16[256,512]{1,0:T(8,128)(2,1)S(1)}, u32[]{:S(2)}, u32[]{:S(2)}) collective-permute-start(bf16[256,512]{1,0:T(8,128)(2,1)S(1)} %get-tuple-element.64), channel_id=1, source_target_pairs={{0,16},{8,120},{16,32},{24,8},{32,48},{40,24},{48,64},{56,40},{64,... | collective-permute-start | bytes 786440 | tf_op jit(solution)/shard_map/ppermute | solution.py:108
  120.9 0.3 collective-permute-start.32
  121.2 9.8 %collective-permute-done.34.four = bf16[128,512]{1,0:T(8,128)(2,1)S(1)} collective-permute-done((bf16[128,512]{1,0:T(8,128)(2,1)S(1)}, bf16[128,512]{1,0:T(8,128)(2,1)S(1)}, u32[]{:S(2)}, u32[]{:S(2)}) %collective-permute-start.34) | collective-permute-done | bytes 131104 | tf_op jit(solution)/shard_map/ppermute | solution.py:108
  130.9 0.1 shard_map.114
  131.0 0.1 collective-permute-start.35
  131.2 1.4 collective-permute-done.32.one
  132.6 6.8 %collective-permute-done.35.two = bf16[256,512]{1,0:T(8,128)(2,1)S(1)} collective-permute-done((bf16[256,512]{1,0:T(8,128)(2,1)S(1)}, bf16[256,512]{1,0:T(8,128)(2,1)S(1)}, u32[]{:S(2)}, u32[]{:S(2)}) %collective-permute-start.35) | collective-permute-done | bytes 262176 | tf_op jit(solution)/shard_map/ppermute | solution.py:108
  139.4 2.1 %collective-permute-start.36 = (bf16[128,512]{1,0:T(8,128)(2,1)S(1)}, bf16[128,512]{1,0:T(8,128)(2,1)S(1)}, u32[]{:S(2)}, u32[]{:S(2)}) collective-permute-start(bf16[128,512]{1,0:T(8,128)(2,1)S(1)} %get-tuple-element.67), channel_id=1, source_target_pairs={{0,8},{8,0},{16,24},{24,16},{32,40},{40,32},{48,56},{56,48},{64,72... | collective-permute-start | bytes 393224 | tf_op jit(solution)/shard_map/ppermute | solution.py:112
  141.5 3.4 %attention.1 = bf16[2,64,128]{2,1,0:T(8,128)(2,1)S(1)} custom-call(s32[2]{0:T(128)S(1)} %copy-done, bf16[2,64,128]{2,1,0:T(8,128)(2,1)} %query.1, bf16[2,768,4,128]{3,2,1,0:T(4,128)(2,1)} %cache_k.1, bf16[2,768,4,128]{3,2,1,0:T(4,128)(2,1)} %cache_v.1), custom_call_target="tpu_custom_call" | custom-call | flops 1000000000 | bytes 3000000 | tf_op jit(solution)/shard_map/attention/pallas_call | solution.py:85
  144.9 0.6 copy.14
  145.6 0.7 shard_map.116
  (43 shorter events, 1.0 us)
Async XLA Ops:
  2.0 21.5 %collective-permute-start = (bf16[136,512]{1,0:T(8,128)(2,1)S(1)}, bf16[136,512]{1,0:T(8,128)(2,1)S(1)}, u32[]{:S(2)}, u32[]{:S(2)}) collective-permute-start(bf16[136,512]{1,0:T(8,128)(2,1)S(1)} %prepare.1.refs_0_), channel_id=1, source_target_pairs={{0,8},{8,0},{16,24},{24,16},{32,40},{40,32},{48,56},{56,48},{64,72... | collective-permute-start | bytes 417800 | tf_op jit(solution)/shard_map/ppermute | solution.py:112
  23.6 6.8 %collective-permute-start.2 = (bf16[272,512]{1,0:T(8,128)(2,1)S(1)}, bf16[272,512]{1,0:T(8,128)(2,1)S(1)}, u32[]{:S(2)}, u32[]{:S(2)}) collective-permute-start(bf16[272,512]{1,0:T(8,128)(2,1)S(1)} %pair.1.refs_0_), channel_id=1, source_target_pairs={{0,32},{8,104},{16,48},{24,120},{32,64},{40,8},{48,80},{56,24},{64... | collective-permute-start | bytes 835592 | tf_op jit(solution)/shard_map/ppermute | solution.py:108
  23.7 9.4 %collective-permute-start.1 = (bf16[272,512]{1,0:T(8,128)(2,1)S(1)}, bf16[272,512]{1,0:T(8,128)(2,1)S(1)}, u32[]{:S(2)}, u32[]{:S(2)}) collective-permute-start(bf16[272,512]{1,0:T(8,128)(2,1)S(1)} %pair.1.refs_0_), channel_id=1, source_target_pairs={{0,16},{8,120},{16,32},{24,8},{32,48},{40,24},{48,64},{56,40},{64,... | collective-permute-start | bytes 835592 | tf_op jit(solution)/shard_map/ppermute | solution.py:108
  30.3 5.4 %collective-permute-start.3 = (bf16[272,512]{1,0:T(8,128)(2,1)S(1)}, bf16[272,512]{1,0:T(8,128)(2,1)S(1)}, u32[]{:S(2)}, u32[]{:S(2)}) collective-permute-start(bf16[272,512]{1,0:T(8,128)(2,1)S(1)} %collective-permute-done.2.refs_2_), channel_id=1, source_target_pairs={{0,16},{8,120},{16,32},{24,8},{32,48},{40,24},{48,64},{56,40},{64,... | collective-permute-start | bytes 835592 | tf_op jit(solution)/shard_map/ppermute | solution.py:108
  30.3 11.7 %collective-permute-start.4 = (bf16[136,512]{1,0:T(8,128)(2,1)S(1)}, bf16[136,512]{1,0:T(8,128)(2,1)S(1)}, u32[]{:S(2)}, u32[]{:S(2)}) collective-permute-start(bf16[136,512]{1,0:T(8,128)(2,1)S(1)} %slice.12), channel_id=1, source_target_pairs={{0,32},{8,104},{16,48},{24,120},{32,64},{40,8},{48,80},{56,24},{64... | collective-permute-start | bytes 417800 | tf_op jit(solution)/shard_map/ppermute | solution.py:108
  31.3 13.6 %collective-permute-start.6 = (bf16[272,512]{1,0:T(8,128)(2,1)S(1)}, bf16[272,512]{1,0:T(8,128)(2,1)S(1)}, u32[]{:S(2)}, u32[]{:S(2)}) collective-permute-start(bf16[272,512]{1,0:T(8,128)(2,1)S(1)} %collective-permute-done.2.refs_2_), channel_id=1, source_target_pairs={{0,8},{8,0},{16,24},{24,16},{32,40},{40,32},{48,56},{56,48},{64,72... | collective-permute-start | bytes 835592 | tf_op jit(solution)/shard_map/ppermute | solution.py:112
  33.1 11.9 %collective-permute-start.5 = (bf16[272,512]{1,0:T(8,128)(2,1)S(1)}, bf16[272,512]{1,0:T(8,128)(2,1)S(1)}, u32[]{:S(2)}, u32[]{:S(2)}) collective-permute-start(bf16[272,512]{1,0:T(8,128)(2,1)S(1)} %collective-permute-done.1.refs_1_), channel_id=1, source_target_pairs={{0,8},{8,0},{16,24},{24,16},{32,40},{40,32},{48,56},{56,48},{64,72... | collective-permute-start | bytes 835592 | tf_op jit(solution)/shard_map/ppermute | solution.py:112
  35.7 9.2 %collective-permute-start.7 = (bf16[272,512]{1,0:T(8,128)(2,1)S(1)}, bf16[272,512]{1,0:T(8,128)(2,1)S(1)}, u32[]{:S(2)}, u32[]{:S(2)}) collective-permute-start(bf16[272,512]{1,0:T(8,128)(2,1)S(1)} %collective-permute-done.3.refs_3_), channel_id=1, source_target_pairs={{0,8},{8,0},{16,24},{24,16},{32,40},{40,32},{48,56},{56,48},{64,72... | collective-permute-start | bytes 835592 | tf_op jit(solution)/shard_map/ppermute | solution.py:112
  42.0 2.9 %collective-permute-start.8 = (bf16[136,512]{1,0:T(8,128)(2,1)S(1)}, bf16[136,512]{1,0:T(8,128)(2,1)S(1)}, u32[]{:S(2)}, u32[]{:S(2)}) collective-permute-start(bf16[136,512]{1,0:T(8,128)(2,1)S(1)} %collective-permute-done.4.refs_4_), channel_id=1, source_target_pairs={{0,8},{8,0},{16,24},{24,16},{32,40},{40,32},{48,56},{56,48},{64,72... | collective-permute-start | bytes 417800 | tf_op jit(solution)/shard_map/ppermute | solution.py:112
  52.6 6.1 %collective-permute-start.19 = (bf16[2,32,1536]{2,1,0:T(8,128)(2,1)S(1)}, bf16[2,32,1536]{2,1,0:T(8,128)(2,1)S(1)}, u32[]{:S(2)}, u32[]{:S(2)}) collective-permute-start(bf16[2,32,1536]{2,1,0:T(8,128)(2,1)S(1)} %get-tuple-element.56), channel_id=1, source_target_pairs={{0,7},{1,0},{2,1},{3,2},{4,3},{5,4},{6,5},{7,6},{8,15},{9,8},{10,9... | collective-permute-start | bytes 589832 | tf_op jit(solution)/shard_map/ppermute | solution.py:102
  52.8 7.6 %collective-permute-start.16 = (bf16[2,32,1536]{2,1,0:T(8,128)(2,1)S(1)}, bf16[2,32,1536]{2,1,0:T(8,128)(2,1)S(1)}, u32[]{:S(2)}, u32[]{:S(2)}) collective-permute-start(bf16[2,32,1536]{2,1,0:T(8,128)(2,1)S(1)} %get-tuple-element.53), channel_id=1, source_target_pairs={{0,1},{1,2},{2,3},{3,4},{4,5},{5,6},{6,7},{7,0},{8,9},{9,10},{10,1... | collective-permute-start | bytes 589832 | tf_op jit(solution)/shard_map/ppermute | solution.py:102
  54.2 8.7 %collective-permute-start.13 = (bf16[2,32,1536]{2,1,0:T(8,128)(2,1)S(1)}, bf16[2,32,1536]{2,1,0:T(8,128)(2,1)S(1)}, u32[]{:S(2)}, u32[]{:S(2)}) collective-permute-start(bf16[2,32,1536]{2,1,0:T(8,128)(2,1)S(1)} %get-tuple-element.48), channel_id=1, source_target_pairs={{0,7},{1,0},{2,1},{3,2},{4,3},{5,4},{6,5},{7,6},{8,15},{9,8},{10,9... | collective-permute-start | bytes 589832 | tf_op jit(solution)/shard_map/ppermute | solution.py:102
  55.6 9.0 %collective-permute-start.9 = (bf16[2,32,1536]{2,1,0:T(8,128)(2,1)S(1)}, bf16[2,32,1536]{2,1,0:T(8,128)(2,1)S(1)}, u32[]{:S(2)}, u32[]{:S(2)}) collective-permute-start(bf16[2,32,1536]{2,1,0:T(8,128)(2,1)S(1)} %get-tuple-element.44), channel_id=1, source_target_pairs={{0,1},{1,2},{2,3},{3,4},{4,5},{5,6},{6,7},{7,0},{8,9},{9,10},{10,1... | collective-permute-start | bytes 589832 | tf_op jit(solution)/shard_map/ppermute | solution.py:102
  58.7 8.4 %collective-permute-start.20 = (bf16[2,32,1536]{2,1,0:T(8,128)(2,1)S(1)}, bf16[2,32,1536]{2,1,0:T(8,128)(2,1)S(1)}, u32[]{:S(2)}, u32[]{:S(2)}) collective-permute-start(bf16[2,32,1536]{2,1,0:T(8,128)(2,1)S(1)} %add_convert_fusion.2), channel_id=1, source_target_pairs={{0,7},{1,0},{2,1},{3,2},{4,3},{5,4},{6,5},{7,6},{8,15},{9,8},{10,9... | collective-permute-start | bytes 589832 | tf_op jit(solution)/shard_map/ppermute | solution.py:102
  60.4 7.7 %collective-permute-start.17 = (bf16[2,32,1536]{2,1,0:T(8,128)(2,1)S(1)}, bf16[2,32,1536]{2,1,0:T(8,128)(2,1)S(1)}, u32[]{:S(2)}, u32[]{:S(2)}) collective-permute-start(bf16[2,32,1536]{2,1,0:T(8,128)(2,1)S(1)} %add_convert_fusion.4), channel_id=1, source_target_pairs={{0,1},{1,2},{2,3},{3,4},{4,5},{5,6},{6,7},{7,0},{8,9},{9,10},{10,1... | collective-permute-start | bytes 589832 | tf_op jit(solution)/shard_map/ppermute | solution.py:102
  63.0 8.4 %collective-permute-start.14 = (bf16[2,32,1536]{2,1,0:T(8,128)(2,1)S(1)}, bf16[2,32,1536]{2,1,0:T(8,128)(2,1)S(1)}, u32[]{:S(2)}, u32[]{:S(2)}) collective-permute-start(bf16[2,32,1536]{2,1,0:T(8,128)(2,1)S(1)} %add_convert_fusion.6), channel_id=1, source_target_pairs={{0,7},{1,0},{2,1},{3,2},{4,3},{5,4},{6,5},{7,6},{8,15},{9,8},{10,9... | collective-permute-start | bytes 589832 | tf_op jit(solution)/shard_map/ppermute | solution.py:102
  64.6 7.6 %collective-permute-start.10 = (bf16[2,32,1536]{2,1,0:T(8,128)(2,1)S(1)}, bf16[2,32,1536]{2,1,0:T(8,128)(2,1)S(1)}, u32[]{:S(2)}, u32[]{:S(2)}) collective-permute-start(bf16[2,32,1536]{2,1,0:T(8,128)(2,1)S(1)} %add_convert_fusion.9), channel_id=1, source_target_pairs={{0,1},{1,2},{2,3},{3,4},{4,5},{5,6},{6,7},{7,0},{8,9},{9,10},{10,1... | collective-permute-start | bytes 589832 | tf_op jit(solution)/shard_map/ppermute | solution.py:102
  67.2 8.4 %collective-permute-start.21 = (bf16[2,32,1536]{2,1,0:T(8,128)(2,1)S(1)}, bf16[2,32,1536]{2,1,0:T(8,128)(2,1)S(1)}, u32[]{:S(2)}, u32[]{:S(2)}) collective-permute-start(bf16[2,32,1536]{2,1,0:T(8,128)(2,1)S(1)} %add_convert_fusion.1), channel_id=1, source_target_pairs={{0,7},{1,0},{2,1},{3,2},{4,3},{5,4},{6,5},{7,6},{8,15},{9,8},{10,9... | collective-permute-start | bytes 589832 | tf_op jit(solution)/shard_map/ppermute | solution.py:102
  68.1 13.0 %collective-permute-start.18 = (bf16[2,32,1536]{2,1,0:T(8,128)(2,1)S(1)}, bf16[2,32,1536]{2,1,0:T(8,128)(2,1)S(1)}, u32[]{:S(2)}, u32[]{:S(2)}) collective-permute-start(bf16[2,32,1536]{2,1,0:T(8,128)(2,1)S(1)} %add_convert_fusion.3), channel_id=1, source_target_pairs={{0,1},{1,2},{2,3},{3,4},{4,5},{5,6},{6,7},{7,0},{8,9},{9,10},{10,1... | collective-permute-start | bytes 589832 | tf_op jit(solution)/shard_map/ppermute | solution.py:102
  71.4 9.7 %collective-permute-start.15 = (bf16[2,32,1536]{2,1,0:T(8,128)(2,1)S(1)}, bf16[2,32,1536]{2,1,0:T(8,128)(2,1)S(1)}, u32[]{:S(2)}, u32[]{:S(2)}) collective-permute-start(bf16[2,32,1536]{2,1,0:T(8,128)(2,1)S(1)} %add_convert_fusion.5), channel_id=1, source_target_pairs={{0,7},{1,0},{2,1},{3,2},{4,3},{5,4},{6,5},{7,6},{8,15},{9,8},{10,9... | collective-permute-start | bytes 589832 | tf_op jit(solution)/shard_map/ppermute | solution.py:102
  72.3 7.3 %collective-permute-start.11 = (bf16[2,32,1536]{2,1,0:T(8,128)(2,1)S(1)}, bf16[2,32,1536]{2,1,0:T(8,128)(2,1)S(1)}, u32[]{:S(2)}, u32[]{:S(2)}) collective-permute-start(bf16[2,32,1536]{2,1,0:T(8,128)(2,1)S(1)} %add_convert_fusion.8), channel_id=1, source_target_pairs={{0,1},{1,2},{2,3},{3,4},{4,5},{5,6},{6,7},{7,0},{8,9},{9,10},{10,1... | collective-permute-start | bytes 589832 | tf_op jit(solution)/shard_map/ppermute | solution.py:102
  75.6 8.4 %collective-permute-start.22 = (bf16[2,32,1536]{2,1,0:T(8,128)(2,1)S(1)}, bf16[2,32,1536]{2,1,0:T(8,128)(2,1)S(1)}, u32[]{:S(2)}, u32[]{:S(2)}) collective-permute-start(bf16[2,32,1536]{2,1,0:T(8,128)(2,1)S(1)} %add_convert_fusion), channel_id=1, source_target_pairs={{0,7},{1,0},{2,1},{3,2},{4,3},{5,4},{6,5},{7,6},{8,15},{9,8},{10,9... | collective-permute-start | bytes 589832 | tf_op jit(solution)/shard_map/ppermute | solution.py:102
  79.7 5.8 %collective-permute-start.12 = (bf16[2,32,1536]{2,1,0:T(8,128)(2,1)S(1)}, bf16[2,32,1536]{2,1,0:T(8,128)(2,1)S(1)}, u32[]{:S(2)}, u32[]{:S(2)}) collective-permute-start(bf16[2,32,1536]{2,1,0:T(8,128)(2,1)S(1)} %add_convert_fusion.7), channel_id=1, source_target_pairs={{0,1},{1,2},{2,3},{3,4},{4,5},{5,6},{6,7},{7,0},{8,9},{9,10},{10,1... | collective-permute-start | bytes 589832 | tf_op jit(solution)/shard_map/ppermute | solution.py:102
  85.8 10.0 %collective-permute-start.25 = (bf16[4,32,768]{2,1,0:T(8,128)(2,1)S(1)}, bf16[4,32,768]{2,1,0:T(8,128)(2,1)S(1)}, u32[]{:S(2)}, u32[]{:S(2)}) collective-permute-start(bf16[4,32,768]{2,1,0:T(8,128)(2,1)S(1)} %hidden.1.refs_0_), channel_id=1, source_target_pairs={{0,2},{1,3},{2,4},{3,5},{4,6},{5,7},{6,0},{7,1},{8,10},{9,11},{10,... | collective-permute-start | bytes 589832 | tf_op jit(solution)/shard_map/ppermute | solution.py:102
  86.6 9.2 %collective-permute-start.26 = (bf16[4,32,768]{2,1,0:T(8,128)(2,1)S(1)}, bf16[4,32,768]{2,1,0:T(8,128)(2,1)S(1)}, u32[]{:S(2)}, u32[]{:S(2)}) collective-permute-start(bf16[4,32,768]{2,1,0:T(8,128)(2,1)S(1)} %hidden.1.refs_0_), channel_id=1, source_target_pairs={{0,6},{1,7},{2,0},{3,1},{4,2},{5,3},{6,4},{7,5},{8,14},{9,15},{10,... | collective-permute-start | bytes 589832 | tf_op jit(solution)/shard_map/ppermute | solution.py:102
  89.5 11.4 %collective-permute-start.23 = (bf16[4,32,768]{2,1,0:T(8,128)(2,1)S(1)}, bf16[4,32,768]{2,1,0:T(8,128)(2,1)S(1)}, u32[]{:S(2)}, u32[]{:S(2)}) collective-permute-start(bf16[4,32,768]{2,1,0:T(8,128)(2,1)S(1)} %hidden.1.refs_0_), channel_id=1, source_target_pairs={{0,1},{1,2},{2,3},{3,4},{4,5},{5,6},{6,7},{7,0},{8,9},{9,10},{10,1... | collective-permute-start | bytes 589832 | tf_op jit(solution)/shard_map/ppermute | solution.py:102
  89.6 17.0 %collective-permute-start.24 = (bf16[4,32,768]{2,1,0:T(8,128)(2,1)S(1)}, bf16[4,32,768]{2,1,0:T(8,128)(2,1)S(1)}, u32[]{:S(2)}, u32[]{:S(2)}) collective-permute-start(bf16[4,32,768]{2,1,0:T(8,128)(2,1)S(1)} %hidden.1.refs_0_), channel_id=1, source_target_pairs={{0,7},{1,0},{2,1},{3,2},{4,3},{5,4},{6,5},{7,6},{8,15},{9,8},{10,9... | collective-permute-start | bytes 589832 | tf_op jit(solution)/shard_map/ppermute | solution.py:102
  95.8 12.6 %collective-permute-start.27 = (bf16[4,32,768]{2,1,0:T(8,128)(2,1)S(1)}, bf16[4,32,768]{2,1,0:T(8,128)(2,1)S(1)}, u32[]{:S(2)}, u32[]{:S(2)}) collective-permute-start(bf16[4,32,768]{2,1,0:T(8,128)(2,1)S(1)} %collective-permute-done.25.refs_3_), channel_id=1, source_target_pairs={{0,1},{1,2},{2,3},{3,4},{4,5},{5,6},{6,7},{7,0},{8,9},{9,10},{10,1... | collective-permute-start | bytes 589832 | tf_op jit(solution)/shard_map/ppermute | solution.py:102
  95.8 12.6 %collective-permute-start.28 = (bf16[4,32,768]{2,1,0:T(8,128)(2,1)S(1)}, bf16[4,32,768]{2,1,0:T(8,128)(2,1)S(1)}, u32[]{:S(2)}, u32[]{:S(2)}) collective-permute-start(bf16[4,32,768]{2,1,0:T(8,128)(2,1)S(1)} %collective-permute-done.26.refs_4_), channel_id=1, source_target_pairs={{0,7},{1,0},{2,1},{3,2},{4,3},{5,4},{6,5},{7,6},{8,15},{9,8},{10,9... | collective-permute-start | bytes 589832 | tf_op jit(solution)/shard_map/ppermute | solution.py:102
  98.5 9.7 %collective-permute-start.29 = (bf16[2,32,768]{2,1,0:T(8,128)(2,1)S(1)}, bf16[2,32,768]{2,1,0:T(8,128)(2,1)S(1)}, u32[]{:S(2)}, u32[]{:S(2)}) collective-permute-start(bf16[2,32,768]{2,1,0:T(8,128)(2,1)S(1)} %slice.13), channel_id=1, source_target_pairs={{0,2},{1,3},{2,4},{3,5},{4,6},{5,7},{6,0},{7,1},{8,10},{9,11},{10,... | collective-permute-start | bytes 294920 | tf_op jit(solution)/shard_map/ppermute | solution.py:102
  100.9 7.5 %collective-permute-start.30 = (bf16[2,32,768]{2,1,0:T(8,128)(2,1)S(1)}, bf16[2,32,768]{2,1,0:T(8,128)(2,1)S(1)}, u32[]{:S(2)}, u32[]{:S(2)}) collective-permute-start(bf16[2,32,768]{2,1,0:T(8,128)(2,1)S(1)} %slice.14), channel_id=1, source_target_pairs={{0,6},{1,7},{2,0},{3,1},{4,2},{5,3},{6,4},{7,5},{8,14},{9,15},{10,... | collective-permute-start | bytes 294920 | tf_op jit(solution)/shard_map/ppermute | solution.py:102
  112.0 7.2 %collective-permute-start.31 = (bf16[8,128,512]{2,1,0:T(8,128)(2,1)S(1)}, bf16[8,128,512]{2,1,0:T(8,128)(2,1)S(1)}, u32[]{:S(2)}, u32[]{:S(2)}) collective-permute-start(bf16[8,128,512]{2,1,0:T(8,128)(2,1)S(1)} %get-tuple-element.62), channel_id=1, source_target_pairs={{0,8},{8,0},{16,24},{24,16},{32,40},{40,32},{48,56},{56,48},{64,72... | collective-permute-start | bytes 3145736 | tf_op jit(solution)/shard_map/ppermute | solution.py:112
  119.4 22.2 %copy-start = (s32[2]{0:T(128)S(1)}, s32[2]{0:T(128)}, u32[]{:S(2)}) copy-start(s32[2]{0:T(128)} %lengths.1) | copy-start | bytes 28
  119.4 11.6 %collective-permute-start.33 = (bf16[256,512]{1,0:T(8,128)(2,1)S(1)}, bf16[256,512]{1,0:T(8,128)(2,1)S(1)}, u32[]{:S(2)}, u32[]{:S(2)}) collective-permute-start(bf16[256,512]{1,0:T(8,128)(2,1)S(1)} %get-tuple-element.64), channel_id=1, source_target_pairs={{0,16},{8,120},{16,32},{24,8},{32,48},{40,24},{48,64},{56,40},{64,... | collective-permute-start | bytes 786440 | tf_op jit(solution)/shard_map/ppermute | solution.py:108
  120.9 10.0 %collective-permute-start.34 = (bf16[128,512]{1,0:T(8,128)(2,1)S(1)}, bf16[128,512]{1,0:T(8,128)(2,1)S(1)}, u32[]{:S(2)}, u32[]{:S(2)}) collective-permute-start(bf16[128,512]{1,0:T(8,128)(2,1)S(1)} %get-tuple-element.65), channel_id=1, source_target_pairs={{0,32},{8,104},{16,48},{24,120},{32,64},{40,8},{48,80},{56,24},{64... | collective-permute-start | bytes 393224 | tf_op jit(solution)/shard_map/ppermute | solution.py:108
  120.9 11.7 %collective-permute-start.32 = (bf16[256,512]{1,0:T(8,128)(2,1)S(1)}, bf16[256,512]{1,0:T(8,128)(2,1)S(1)}, u32[]{:S(2)}, u32[]{:S(2)}) collective-permute-start(bf16[256,512]{1,0:T(8,128)(2,1)S(1)} %get-tuple-element.63), channel_id=1, source_target_pairs={{0,16},{8,120},{16,32},{24,8},{32,48},{40,24},{48,64},{56,40},{64,... | collective-permute-start | bytes 786440 | tf_op jit(solution)/shard_map/ppermute | solution.py:108
  131.0 8.3 %collective-permute-start.35 = (bf16[256,512]{1,0:T(8,128)(2,1)S(1)}, bf16[256,512]{1,0:T(8,128)(2,1)S(1)}, u32[]{:S(2)}, u32[]{:S(2)}) collective-permute-start(bf16[256,512]{1,0:T(8,128)(2,1)S(1)} %shard_map.114), channel_id=1, source_target_pairs={{0,32},{8,104},{16,48},{24,120},{32,64},{40,8},{48,80},{56,24},{64... | collective-permute-start | bytes 786440 | tf_op jit(solution)/shard_map/ppermute | solution.py:108
  139.4 6.1 %collective-permute-start.36 = (bf16[128,512]{1,0:T(8,128)(2,1)S(1)}, bf16[128,512]{1,0:T(8,128)(2,1)S(1)}, u32[]{:S(2)}, u32[]{:S(2)}) collective-permute-start(bf16[128,512]{1,0:T(8,128)(2,1)S(1)} %get-tuple-element.67), channel_id=1, source_target_pairs={{0,8},{8,0},{16,24},{24,16},{32,40},{40,32},{48,56},{56,48},{64,72... | collective-permute-start | bytes 393224 | tf_op jit(solution)/shard_map/ppermute | solution.py:112

commit v4 on v3

--- a/solution.py
+++ b/solution.py
@@ -21,32 +21,28 @@
     return home[i].astype(F32) + swapped[i].astype(F32)
 
 
-def first_kernel(home, swapped, three, four, one):
+def far_kernel(home, swapped, three, four):
     rows = home.shape[1]
-    four[...] = both_cores(home, swapped, 6).astype(BF16)
+    four[...] = both_cores(home, swapped, 2).astype(BF16)
     for c in range(2):
-        three[c * rows : (c + 1) * rows, :] = both_cores(home, swapped, 4 + c).astype(BF16)
-        one[c * rows : (c + 1) * rows, :] = both_cores(home, swapped, c).astype(BF16)
-
-
-def relay_kernel(home, swapped, three, four, two):
+        three[c * rows : (c + 1) * rows, :] = both_cores(home, swapped, c).astype(BF16)
+
+
+def one_kernel(home, swapped, own, other):
+    own[...] = both_cores(home, swapped, 0).astype(BF16)
+    other[...] = both_cores(home, swapped, 1).astype(BF16)
+
+
+def relay_kernel(home, swapped, three, four, own, other):
     rows = home.shape[1]
     came = three[...].astype(F32)
-    two[0:rows, :] = (
-        both_cores(home, swapped, 2) + (came[0:rows] + four[...].astype(F32))
-    ).astype(BF16)
-    two[rows:, :] = (both_cores(home, swapped, 3) + came[rows:]).astype(BF16)
-
-
-def cross_kernel(home, swapped, one, two, own, other):
-    rows = home.shape[1]
-    total = one[...].astype(F32) + two[...].astype(F32)
-    other[...] = total[rows:].astype(BF16)
-    own[...] = total[0:rows] + both_cores(home, swapped, 7)
-
-
-def finish_kernel(own, came, out):
-    out[...] = (own[...] + came[...].astype(F32)).astype(BF16)
+    own[...] = (both_cores(home, swapped, 2) + (came[0:rows] + four[...].astype(F32))).astype(BF16)
+    other[...] = (both_cores(home, swapped, 3) + came[rows:]).astype(BF16)
+
+
+def finish_kernel(home, swapped, a, b, c, d, out):
+    came = (a[...].astype(F32) + b[...].astype(F32)) + (c[...].astype(F32) + d[...].astype(F32))
+    out[...] = (both_cores(home, swapped, 3) + came).astype(BF16)
 
 
 def in_hbm(value):
@@ -102,9 +98,9 @@
     return lax.ppermute(value, axis, [(i, (i + step) % count) for i in range(count)])
 
 
-def both_ways(value, places):
+def both_ways(value, places, cross=0):
     count = lax.axis_size("attn")
-    pairs = [(i, (i + (-2 if i % 2 else 2) * places) % count) for i in range(count)]
+    pairs = [(i, (i + (-2 if i % 2 else 2) * places) % count ^ cross) for i in range(count)]
     return lax.ppermute(value, "attn", pairs)
 
 
@@ -136,7 +132,7 @@
         out[i * height : (i + 1) * height, :] = ref[...]
 
 
-def expert_parts(j0, info, place, tok, wg, wu, onehot, packed, out):
+def expert_parts(j0, info, place, tok, wg, wu, onehot, out):
     n_blocks = place.shape[0]
     rows = tok.shape[0] // n_blocks
     n_dest = len(out)
@@ -146,21 +142,11 @@
     row_id = lax.broadcasted_iota(jnp.int32, (capacity, rows), 0) + info[1 + n_blocks]
     row_id = jnp.where(row_id < capacity, row_id, row_id - capacity).astype(F32)
 
-    def select(i, carry):
-        at = pl.ds(pl.multiple_of(i * rows, rows), rows)
-        block = info[1 + i]
-        for j in range(here_count):
-            spot = place[block, j0 + j : j0 + j + 1, :]
-            onehot[j * capacity : (j + 1) * capacity, at] = jnp.where(
-                row_id == spot, 1.0, 0.0
-            ).astype(BF16)
-        return carry
-
-    lax.fori_loop(0, n_blocks, select, 0, unroll=2)
-    packed[...] = jnp.dot(onehot[...], tok[...], preferred_element_type=F32).astype(BF16)
-
     def expert(j, carry):
-        mine = packed[pl.ds(pl.multiple_of(j * capacity, capacity), capacity), :]
+        for i in range(n_blocks):
+            spot = place[info[1 + i], pl.ds(j0 + j, 1), :]
+            onehot[:, i * rows : (i + 1) * rows] = jnp.where(row_id == spot, 1.0, 0.0).astype(BF16)
+        mine = jnp.dot(onehot[...], tok[...], preferred_element_type=F32).astype(BF16)
         gate = jnp.dot(mine, wg[j0 + j], preferred_element_type=F32).astype(BF16)
         up = jnp.dot(mine, wu[j0 + j], preferred_element_type=F32).astype(BF16)
         for d in range(n_dest):
@@ -187,7 +173,7 @@
     ops = refs[:n_ops]
     wg, wu = refs[n_ops : n_ops + 2]
     out = refs[n_ops + 2 : n_ops + 2 + n_dest]
-    route, tok, meta, onehot, packed = refs[n_ops + 2 + n_dest :]
+    route, tok, meta, onehot = refs[n_ops + 2 + n_dest :]
     n_blocks = len(plan)
     rows = tok.shape[0] // n_blocks
     capacity = n_dest * out[0].shape[1]
@@ -227,12 +213,12 @@
     row = lax.broadcasted_iota(jnp.int32, (size, rows), 0)
     route[...] = jnp.where(row % 8 < local, place, member).reshape(n_blocks, 8, rows)
 
-    expert_parts(0, info, route, tok, wg, wu, onehot, packed, out)
+    expert_parts(0, info, route, tok, wg, wu, onehot, out)
 
 
 def pack_more_kernel(j0, info, tok, route, wg, wu, *refs):
-    *out, onehot, packed = refs
-    expert_parts(j0, info, route, tok, wg, wu, onehot, packed, out)
+    *out, onehot = refs
+    expert_parts(j0, info, route, tok, wg, wu, onehot, out)
 
 
 def hidden_kernel(*refs):
@@ -274,12 +260,13 @@
     copy.wait()
 
 
-def mix_rows(first, mix, res, ref):
+def mix_rows(quarter, mix, res, ref):
     n_dest, rows, feat = ref.shape
-    group = 4
+    group = 2
 
     def some(g, carry):
-        at = pl.ds(pl.multiple_of(first + g * group * rows, group * rows), group * rows)
+        at = (quarter * n_dest + g * group) * rows
+        at = pl.ds(pl.multiple_of(at, group * rows), group * rows)
         got = jnp.dot(mix[at, :], res[...], preferred_element_type=F32).astype(BF16)
         ref[pl.ds(g * group, group)] = got.reshape(group, rows, feat)
         return carry
@@ -308,8 +295,13 @@
     mix_rows(0, mix, res, away)
 
 
-def home_kernel(mix, res, home):
-    mix_rows(mix.shape[0] // 2, mix, res, home)
+def second_kernel(mix, res, home, away):
+    mix_rows(1, mix, res, away)
+    mix_rows(2, mix, res, home)
+
+
+def third_kernel(mix, res, home):
+    mix_rows(3, mix, res, home)
 
 
 def scatter_sum(pieces, axis):
@@ -359,9 +351,10 @@
     order += [(-k, flip) for k in (1, 2, 3) for flip in (0, 1)] + [(far, 0)]
     order += [(k, flip) for k in (1, 2, 3) for flip in (1, 0)] + [(far, 1)]
     pack_info = [local * me] + [token_block(*at) for at in order]
-    onward = [(k, flip) for k in (1, 2, 3) for flip in (0, 1)] + [(far, 0), (0, 0)]
-    mix_info = [token_block(-k, 1 - flip) for k, flip in onward]
-    mix_info += [token_block(k, flip) for k, flip in onward]
+    onward = [(3, 0), (3, 1), (far, 0), (0, 0)], [(1, 0), (1, 1), (2, 0), (2, 1)]
+    for_other = [[token_block(-k, 1 - flip) for k, flip in part] for part in onward]
+    for_own = [[token_block(k, flip) for k, flip in part] for part in onward]
+    mix_info = for_other[0] + for_other[1] + for_own[0] + for_own[1]
     row_at = [x * dest_rows for x in x_at]
     pack_info.append(col * dest_rows)
     pack_info = jnp.stack(pack_info).astype(jnp.int32)
@@ -387,6 +380,9 @@
     )(in_hbm(tokens), in_hbm(expert_ids.T), in_hbm(gate_weight.T))
     attn_out = grouped_attention(query, cache_k, cache_v, lengths)
 
+    def pass_on(value, places, cross=0):
+        return both_ways(value, places, cross)
+
     pair = pl.pallas_call(
         bundle_kernel,
         out_shape=jax.ShapeDtypeStruct((2 * height, feat), BF16),
@@ -395,8 +391,8 @@
         name="pair",
         **SMALL,
     )(*map(in_vmem, (block, swap_cores(block))))
-    two, one = both_ways(pair, 2), both_ways(pair, 1)
-    four, three = both_ways(two[:height], 2), both_ways(two, 1)
+    two, one = pass_on(pair, 2), pass_on(pair, 1)
+    four, three = pass_on(two[:height], 2), pass_on(two, 1)
     operands = [pair, one, two, three, four]
     operands += [swap_cores(one), swap_cores(two), swap_cores(three), swap_cores(four)]
     pairs = [((i, 0), (i, height)) for i in range(8) if i != 4]
@@ -404,8 +400,7 @@
 
     cut = local // 2
     pack_scratch = [
-        pltpu.VMEM((cut * capacity, attn_count * rows), BF16),
-        pltpu.VMEM((cut * capacity, feat), BF16),
+        pltpu.VMEM((capacity, attn_count * rows), BF16),
     ]
     wg, wu = pl.pallas_call(
         fetch_kernel,
@@ -475,12 +470,10 @@
         name="mix",
         **SMALL,
     )(mix_info, in_vmem(route), in_hbm(w_down))
-    away, res = pl.pallas_call(
+    quarter = jax.ShapeDtypeStruct((attn_count // 4, rows, feat), BF16)
+    away_far, res = pl.pallas_call(
         functools.partial(down_kernel, where),
-        out_shape=(
-            jax.ShapeDtypeStruct((chips, rows, feat), BF16),
-            jax.ShapeDtypeStruct((local * capacity, feat), BF16),
-        ),
+        out_shape=(quarter, jax.ShapeDtypeStruct((local * capacity, feat), BF16)),
         in_specs=[SMEM_SPEC] + [VMEM_SPEC] * (len(pieces_in) + 2),
         out_specs=(VMEM_SPEC, VMEM_SPEC),
         scratch_shapes=[pltpu.VMEM((local, capacity, ff), BF16)],
@@ -488,35 +481,30 @@
         cost_estimate=pl.CostEstimate(flops=2 * 10**9, bytes_accessed=6 * 10**6, transcendentals=0),
         name="down",
     )(row_at, *map(in_vmem, pieces_in), in_vmem(wd), in_vmem(mix))
-    swapped = swap_cores(away)
-    home = pl.pallas_call(
-        home_kernel,
-        out_shape=jax.ShapeDtypeStruct((chips, rows, feat), BF16),
-        in_specs=[VMEM_SPEC, VMEM_SPEC],
-        out_specs=VMEM_SPEC,
-        cost_estimate=pl.CostEstimate(flops=10**9, bytes_accessed=2 * 10**6, transcendentals=0),
-        name="home",
-        **SMALL,
-    )(in_vmem(mix), in_vmem(res))
 
     def small_call(kernel, shapes, *operands):
         out = pl.pallas_call(
             kernel,
-            out_shape=tuple(jax.ShapeDtypeStruct((r, feat), t) for r, t in shapes),
+            out_shape=shapes,
             in_specs=[VMEM_SPEC] * len(operands),
             out_specs=(VMEM_SPEC,) * len(shapes),
             **SMALL,
         )(*map(in_vmem, operands))
         return out if len(shapes) > 1 else out[0]
 
-    twice = (2 * rows, BF16)
-    once = (rows, BF16)
-    three, four, one = small_call(first_kernel, (twice, once, twice), home, swapped)
-    four, three, one = both_ways(four, 2), both_ways(three, 1), both_ways(one, 1)
-    two = small_call(relay_kernel, (twice,), home, swapped, three, four)
-    two = both_ways(two, 2)
-    own, other = small_call(cross_kernel, ((rows, F32), once), home, swapped, one, two)
-    moe_out = small_call(finish_kernel, (once,), own, swap_cores(other))
+    once = jax.ShapeDtypeStruct((rows, feat), BF16)
+    twice = jax.ShapeDtypeStruct((2 * rows, feat), BF16)
+    came_far = swap_cores(away_far)
+    home_far, away_near = small_call(second_kernel, (quarter, quarter), mix, res)
+    came_near = swap_cores(away_near)
+    three, four = small_call(far_kernel, (twice, once), home_far, came_far)
+    four, three = pass_on(four, 2), pass_on(three, 1)
+    home_near = small_call(third_kernel, (quarter,), mix, res)
+    own, other = small_call(one_kernel, (once, once), home_near, came_near)
+    last = [pass_on(own, 1), pass_on(other, 1, 1)]
+    own, other = small_call(relay_kernel, (once, once), home_near, came_near, three, four)
+    last += [pass_on(own, 2), pass_on(other, 2, 1)]
+    moe_out = small_call(finish_kernel, (once,), home_far, came_far, *last)
     return (moe_out, attn_out)
 
 

time: 146 us -> 140 us (0.959)
  waiting for transfers between devices: 55.1 us -> 40.9 us
  starting transfers between devices: 63.4 us -> 71.2 us
    ppermute x8 -> x10, waiting for transfers between devices: 25.2 us -> 12.6 us  [both_ways(): return lax.ppermute(value, 'attn', pairs)]
    ppermute x8 -> x10, starting transfers between devices: 3.2 us -> 12.3 us  [both_ways(): return lax.ppermute(value, 'attn', pairs)]
    ppermute x7, starting transfers between devices: 37.5 us -> 35.5 us  [swap_cores(): lax.ppermute(value, 'attn', [(i, i ^ 1) for i in range(lax.axis_size('att...]
    pallas_call x6 -> x7, Pallas kernels: 5.99 us -> 6.64 us  [the longest x6 3.64 us: small_call(): pl.pallas_call(kernel, out_shape=shapes, in_specs=[VMEM_SPEC] * len(opera...]
  transfers between devices with their start and end apart: 37 -> 39, of which waited for: 19 -> 16; matrix products, arithmetic and copies ran while one was open for 1% -> 1% of each run, Pallas kernels for 8% -> 10%
where the time goes in v4:
time: 140 us
  starting transfers between devices  71.2 us (51%)
  waiting for transfers between devices  40.9 us (29%)
  Pallas kernels  25 us (18%)
    ppermute x7, starting transfers between devices, swap_cores(): lax.ppermute(value, 'attn', [(i, i ^ 1) for i in range(lax.axis_size('att...  35.5 us
    ppermute x22, waiting for transfers between devices, shift(): lax.ppermute(value, axis, [(i, (i + step) % count) for i in range(count)])  27.2 us
    ppermute x22, starting transfers between devices, shift(): lax.ppermute(value, axis, [(i, (i + step) % count) for i in range(count)])  23.5 us
    ppermute x10, waiting for transfers between devices, both_ways(): return lax.ppermute(value, 'attn', pairs)  12.6 us
    ppermute x10, starting transfers between devices, both_ways(): return lax.ppermute(value, 'attn', pairs)  12.3 us
    pallas_call x1, Pallas kernels, step(): pl.pallas_call(mix_kernel, out_shape=(jax.ShapeDtypeStruct((attn_count *...  4.25 us
    pallas_call x6, Pallas kernels, small_call(): pl.pallas_call(kernel, out_shape=shapes, in_specs=[VMEM_SPEC] * len(opera...  3.64 us
    pallas_call x1, Pallas kernels, step(): pl.pallas_call(functools.partial(pack_kernel, plan, local, n_expert), out...  3.63 us
  transfers between devices with their start and end apart: 39, of which 16 were waited for; matrix products, arithmetic and copies ran while one was open for 1% of the time, Pallas kernels for 10%

profile of v4, /device:TPU:513, one launch (start us, length us, event | category | flops | bytes accessed | tf_op | source)
XLA Modules:
  0.0 139.6 jit_solution(8199768225195362237)
XLA Ops:
  1.1 0.9 prepare.1.refs_0_
  2.0 20.5 %collective-permute-start = (bf16[136,512]{1,0:T(8,128)(2,1)S(1)}, bf16[136,512]{1,0:T(8,128)(2,1)S(1)}, u32[]{:S(2)}, u32[]{:S(2)}) collective-permute-start(bf16[136,512]{1,0:T(8,128)(2,1)S(1)} %prepare.1.refs_0_), channel_id=1, source_target_pairs={{0,8},{8,0},{16,24},{24,16},{32,40},{40,32},{48,56},{56,48},{64,72... | collective-permute-start | bytes 417800 | tf_op jit(solution)/shard_map/ppermute | solution.py:108
  22.5 1.0 collective-permute-done.refs_1_
  23.6 0.1 collective-permute-start.2
  23.7 0.1 collective-permute-start.1
  23.8 6.5 %collective-permute-done.2.refs_2_ = bf16[272,512]{1,0:T(8,128)(2,1)S(1)} collective-permute-done((bf16[272,512]{1,0:T(8,128)(2,1)S(1)}, bf16[272,512]{1,0:T(8,128)(2,1)S(1)}, u32[]{:S(2)}, u32[]{:S(2)}) %collective-permute-start.2) | collective-permute-done | bytes 278560 | tf_op jit(solution)/shard_map/ppermute | solution.py:104
  30.3 1.0 collective-permute-start.4
  31.3 1.7 %collective-permute-start.6 = (bf16[272,512]{1,0:T(8,128)(2,1)S(1)}, bf16[272,512]{1,0:T(8,128)(2,1)S(1)}, u32[]{:S(2)}, u32[]{:S(2)}) collective-permute-start(bf16[272,512]{1,0:T(8,128)(2,1)S(1)} %collective-permute-done.2.refs_2_), channel_id=1, source_target_pairs={{0,8},{8,0},{16,24},{24,16},{32,40},{40,32},{48,56},{56,48},{64,72... | collective-permute-start | bytes 835592 | tf_op jit(solution)/shard_map/ppermute | solution.py:108
  33.1 1.8 %collective-permute-start.5 = (bf16[272,512]{1,0:T(8,128)(2,1)S(1)}, bf16[272,512]{1,0:T(8,128)(2,1)S(1)}, u32[]{:S(2)}, u32[]{:S(2)}) collective-permute-start(bf16[272,512]{1,0:T(8,128)(2,1)S(1)} %collective-permute-done.1.refs_1_), channel_id=1, source_target_pairs={{0,8},{8,0},{16,24},{24,16},{32,40},{40,32},{48,56},{56,48},{64,72... | collective-permute-start | bytes 835592 | tf_op jit(solution)/shard_map/ppermute | solution.py:108
  34.9 0.8 collective-permute-done.3.refs_3_
  35.7 6.3 %collective-permute-start.7 = (bf16[272,512]{1,0:T(8,128)(2,1)S(1)}, bf16[272,512]{1,0:T(8,128)(2,1)S(1)}, u32[]{:S(2)}, u32[]{:S(2)}) collective-permute-start(bf16[272,512]{1,0:T(8,128)(2,1)S(1)} %collective-permute-done.3.refs_3_), channel_id=1, source_target_pairs={{0,8},{8,0},{16,24},{24,16},{32,40},{40,32},{48,56},{56,48},{64,72... | collective-permute-start | bytes 835592 | tf_op jit(solution)/shard_map/ppermute | solution.py:108
  42.1 2.9 %weights.1 = (bf16[4,512,768]{2,1,0:T(8,128)(2,1)S(1)}, bf16[4,512,768]{2,1,0:T(8,128)(2,1)S(1)}) custom-call(bf16[4,512,768]{2,1,0:T(8,128)(2,1)} %wg_hbm.1, bf16[4,512,768]{2,1,0:T(8,128)(2,1)} %wu_hbm.1), custom_call_target="tpu_custom_call" | custom-call | tf_op jit(solution)/shard_map/weights/pallas_call | solution.py:405
  45.0 3.6 %pack.1 = (bf16[2,32,1536]{2,1,0:T(8,128)(2,1)S(1)}, bf16[2,32,1536]{2,1,0:T(8,128)(2,1)S(1)}, bf16[2,32,1536]{2,1,0:T(8,128)(2,1)S(1)}, bf16[2,32,1536]{2,1,0:T...) custom-call(s32[18]{0:T(128)S(1)} %stack.123.info, ...), custom_call_target="tpu_custom_call" | custom-call | flops 2000000000 | bytes 6000000 | tf_op jit(solution)/shard_map/pack/pallas_call | solution.py:416
  48.6 3.0 %pack_more.1 = (bf16[2,32,1536]{2,1,0:T(8,128)(2,1)S(1)}, bf16[2,32,1536]{2,1,0:T(8,128)(2,1)S(1)}, bf16[2,32,1536]{2,1,0:T(8,128)(2,1)S(1)}, bf16[2,32,1536]{2,...) custom-call(s32[18]{0:T(128)S(1)} %stack.123.info, ...), custom_call_target="tpu_custom_call" | custom-call | flops 2000000000 | bytes 6000000 | tf_op jit(solution)/shard_map/pack_more/pallas_call | solution.py:433
  51.7 0.1 collective-permute-start.19
  51.8 1.4 %collective-permute-start.16 = (bf16[2,32,1536]{2,1,0:T(8,128)(2,1)S(1)}, bf16[2,32,1536]{2,1,0:T(8,128)(2,1)S(1)}, u32[]{:S(2)}, u32[]{:S(2)}) collective-permute-start(bf16[2,32,1536]{2,1,0:T(8,128)(2,1)S(1)} %get-tuple-element.56), channel_id=1, source_target_pairs={{0,1},{1,2},{2,3},{3,4},{4,5},{5,6},{6,7},{7,0},{8,9},{9,10},{10,1... | collective-permute-start | bytes 589832 | tf_op jit(solution)/shard_map/ppermute | solution.py:98
  53.2 1.3 collective-permute-start.13
  54.6 0.1 collective-permute-start.9
  54.7 3.0 %collective-permute-done.19 = bf16[2,32,1536]{2,1,0:T(8,128)(2,1)S(1)} collective-permute-done((bf16[2,32,1536]{2,1,0:T(8,128)(2,1)S(1)}, bf16[2,32,1536]{2,1,0:T(8,128)(2,1)S(1)}, u32[]{:S(2)}, u32[]{:S(2)}) %collective-permute-start.19) | collective-permute-done | bytes 196640 | tf_op jit(solution)/shard_map/ppermute | solution.py:98
  57.8 1.8 %collective-permute-start.20 = (bf16[2,32,1536]{2,1,0:T(8,128)(2,1)S(1)}, bf16[2,32,1536]{2,1,0:T(8,128)(2,1)S(1)}, u32[]{:S(2)}, u32[]{:S(2)}) collective-permute-start(bf16[2,32,1536]{2,1,0:T(8,128)(2,1)S(1)} %add_convert_fusion.2), channel_id=1, source_target_pairs={{0,7},{1,0},{2,1},{3,2},{4,3},{5,4},{6,5},{7,6},{8,15},{9,8},{10,9... | collective-permute-start | bytes 589832 | tf_op jit(solution)/shard_map/ppermute | solution.py:98
  59.6 0.1 collective-permute-start.17
  59.8 2.2 %collective-permute-done.13 = bf16[2,32,1536]{2,1,0:T(8,128)(2,1)S(1)} collective-permute-done((bf16[2,32,1536]{2,1,0:T(8,128)(2,1)S(1)}, bf16[2,32,1536]{2,1,0:T(8,128)(2,1)S(1)}, u32[]{:S(2)}, u32[]{:S(2)}) %collective-permute-start.13) | collective-permute-done | bytes 196640 | tf_op jit(solution)/shard_map/ppermute | solution.py:98
  62.0 1.6 %collective-permute-start.14 = (bf16[2,32,1536]{2,1,0:T(8,128)(2,1)S(1)}, bf16[2,32,1536]{2,1,0:T(8,128)(2,1)S(1)}, u32[]{:S(2)}, u32[]{:S(2)}) collective-permute-start(bf16[2,32,1536]{2,1,0:T(8,128)(2,1)S(1)} %add_convert_fusion.6), channel_id=1, source_target_pairs={{0,7},{1,0},{2,1},{3,2},{4,3},{5,4},{6,5},{7,6},{8,15},{9,8},{10,9... | collective-permute-start | bytes 589832 | tf_op jit(solution)/shard_map/ppermute | solution.py:98
  63.7 0.1 collective-permute-start.10
  63.8 2.3 %collective-permute-done.20 = bf16[2,32,1536]{2,1,0:T(8,128)(2,1)S(1)} collective-permute-done((bf16[2,32,1536]{2,1,0:T(8,128)(2,1)S(1)}, bf16[2,32,1536]{2,1,0:T(8,128)(2,1)S(1)}, u32[]{:S(2)}, u32[]{:S(2)}) %collective-permute-start.20) | collective-permute-done | bytes 196640 | tf_op jit(solution)/shard_map/ppermute | solution.py:98
  66.2 0.7 collective-permute-start.21
  67.0 1.0 collective-permute-start.18
  68.0 2.4 %collective-permute-done.14 = bf16[2,32,1536]{2,1,0:T(8,128)(2,1)S(1)} collective-permute-done((bf16[2,32,1536]{2,1,0:T(8,128)(2,1)S(1)}, bf16[2,32,1536]{2,1,0:T(8,128)(2,1)S(1)}, u32[]{:S(2)}, u32[]{:S(2)}) %collective-permute-start.14) | collective-permute-done | bytes 196640 | tf_op jit(solution)/shard_map/ppermute | solution.py:98
  70.4 0.9 collective-permute-start.15
  71.4 0.7 collective-permute-start.11
  72.2 2.4 %collective-permute-done.21 = bf16[2,32,1536]{2,1,0:T(8,128)(2,1)S(1)} collective-permute-done((bf16[2,32,1536]{2,1,0:T(8,128)(2,1)S(1)}, bf16[2,32,1536]{2,1,0:T(8,128)(2,1)S(1)}, u32[]{:S(2)}, u32[]{:S(2)}) %collective-permute-start.21) | collective-permute-done | bytes 196640 | tf_op jit(solution)/shard_map/ppermute | solution.py:98
  74.6 0.8 collective-permute-start.22
  75.4 3.3 %collective-permute-done.11 = bf16[2,32,1536]{2,1,0:T(8,128)(2,1)S(1)} collective-permute-done((bf16[2,32,1536]{2,1,0:T(8,128)(2,1)S(1)}, bf16[2,32,1536]{2,1,0:T(8,128)(2,1)S(1)}, u32[]{:S(2)}, u32[]{:S(2)}) %collective-permute-start.11) | collective-permute-done | bytes 196640 | tf_op jit(solution)/shard_map/ppermute | solution.py:98
  78.8 1.4 collective-permute-start.12
  80.2 2.9 %collective-permute-done.22.refs_5_ = bf16[2,32,1536]{2,1,0:T(8,128)(2,1)S(1)} collective-permute-done((bf16[2,32,1536]{2,1,0:T(8,128)(2,1)S(1)}, bf16[2,32,1536]{2,1,0:T(8,128)(2,1)S(1)}, u32[]{:S(2)}, u32[]{:S(2)}) %collective-permute-start.22) | collective-permute-done | bytes 196640 | tf_op jit(solution)/shard_map/ppermute | solution.py:98
  83.0 1.6 %collective-permute-done.12.refs_1_ = bf16[2,32,1536]{2,1,0:T(8,128)(2,1)S(1)} collective-permute-done((bf16[2,32,1536]{2,1,0:T(8,128)(2,1)S(1)}, bf16[2,32,1536]{2,1,0:T(8,128)(2,1)S(1)}, u32[]{:S(2)}, u32[]{:S(2)}) %collective-permute-start.12) | collective-permute-done | bytes 196640 | tf_op jit(solution)/shard_map/ppermute | solution.py:98
  84.6 0.2 hidden.1.refs_0_
  84.8 0.8 collective-permute-start.25
  85.6 2.9 %collective-permute-start.26 = (bf16[4,32,768]{2,1,0:T(8,128)(2,1)S(1)}, bf16[4,32,768]{2,1,0:T(8,128)(2,1)S(1)}, u32[]{:S(2)}, u32[]{:S(2)}) collective-permute-start(bf16[4,32,768]{2,1,0:T(8,128)(2,1)S(1)} %hidden.1.refs_0_), channel_id=1, source_target_pairs={{0,6},{1,7},{2,0},{3,1},{4,2},{5,3},{6,4},{7,5},{8,14},{9,15},{10,... | collective-permute-start | bytes 589832 | tf_op jit(solution)/shard_map/ppermute | solution.py:98
  88.5 0.4 collective-permute-start.23
  88.9 2.3 %collective-permute-start.24 = (bf16[4,32,768]{2,1,0:T(8,128)(2,1)S(1)}, bf16[4,32,768]{2,1,0:T(8,128)(2,1)S(1)}, u32[]{:S(2)}, u32[]{:S(2)}) collective-permute-start(bf16[4,32,768]{2,1,0:T(8,128)(2,1)S(1)} %hidden.1.refs_0_), channel_id=1, source_target_pairs={{0,7},{1,0},{2,1},{3,2},{4,3},{5,4},{6,5},{7,6},{8,15},{9,8},{10,9... | collective-permute-start | bytes 589832 | tf_op jit(solution)/shard_map/ppermute | solution.py:98
  91.2 4.1 %collective-permute-done.25.refs_3_ = bf16[4,32,768]{2,1,0:T(8,128)(2,1)S(1)} collective-permute-done((bf16[4,32,768]{2,1,0:T(8,128)(2,1)S(1)}, bf16[4,32,768]{2,1,0:T(8,128)(2,1)S(1)}, u32[]{:S(2)}, u32[]{:S(2)}) %collective-permute-start.25) | collective-permute-done | bytes 196640 | tf_op jit(solution)/shard_map/ppermute | solution.py:98
  95.3 2.7 %collective-permute-start.28 = (bf16[4,32,768]{2,1,0:T(8,128)(2,1)S(1)}, bf16[4,32,768]{2,1,0:T(8,128)(2,1)S(1)}, u32[]{:S(2)}, u32[]{:S(2)}) collective-permute-start(bf16[4,32,768]{2,1,0:T(8,128)(2,1)S(1)} %collective-permute-done.26.refs_4_), channel_id=1, source_target_pairs={{0,7},{1,0},{2,1},{3,2},{4,3},{5,4},{6,5},{7,6},{8,15},{9,8},{10,9... | collective-permute-start | bytes 589832 | tf_op jit(solution)/shard_map/ppermute | solution.py:98
  98.0 0.1 collective-permute-start.29
  98.1 1.6 %collective-permute-done.23.refs_1_ = bf16[4,32,768]{2,1,0:T(8,128)(2,1)S(1)} collective-permute-done((bf16[4,32,768]{2,1,0:T(8,128)(2,1)S(1)}, bf16[4,32,768]{2,1,0:T(8,128)(2,1)S(1)}, u32[]{:S(2)}, u32[]{:S(2)}) %collective-permute-start.23) | collective-permute-done | bytes 196640 | tf_op jit(solution)/shard_map/ppermute | solution.py:98
  99.7 2.0 %collective-permute-start.30 = (bf16[2,32,768]{2,1,0:T(8,128)(2,1)S(1)}, bf16[2,32,768]{2,1,0:T(8,128)(2,1)S(1)}, u32[]{:S(2)}, u32[]{:S(2)}) collective-permute-start(bf16[2,32,768]{2,1,0:T(8,128)(2,1)S(1)} %slice.14), channel_id=1, source_target_pairs={{0,6},{1,7},{2,0},{3,1},{4,2},{5,3},{6,4},{7,5},{8,14},{9,15},{10,... | collective-permute-start | bytes 294920 | tf_op jit(solution)/shard_map/ppermute | solution.py:98
  101.8 4.3 %mix.1 = (bf16[2048,1024]{1,0:T(8,128)(2,1)S(1)}, bf16[4,768,512]{2,1,0:T(8,128)(2,1)S(1)}) custom-call(s32[16]{0:T(128)S(1)} %stack.125.info, f32[16,8,128]{2,1,0:T(8,128)S(1)} %get-tuple-element.43.route, bf16[4,768,512]{2,1,0:T(8,128)(2,1)} %wd_hbm.1), custom_call_target="tpu_custom_call" | custom-call | tf_op jit(solution)/shard_map/mix/pallas_call | solution.py:461
  106.1 1.4 %collective-permute-done.29.refs_7_ = bf16[2,32,768]{2,1,0:T(8,128)(2,1)S(1)} collective-permute-done((bf16[2,32,768]{2,1,0:T(8,128)(2,1)S(1)}, bf16[2,32,768]{2,1,0:T(8,128)(2,1)S(1)}, u32[]{:S(2)}, u32[]{:S(2)}) %collective-permute-start.29) | collective-permute-done | bytes 98336 | tf_op jit(solution)/shard_map/ppermute | solution.py:98
  107.5 3.0 %down.1 = (bf16[4,128,512]{2,1,0:T(8,128)(2,1)S(1)}, bf16[1024,512]{1,0:T(8,128)(2,1)S(1)}) custom-call(s32[8]{0:T(128)S(1)} %stack.134.info, bf16[4,32,768]{2,1,0:T(8,128)(2,1)S(1)} %hidden.1.refs_0_, bf16[4,32,768]{2,1,0:T(8,128)(2,1)S(1)} %collective-permute-done.23.refs_1_, bf16[4,32,768]{2,1,0:T(8,128)(2,1)S(1)} %collective-permute-done.24.refs_2_, ...), custom_call_target="tpu_custom_call" | custom-call | flops 2000000000 | bytes 6000000 | tf_op jit(solution)/shard_map/down/pallas_call | solution.py:474
  110.5 4.9 %collective-permute-start.31 = (bf16[4,128,512]{2,1,0:T(8,128)(2,1)S(1)}, bf16[4,128,512]{2,1,0:T(8,128)(2,1)S(1)}, u32[]{:S(2)}, u32[]{:S(2)}) collective-permute-start(bf16[4,128,512]{2,1,0:T(8,128)(2,1)S(1)} %get-tuple-element.66), channel_id=1, source_target_pairs={{0,8},{8,0},{16,24},{24,16},{32,40},{40,32},{48,56},{56,48},{64,72... | collective-permute-start | bytes 1572872 | tf_op jit(solution)/shard_map/ppermute | solution.py:108
  115.4 1.7 %shard_map.113 = (bf16[4,128,512]{2,1,0:T(8,128)(2,1)S(1)}, bf16[4,128,512]{2,1,0:T(8,128)(2,1)S(1)}) custom-call(bf16[2048,1024]{1,0:T(8,128)(2,1)S(1)} %get-tuple-element.44.refs_10_.mix, bf16[1024,512]{1,0:T(8,128)(2,1)S(1)} %get-tuple-element.64.res), custom_call_target="tpu_custom_call" | custom-call | tf_op jit(solution)/shard_map/pallas_call | solution.py:486
  117.1 0.1 collective-permute-start.32
  117.4 1.6 %collective-permute-start.35 = (bf16[256,512]{1,0:T(8,128)(2,1)S(1)}, bf16[256,512]{1,0:T(8,128)(2,1)S(1)}, u32[]{:S(2)}, u32[]{:S(2)}) collective-permute-start(bf16[256,512]{1,0:T(8,128)(2,1)S(1)} %get-tuple-element.70), channel_id=1, source_target_pairs={{0,16},{8,120},{16,32},{24,8},{32,48},{40,24},{48,64},{56,40},{64,... | collective-permute-start | bytes 786440 | tf_op jit(solution)/shard_map/ppermute | solution.py:104
  119.0 0.9 shard_map.114.home
  120.0 0.9 collective-permute-start.33
  120.8 4.7 %collective-permute-start.34 = (bf16[128,512]{1,0:T(8,128)(2,1)S(1)}, bf16[128,512]{1,0:T(8,128)(2,1)S(1)}, u32[]{:S(2)}, u32[]{:S(2)}) collective-permute-start(bf16[128,512]{1,0:T(8,128)(2,1)S(1)} %get-tuple-element.69), channel_id=1, source_target_pairs={{0,24},{8,112},{16,40},{24,0},{32,56},{40,16},{48,72},{56,32},{64,... | collective-permute-start | bytes 393224 | tf_op jit(solution)/shard_map/ppermute | solution.py:104
  125.6 3.4 %collective-permute-done.36.four = bf16[128,512]{1,0:T(8,128)(2,1)S(1)} collective-permute-done((bf16[128,512]{1,0:T(8,128)(2,1)S(1)}, bf16[128,512]{1,0:T(8,128)(2,1)S(1)}, u32[]{:S(2)}, u32[]{:S(2)}) %collective-permute-start.36) | collective-permute-done | bytes 131104 | tf_op jit(solution)/shard_map/ppermute | solution.py:104
  129.0 0.1 shard_map.117
  129.1 0.1 collective-permute-start.37
  129.3 3.6 %collective-permute-start.38 = (bf16[128,512]{1,0:T(8,128)(2,1)S(1)}, bf16[128,512]{1,0:T(8,128)(2,1)S(1)}, u32[]{:S(2)}, u32[]{:S(2)}) collective-permute-start(bf16[128,512]{1,0:T(8,128)(2,1)S(1)} %get-tuple-element.73), channel_id=1, source_target_pairs={{0,40},{8,96},{16,56},{24,112},{32,72},{40,0},{48,88},{56,16},{64,... | collective-permute-start | bytes 393224 | tf_op jit(solution)/shard_map/ppermute | solution.py:104
  132.9 3.4 %attention.1 = bf16[2,64,128]{2,1,0:T(8,128)(2,1)S(1)} custom-call(s32[2]{0:T(128)S(1)} %copy-done, bf16[2,64,128]{2,1,0:T(8,128)(2,1)} %query.1, bf16[2,768,4,128]{3,2,1,0:T(4,128)(2,1)} %cache_k.1, bf16[2,768,4,128]{3,2,1,0:T(4,128)(2,1)} %cache_v.1), custom_call_target="tpu_custom_call" | custom-call | flops 1000000000 | bytes 3000000 | tf_op jit(solution)/shard_map/attention/pallas_call | solution.py:81
  136.3 0.6 copy.14
  136.9 1.9 %collective-permute-done.38.d = bf16[128,512]{1,0:T(8,128)(2,1)S(1)} collective-permute-done((bf16[128,512]{1,0:T(8,128)(2,1)S(1)}, bf16[128,512]{1,0:T(8,128)(2,1)S(1)}, u32[]{:S(2)}, u32[]{:S(2)}) %collective-permute-start.38) | collective-permute-done | bytes 131104 | tf_op jit(solution)/shard_map/ppermute | solution.py:104
  138.9 0.8 shard_map.118
  (48 shorter events, 1.1 us)
Async XLA Ops:
  2.0 21.5 %collective-permute-start = (bf16[136,512]{1,0:T(8,128)(2,1)S(1)}, bf16[136,512]{1,0:T(8,128)(2,1)S(1)}, u32[]{:S(2)}, u32[]{:S(2)}) collective-permute-start(bf16[136,512]{1,0:T(8,128)(2,1)S(1)} %prepare.1.refs_0_), channel_id=1, source_target_pairs={{0,8},{8,0},{16,24},{24,16},{32,40},{40,32},{48,56},{56,48},{64,72... | collective-permute-start | bytes 417800 | tf_op jit(solution)/shard_map/ppermute | solution.py:108
  23.6 6.8 %collective-permute-start.2 = (bf16[272,512]{1,0:T(8,128)(2,1)S(1)}, bf16[272,512]{1,0:T(8,128)(2,1)S(1)}, u32[]{:S(2)}, u32[]{:S(2)}) collective-permute-start(bf16[272,512]{1,0:T(8,128)(2,1)S(1)} %pair.1.refs_0_), channel_id=1, source_target_pairs={{0,32},{8,104},{16,48},{24,120},{32,64},{40,8},{48,80},{56,24},{64... | collective-permute-start | bytes 835592 | tf_op jit(solution)/shard_map/ppermute | solution.py:104
  23.7 9.4 %collective-permute-start.1 = (bf16[272,512]{1,0:T(8,128)(2,1)S(1)}, bf16[272,512]{1,0:T(8,128)(2,1)S(1)}, u32[]{:S(2)}, u32[]{:S(2)}) collective-permute-start(bf16[272,512]{1,0:T(8,128)(2,1)S(1)} %pair.1.refs_0_), channel_id=1, source_target_pairs={{0,16},{8,120},{16,32},{24,8},{32,48},{40,24},{48,64},{56,40},{64,... | collective-permute-start | bytes 835592 | tf_op jit(solution)/shard_map/ppermute | solution.py:104
  30.3 5.4 %collective-permute-start.3 = (bf16[272,512]{1,0:T(8,128)(2,1)S(1)}, bf16[272,512]{1,0:T(8,128)(2,1)S(1)}, u32[]{:S(2)}, u32[]{:S(2)}) collective-permute-start(bf16[272,512]{1,0:T(8,128)(2,1)S(1)} %collective-permute-done.2.refs_2_), channel_id=1, source_target_pairs={{0,16},{8,120},{16,32},{24,8},{32,48},{40,24},{48,64},{56,40},{64,... | collective-permute-start | bytes 835592 | tf_op jit(solution)/shard_map/ppermute | solution.py:104
  30.3 11.7 %collective-permute-start.4 = (bf16[136,512]{1,0:T(8,128)(2,1)S(1)}, bf16[136,512]{1,0:T(8,128)(2,1)S(1)}, u32[]{:S(2)}, u32[]{:S(2)}) collective-permute-start(bf16[136,512]{1,0:T(8,128)(2,1)S(1)} %slice.12), channel_id=1, source_target_pairs={{0,32},{8,104},{16,48},{24,120},{32,64},{40,8},{48,80},{56,24},{64... | collective-permute-start | bytes 417800 | tf_op jit(solution)/shard_map/ppermute | solution.py:104
  31.3 13.6 %collective-permute-start.6 = (bf16[272,512]{1,0:T(8,128)(2,1)S(1)}, bf16[272,512]{1,0:T(8,128)(2,1)S(1)}, u32[]{:S(2)}, u32[]{:S(2)}) collective-permute-start(bf16[272,512]{1,0:T(8,128)(2,1)S(1)} %collective-permute-done.2.refs_2_), channel_id=1, source_target_pairs={{0,8},{8,0},{16,24},{24,16},{32,40},{40,32},{48,56},{56,48},{64,72... | collective-permute-start | bytes 835592 | tf_op jit(solution)/shard_map/ppermute | solution.py:108
  33.1 11.9 %collective-permute-start.5 = (bf16[272,512]{1,0:T(8,128)(2,1)S(1)}, bf16[272,512]{1,0:T(8,128)(2,1)S(1)}, u32[]{:S(2)}, u32[]{:S(2)}) collective-permute-start(bf16[272,512]{1,0:T(8,128)(2,1)S(1)} %collective-permute-done.1.refs_1_), channel_id=1, source_target_pairs={{0,8},{8,0},{16,24},{24,16},{32,40},{40,32},{48,56},{56,48},{64,72... | collective-permute-start | bytes 835592 | tf_op jit(solution)/shard_map/ppermute | solution.py:108
  35.7 9.2 %collective-permute-start.7 = (bf16[272,512]{1,0:T(8,128)(2,1)S(1)}, bf16[272,512]{1,0:T(8,128)(2,1)S(1)}, u32[]{:S(2)}, u32[]{:S(2)}) collective-permute-start(bf16[272,512]{1,0:T(8,128)(2,1)S(1)} %collective-permute-done.3.refs_3_), channel_id=1, source_target_pairs={{0,8},{8,0},{16,24},{24,16},{32,40},{40,32},{48,56},{56,48},{64,72... | collective-permute-start | bytes 835592 | tf_op jit(solution)/shard_map/ppermute | solution.py:108
  42.0 2.9 %collective-permute-start.8 = (bf16[136,512]{1,0:T(8,128)(2,1)S(1)}, bf16[136,512]{1,0:T(8,128)(2,1)S(1)}, u32[]{:S(2)}, u32[]{:S(2)}) collective-permute-start(bf16[136,512]{1,0:T(8,128)(2,1)S(1)} %collective-permute-done.4.refs_4_), channel_id=1, source_target_pairs={{0,8},{8,0},{16,24},{24,16},{32,40},{40,32},{48,56},{56,48},{64,72... | collective-permute-start | bytes 417800 | tf_op jit(solution)/shard_map/ppermute | solution.py:108
  51.7 6.1 %collective-permute-start.19 = (bf16[2,32,1536]{2,1,0:T(8,128)(2,1)S(1)}, bf16[2,32,1536]{2,1,0:T(8,128)(2,1)S(1)}, u32[]{:S(2)}, u32[]{:S(2)}) collective-permute-start(bf16[2,32,1536]{2,1,0:T(8,128)(2,1)S(1)} %get-tuple-element.59), channel_id=1, source_target_pairs={{0,7},{1,0},{2,1},{3,2},{4,3},{5,4},{6,5},{7,6},{8,15},{9,8},{10,9... | collective-permute-start | bytes 589832 | tf_op jit(solution)/shard_map/ppermute | solution.py:98
  51.8 7.8 %collective-permute-start.16 = (bf16[2,32,1536]{2,1,0:T(8,128)(2,1)S(1)}, bf16[2,32,1536]{2,1,0:T(8,128)(2,1)S(1)}, u32[]{:S(2)}, u32[]{:S(2)}) collective-permute-start(bf16[2,32,1536]{2,1,0:T(8,128)(2,1)S(1)} %get-tuple-element.56), channel_id=1, source_target_pairs={{0,1},{1,2},{2,3},{3,4},{4,5},{5,6},{6,7},{7,0},{8,9},{9,10},{10,1... | collective-permute-start | bytes 589832 | tf_op jit(solution)/shard_map/ppermute | solution.py:98
  53.2 8.7 %collective-permute-start.13 = (bf16[2,32,1536]{2,1,0:T(8,128)(2,1)S(1)}, bf16[2,32,1536]{2,1,0:T(8,128)(2,1)S(1)}, u32[]{:S(2)}, u32[]{:S(2)}) collective-permute-start(bf16[2,32,1536]{2,1,0:T(8,128)(2,1)S(1)} %get-tuple-element.51), channel_id=1, source_target_pairs={{0,7},{1,0},{2,1},{3,2},{4,3},{5,4},{6,5},{7,6},{8,15},{9,8},{10,9... | collective-permute-start | bytes 589832 | tf_op jit(solution)/shard_map/ppermute | solution.py:98
  54.6 9.0 %collective-permute-start.9 = (bf16[2,32,1536]{2,1,0:T(8,128)(2,1)S(1)}, bf16[2,32,1536]{2,1,0:T(8,128)(2,1)S(1)}, u32[]{:S(2)}, u32[]{:S(2)}) collective-permute-start(bf16[2,32,1536]{2,1,0:T(8,128)(2,1)S(1)} %get-tuple-element.47), channel_id=1, source_target_pairs={{0,1},{1,2},{2,3},{3,4},{4,5},{5,6},{6,7},{7,0},{8,9},{9,10},{10,1... | collective-permute-start | bytes 589832 | tf_op jit(solution)/shard_map/ppermute | solution.py:98
  57.8 8.4 %collective-permute-start.20 = (bf16[2,32,1536]{2,1,0:T(8,128)(2,1)S(1)}, bf16[2,32,1536]{2,1,0:T(8,128)(2,1)S(1)}, u32[]{:S(2)}, u32[]{:S(2)}) collective-permute-start(bf16[2,32,1536]{2,1,0:T(8,128)(2,1)S(1)} %add_convert_fusion.2), channel_id=1, source_target_pairs={{0,7},{1,0},{2,1},{3,2},{4,3},{5,4},{6,5},{7,6},{8,15},{9,8},{10,9... | collective-permute-start | bytes 589832 | tf_op jit(solution)/shard_map/ppermute | solution.py:98
  59.6 7.3 %collective-permute-start.17 = (bf16[2,32,1536]{2,1,0:T(8,128)(2,1)S(1)}, bf16[2,32,1536]{2,1,0:T(8,128)(2,1)S(1)}, u32[]{:S(2)}, u32[]{:S(2)}) collective-permute-start(bf16[2,32,1536]{2,1,0:T(8,128)(2,1)S(1)} %add_convert_fusion.4), channel_id=1, source_target_pairs={{0,1},{1,2},{2,3},{3,4},{4,5},{5,6},{6,7},{7,0},{8,9},{9,10},{10,1... | collective-permute-start | bytes 589832 | tf_op jit(solution)/shard_map/ppermute | solution.py:98
  62.0 8.4 %collective-permute-start.14 = (bf16[2,32,1536]{2,1,0:T(8,128)(2,1)S(1)}, bf16[2,32,1536]{2,1,0:T(8,128)(2,1)S(1)}, u32[]{:S(2)}, u32[]{:S(2)}) collective-permute-start(bf16[2,32,1536]{2,1,0:T(8,128)(2,1)S(1)} %add_convert_fusion.6), channel_id=1, source_target_pairs={{0,7},{1,0},{2,1},{3,2},{4,3},{5,4},{6,5},{7,6},{8,15},{9,8},{10,9... | collective-permute-start | bytes 589832 | tf_op jit(solution)/shard_map/ppermute | solution.py:98
  63.7 7.7 %collective-permute-start.10 = (bf16[2,32,1536]{2,1,0:T(8,128)(2,1)S(1)}, bf16[2,32,1536]{2,1,0:T(8,128)(2,1)S(1)}, u32[]{:S(2)}, u32[]{:S(2)}) collective-permute-start(bf16[2,32,1536]{2,1,0:T(8,128)(2,1)S(1)} %add_convert_fusion.9), channel_id=1, source_target_pairs={{0,1},{1,2},{2,3},{3,4},{4,5},{5,6},{6,7},{7,0},{8,9},{9,10},{10,1... | collective-permute-start | bytes 589832 | tf_op jit(solution)/shard_map/ppermute | solution.py:98
  66.2 8.4 %collective-permute-start.21 = (bf16[2,32,1536]{2,1,0:T(8,128)(2,1)S(1)}, bf16[2,32,1536]{2,1,0:T(8,128)(2,1)S(1)}, u32[]{:S(2)}, u32[]{:S(2)}) collective-permute-start(bf16[2,32,1536]{2,1,0:T(8,128)(2,1)S(1)} %add_convert_fusion.1), channel_id=1, source_target_pairs={{0,7},{1,0},{2,1},{3,2},{4,3},{5,4},{6,5},{7,6},{8,15},{9,8},{10,9... | collective-permute-start | bytes 589832 | tf_op jit(solution)/shard_map/ppermute | solution.py:98
  67.0 13.2 %collective-permute-start.18 = (bf16[2,32,1536]{2,1,0:T(8,128)(2,1)S(1)}, bf16[2,32,1536]{2,1,0:T(8,128)(2,1)S(1)}, u32[]{:S(2)}, u32[]{:S(2)}) collective-permute-start(bf16[2,32,1536]{2,1,0:T(8,128)(2,1)S(1)} %add_convert_fusion.3), channel_id=1, source_target_pairs={{0,1},{1,2},{2,3},{3,4},{4,5},{5,6},{6,7},{7,0},{8,9},{9,10},{10,1... | collective-permute-start | bytes 589832 | tf_op jit(solution)/shard_map/ppermute | solution.py:98
  70.4 9.7 %collective-permute-start.15 = (bf16[2,32,1536]{2,1,0:T(8,128)(2,1)S(1)}, bf16[2,32,1536]{2,1,0:T(8,128)(2,1)S(1)}, u32[]{:S(2)}, u32[]{:S(2)}) collective-permute-start(bf16[2,32,1536]{2,1,0:T(8,128)(2,1)S(1)} %add_convert_fusion.5), channel_id=1, source_target_pairs={{0,7},{1,0},{2,1},{3,2},{4,3},{5,4},{6,5},{7,6},{8,15},{9,8},{10,9... | collective-permute-start | bytes 589832 | tf_op jit(solution)/shard_map/ppermute | solution.py:98
  71.4 7.3 %collective-permute-start.11 = (bf16[2,32,1536]{2,1,0:T(8,128)(2,1)S(1)}, bf16[2,32,1536]{2,1,0:T(8,128)(2,1)S(1)}, u32[]{:S(2)}, u32[]{:S(2)}) collective-permute-start(bf16[2,32,1536]{2,1,0:T(8,128)(2,1)S(1)} %add_convert_fusion.8), channel_id=1, source_target_pairs={{0,1},{1,2},{2,3},{3,4},{4,5},{5,6},{6,7},{7,0},{8,9},{9,10},{10,1... | collective-permute-start | bytes 589832 | tf_op jit(solution)/shard_map/ppermute | solution.py:98
  74.6 8.4 %collective-permute-start.22 = (bf16[2,32,1536]{2,1,0:T(8,128)(2,1)S(1)}, bf16[2,32,1536]{2,1,0:T(8,128)(2,1)S(1)}, u32[]{:S(2)}, u32[]{:S(2)}) collective-permute-start(bf16[2,32,1536]{2,1,0:T(8,128)(2,1)S(1)} %add_convert_fusion), channel_id=1, source_target_pairs={{0,7},{1,0},{2,1},{3,2},{4,3},{5,4},{6,5},{7,6},{8,15},{9,8},{10,9... | collective-permute-start | bytes 589832 | tf_op jit(solution)/shard_map/ppermute | solution.py:98
  78.8 5.8 %collective-permute-start.12 = (bf16[2,32,1536]{2,1,0:T(8,128)(2,1)S(1)}, bf16[2,32,1536]{2,1,0:T(8,128)(2,1)S(1)}, u32[]{:S(2)}, u32[]{:S(2)}) collective-permute-start(bf16[2,32,1536]{2,1,0:T(8,128)(2,1)S(1)} %add_convert_fusion.7), channel_id=1, source_target_pairs={{0,1},{1,2},{2,3},{3,4},{4,5},{5,6},{6,7},{7,0},{8,9},{9,10},{10,1... | collective-permute-start | bytes 589832 | tf_op jit(solution)/shard_map/ppermute | solution.py:98
  84.8 10.4 %collective-permute-start.25 = (bf16[4,32,768]{2,1,0:T(8,128)(2,1)S(1)}, bf16[4,32,768]{2,1,0:T(8,128)(2,1)S(1)}, u32[]{:S(2)}, u32[]{:S(2)}) collective-permute-start(bf16[4,32,768]{2,1,0:T(8,128)(2,1)S(1)} %hidden.1.refs_0_), channel_id=1, source_target_pairs={{0,2},{1,3},{2,4},{3,5},{4,6},{5,7},{6,0},{7,1},{8,10},{9,11},{10,... | collective-permute-start | bytes 589832 | tf_op jit(solution)/shard_map/ppermute | solution.py:98
  85.6 9.7 %collective-permute-start.26 = (bf16[4,32,768]{2,1,0:T(8,128)(2,1)S(1)}, bf16[4,32,768]{2,1,0:T(8,128)(2,1)S(1)}, u32[]{:S(2)}, u32[]{:S(2)}) collective-permute-start(bf16[4,32,768]{2,1,0:T(8,128)(2,1)S(1)} %hidden.1.refs_0_), channel_id=1, source_target_pairs={{0,6},{1,7},{2,0},{3,1},{4,2},{5,3},{6,4},{7,5},{8,14},{9,15},{10,... | collective-permute-start | bytes 589832 | tf_op jit(solution)/shard_map/ppermute | solution.py:98
  88.5 11.2 %collective-permute-start.23 = (bf16[4,32,768]{2,1,0:T(8,128)(2,1)S(1)}, bf16[4,32,768]{2,1,0:T(8,128)(2,1)S(1)}, u32[]{:S(2)}, u32[]{:S(2)}) collective-permute-start(bf16[4,32,768]{2,1,0:T(8,128)(2,1)S(1)} %hidden.1.refs_0_), channel_id=1, source_target_pairs={{0,1},{1,2},{2,3},{3,4},{4,5},{5,6},{6,7},{7,0},{8,9},{9,10},{10,1... | collective-permute-start | bytes 589832 | tf_op jit(solution)/shard_map/ppermute | solution.py:98
  88.9 17.1 %collective-permute-start.24 = (bf16[4,32,768]{2,1,0:T(8,128)(2,1)S(1)}, bf16[4,32,768]{2,1,0:T(8,128)(2,1)S(1)}, u32[]{:S(2)}, u32[]{:S(2)}) collective-permute-start(bf16[4,32,768]{2,1,0:T(8,128)(2,1)S(1)} %hidden.1.refs_0_), channel_id=1, source_target_pairs={{0,7},{1,0},{2,1},{3,2},{4,3},{5,4},{6,5},{7,6},{8,15},{9,8},{10,9... | collective-permute-start | bytes 589832 | tf_op jit(solution)/shard_map/ppermute | solution.py:98
  95.3 12.2 %collective-permute-start.27 = (bf16[4,32,768]{2,1,0:T(8,128)(2,1)S(1)}, bf16[4,32,768]{2,1,0:T(8,128)(2,1)S(1)}, u32[]{:S(2)}, u32[]{:S(2)}) collective-permute-start(bf16[4,32,768]{2,1,0:T(8,128)(2,1)S(1)} %collective-permute-done.25.refs_3_), channel_id=1, source_target_pairs={{0,1},{1,2},{2,3},{3,4},{4,5},{5,6},{6,7},{7,0},{8,9},{9,10},{10,1... | collective-permute-start | bytes 589832 | tf_op jit(solution)/shard_map/ppermute | solution.py:98
  95.3 12.2 %collective-permute-start.28 = (bf16[4,32,768]{2,1,0:T(8,128)(2,1)S(1)}, bf16[4,32,768]{2,1,0:T(8,128)(2,1)S(1)}, u32[]{:S(2)}, u32[]{:S(2)}) collective-permute-start(bf16[4,32,768]{2,1,0:T(8,128)(2,1)S(1)} %collective-permute-done.26.refs_4_), channel_id=1, source_target_pairs={{0,7},{1,0},{2,1},{3,2},{4,3},{5,4},{6,5},{7,6},{8,15},{9,8},{10,9... | collective-permute-start | bytes 589832 | tf_op jit(solution)/shard_map/ppermute | solution.py:98
  98.0 9.5 %collective-permute-start.29 = (bf16[2,32,768]{2,1,0:T(8,128)(2,1)S(1)}, bf16[2,32,768]{2,1,0:T(8,128)(2,1)S(1)}, u32[]{:S(2)}, u32[]{:S(2)}) collective-permute-start(bf16[2,32,768]{2,1,0:T(8,128)(2,1)S(1)} %slice.13), channel_id=1, source_target_pairs={{0,2},{1,3},{2,4},{3,5},{4,6},{5,7},{6,0},{7,1},{8,10},{9,11},{10,... | collective-permute-start | bytes 294920 | tf_op jit(solution)/shard_map/ppermute | solution.py:98
  99.7 7.7 %collective-permute-start.30 = (bf16[2,32,768]{2,1,0:T(8,128)(2,1)S(1)}, bf16[2,32,768]{2,1,0:T(8,128)(2,1)S(1)}, u32[]{:S(2)}, u32[]{:S(2)}) collective-permute-start(bf16[2,32,768]{2,1,0:T(8,128)(2,1)S(1)} %slice.14), channel_id=1, source_target_pairs={{0,6},{1,7},{2,0},{3,1},{4,2},{5,3},{6,4},{7,5},{8,14},{9,15},{10,... | collective-permute-start | bytes 294920 | tf_op jit(solution)/shard_map/ppermute | solution.py:98
  110.5 6.8 %collective-permute-start.31 = (bf16[4,128,512]{2,1,0:T(8,128)(2,1)S(1)}, bf16[4,128,512]{2,1,0:T(8,128)(2,1)S(1)}, u32[]{:S(2)}, u32[]{:S(2)}) collective-permute-start(bf16[4,128,512]{2,1,0:T(8,128)(2,1)S(1)} %get-tuple-element.66), channel_id=1, source_target_pairs={{0,8},{8,0},{16,24},{24,16},{32,40},{40,32},{48,56},{56,48},{64,72... | collective-permute-start | bytes 1572872 | tf_op jit(solution)/shard_map/ppermute | solution.py:108
  117.1 2.8 %collective-permute-start.32 = (bf16[4,128,512]{2,1,0:T(8,128)(2,1)S(1)}, bf16[4,128,512]{2,1,0:T(8,128)(2,1)S(1)}, u32[]{:S(2)}, u32[]{:S(2)}) collective-permute-start(bf16[4,128,512]{2,1,0:T(8,128)(2,1)S(1)} %get-tuple-element.67), channel_id=1, source_target_pairs={{0,8},{8,0},{16,24},{24,16},{32,40},{40,32},{48,56},{56,48},{64,72... | collective-permute-start | bytes 1572872 | tf_op jit(solution)/shard_map/ppermute | solution.py:108
  117.4 11.6 %collective-permute-start.35 = (bf16[256,512]{1,0:T(8,128)(2,1)S(1)}, bf16[256,512]{1,0:T(8,128)(2,1)S(1)}, u32[]{:S(2)}, u32[]{:S(2)}) collective-permute-start(bf16[256,512]{1,0:T(8,128)(2,1)S(1)} %get-tuple-element.70), channel_id=1, source_target_pairs={{0,16},{8,120},{16,32},{24,8},{32,48},{40,24},{48,64},{56,40},{64,... | collective-permute-start | bytes 786440 | tf_op jit(solution)/shard_map/ppermute | solution.py:104
  119.0 13.9 %copy-start = (s32[2]{0:T(128)S(1)}, s32[2]{0:T(128)}, u32[]{:S(2)}) copy-start(s32[2]{0:T(128)} %lengths.1) | copy-start | bytes 28
  119.0 10.0 %collective-permute-start.36 = (bf16[128,512]{1,0:T(8,128)(2,1)S(1)}, bf16[128,512]{1,0:T(8,128)(2,1)S(1)}, u32[]{:S(2)}, u32[]{:S(2)}) collective-permute-start(bf16[128,512]{1,0:T(8,128)(2,1)S(1)} %get-tuple-element.71), channel_id=1, source_target_pairs={{0,32},{8,104},{16,48},{24,120},{32,64},{40,8},{48,80},{56,24},{64... | collective-permute-start | bytes 393224 | tf_op jit(solution)/shard_map/ppermute | solution.py:104
  120.0 17.0 %collective-permute-start.33 = (bf16[128,512]{1,0:T(8,128)(2,1)S(1)}, bf16[128,512]{1,0:T(8,128)(2,1)S(1)}, u32[]{:S(2)}, u32[]{:S(2)}) collective-permute-start(bf16[128,512]{1,0:T(8,128)(2,1)S(1)} %get-tuple-element.68), channel_id=1, source_target_pairs={{0,16},{8,120},{16,32},{24,8},{32,48},{40,24},{48,64},{56,40},{64,... | collective-permute-start | bytes 393224 | tf_op jit(solution)/shard_map/ppermute | solution.py:104
  120.8 16.1 %collective-permute-start.34 = (bf16[128,512]{1,0:T(8,128)(2,1)S(1)}, bf16[128,512]{1,0:T(8,128)(2,1)S(1)}, u32[]{:S(2)}, u32[]{:S(2)}) collective-permute-start(bf16[128,512]{1,0:T(8,128)(2,1)S(1)} %get-tuple-element.69), channel_id=1, source_target_pairs={{0,24},{8,112},{16,40},{24,0},{32,56},{40,16},{48,72},{56,32},{64,... | collective-permute-start | bytes 393224 | tf_op jit(solution)/shard_map/ppermute | solution.py:104
  129.1 7.8 %collective-permute-start.37 = (bf16[128,512]{1,0:T(8,128)(2,1)S(1)}, bf16[128,512]{1,0:T(8,128)(2,1)S(1)}, u32[]{:S(2)}, u32[]{:S(2)}) collective-permute-start(bf16[128,512]{1,0:T(8,128)(2,1)S(1)} %get-tuple-element.72), channel_id=1, source_target_pairs={{0,32},{8,104},{16,48},{24,120},{32,64},{40,8},{48,80},{56,24},{64... | collective-permute-start | bytes 393224 | tf_op jit(solution)/shard_map/ppermute | solution.py:104
  129.3 9.6 %collective-permute-start.38 = (bf16[128,512]{1,0:T(8,128)(2,1)S(1)}, bf16[128,512]{1,0:T(8,128)(2,1)S(1)}, u32[]{:S(2)}, u32[]{:S(2)}) collective-permute-start(bf16[128,512]{1,0:T(8,128)(2,1)S(1)} %get-tuple-element.73), channel_id=1, source_target_pairs={{0,40},{8,96},{16,56},{24,112},{32,72},{40,0},{48,88},{56,16},{64,... | collective-permute-start | bytes 393224 | tf_op jit(solution)/shard_map/ppermute | solution.py:104

commit v5 on v4

--- a/solution.py
+++ b/solution.py
@@ -143,9 +143,13 @@
     row_id = jnp.where(row_id < capacity, row_id, row_id - capacity).astype(F32)
 
     def expert(j, carry):
-        for i in range(n_blocks):
+        def select(i, carry):
             spot = place[info[1 + i], pl.ds(j0 + j, 1), :]
-            onehot[:, i * rows : (i + 1) * rows] = jnp.where(row_id == spot, 1.0, 0.0).astype(BF16)
+            at = pl.ds(pl.multiple_of(i * rows, rows), rows)
+            onehot[:, at] = jnp.where(row_id == spot, 1.0, 0.0).astype(BF16)
+            return carry
+
+        lax.fori_loop(0, n_blocks, select, 0, unroll=2)
         mine = jnp.dot(onehot[...], tok[...], preferred_element_type=F32).astype(BF16)
         gate = jnp.dot(mine, wg[j0 + j], preferred_element_type=F32).astype(BF16)
         up = jnp.dot(mine, wu[j0 + j], preferred_element_type=F32).astype(BF16)
@@ -383,20 +387,27 @@
     def pass_on(value, places, cross=0):
         return both_ways(value, places, cross)
 
-    pair = pl.pallas_call(
-        bundle_kernel,
-        out_shape=jax.ShapeDtypeStruct((2 * height, feat), BF16),
-        in_specs=[VMEM_SPEC] * 2,
-        out_specs=VMEM_SPEC,
-        name="pair",
-        **SMALL,
-    )(*map(in_vmem, (block, swap_cores(block))))
-    two, one = pass_on(pair, 2), pass_on(pair, 1)
-    four, three = pass_on(two[:height], 2), pass_on(two, 1)
-    operands = [pair, one, two, three, four]
+    def paired(one, two):
+        return pl.pallas_call(
+            bundle_kernel,
+            out_shape=jax.ShapeDtypeStruct((2 * height, feat), BF16),
+            in_specs=[VMEM_SPEC] * 2,
+            out_specs=VMEM_SPEC,
+            name="pair",
+            **SMALL,
+        )(in_vmem(one), in_vmem(two))
+
+    two_own = pass_on(block, 2)
+    other = swap_cores(block)
+    two_other = pass_on(other, 2)
+    one = pass_on(paired(block, other), 1)
+    four = pass_on(two_own, 2)
+    two = paired(two_own, two_other)
+    three = pass_on(two, 1)
+    operands = [block, other, one, two_own, two_other, three, four]
     operands += [swap_cores(one), swap_cores(two), swap_cores(three), swap_cores(four)]
-    pairs = [((i, 0), (i, height)) for i in range(8) if i != 4]
-    plan = [at for p in pairs[:4] for at in p] + [(4, 0)] + [at for p in pairs[4:] for at in p] + [(8, 0)]
+    plan = [(0, 0), (1, 0), (2, 0), (2, height), (3, 0), (4, 0), (5, 0), (5, height), (6, 0)]
+    plan += [(i, r) for i in (7, 8, 9) for r in (0, height)] + [(10, 0)]
 
     cut = local // 2
     pack_scratch = [

time: 140 us -> 140 us (level)
  waiting for transfers between devices: 40.9 us -> 39.1 us
    ppermute x10 -> x11, waiting for transfers between devices: 12.6 us -> 11.3 us  [both_ways(): return lax.ppermute(value, 'attn', pairs)]
    ppermute x10 -> x11, starting transfers between devices: 12.3 us -> 12.4 us  [both_ways(): return lax.ppermute(value, 'attn', pairs)]
  transfers between devices with their start and end apart: 39 -> 40, of which waited for: 16 -> 18; matrix products, arithmetic and copies ran while one was open for 1% -> 1% of each run, Pallas kernels for 10% -> 10%
where the time goes in v5:
time: 140 us
  starting transfers between devices  71.7 us (51%)
  waiting for transfers between devices  39.1 us (28%)
  Pallas kernels  26.3 us (19%)
    ppermute x7, starting transfers between devices, swap_cores(): lax.ppermute(value, 'attn', [(i, i ^ 1) for i in range(lax.axis_size('att...  35.7 us
    ppermute x22, waiting for transfers between devices, shift(): lax.ppermute(value, axis, [(i, (i + step) % count) for i in range(count)])  26.8 us
    ppermute x22, starting transfers between devices, shift(): lax.ppermute(value, axis, [(i, (i + step) % count) for i in range(count)])  23.5 us
    ppermute x11, starting transfers between devices, both_ways(): return lax.ppermute(value, 'attn', pairs)  12.4 us
    ppermute x11, waiting for transfers between devices, both_ways(): return lax.ppermute(value, 'attn', pairs)  11.3 us
    pallas_call x1, Pallas kernels, step(): pl.pallas_call(mix_kernel, out_shape=(jax.ShapeDtypeStruct((attn_count *...  4.25 us
    pallas_call x1, Pallas kernels, step(): pl.pallas_call(functools.partial(pack_kernel, plan, local, n_expert), out...  4.24 us
    pallas_call x1, Pallas kernels, step(): pl.pallas_call(functools.partial(pack_more_kernel, cut), out_shape=part_s...  3.7 us
  transfers between devices with their start and end apart: 40, of which 18 were waited for; matrix products, arithmetic and copies ran while one was open for 1% of the time, Pallas kernels for 10%

profile of v5, /device:TPU:513, one launch (start us, length us, event | category | flops | bytes accessed | tf_op | source)
XLA Modules:
  0.0 139.6 jit_solution(5857288258907382418)
XLA Ops:
  1.1 0.9 prepare.1.refs_0_
  2.0 20.5 %collective-permute-start = (bf16[136,512]{1,0:T(8,128)(2,1)S(1)}, bf16[136,512]{1,0:T(8,128)(2,1)S(1)}, u32[]{:S(2)}, u32[]{:S(2)}) collective-permute-start(bf16[136,512]{1,0:T(8,128)(2,1)S(1)} %prepare.1.refs_0_), channel_id=1, source_target_pairs={{0,8},{8,0},{16,24},{24,16},{32,40},{40,32},{48,56},{56,48},{64,72... | collective-permute-start | bytes 417800 | tf_op jit(solution)/shard_map/ppermute | solution.py:108
  22.5 1.0 collective-permute-done.refs_1_
  23.6 0.1 collective-permute-start.1
  23.7 3.7 %collective-permute-done.2.refs_0_.refs_3_ = bf16[136,512]{1,0:T(8,128)(2,1)S(1)} collective-permute-done((bf16[136,512]{1,0:T(8,128)(2,1)S(1)}, bf16[136,512]{1,0:T(8,128)(2,1)S(1)}, u32[]{:S(2)}, u32[]{:S(2)}) %collective-permute-start.2) | collective-permute-done | bytes 139296 | tf_op jit(solution)/shard_map/ppermute | solution.py:104
  27.4 1.7 %collective-permute-done.3.refs_1_.refs_4_ = bf16[136,512]{1,0:T(8,128)(2,1)S(1)} collective-permute-done((bf16[136,512]{1,0:T(8,128)(2,1)S(1)}, bf16[136,512]{1,0:T(8,128)(2,1)S(1)}, u32[]{:S(2)}, u32[]{:S(2)}) %collective-permute-start.3) | collective-permute-done | bytes 139296 | tf_op jit(solution)/shard_map/ppermute | solution.py:104
  29.2 0.1 collective-permute-start.4
  29.3 1.0 collective-permute-start.5
  30.3 1.5 %collective-permute-start.7 = (bf16[272,512]{1,0:T(8,128)(2,1)S(1)}, bf16[272,512]{1,0:T(8,128)(2,1)S(1)}, u32[]{:S(2)}, u32[]{:S(2)}) collective-permute-start(bf16[272,512]{1,0:T(8,128)(2,1)S(1)} %pair.3), channel_id=1, source_target_pairs={{0,8},{8,0},{16,24},{24,16},{32,40},{40,32},{48,56},{56,48},{64,72... | collective-permute-start | bytes 835592 | tf_op jit(solution)/shard_map/ppermute | solution.py:108
  31.9 0.3 collective-permute-done.1.refs_2_
  32.1 2.2 %collective-permute-start.6 = (bf16[272,512]{1,0:T(8,128)(2,1)S(1)}, bf16[272,512]{1,0:T(8,128)(2,1)S(1)}, u32[]{:S(2)}, u32[]{:S(2)}) collective-permute-start(bf16[272,512]{1,0:T(8,128)(2,1)S(1)} %collective-permute-done.1.refs_2_), channel_id=1, source_target_pairs={{0,8},{8,0},{16,24},{24,16},{32,40},{40,32},{48,56},{56,48},{64,72... | collective-permute-start | bytes 835592 | tf_op jit(solution)/shard_map/ppermute | solution.py:108
  34.3 0.5 collective-permute-done.4.refs_5_
  34.8 6.0 %collective-permute-start.8 = (bf16[272,512]{1,0:T(8,128)(2,1)S(1)}, bf16[272,512]{1,0:T(8,128)(2,1)S(1)}, u32[]{:S(2)}, u32[]{:S(2)}) collective-permute-start(bf16[272,512]{1,0:T(8,128)(2,1)S(1)} %collective-permute-done.4.refs_5_), channel_id=1, source_target_pairs={{0,8},{8,0},{16,24},{24,16},{32,40},{40,32},{48,56},{56,48},{64,72... | collective-permute-start | bytes 835592 | tf_op jit(solution)/shard_map/ppermute | solution.py:108
  40.8 2.9 %weights.1 = (bf16[4,512,768]{2,1,0:T(8,128)(2,1)S(1)}, bf16[4,512,768]{2,1,0:T(8,128)(2,1)S(1)}) custom-call(bf16[4,512,768]{2,1,0:T(8,128)(2,1)} %wg_hbm.1, bf16[4,512,768]{2,1,0:T(8,128)(2,1)} %wu_hbm.1), custom_call_target="tpu_custom_call" | custom-call | tf_op jit(solution)/shard_map/weights/pallas_call | solution.py:416
  43.7 4.2 %pack.1 = (bf16[2,32,1536]{2,1,0:T(8,128)(2,1)S(1)}, bf16[2,32,1536]{2,1,0:T(8,128)(2,1)S(1)}, bf16[2,32,1536]{2,1,0:T(8,128)(2,1)S(1)}, bf16[2,32,1536]{2,1,0:T...) custom-call(s32[18]{0:T(128)S(1)} %stack.123.info, ...), custom_call_target="tpu_custom_call" | custom-call | flops 2000000000 | bytes 6000000 | tf_op jit(solution)/shard_map/pack/pallas_call | solution.py:427
  48.0 3.7 %pack_more.1 = (bf16[2,32,1536]{2,1,0:T(8,128)(2,1)S(1)}, bf16[2,32,1536]{2,1,0:T(8,128)(2,1)S(1)}, bf16[2,32,1536]{2,1,0:T(8,128)(2,1)S(1)}, bf16[2,32,1536]{2,...) custom-call(s32[18]{0:T(128)S(1)} %stack.123.info, ...), custom_call_target="tpu_custom_call" | custom-call | flops 2000000000 | bytes 6000000 | tf_op jit(solution)/shard_map/pack_more/pallas_call | solution.py:444
  51.7 0.1 collective-permute-start.20
  51.8 1.4 %collective-permute-start.17 = (bf16[2,32,1536]{2,1,0:T(8,128)(2,1)S(1)}, bf16[2,32,1536]{2,1,0:T(8,128)(2,1)S(1)}, u32[]{:S(2)}, u32[]{:S(2)}) collective-permute-start(bf16[2,32,1536]{2,1,0:T(8,128)(2,1)S(1)} %get-tuple-element.56), channel_id=1, source_target_pairs={{0,1},{1,2},{2,3},{3,4},{4,5},{5,6},{6,7},{7,0},{8,9},{9,10},{10,1... | collective-permute-start | bytes 589832 | tf_op jit(solution)/shard_map/ppermute | solution.py:98
  53.3 1.3 collective-permute-start.14
  54.7 3.0 %collective-permute-done.20 = bf16[2,32,1536]{2,1,0:T(8,128)(2,1)S(1)} collective-permute-done((bf16[2,32,1536]{2,1,0:T(8,128)(2,1)S(1)}, bf16[2,32,1536]{2,1,0:T(8,128)(2,1)S(1)}, u32[]{:S(2)}, u32[]{:S(2)}) %collective-permute-start.20) | collective-permute-done | bytes 196640 | tf_op jit(solution)/shard_map/ppermute | solution.py:98
  57.8 1.6 %collective-permute-start.21 = (bf16[2,32,1536]{2,1,0:T(8,128)(2,1)S(1)}, bf16[2,32,1536]{2,1,0:T(8,128)(2,1)S(1)}, u32[]{:S(2)}, u32[]{:S(2)}) collective-permute-start(bf16[2,32,1536]{2,1,0:T(8,128)(2,1)S(1)} %add_convert_fusion.2), channel_id=1, source_target_pairs={{0,7},{1,0},{2,1},{3,2},{4,3},{5,4},{6,5},{7,6},{8,15},{9,8},{10,9... | collective-permute-start | bytes 589832 | tf_op jit(solution)/shard_map/ppermute | solution.py:98
  59.5 0.1 collective-permute-start.18
  59.6 2.3 %collective-permute-done.14 = bf16[2,32,1536]{2,1,0:T(8,128)(2,1)S(1)} collective-permute-done((bf16[2,32,1536]{2,1,0:T(8,128)(2,1)S(1)}, bf16[2,32,1536]{2,1,0:T(8,128)(2,1)S(1)}, u32[]{:S(2)}, u32[]{:S(2)}) %collective-permute-start.14) | collective-permute-done | bytes 196640 | tf_op jit(solution)/shard_map/ppermute | solution.py:98
  62.0 1.6 %collective-permute-start.15 = (bf16[2,32,1536]{2,1,0:T(8,128)(2,1)S(1)}, bf16[2,32,1536]{2,1,0:T(8,128)(2,1)S(1)}, u32[]{:S(2)}, u32[]{:S(2)}) collective-permute-start(bf16[2,32,1536]{2,1,0:T(8,128)(2,1)S(1)} %add_convert_fusion.6), channel_id=1, source_target_pairs={{0,7},{1,0},{2,1},{3,2},{4,3},{5,4},{6,5},{7,6},{8,15},{9,8},{10,9... | collective-permute-start | bytes 589832 | tf_op jit(solution)/shard_map/ppermute | solution.py:98
  63.7 0.1 collective-permute-start.11
  63.8 2.3 %collective-permute-done.21 = bf16[2,32,1536]{2,1,0:T(8,128)(2,1)S(1)} collective-permute-done((bf16[2,32,1536]{2,1,0:T(8,128)(2,1)S(1)}, bf16[2,32,1536]{2,1,0:T(8,128)(2,1)S(1)}, u32[]{:S(2)}, u32[]{:S(2)}) %collective-permute-start.21) | collective-permute-done | bytes 196640 | tf_op jit(solution)/shard_map/ppermute | solution.py:98
  66.2 0.9 collective-permute-start.22
  67.2 0.8 collective-permute-start.19
  68.0 2.4 %collective-permute-done.15 = bf16[2,32,1536]{2,1,0:T(8,128)(2,1)S(1)} collective-permute-done((bf16[2,32,1536]{2,1,0:T(8,128)(2,1)S(1)}, bf16[2,32,1536]{2,1,0:T(8,128)(2,1)S(1)}, u32[]{:S(2)}, u32[]{:S(2)}) %collective-permute-start.15) | collective-permute-done | bytes 196640 | tf_op jit(solution)/shard_map/ppermute | solution.py:98
  70.5 0.9 collective-permute-start.16
  71.4 0.8 collective-permute-start.12
  72.2 2.4 %collective-permute-done.22 = bf16[2,32,1536]{2,1,0:T(8,128)(2,1)S(1)} collective-permute-done((bf16[2,32,1536]{2,1,0:T(8,128)(2,1)S(1)}, bf16[2,32,1536]{2,1,0:T(8,128)(2,1)S(1)}, u32[]{:S(2)}, u32[]{:S(2)}) %collective-permute-start.22) | collective-permute-done | bytes 196640 | tf_op jit(solution)/shard_map/ppermute | solution.py:98
  74.7 0.8 collective-permute-start.23
  75.4 3.3 %collective-permute-done.12 = bf16[2,32,1536]{2,1,0:T(8,128)(2,1)S(1)} collective-permute-done((bf16[2,32,1536]{2,1,0:T(8,128)(2,1)S(1)}, bf16[2,32,1536]{2,1,0:T(8,128)(2,1)S(1)}, u32[]{:S(2)}, u32[]{:S(2)}) %collective-permute-start.12) | collective-permute-done | bytes 196640 | tf_op jit(solution)/shard_map/ppermute | solution.py:98
  78.8 1.4 collective-permute-start.13
  80.2 2.9 %collective-permute-done.23.refs_5_ = bf16[2,32,1536]{2,1,0:T(8,128)(2,1)S(1)} collective-permute-done((bf16[2,32,1536]{2,1,0:T(8,128)(2,1)S(1)}, bf16[2,32,1536]{2,1,0:T(8,128)(2,1)S(1)}, u32[]{:S(2)}, u32[]{:S(2)}) %collective-permute-start.23) | collective-permute-done | bytes 196640 | tf_op jit(solution)/shard_map/ppermute | solution.py:98
  83.0 1.6 %collective-permute-done.13.refs_1_ = bf16[2,32,1536]{2,1,0:T(8,128)(2,1)S(1)} collective-permute-done((bf16[2,32,1536]{2,1,0:T(8,128)(2,1)S(1)}, bf16[2,32,1536]{2,1,0:T(8,128)(2,1)S(1)}, u32[]{:S(2)}, u32[]{:S(2)}) %collective-permute-start.13) | collective-permute-done | bytes 196640 | tf_op jit(solution)/shard_map/ppermute | solution.py:98
  84.6 0.2 hidden.1.refs_0_
  84.9 0.8 collective-permute-start.26
  85.6 2.9 %collective-permute-start.27 = (bf16[4,32,768]{2,1,0:T(8,128)(2,1)S(1)}, bf16[4,32,768]{2,1,0:T(8,128)(2,1)S(1)}, u32[]{:S(2)}, u32[]{:S(2)}) collective-permute-start(bf16[4,32,768]{2,1,0:T(8,128)(2,1)S(1)} %hidden.1.refs_0_), channel_id=1, source_target_pairs={{0,6},{1,7},{2,0},{3,1},{4,2},{5,3},{6,4},{7,5},{8,14},{9,15},{10,... | collective-permute-start | bytes 589832 | tf_op jit(solution)/shard_map/ppermute | solution.py:98
  88.6 0.4 collective-permute-start.24
  88.9 2.3 %collective-permute-start.25 = (bf16[4,32,768]{2,1,0:T(8,128)(2,1)S(1)}, bf16[4,32,768]{2,1,0:T(8,128)(2,1)S(1)}, u32[]{:S(2)}, u32[]{:S(2)}) collective-permute-start(bf16[4,32,768]{2,1,0:T(8,128)(2,1)S(1)} %hidden.1.refs_0_), channel_id=1, source_target_pairs={{0,7},{1,0},{2,1},{3,2},{4,3},{5,4},{6,5},{7,6},{8,15},{9,8},{10,9... | collective-permute-start | bytes 589832 | tf_op jit(solution)/shard_map/ppermute | solution.py:98
  91.3 3.5 %collective-permute-done.26.refs_3_ = bf16[4,32,768]{2,1,0:T(8,128)(2,1)S(1)} collective-permute-done((bf16[4,32,768]{2,1,0:T(8,128)(2,1)S(1)}, bf16[4,32,768]{2,1,0:T(8,128)(2,1)S(1)}, u32[]{:S(2)}, u32[]{:S(2)}) %collective-permute-start.26) | collective-permute-done | bytes 196640 | tf_op jit(solution)/shard_map/ppermute | solution.py:98
  94.7 3.2 %collective-permute-start.29 = (bf16[4,32,768]{2,1,0:T(8,128)(2,1)S(1)}, bf16[4,32,768]{2,1,0:T(8,128)(2,1)S(1)}, u32[]{:S(2)}, u32[]{:S(2)}) collective-permute-start(bf16[4,32,768]{2,1,0:T(8,128)(2,1)S(1)} %collective-permute-done.27.refs_4_), channel_id=1, source_target_pairs={{0,7},{1,0},{2,1},{3,2},{4,3},{5,4},{6,5},{7,6},{8,15},{9,8},{10,9... | collective-permute-start | bytes 589832 | tf_op jit(solution)/shard_map/ppermute | solution.py:98
  98.1 1.9 %collective-permute-done.24.refs_1_ = bf16[4,32,768]{2,1,0:T(8,128)(2,1)S(1)} collective-permute-done((bf16[4,32,768]{2,1,0:T(8,128)(2,1)S(1)}, bf16[4,32,768]{2,1,0:T(8,128)(2,1)S(1)}, u32[]{:S(2)}, u32[]{:S(2)}) %collective-permute-start.24) | collective-permute-done | bytes 196640 | tf_op jit(solution)/shard_map/ppermute | solution.py:98
  99.9 1.8 %collective-permute-start.31 = (bf16[2,32,768]{2,1,0:T(8,128)(2,1)S(1)}, bf16[2,32,768]{2,1,0:T(8,128)(2,1)S(1)}, u32[]{:S(2)}, u32[]{:S(2)}) collective-permute-start(bf16[2,32,768]{2,1,0:T(8,128)(2,1)S(1)} %slice.9), channel_id=1, source_target_pairs={{0,6},{1,7},{2,0},{3,1},{4,2},{5,3},{6,4},{7,5},{8,14},{9,15},{10,... | collective-permute-start | bytes 294920 | tf_op jit(solution)/shard_map/ppermute | solution.py:98
  101.7 4.3 %mix.1 = (bf16[2048,1024]{1,0:T(8,128)(2,1)S(1)}, bf16[4,768,512]{2,1,0:T(8,128)(2,1)S(1)}) custom-call(s32[16]{0:T(128)S(1)} %stack.125.info, f32[16,8,128]{2,1,0:T(8,128)S(1)} %get-tuple-element.43.route, bf16[4,768,512]{2,1,0:T(8,128)(2,1)} %wd_hbm.1), custom_call_target="tpu_custom_call" | custom-call | tf_op jit(solution)/shard_map/mix/pallas_call | solution.py:472
  106.0 1.2 collective-permute-done.30.refs_7_
  107.2 3.0 %down.1 = (bf16[4,128,512]{2,1,0:T(8,128)(2,1)S(1)}, bf16[1024,512]{1,0:T(8,128)(2,1)S(1)}) custom-call(s32[8]{0:T(128)S(1)} %stack.134.info, bf16[4,32,768]{2,1,0:T(8,128)(2,1)S(1)} %hidden.1.refs_0_, bf16[4,32,768]{2,1,0:T(8,128)(2,1)S(1)} %collective-permute-done.24.refs_1_, bf16[4,32,768]{2,1,0:T(8,128)(2,1)S(1)} %collective-permute-done.25.refs_2_, ...), custom_call_target="tpu_custom_call" | custom-call | flops 2000000000 | bytes 6000000 | tf_op jit(solution)/shard_map/down/pallas_call | solution.py:485
  110.2 5.3 %collective-permute-start.32 = (bf16[4,128,512]{2,1,0:T(8,128)(2,1)S(1)}, bf16[4,128,512]{2,1,0:T(8,128)(2,1)S(1)}, u32[]{:S(2)}, u32[]{:S(2)}) collective-permute-start(bf16[4,128,512]{2,1,0:T(8,128)(2,1)S(1)} %get-tuple-element.66), channel_id=1, source_target_pairs={{0,8},{8,0},{16,24},{24,16},{32,40},{40,32},{48,56},{56,48},{64,72... | collective-permute-start | bytes 1572872 | tf_op jit(solution)/shard_map/ppermute | solution.py:108
  115.4 1.7 %shard_map.113 = (bf16[4,128,512]{2,1,0:T(8,128)(2,1)S(1)}, bf16[4,128,512]{2,1,0:T(8,128)(2,1)S(1)}) custom-call(bf16[2048,1024]{1,0:T(8,128)(2,1)S(1)} %get-tuple-element.44.refs_10_.mix, bf16[1024,512]{1,0:T(8,128)(2,1)S(1)} %get-tuple-element.64.res), custom_call_target="tpu_custom_call" | custom-call | tf_op jit(solution)/shard_map/pallas_call | solution.py:497
  117.2 0.1 collective-permute-start.33
  117.5 2.2 %collective-permute-start.36 = (bf16[256,512]{1,0:T(8,128)(2,1)S(1)}, bf16[256,512]{1,0:T(8,128)(2,1)S(1)}, u32[]{:S(2)}, u32[]{:S(2)}) collective-permute-start(bf16[256,512]{1,0:T(8,128)(2,1)S(1)} %get-tuple-element.70), channel_id=1, source_target_pairs={{0,16},{8,120},{16,32},{24,8},{32,48},{40,24},{48,64},{56,40},{64,... | collective-permute-start | bytes 786440 | tf_op jit(solution)/shard_map/ppermute | solution.py:104
  119.7 0.8 collective-permute-start.37
  120.5 0.9 shard_map.114.home
  121.4 0.3 collective-permute-start.34
  121.7 3.9 %collective-permute-start.35 = (bf16[128,512]{1,0:T(8,128)(2,1)S(1)}, bf16[128,512]{1,0:T(8,128)(2,1)S(1)}, u32[]{:S(2)}, u32[]{:S(2)}) collective-permute-start(bf16[128,512]{1,0:T(8,128)(2,1)S(1)} %get-tuple-element.69), channel_id=1, source_target_pairs={{0,24},{8,112},{16,40},{24,0},{32,56},{40,16},{48,72},{56,32},{64,... | collective-permute-start | bytes 393224 | tf_op jit(solution)/shard_map/ppermute | solution.py:104
  125.6 3.4 %collective-permute-done.37.four = bf16[128,512]{1,0:T(8,128)(2,1)S(1)} collective-permute-done((bf16[128,512]{1,0:T(8,128)(2,1)S(1)}, bf16[128,512]{1,0:T(8,128)(2,1)S(1)}, u32[]{:S(2)}, u32[]{:S(2)}) %collective-permute-start.37) | collective-permute-done | bytes 131104 | tf_op jit(solution)/shard_map/ppermute | solution.py:104
  129.1 1.0 collective-permute-start.38
  130.2 3.0 %collective-permute-start.39 = (bf16[128,512]{1,0:T(8,128)(2,1)S(1)}, bf16[128,512]{1,0:T(8,128)(2,1)S(1)}, u32[]{:S(2)}, u32[]{:S(2)}) collective-permute-start(bf16[128,512]{1,0:T(8,128)(2,1)S(1)} %get-tuple-element.73), channel_id=1, source_target_pairs={{0,40},{8,96},{16,56},{24,112},{32,72},{40,0},{48,88},{56,16},{64,... | collective-permute-start | bytes 393224 | tf_op jit(solution)/shard_map/ppermute | solution.py:104
  133.1 3.4 %attention.1 = bf16[2,64,128]{2,1,0:T(8,128)(2,1)S(1)} custom-call(s32[2]{0:T(128)S(1)} %copy-done, bf16[2,64,128]{2,1,0:T(8,128)(2,1)} %query.1, bf16[2,768,4,128]{3,2,1,0:T(4,128)(2,1)} %cache_k.1, bf16[2,768,4,128]{3,2,1,0:T(4,128)(2,1)} %cache_v.1), custom_call_target="tpu_custom_call" | custom-call | flops 1000000000 | bytes 3000000 | tf_op jit(solution)/shard_map/attention/pallas_call | solution.py:81
  136.5 0.6 copy.14
  137.2 1.6 %collective-permute-done.39.d = bf16[128,512]{1,0:T(8,128)(2,1)S(1)} collective-permute-done((bf16[128,512]{1,0:T(8,128)(2,1)S(1)}, bf16[128,512]{1,0:T(8,128)(2,1)S(1)}, u32[]{:S(2)}, u32[]{:S(2)}) %collective-permute-start.39) | collective-permute-done | bytes 131104 | tf_op jit(solution)/shard_map/ppermute | solution.py:104
  138.8 0.8 shard_map.118
  (50 shorter events, 1.4 us)
Async XLA Ops:
  2.0 21.5 %collective-permute-start = (bf16[136,512]{1,0:T(8,128)(2,1)S(1)}, bf16[136,512]{1,0:T(8,128)(2,1)S(1)}, u32[]{:S(2)}, u32[]{:S(2)}) collective-permute-start(bf16[136,512]{1,0:T(8,128)(2,1)S(1)} %prepare.1.refs_0_), channel_id=1, source_target_pairs={{0,8},{8,0},{16,24},{24,16},{32,40},{40,32},{48,56},{56,48},{64,72... | collective-permute-start | bytes 417800 | tf_op jit(solution)/shard_map/ppermute | solution.py:108
  22.5 4.9 %collective-permute-start.2 = (bf16[136,512]{1,0:T(8,128)(2,1)S(1)}, bf16[136,512]{1,0:T(8,128)(2,1)S(1)}, u32[]{:S(2)}, u32[]{:S(2)}) collective-permute-start(bf16[136,512]{1,0:T(8,128)(2,1)S(1)} %prepare.1.refs_0_), channel_id=1, source_target_pairs={{0,32},{8,104},{16,48},{24,120},{32,64},{40,8},{48,80},{56,24},{64... | collective-permute-start | bytes 417800 | tf_op jit(solution)/shard_map/ppermute | solution.py:104
  23.5 5.6 %collective-permute-start.3 = (bf16[136,512]{1,0:T(8,128)(2,1)S(1)}, bf16[136,512]{1,0:T(8,128)(2,1)S(1)}, u32[]{:S(2)}, u32[]{:S(2)}) collective-permute-start(bf16[136,512]{1,0:T(8,128)(2,1)S(1)} %collective-permute-done.refs_1_), channel_id=1, source_target_pairs={{0,32},{8,104},{16,48},{24,120},{32,64},{40,8},{48,80},{56,24},{64... | collective-permute-start | bytes 417800 | tf_op jit(solution)/shard_map/ppermute | solution.py:104
  23.6 8.6 %collective-permute-start.1 = (bf16[272,512]{1,0:T(8,128)(2,1)S(1)}, bf16[272,512]{1,0:T(8,128)(2,1)S(1)}, u32[]{:S(2)}, u32[]{:S(2)}) collective-permute-start(bf16[272,512]{1,0:T(8,128)(2,1)S(1)} %pair.2), channel_id=1, source_target_pairs={{0,16},{8,120},{16,32},{24,8},{32,48},{40,24},{48,64},{56,40},{64,... | collective-permute-start | bytes 835592 | tf_op jit(solution)/shard_map/ppermute | solution.py:104
  29.2 5.6 %collective-permute-start.4 = (bf16[272,512]{1,0:T(8,128)(2,1)S(1)}, bf16[272,512]{1,0:T(8,128)(2,1)S(1)}, u32[]{:S(2)}, u32[]{:S(2)}) collective-permute-start(bf16[272,512]{1,0:T(8,128)(2,1)S(1)} %pair.3), channel_id=1, source_target_pairs={{0,16},{8,120},{16,32},{24,8},{32,48},{40,24},{48,64},{56,40},{64,... | collective-permute-start | bytes 835592 | tf_op jit(solution)/shard_map/ppermute | solution.py:104
  29.3 11.5 %collective-permute-start.5 = (bf16[136,512]{1,0:T(8,128)(2,1)S(1)}, bf16[136,512]{1,0:T(8,128)(2,1)S(1)}, u32[]{:S(2)}, u32[]{:S(2)}) collective-permute-start(bf16[136,512]{1,0:T(8,128)(2,1)S(1)} %collective-permute-done.2.refs_0_.refs_3_), channel_id=1, source_target_pairs={{0,32},{8,104},{16,48},{24,120},{32,64},{40,8},{48,80},{56,24},{64... | collective-permute-start | bytes 417800 | tf_op jit(solution)/shard_map/ppermute | solution.py:104
  30.3 13.4 %collective-permute-start.7 = (bf16[272,512]{1,0:T(8,128)(2,1)S(1)}, bf16[272,512]{1,0:T(8,128)(2,1)S(1)}, u32[]{:S(2)}, u32[]{:S(2)}) collective-permute-start(bf16[272,512]{1,0:T(8,128)(2,1)S(1)} %pair.3), channel_id=1, source_target_pairs={{0,8},{8,0},{16,24},{24,16},{32,40},{40,32},{48,56},{56,48},{64,72... | collective-permute-start | bytes 835592 | tf_op jit(solution)/shard_map/ppermute | solution.py:108
  32.1 11.6 %collective-permute-start.6 = (bf16[272,512]{1,0:T(8,128)(2,1)S(1)}, bf16[272,512]{1,0:T(8,128)(2,1)S(1)}, u32[]{:S(2)}, u32[]{:S(2)}) collective-permute-start(bf16[272,512]{1,0:T(8,128)(2,1)S(1)} %collective-permute-done.1.refs_2_), channel_id=1, source_target_pairs={{0,8},{8,0},{16,24},{24,16},{32,40},{40,32},{48,56},{56,48},{64,72... | collective-permute-start | bytes 835592 | tf_op jit(solution)/shard_map/ppermute | solution.py:108
  34.8 8.9 %collective-permute-start.8 = (bf16[272,512]{1,0:T(8,128)(2,1)S(1)}, bf16[272,512]{1,0:T(8,128)(2,1)S(1)}, u32[]{:S(2)}, u32[]{:S(2)}) collective-permute-start(bf16[272,512]{1,0:T(8,128)(2,1)S(1)} %collective-permute-done.4.refs_5_), channel_id=1, source_target_pairs={{0,8},{8,0},{16,24},{24,16},{32,40},{40,32},{48,56},{56,48},{64,72... | collective-permute-start | bytes 835592 | tf_op jit(solution)/shard_map/ppermute | solution.py:108
  40.8 2.9 %collective-permute-start.9 = (bf16[136,512]{1,0:T(8,128)(2,1)S(1)}, bf16[136,512]{1,0:T(8,128)(2,1)S(1)}, u32[]{:S(2)}, u32[]{:S(2)}) collective-permute-start(bf16[136,512]{1,0:T(8,128)(2,1)S(1)} %collective-permute-done.5.refs_6_), channel_id=1, source_target_pairs={{0,8},{8,0},{16,24},{24,16},{32,40},{40,32},{48,56},{56,48},{64,72... | collective-permute-start | bytes 417800 | tf_op jit(solution)/shard_map/ppermute | solution.py:108
  51.7 6.1 %collective-permute-start.20 = (bf16[2,32,1536]{2,1,0:T(8,128)(2,1)S(1)}, bf16[2,32,1536]{2,1,0:T(8,128)(2,1)S(1)}, u32[]{:S(2)}, u32[]{:S(2)}) collective-permute-start(bf16[2,32,1536]{2,1,0:T(8,128)(2,1)S(1)} %get-tuple-element.59), channel_id=1, source_target_pairs={{0,7},{1,0},{2,1},{3,2},{4,3},{5,4},{6,5},{7,6},{8,15},{9,8},{10,9... | collective-permute-start | bytes 589832 | tf_op jit(solution)/shard_map/ppermute | solution.py:98
  51.8 7.6 %collective-permute-start.17 = (bf16[2,32,1536]{2,1,0:T(8,128)(2,1)S(1)}, bf16[2,32,1536]{2,1,0:T(8,128)(2,1)S(1)}, u32[]{:S(2)}, u32[]{:S(2)}) collective-permute-start(bf16[2,32,1536]{2,1,0:T(8,128)(2,1)S(1)} %get-tuple-element.56), channel_id=1, source_target_pairs={{0,1},{1,2},{2,3},{3,4},{4,5},{5,6},{6,7},{7,0},{8,9},{9,10},{10,1... | collective-permute-start | bytes 589832 | tf_op jit(solution)/shard_map/ppermute | solution.py:98
  53.3 8.7 %collective-permute-start.14 = (bf16[2,32,1536]{2,1,0:T(8,128)(2,1)S(1)}, bf16[2,32,1536]{2,1,0:T(8,128)(2,1)S(1)}, u32[]{:S(2)}, u32[]{:S(2)}) collective-permute-start(bf16[2,32,1536]{2,1,0:T(8,128)(2,1)S(1)} %get-tuple-element.51), channel_id=1, source_target_pairs={{0,7},{1,0},{2,1},{3,2},{4,3},{5,4},{6,5},{7,6},{8,15},{9,8},{10,9... | collective-permute-start | bytes 589832 | tf_op jit(solution)/shard_map/ppermute | solution.py:98
  54.6 9.0 %collective-permute-start.10 = (bf16[2,32,1536]{2,1,0:T(8,128)(2,1)S(1)}, bf16[2,32,1536]{2,1,0:T(8,128)(2,1)S(1)}, u32[]{:S(2)}, u32[]{:S(2)}) collective-permute-start(bf16[2,32,1536]{2,1,0:T(8,128)(2,1)S(1)} %get-tuple-element.47), channel_id=1, source_target_pairs={{0,1},{1,2},{2,3},{3,4},{4,5},{5,6},{6,7},{7,0},{8,9},{9,10},{10,1... | collective-permute-start | bytes 589832 | tf_op jit(solution)/shard_map/ppermute | solution.py:98
  57.8 8.4 %collective-permute-start.21 = (bf16[2,32,1536]{2,1,0:T(8,128)(2,1)S(1)}, bf16[2,32,1536]{2,1,0:T(8,128)(2,1)S(1)}, u32[]{:S(2)}, u32[]{:S(2)}) collective-permute-start(bf16[2,32,1536]{2,1,0:T(8,128)(2,1)S(1)} %add_convert_fusion.2), channel_id=1, source_target_pairs={{0,7},{1,0},{2,1},{3,2},{4,3},{5,4},{6,5},{7,6},{8,15},{9,8},{10,9... | collective-permute-start | bytes 589832 | tf_op jit(solution)/shard_map/ppermute | solution.py:98
  59.5 7.6 %collective-permute-start.18 = (bf16[2,32,1536]{2,1,0:T(8,128)(2,1)S(1)}, bf16[2,32,1536]{2,1,0:T(8,128)(2,1)S(1)}, u32[]{:S(2)}, u32[]{:S(2)}) collective-permute-start(bf16[2,32,1536]{2,1,0:T(8,128)(2,1)S(1)} %add_convert_fusion.4), channel_id=1, source_target_pairs={{0,1},{1,2},{2,3},{3,4},{4,5},{5,6},{6,7},{7,0},{8,9},{9,10},{10,1... | collective-permute-start | bytes 589832 | tf_op jit(solution)/shard_map/ppermute | solution.py:98
  62.0 8.4 %collective-permute-start.15 = (bf16[2,32,1536]{2,1,0:T(8,128)(2,1)S(1)}, bf16[2,32,1536]{2,1,0:T(8,128)(2,1)S(1)}, u32[]{:S(2)}, u32[]{:S(2)}) collective-permute-start(bf16[2,32,1536]{2,1,0:T(8,128)(2,1)S(1)} %add_convert_fusion.6), channel_id=1, source_target_pairs={{0,7},{1,0},{2,1},{3,2},{4,3},{5,4},{6,5},{7,6},{8,15},{9,8},{10,9... | collective-permute-start | bytes 589832 | tf_op jit(solution)/shard_map/ppermute | solution.py:98
  63.7 7.7 %collective-permute-start.11 = (bf16[2,32,1536]{2,1,0:T(8,128)(2,1)S(1)}, bf16[2,32,1536]{2,1,0:T(8,128)(2,1)S(1)}, u32[]{:S(2)}, u32[]{:S(2)}) collective-permute-start(bf16[2,32,1536]{2,1,0:T(8,128)(2,1)S(1)} %add_convert_fusion.9), channel_id=1, source_target_pairs={{0,1},{1,2},{2,3},{3,4},{4,5},{5,6},{6,7},{7,0},{8,9},{9,10},{10,1... | collective-permute-start | bytes 589832 | tf_op jit(solution)/shard_map/ppermute | solution.py:98
  66.2 8.4 %collective-permute-start.22 = (bf16[2,32,1536]{2,1,0:T(8,128)(2,1)S(1)}, bf16[2,32,1536]{2,1,0:T(8,128)(2,1)S(1)}, u32[]{:S(2)}, u32[]{:S(2)}) collective-permute-start(bf16[2,32,1536]{2,1,0:T(8,128)(2,1)S(1)} %add_convert_fusion.1), channel_id=1, source_target_pairs={{0,7},{1,0},{2,1},{3,2},{4,3},{5,4},{6,5},{7,6},{8,15},{9,8},{10,9... | collective-permute-start | bytes 589832 | tf_op jit(solution)/shard_map/ppermute | solution.py:98
  67.2 13.0 %collective-permute-start.19 = (bf16[2,32,1536]{2,1,0:T(8,128)(2,1)S(1)}, bf16[2,32,1536]{2,1,0:T(8,128)(2,1)S(1)}, u32[]{:S(2)}, u32[]{:S(2)}) collective-permute-start(bf16[2,32,1536]{2,1,0:T(8,128)(2,1)S(1)} %add_convert_fusion.3), channel_id=1, source_target_pairs={{0,1},{1,2},{2,3},{3,4},{4,5},{5,6},{6,7},{7,0},{8,9},{9,10},{10,1... | collective-permute-start | bytes 589832 | tf_op jit(solution)/shard_map/ppermute | solution.py:98
  70.5 9.7 %collective-permute-start.16 = (bf16[2,32,1536]{2,1,0:T(8,128)(2,1)S(1)}, bf16[2,32,1536]{2,1,0:T(8,128)(2,1)S(1)}, u32[]{:S(2)}, u32[]{:S(2)}) collective-permute-start(bf16[2,32,1536]{2,1,0:T(8,128)(2,1)S(1)} %add_convert_fusion.5), channel_id=1, source_target_pairs={{0,7},{1,0},{2,1},{3,2},{4,3},{5,4},{6,5},{7,6},{8,15},{9,8},{10,9... | collective-permute-start | bytes 589832 | tf_op jit(solution)/shard_map/ppermute | solution.py:98
  71.4 7.3 %collective-permute-start.12 = (bf16[2,32,1536]{2,1,0:T(8,128)(2,1)S(1)}, bf16[2,32,1536]{2,1,0:T(8,128)(2,1)S(1)}, u32[]{:S(2)}, u32[]{:S(2)}) collective-permute-start(bf16[2,32,1536]{2,1,0:T(8,128)(2,1)S(1)} %add_convert_fusion.8), channel_id=1, source_target_pairs={{0,1},{1,2},{2,3},{3,4},{4,5},{5,6},{6,7},{7,0},{8,9},{9,10},{10,1... | collective-permute-start | bytes 589832 | tf_op jit(solution)/shard_map/ppermute | solution.py:98
  74.7 8.4 %collective-permute-start.23 = (bf16[2,32,1536]{2,1,0:T(8,128)(2,1)S(1)}, bf16[2,32,1536]{2,1,0:T(8,128)(2,1)S(1)}, u32[]{:S(2)}, u32[]{:S(2)}) collective-permute-start(bf16[2,32,1536]{2,1,0:T(8,128)(2,1)S(1)} %add_convert_fusion), channel_id=1, source_target_pairs={{0,7},{1,0},{2,1},{3,2},{4,3},{5,4},{6,5},{7,6},{8,15},{9,8},{10,9... | collective-permute-start | bytes 589832 | tf_op jit(solution)/shard_map/ppermute | solution.py:98
  78.8 5.8 %collective-permute-start.13 = (bf16[2,32,1536]{2,1,0:T(8,128)(2,1)S(1)}, bf16[2,32,1536]{2,1,0:T(8,128)(2,1)S(1)}, u32[]{:S(2)}, u32[]{:S(2)}) collective-permute-start(bf16[2,32,1536]{2,1,0:T(8,128)(2,1)S(1)} %add_convert_fusion.7), channel_id=1, source_target_pairs={{0,1},{1,2},{2,3},{3,4},{4,5},{5,6},{6,7},{7,0},{8,9},{9,10},{10,1... | collective-permute-start | bytes 589832 | tf_op jit(solution)/shard_map/ppermute | solution.py:98
  84.9 9.8 %collective-permute-start.26 = (bf16[4,32,768]{2,1,0:T(8,128)(2,1)S(1)}, bf16[4,32,768]{2,1,0:T(8,128)(2,1)S(1)}, u32[]{:S(2)}, u32[]{:S(2)}) collective-permute-start(bf16[4,32,768]{2,1,0:T(8,128)(2,1)S(1)} %hidden.1.refs_0_), channel_id=1, source_target_pairs={{0,2},{1,3},{2,4},{3,5},{4,6},{5,7},{6,0},{7,1},{8,10},{9,11},{10,... | collective-permute-start | bytes 589832 | tf_op jit(solution)/shard_map/ppermute | solution.py:98
  85.6 9.1 %collective-permute-start.27 = (bf16[4,32,768]{2,1,0:T(8,128)(2,1)S(1)}, bf16[4,32,768]{2,1,0:T(8,128)(2,1)S(1)}, u32[]{:S(2)}, u32[]{:S(2)}) collective-permute-start(bf16[4,32,768]{2,1,0:T(8,128)(2,1)S(1)} %hidden.1.refs_0_), channel_id=1, source_target_pairs={{0,6},{1,7},{2,0},{3,1},{4,2},{5,3},{6,4},{7,5},{8,14},{9,15},{10,... | collective-permute-start | bytes 589832 | tf_op jit(solution)/shard_map/ppermute | solution.py:98
  88.6 11.4 %collective-permute-start.24 = (bf16[4,32,768]{2,1,0:T(8,128)(2,1)S(1)}, bf16[4,32,768]{2,1,0:T(8,128)(2,1)S(1)}, u32[]{:S(2)}, u32[]{:S(2)}) collective-permute-start(bf16[4,32,768]{2,1,0:T(8,128)(2,1)S(1)} %hidden.1.refs_0_), channel_id=1, source_target_pairs={{0,1},{1,2},{2,3},{3,4},{4,5},{5,6},{6,7},{7,0},{8,9},{9,10},{10,1... | collective-permute-start | bytes 589832 | tf_op jit(solution)/shard_map/ppermute | solution.py:98
  88.9 17.0 %collective-permute-start.25 = (bf16[4,32,768]{2,1,0:T(8,128)(2,1)S(1)}, bf16[4,32,768]{2,1,0:T(8,128)(2,1)S(1)}, u32[]{:S(2)}, u32[]{:S(2)}) collective-permute-start(bf16[4,32,768]{2,1,0:T(8,128)(2,1)S(1)} %hidden.1.refs_0_), channel_id=1, source_target_pairs={{0,7},{1,0},{2,1},{3,2},{4,3},{5,4},{6,5},{7,6},{8,15},{9,8},{10,9... | collective-permute-start | bytes 589832 | tf_op jit(solution)/shard_map/ppermute | solution.py:98
  94.7 12.5 %collective-permute-start.28 = (bf16[4,32,768]{2,1,0:T(8,128)(2,1)S(1)}, bf16[4,32,768]{2,1,0:T(8,128)(2,1)S(1)}, u32[]{:S(2)}, u32[]{:S(2)}) collective-permute-start(bf16[4,32,768]{2,1,0:T(8,128)(2,1)S(1)} %collective-permute-done.26.refs_3_), channel_id=1, source_target_pairs={{0,1},{1,2},{2,3},{3,4},{4,5},{5,6},{6,7},{7,0},{8,9},{9,10},{10,1... | collective-permute-start | bytes 589832 | tf_op jit(solution)/shard_map/ppermute | solution.py:98
  94.7 12.4 %collective-permute-start.29 = (bf16[4,32,768]{2,1,0:T(8,128)(2,1)S(1)}, bf16[4,32,768]{2,1,0:T(8,128)(2,1)S(1)}, u32[]{:S(2)}, u32[]{:S(2)}) collective-permute-start(bf16[4,32,768]{2,1,0:T(8,128)(2,1)S(1)} %collective-permute-done.27.refs_4_), channel_id=1, source_target_pairs={{0,7},{1,0},{2,1},{3,2},{4,3},{5,4},{6,5},{7,6},{8,15},{9,8},{10,9... | collective-permute-start | bytes 589832 | tf_op jit(solution)/shard_map/ppermute | solution.py:98
  97.9 9.2 %collective-permute-start.30 = (bf16[2,32,768]{2,1,0:T(8,128)(2,1)S(1)}, bf16[2,32,768]{2,1,0:T(8,128)(2,1)S(1)}, u32[]{:S(2)}, u32[]{:S(2)}) collective-permute-start(bf16[2,32,768]{2,1,0:T(8,128)(2,1)S(1)} %slice.8), channel_id=1, source_target_pairs={{0,2},{1,3},{2,4},{3,5},{4,6},{5,7},{6,0},{7,1},{8,10},{9,11},{10,... | collective-permute-start | bytes 294920 | tf_op jit(solution)/shard_map/ppermute | solution.py:98
  99.9 7.2 %collective-permute-start.31 = (bf16[2,32,768]{2,1,0:T(8,128)(2,1)S(1)}, bf16[2,32,768]{2,1,0:T(8,128)(2,1)S(1)}, u32[]{:S(2)}, u32[]{:S(2)}) collective-permute-start(bf16[2,32,768]{2,1,0:T(8,128)(2,1)S(1)} %slice.9), channel_id=1, source_target_pairs={{0,6},{1,7},{2,0},{3,1},{4,2},{5,3},{6,4},{7,5},{8,14},{9,15},{10,... | collective-permute-start | bytes 294920 | tf_op jit(solution)/shard_map/ppermute | solution.py:98
  110.2 7.2 %collective-permute-start.32 = (bf16[4,128,512]{2,1,0:T(8,128)(2,1)S(1)}, bf16[4,128,512]{2,1,0:T(8,128)(2,1)S(1)}, u32[]{:S(2)}, u32[]{:S(2)}) collective-permute-start(bf16[4,128,512]{2,1,0:T(8,128)(2,1)S(1)} %get-tuple-element.66), channel_id=1, source_target_pairs={{0,8},{8,0},{16,24},{24,16},{32,40},{40,32},{48,56},{56,48},{64,72... | collective-permute-start | bytes 1572872 | tf_op jit(solution)/shard_map/ppermute | solution.py:108
  117.2 4.2 %collective-permute-start.33 = (bf16[4,128,512]{2,1,0:T(8,128)(2,1)S(1)}, bf16[4,128,512]{2,1,0:T(8,128)(2,1)S(1)}, u32[]{:S(2)}, u32[]{:S(2)}) collective-permute-start(bf16[4,128,512]{2,1,0:T(8,128)(2,1)S(1)} %get-tuple-element.67), channel_id=1, source_target_pairs={{0,8},{8,0},{16,24},{24,16},{32,40},{40,32},{48,56},{56,48},{64,72... | collective-permute-start | bytes 1572872 | tf_op jit(solution)/shard_map/ppermute | solution.py:108
  117.5 11.6 %collective-permute-start.36 = (bf16[256,512]{1,0:T(8,128)(2,1)S(1)}, bf16[256,512]{1,0:T(8,128)(2,1)S(1)}, u32[]{:S(2)}, u32[]{:S(2)}) collective-permute-start(bf16[256,512]{1,0:T(8,128)(2,1)S(1)} %get-tuple-element.70), channel_id=1, source_target_pairs={{0,16},{8,120},{16,32},{24,8},{32,48},{40,24},{48,64},{56,40},{64,... | collective-permute-start | bytes 786440 | tf_op jit(solution)/shard_map/ppermute | solution.py:104
  119.7 13.4 %copy-start = (s32[2]{0:T(128)S(1)}, s32[2]{0:T(128)}, u32[]{:S(2)}) copy-start(s32[2]{0:T(128)} %lengths.1) | copy-start | bytes 28
  119.7 9.3 %collective-permute-start.37 = (bf16[128,512]{1,0:T(8,128)(2,1)S(1)}, bf16[128,512]{1,0:T(8,128)(2,1)S(1)}, u32[]{:S(2)}, u32[]{:S(2)}) collective-permute-start(bf16[128,512]{1,0:T(8,128)(2,1)S(1)} %get-tuple-element.71), channel_id=1, source_target_pairs={{0,32},{8,104},{16,48},{24,120},{32,64},{40,8},{48,80},{56,24},{64... | collective-permute-start | bytes 393224 | tf_op jit(solution)/shard_map/ppermute | solution.py:104
  121.4 15.7 %collective-permute-start.34 = (bf16[128,512]{1,0:T(8,128)(2,1)S(1)}, bf16[128,512]{1,0:T(8,128)(2,1)S(1)}, u32[]{:S(2)}, u32[]{:S(2)}) collective-permute-start(bf16[128,512]{1,0:T(8,128)(2,1)S(1)} %get-tuple-element.68), channel_id=1, source_target_pairs={{0,16},{8,120},{16,32},{24,8},{32,48},{40,24},{48,64},{56,40},{64,... | collective-permute-start | bytes 393224 | tf_op jit(solution)/shard_map/ppermute | solution.py:104
  121.7 15.5 %collective-permute-start.35 = (bf16[128,512]{1,0:T(8,128)(2,1)S(1)}, bf16[128,512]{1,0:T(8,128)(2,1)S(1)}, u32[]{:S(2)}, u32[]{:S(2)}) collective-permute-start(bf16[128,512]{1,0:T(8,128)(2,1)S(1)} %get-tuple-element.69), channel_id=1, source_target_pairs={{0,24},{8,112},{16,40},{24,0},{32,56},{40,16},{48,72},{56,32},{64,... | collective-permute-start | bytes 393224 | tf_op jit(solution)/shard_map/ppermute | solution.py:104
  129.1 8.0 %collective-permute-start.38 = (bf16[128,512]{1,0:T(8,128)(2,1)S(1)}, bf16[128,512]{1,0:T(8,128)(2,1)S(1)}, u32[]{:S(2)}, u32[]{:S(2)}) collective-permute-start(bf16[128,512]{1,0:T(8,128)(2,1)S(1)} %get-tuple-element.72), channel_id=1, source_target_pairs={{0,32},{8,104},{16,48},{24,120},{32,64},{40,8},{48,80},{56,24},{64... | collective-permute-start | bytes 393224 | tf_op jit(solution)/shard_map/ppermute | solution.py:104
  130.2 8.7 %collective-permute-start.39 = (bf16[128,512]{1,0:T(8,128)(2,1)S(1)}, bf16[128,512]{1,0:T(8,128)(2,1)S(1)}, u32[]{:S(2)}, u32[]{:S(2)}) collective-permute-start(bf16[128,512]{1,0:T(8,128)(2,1)S(1)} %get-tuple-element.73), channel_id=1, source_target_pairs={{0,40},{8,96},{16,56},{24,112},{32,72},{40,0},{48,88},{56,16},{64,... | collective-permute-start | bytes 393224 | tf_op jit(solution)/shard_map/ppermute | solution.py:104

commit v6 on v5

--- a/solution.py
+++ b/solution.py
@@ -143,13 +143,9 @@
     row_id = jnp.where(row_id < capacity, row_id, row_id - capacity).astype(F32)
 
     def expert(j, carry):
-        def select(i, carry):
+        for i in range(n_blocks):
             spot = place[info[1 + i], pl.ds(j0 + j, 1), :]
-            at = pl.ds(pl.multiple_of(i * rows, rows), rows)
-            onehot[:, at] = jnp.where(row_id == spot, 1.0, 0.0).astype(BF16)
-            return carry
-
-        lax.fori_loop(0, n_blocks, select, 0, unroll=2)
+            onehot[:, i * rows : (i + 1) * rows] = jnp.where(row_id == spot, 1.0, 0.0).astype(BF16)
         mine = jnp.dot(onehot[...], tok[...], preferred_element_type=F32).astype(BF16)
         gate = jnp.dot(mine, wg[j0 + j], preferred_element_type=F32).astype(BF16)
         up = jnp.dot(mine, wu[j0 + j], preferred_element_type=F32).astype(BF16)

time: 140 us -> 138 us (0.986)
  transfers between devices with their start and end apart: 40 -> 40, of which waited for: 18 -> 19; matrix products, arithmetic and copies ran while one was open for 1% -> 1% of each run, Pallas kernels for 10% -> 10%
where the time goes in v6:
time: 138 us
  starting transfers between devices  71.6 us (52%)
  waiting for transfers between devices  39.2 us (28%)
  Pallas kernels  25 us (18%)
    ppermute x7, starting transfers between devices, swap_cores(): lax.ppermute(value, 'attn', [(i, i ^ 1) for i in range(lax.axis_size('att...  35.4 us
    ppermute x22, waiting for transfers between devices, shift(): lax.ppermute(value, axis, [(i, (i + step) % count) for i in range(count)])  27 us
    ppermute x22, starting transfers between devices, shift(): lax.ppermute(value, axis, [(i, (i + step) % count) for i in range(count)])  23.7 us
    ppermute x11, starting transfers between devices, both_ways(): return lax.ppermute(value, 'attn', pairs)  12.5 us
    ppermute x11, waiting for transfers between devices, both_ways(): return lax.ppermute(value, 'attn', pairs)  11.3 us
    pallas_call x1, Pallas kernels, step(): pl.pallas_call(mix_kernel, out_shape=(jax.ShapeDtypeStruct((attn_count *...  4.25 us
    pallas_call x6, Pallas kernels, small_call(): pl.pallas_call(kernel, out_shape=shapes, in_specs=[VMEM_SPEC] * len(opera...  3.64 us
    pallas_call x1, Pallas kernels, step(): pl.pallas_call(functools.partial(pack_kernel, plan, local, n_expert), out...  3.62 us
  transfers between devices with their start and end apart: 40, of which 19 were waited for; matrix products, arithmetic and copies ran while one was open for 1% of the time, Pallas kernels for 10%

profile of v6, /device:TPU:513, one launch (start us, length us, event | category | flops | bytes accessed | tf_op | source)
XLA Modules:
  0.0 138.4 jit_solution(16075712125414256215)
XLA Ops:
  1.1 0.9 prepare.1.refs_0_
  2.0 20.5 %collective-permute-start = (bf16[136,512]{1,0:T(8,128)(2,1)S(1)}, bf16[136,512]{1,0:T(8,128)(2,1)S(1)}, u32[]{:S(2)}, u32[]{:S(2)}) collective-permute-start(bf16[136,512]{1,0:T(8,128)(2,1)S(1)} %prepare.1.refs_0_), channel_id=1, source_target_pairs={{0,8},{8,0},{16,24},{24,16},{32,40},{40,32},{48,56},{56,48},{64,72... | collective-permute-start | bytes 417800 | tf_op jit(solution)/shard_map/ppermute | solution.py:108
  22.5 1.0 collective-permute-done.refs_1_
  23.6 0.1 collective-permute-start.1
  23.7 3.7 %collective-permute-done.2.refs_0_.refs_3_ = bf16[136,512]{1,0:T(8,128)(2,1)S(1)} collective-permute-done((bf16[136,512]{1,0:T(8,128)(2,1)S(1)}, bf16[136,512]{1,0:T(8,128)(2,1)S(1)}, u32[]{:S(2)}, u32[]{:S(2)}) %collective-permute-start.2) | collective-permute-done | bytes 139296 | tf_op jit(solution)/shard_map/ppermute | solution.py:104
  27.4 1.7 %collective-permute-done.3.refs_1_.refs_4_ = bf16[136,512]{1,0:T(8,128)(2,1)S(1)} collective-permute-done((bf16[136,512]{1,0:T(8,128)(2,1)S(1)}, bf16[136,512]{1,0:T(8,128)(2,1)S(1)}, u32[]{:S(2)}, u32[]{:S(2)}) %collective-permute-start.3) | collective-permute-done | bytes 139296 | tf_op jit(solution)/shard_map/ppermute | solution.py:104
  29.2 0.1 collective-permute-start.4
  29.3 1.0 collective-permute-start.5
  30.3 1.5 %collective-permute-start.7 = (bf16[272,512]{1,0:T(8,128)(2,1)S(1)}, bf16[272,512]{1,0:T(8,128)(2,1)S(1)}, u32[]{:S(2)}, u32[]{:S(2)}) collective-permute-start(bf16[272,512]{1,0:T(8,128)(2,1)S(1)} %pair.3), channel_id=1, source_target_pairs={{0,8},{8,0},{16,24},{24,16},{32,40},{40,32},{48,56},{56,48},{64,72... | collective-permute-start | bytes 835592 | tf_op jit(solution)/shard_map/ppermute | solution.py:108
  31.9 0.3 collective-permute-done.1.refs_2_
  32.1 2.2 %collective-permute-start.6 = (bf16[272,512]{1,0:T(8,128)(2,1)S(1)}, bf16[272,512]{1,0:T(8,128)(2,1)S(1)}, u32[]{:S(2)}, u32[]{:S(2)}) collective-permute-start(bf16[272,512]{1,0:T(8,128)(2,1)S(1)} %collective-permute-done.1.refs_2_), channel_id=1, source_target_pairs={{0,8},{8,0},{16,24},{24,16},{32,40},{40,32},{48,56},{56,48},{64,72... | collective-permute-start | bytes 835592 | tf_op jit(solution)/shard_map/ppermute | solution.py:108
  34.3 0.5 collective-permute-done.4.refs_5_
  34.8 6.0 %collective-permute-start.8 = (bf16[272,512]{1,0:T(8,128)(2,1)S(1)}, bf16[272,512]{1,0:T(8,128)(2,1)S(1)}, u32[]{:S(2)}, u32[]{:S(2)}) collective-permute-start(bf16[272,512]{1,0:T(8,128)(2,1)S(1)} %collective-permute-done.4.refs_5_), channel_id=1, source_target_pairs={{0,8},{8,0},{16,24},{24,16},{32,40},{40,32},{48,56},{56,48},{64,72... | collective-permute-start | bytes 835592 | tf_op jit(solution)/shard_map/ppermute | solution.py:108
  40.8 2.9 %weights.1 = (bf16[4,512,768]{2,1,0:T(8,128)(2,1)S(1)}, bf16[4,512,768]{2,1,0:T(8,128)(2,1)S(1)}) custom-call(bf16[4,512,768]{2,1,0:T(8,128)(2,1)} %wg_hbm.1, bf16[4,512,768]{2,1,0:T(8,128)(2,1)} %wu_hbm.1), custom_call_target="tpu_custom_call" | custom-call | tf_op jit(solution)/shard_map/weights/pallas_call | solution.py:412
  43.7 3.6 %pack.1 = (bf16[2,32,1536]{2,1,0:T(8,128)(2,1)S(1)}, bf16[2,32,1536]{2,1,0:T(8,128)(2,1)S(1)}, bf16[2,32,1536]{2,1,0:T(8,128)(2,1)S(1)}, bf16[2,32,1536]{2,1,0:T...) custom-call(s32[18]{0:T(128)S(1)} %stack.123.info, ...), custom_call_target="tpu_custom_call" | custom-call | flops 2000000000 | bytes 6000000 | tf_op jit(solution)/shard_map/pack/pallas_call | solution.py:423
  47.4 3.1 %pack_more.1 = (bf16[2,32,1536]{2,1,0:T(8,128)(2,1)S(1)}, bf16[2,32,1536]{2,1,0:T(8,128)(2,1)S(1)}, bf16[2,32,1536]{2,1,0:T(8,128)(2,1)S(1)}, bf16[2,32,1536]{2,...) custom-call(s32[18]{0:T(128)S(1)} %stack.123.info, ...), custom_call_target="tpu_custom_call" | custom-call | flops 2000000000 | bytes 6000000 | tf_op jit(solution)/shard_map/pack_more/pallas_call | solution.py:440
  50.4 0.1 collective-permute-start.20
  50.6 1.4 %collective-permute-start.17 = (bf16[2,32,1536]{2,1,0:T(8,128)(2,1)S(1)}, bf16[2,32,1536]{2,1,0:T(8,128)(2,1)S(1)}, u32[]{:S(2)}, u32[]{:S(2)}) collective-permute-start(bf16[2,32,1536]{2,1,0:T(8,128)(2,1)S(1)} %get-tuple-element.56), channel_id=1, source_target_pairs={{0,1},{1,2},{2,3},{3,4},{4,5},{5,6},{6,7},{7,0},{8,9},{9,10},{10,1... | collective-permute-start | bytes 589832 | tf_op jit(solution)/shard_map/ppermute | solution.py:98
  52.0 1.3 collective-permute-start.14
  53.5 3.1 %collective-permute-done.20 = bf16[2,32,1536]{2,1,0:T(8,128)(2,1)S(1)} collective-permute-done((bf16[2,32,1536]{2,1,0:T(8,128)(2,1)S(1)}, bf16[2,32,1536]{2,1,0:T(8,128)(2,1)S(1)}, u32[]{:S(2)}, u32[]{:S(2)}) %collective-permute-start.20) | collective-permute-done | bytes 196640 | tf_op jit(solution)/shard_map/ppermute | solution.py:98
  56.6 1.6 %collective-permute-start.21 = (bf16[2,32,1536]{2,1,0:T(8,128)(2,1)S(1)}, bf16[2,32,1536]{2,1,0:T(8,128)(2,1)S(1)}, u32[]{:S(2)}, u32[]{:S(2)}) collective-permute-start(bf16[2,32,1536]{2,1,0:T(8,128)(2,1)S(1)} %add_convert_fusion.2), channel_id=1, source_target_pairs={{0,7},{1,0},{2,1},{3,2},{4,3},{5,4},{6,5},{7,6},{8,15},{9,8},{10,9... | collective-permute-start | bytes 589832 | tf_op jit(solution)/shard_map/ppermute | solution.py:98
  58.3 0.1 collective-permute-start.18
  58.4 2.3 %collective-permute-done.14 = bf16[2,32,1536]{2,1,0:T(8,128)(2,1)S(1)} collective-permute-done((bf16[2,32,1536]{2,1,0:T(8,128)(2,1)S(1)}, bf16[2,32,1536]{2,1,0:T(8,128)(2,1)S(1)}, u32[]{:S(2)}, u32[]{:S(2)}) %collective-permute-start.14) | collective-permute-done | bytes 196640 | tf_op jit(solution)/shard_map/ppermute | solution.py:98
  60.8 1.6 %collective-permute-start.15 = (bf16[2,32,1536]{2,1,0:T(8,128)(2,1)S(1)}, bf16[2,32,1536]{2,1,0:T(8,128)(2,1)S(1)}, u32[]{:S(2)}, u32[]{:S(2)}) collective-permute-start(bf16[2,32,1536]{2,1,0:T(8,128)(2,1)S(1)} %add_convert_fusion.6), channel_id=1, source_target_pairs={{0,7},{1,0},{2,1},{3,2},{4,3},{5,4},{6,5},{7,6},{8,15},{9,8},{10,9... | collective-permute-start | bytes 589832 | tf_op jit(solution)/shard_map/ppermute | solution.py:98
  62.5 0.1 collective-permute-start.11
  62.6 2.3 %collective-permute-done.21 = bf16[2,32,1536]{2,1,0:T(8,128)(2,1)S(1)} collective-permute-done((bf16[2,32,1536]{2,1,0:T(8,128)(2,1)S(1)}, bf16[2,32,1536]{2,1,0:T(8,128)(2,1)S(1)}, u32[]{:S(2)}, u32[]{:S(2)}) %collective-permute-start.21) | collective-permute-done | bytes 196640 | tf_op jit(solution)/shard_map/ppermute | solution.py:98
  65.0 0.9 collective-permute-start.22
  66.0 0.8 collective-permute-start.19
  66.8 2.4 %collective-permute-done.15 = bf16[2,32,1536]{2,1,0:T(8,128)(2,1)S(1)} collective-permute-done((bf16[2,32,1536]{2,1,0:T(8,128)(2,1)S(1)}, bf16[2,32,1536]{2,1,0:T(8,128)(2,1)S(1)}, u32[]{:S(2)}, u32[]{:S(2)}) %collective-permute-start.15) | collective-permute-done | bytes 196640 | tf_op jit(solution)/shard_map/ppermute | solution.py:98
  69.2 0.9 collective-permute-start.16
  70.2 0.8 collective-permute-start.12
  71.0 2.4 %collective-permute-done.22 = bf16[2,32,1536]{2,1,0:T(8,128)(2,1)S(1)} collective-permute-done((bf16[2,32,1536]{2,1,0:T(8,128)(2,1)S(1)}, bf16[2,32,1536]{2,1,0:T(8,128)(2,1)S(1)}, u32[]{:S(2)}, u32[]{:S(2)}) %collective-permute-start.22) | collective-permute-done | bytes 196640 | tf_op jit(solution)/shard_map/ppermute | solution.py:98
  73.4 0.8 collective-permute-start.23
  74.2 3.3 %collective-permute-done.12 = bf16[2,32,1536]{2,1,0:T(8,128)(2,1)S(1)} collective-permute-done((bf16[2,32,1536]{2,1,0:T(8,128)(2,1)S(1)}, bf16[2,32,1536]{2,1,0:T(8,128)(2,1)S(1)}, u32[]{:S(2)}, u32[]{:S(2)}) %collective-permute-start.12) | collective-permute-done | bytes 196640 | tf_op jit(solution)/shard_map/ppermute | solution.py:98
  77.5 1.4 %collective-permute-start.13 = (bf16[2,32,1536]{2,1,0:T(8,128)(2,1)S(1)}, bf16[2,32,1536]{2,1,0:T(8,128)(2,1)S(1)}, u32[]{:S(2)}, u32[]{:S(2)}) collective-permute-start(bf16[2,32,1536]{2,1,0:T(8,128)(2,1)S(1)} %add_convert_fusion.7), channel_id=1, source_target_pairs={{0,1},{1,2},{2,3},{3,4},{4,5},{5,6},{6,7},{7,0},{8,9},{9,10},{10,1... | collective-permute-start | bytes 589832 | tf_op jit(solution)/shard_map/ppermute | solution.py:98
  79.0 2.9 %collective-permute-done.23.refs_5_ = bf16[2,32,1536]{2,1,0:T(8,128)(2,1)S(1)} collective-permute-done((bf16[2,32,1536]{2,1,0:T(8,128)(2,1)S(1)}, bf16[2,32,1536]{2,1,0:T(8,128)(2,1)S(1)}, u32[]{:S(2)}, u32[]{:S(2)}) %collective-permute-start.23) | collective-permute-done | bytes 196640 | tf_op jit(solution)/shard_map/ppermute | solution.py:98
  81.8 1.6 %collective-permute-done.13.refs_1_ = bf16[2,32,1536]{2,1,0:T(8,128)(2,1)S(1)} collective-permute-done((bf16[2,32,1536]{2,1,0:T(8,128)(2,1)S(1)}, bf16[2,32,1536]{2,1,0:T(8,128)(2,1)S(1)}, u32[]{:S(2)}, u32[]{:S(2)}) %collective-permute-start.13) | collective-permute-done | bytes 196640 | tf_op jit(solution)/shard_map/ppermute | solution.py:98
  83.4 0.2 hidden.1.refs_0_
  83.6 0.8 collective-permute-start.26
  84.4 2.9 %collective-permute-start.27 = (bf16[4,32,768]{2,1,0:T(8,128)(2,1)S(1)}, bf16[4,32,768]{2,1,0:T(8,128)(2,1)S(1)}, u32[]{:S(2)}, u32[]{:S(2)}) collective-permute-start(bf16[4,32,768]{2,1,0:T(8,128)(2,1)S(1)} %hidden.1.refs_0_), channel_id=1, source_target_pairs={{0,6},{1,7},{2,0},{3,1},{4,2},{5,3},{6,4},{7,5},{8,14},{9,15},{10,... | collective-permute-start | bytes 589832 | tf_op jit(solution)/shard_map/ppermute | solution.py:98
  87.3 0.4 collective-permute-start.24
  87.7 2.2 %collective-permute-start.25 = (bf16[4,32,768]{2,1,0:T(8,128)(2,1)S(1)}, bf16[4,32,768]{2,1,0:T(8,128)(2,1)S(1)}, u32[]{:S(2)}, u32[]{:S(2)}) collective-permute-start(bf16[4,32,768]{2,1,0:T(8,128)(2,1)S(1)} %hidden.1.refs_0_), channel_id=1, source_target_pairs={{0,7},{1,0},{2,1},{3,2},{4,3},{5,4},{6,5},{7,6},{8,15},{9,8},{10,9... | collective-permute-start | bytes 589832 | tf_op jit(solution)/shard_map/ppermute | solution.py:98
  90.0 3.7 %collective-permute-done.26.refs_3_ = bf16[4,32,768]{2,1,0:T(8,128)(2,1)S(1)} collective-permute-done((bf16[4,32,768]{2,1,0:T(8,128)(2,1)S(1)}, bf16[4,32,768]{2,1,0:T(8,128)(2,1)S(1)}, u32[]{:S(2)}, u32[]{:S(2)}) %collective-permute-start.26) | collective-permute-done | bytes 196640 | tf_op jit(solution)/shard_map/ppermute | solution.py:98
  93.7 3.0 %collective-permute-start.29 = (bf16[4,32,768]{2,1,0:T(8,128)(2,1)S(1)}, bf16[4,32,768]{2,1,0:T(8,128)(2,1)S(1)}, u32[]{:S(2)}, u32[]{:S(2)}) collective-permute-start(bf16[4,32,768]{2,1,0:T(8,128)(2,1)S(1)} %collective-permute-done.27.refs_4_), channel_id=1, source_target_pairs={{0,7},{1,0},{2,1},{3,2},{4,3},{5,4},{6,5},{7,6},{8,15},{9,8},{10,9... | collective-permute-start | bytes 589832 | tf_op jit(solution)/shard_map/ppermute | solution.py:98
  96.9 1.6 %collective-permute-done.24.refs_1_ = bf16[4,32,768]{2,1,0:T(8,128)(2,1)S(1)} collective-permute-done((bf16[4,32,768]{2,1,0:T(8,128)(2,1)S(1)}, bf16[4,32,768]{2,1,0:T(8,128)(2,1)S(1)}, u32[]{:S(2)}, u32[]{:S(2)}) %collective-permute-start.24) | collective-permute-done | bytes 196640 | tf_op jit(solution)/shard_map/ppermute | solution.py:98
  98.5 2.1 %collective-permute-start.31 = (bf16[2,32,768]{2,1,0:T(8,128)(2,1)S(1)}, bf16[2,32,768]{2,1,0:T(8,128)(2,1)S(1)}, u32[]{:S(2)}, u32[]{:S(2)}) collective-permute-start(bf16[2,32,768]{2,1,0:T(8,128)(2,1)S(1)} %slice.9), channel_id=1, source_target_pairs={{0,6},{1,7},{2,0},{3,1},{4,2},{5,3},{6,4},{7,5},{8,14},{9,15},{10,... | collective-permute-start | bytes 294920 | tf_op jit(solution)/shard_map/ppermute | solution.py:98
  100.6 4.2 %mix.1 = (bf16[2048,1024]{1,0:T(8,128)(2,1)S(1)}, bf16[4,768,512]{2,1,0:T(8,128)(2,1)S(1)}) custom-call(s32[16]{0:T(128)S(1)} %stack.125.info, f32[16,8,128]{2,1,0:T(8,128)S(1)} %get-tuple-element.43.route, bf16[4,768,512]{2,1,0:T(8,128)(2,1)} %wd_hbm.1), custom_call_target="tpu_custom_call" | custom-call | tf_op jit(solution)/shard_map/mix/pallas_call | solution.py:468
  104.8 1.2 collective-permute-done.30.refs_7_
  106.2 3.0 %down.1 = (bf16[4,128,512]{2,1,0:T(8,128)(2,1)S(1)}, bf16[1024,512]{1,0:T(8,128)(2,1)S(1)}) custom-call(s32[8]{0:T(128)S(1)} %stack.134.info, bf16[4,32,768]{2,1,0:T(8,128)(2,1)S(1)} %hidden.1.refs_0_, bf16[4,32,768]{2,1,0:T(8,128)(2,1)S(1)} %collective-permute-done.24.refs_1_, bf16[4,32,768]{2,1,0:T(8,128)(2,1)S(1)} %collective-permute-done.25.refs_2_, ...), custom_call_target="tpu_custom_call" | custom-call | flops 2000000000 | bytes 6000000 | tf_op jit(solution)/shard_map/down/pallas_call | solution.py:481
  109.2 5.0 %collective-permute-start.32 = (bf16[4,128,512]{2,1,0:T(8,128)(2,1)S(1)}, bf16[4,128,512]{2,1,0:T(8,128)(2,1)S(1)}, u32[]{:S(2)}, u32[]{:S(2)}) collective-permute-start(bf16[4,128,512]{2,1,0:T(8,128)(2,1)S(1)} %get-tuple-element.66), channel_id=1, source_target_pairs={{0,8},{8,0},{16,24},{24,16},{32,40},{40,32},{48,56},{56,48},{64,72... | collective-permute-start | bytes 1572872 | tf_op jit(solution)/shard_map/ppermute | solution.py:108
  114.2 1.7 %shard_map.113 = (bf16[4,128,512]{2,1,0:T(8,128)(2,1)S(1)}, bf16[4,128,512]{2,1,0:T(8,128)(2,1)S(1)}) custom-call(bf16[2048,1024]{1,0:T(8,128)(2,1)S(1)} %get-tuple-element.44.refs_10_.mix, bf16[1024,512]{1,0:T(8,128)(2,1)S(1)} %get-tuple-element.64.res), custom_call_target="tpu_custom_call" | custom-call | tf_op jit(solution)/shard_map/pallas_call | solution.py:493
  115.9 0.1 collective-permute-start.33
  116.2 2.3 %collective-permute-start.36 = (bf16[256,512]{1,0:T(8,128)(2,1)S(1)}, bf16[256,512]{1,0:T(8,128)(2,1)S(1)}, u32[]{:S(2)}, u32[]{:S(2)}) collective-permute-start(bf16[256,512]{1,0:T(8,128)(2,1)S(1)} %get-tuple-element.70), channel_id=1, source_target_pairs={{0,16},{8,120},{16,32},{24,8},{32,48},{40,24},{48,64},{56,40},{64,... | collective-permute-start | bytes 786440 | tf_op jit(solution)/shard_map/ppermute | solution.py:104
  118.5 0.8 collective-permute-start.37
  119.3 0.9 shard_map.114.home
  120.2 0.3 collective-permute-start.34
  120.5 3.9 %collective-permute-start.35 = (bf16[128,512]{1,0:T(8,128)(2,1)S(1)}, bf16[128,512]{1,0:T(8,128)(2,1)S(1)}, u32[]{:S(2)}, u32[]{:S(2)}) collective-permute-start(bf16[128,512]{1,0:T(8,128)(2,1)S(1)} %get-tuple-element.69), channel_id=1, source_target_pairs={{0,24},{8,112},{16,40},{24,0},{32,56},{40,16},{48,72},{56,32},{64,... | collective-permute-start | bytes 393224 | tf_op jit(solution)/shard_map/ppermute | solution.py:104
  124.4 3.4 %collective-permute-done.37.four = bf16[128,512]{1,0:T(8,128)(2,1)S(1)} collective-permute-done((bf16[128,512]{1,0:T(8,128)(2,1)S(1)}, bf16[128,512]{1,0:T(8,128)(2,1)S(1)}, u32[]{:S(2)}, u32[]{:S(2)}) %collective-permute-start.37) | collective-permute-done | bytes 131104 | tf_op jit(solution)/shard_map/ppermute | solution.py:104
  127.9 1.1 collective-permute-start.38
  128.9 3.0 %collective-permute-start.39 = (bf16[128,512]{1,0:T(8,128)(2,1)S(1)}, bf16[128,512]{1,0:T(8,128)(2,1)S(1)}, u32[]{:S(2)}, u32[]{:S(2)}) collective-permute-start(bf16[128,512]{1,0:T(8,128)(2,1)S(1)} %get-tuple-element.73), channel_id=1, source_target_pairs={{0,40},{8,96},{16,56},{24,112},{32,72},{40,0},{48,88},{56,16},{64,... | collective-permute-start | bytes 393224 | tf_op jit(solution)/shard_map/ppermute | solution.py:104
  131.9 3.4 %attention.1 = bf16[2,64,128]{2,1,0:T(8,128)(2,1)S(1)} custom-call(s32[2]{0:T(128)S(1)} %copy-done, bf16[2,64,128]{2,1,0:T(8,128)(2,1)} %query.1, bf16[2,768,4,128]{3,2,1,0:T(4,128)(2,1)} %cache_k.1, bf16[2,768,4,128]{3,2,1,0:T(4,128)(2,1)} %cache_v.1), custom_call_target="tpu_custom_call" | custom-call | flops 1000000000 | bytes 3000000 | tf_op jit(solution)/shard_map/attention/pallas_call | solution.py:81
  135.3 0.6 copy.14
  136.0 1.6 %collective-permute-done.39.d = bf16[128,512]{1,0:T(8,128)(2,1)S(1)} collective-permute-done((bf16[128,512]{1,0:T(8,128)(2,1)S(1)}, bf16[128,512]{1,0:T(8,128)(2,1)S(1)}, u32[]{:S(2)}, u32[]{:S(2)}) %collective-permute-start.39) | collective-permute-done | bytes 131104 | tf_op jit(solution)/shard_map/ppermute | solution.py:104
  137.6 0.8 shard_map.118
  (50 shorter events, 1.5 us)
Async XLA Ops:
  2.0 21.5 %collective-permute-start = (bf16[136,512]{1,0:T(8,128)(2,1)S(1)}, bf16[136,512]{1,0:T(8,128)(2,1)S(1)}, u32[]{:S(2)}, u32[]{:S(2)}) collective-permute-start(bf16[136,512]{1,0:T(8,128)(2,1)S(1)} %prepare.1.refs_0_), channel_id=1, source_target_pairs={{0,8},{8,0},{16,24},{24,16},{32,40},{40,32},{48,56},{56,48},{64,72... | collective-permute-start | bytes 417800 | tf_op jit(solution)/shard_map/ppermute | solution.py:108
  22.5 4.9 %collective-permute-start.2 = (bf16[136,512]{1,0:T(8,128)(2,1)S(1)}, bf16[136,512]{1,0:T(8,128)(2,1)S(1)}, u32[]{:S(2)}, u32[]{:S(2)}) collective-permute-start(bf16[136,512]{1,0:T(8,128)(2,1)S(1)} %prepare.1.refs_0_), channel_id=1, source_target_pairs={{0,32},{8,104},{16,48},{24,120},{32,64},{40,8},{48,80},{56,24},{64... | collective-permute-start | bytes 417800 | tf_op jit(solution)/shard_map/ppermute | solution.py:104
  23.5 5.6 %collective-permute-start.3 = (bf16[136,512]{1,0:T(8,128)(2,1)S(1)}, bf16[136,512]{1,0:T(8,128)(2,1)S(1)}, u32[]{:S(2)}, u32[]{:S(2)}) collective-permute-start(bf16[136,512]{1,0:T(8,128)(2,1)S(1)} %collective-permute-done.refs_1_), channel_id=1, source_target_pairs={{0,32},{8,104},{16,48},{24,120},{32,64},{40,8},{48,80},{56,24},{64... | collective-permute-start | bytes 417800 | tf_op jit(solution)/shard_map/ppermute | solution.py:104
  23.6 8.6 %collective-permute-start.1 = (bf16[272,512]{1,0:T(8,128)(2,1)S(1)}, bf16[272,512]{1,0:T(8,128)(2,1)S(1)}, u32[]{:S(2)}, u32[]{:S(2)}) collective-permute-start(bf16[272,512]{1,0:T(8,128)(2,1)S(1)} %pair.2), channel_id=1, source_target_pairs={{0,16},{8,120},{16,32},{24,8},{32,48},{40,24},{48,64},{56,40},{64,... | collective-permute-start | bytes 835592 | tf_op jit(solution)/shard_map/ppermute | solution.py:104
  29.2 5.6 %collective-permute-start.4 = (bf16[272,512]{1,0:T(8,128)(2,1)S(1)}, bf16[272,512]{1,0:T(8,128)(2,1)S(1)}, u32[]{:S(2)}, u32[]{:S(2)}) collective-permute-start(bf16[272,512]{1,0:T(8,128)(2,1)S(1)} %pair.3), channel_id=1, source_target_pairs={{0,16},{8,120},{16,32},{24,8},{32,48},{40,24},{48,64},{56,40},{64,... | collective-permute-start | bytes 835592 | tf_op jit(solution)/shard_map/ppermute | solution.py:104
  29.3 11.5 %collective-permute-start.5 = (bf16[136,512]{1,0:T(8,128)(2,1)S(1)}, bf16[136,512]{1,0:T(8,128)(2,1)S(1)}, u32[]{:S(2)}, u32[]{:S(2)}) collective-permute-start(bf16[136,512]{1,0:T(8,128)(2,1)S(1)} %collective-permute-done.2.refs_0_.refs_3_), channel_id=1, source_target_pairs={{0,32},{8,104},{16,48},{24,120},{32,64},{40,8},{48,80},{56,24},{64... | collective-permute-start | bytes 417800 | tf_op jit(solution)/shard_map/ppermute | solution.py:104
  30.3 13.4 %collective-permute-start.7 = (bf16[272,512]{1,0:T(8,128)(2,1)S(1)}, bf16[272,512]{1,0:T(8,128)(2,1)S(1)}, u32[]{:S(2)}, u32[]{:S(2)}) collective-permute-start(bf16[272,512]{1,0:T(8,128)(2,1)S(1)} %pair.3), channel_id=1, source_target_pairs={{0,8},{8,0},{16,24},{24,16},{32,40},{40,32},{48,56},{56,48},{64,72... | collective-permute-start | bytes 835592 | tf_op jit(solution)/shard_map/ppermute | solution.py:108
  32.1 11.6 %collective-permute-start.6 = (bf16[272,512]{1,0:T(8,128)(2,1)S(1)}, bf16[272,512]{1,0:T(8,128)(2,1)S(1)}, u32[]{:S(2)}, u32[]{:S(2)}) collective-permute-start(bf16[272,512]{1,0:T(8,128)(2,1)S(1)} %collective-permute-done.1.refs_2_), channel_id=1, source_target_pairs={{0,8},{8,0},{16,24},{24,16},{32,40},{40,32},{48,56},{56,48},{64,72... | collective-permute-start | bytes 835592 | tf_op jit(solution)/shard_map/ppermute | solution.py:108
  34.8 8.9 %collective-permute-start.8 = (bf16[272,512]{1,0:T(8,128)(2,1)S(1)}, bf16[272,512]{1,0:T(8,128)(2,1)S(1)}, u32[]{:S(2)}, u32[]{:S(2)}) collective-permute-start(bf16[272,512]{1,0:T(8,128)(2,1)S(1)} %collective-permute-done.4.refs_5_), channel_id=1, source_target_pairs={{0,8},{8,0},{16,24},{24,16},{32,40},{40,32},{48,56},{56,48},{64,72... | collective-permute-start | bytes 835592 | tf_op jit(solution)/shard_map/ppermute | solution.py:108
  40.8 2.9 %collective-permute-start.9 = (bf16[136,512]{1,0:T(8,128)(2,1)S(1)}, bf16[136,512]{1,0:T(8,128)(2,1)S(1)}, u32[]{:S(2)}, u32[]{:S(2)}) collective-permute-start(bf16[136,512]{1,0:T(8,128)(2,1)S(1)} %collective-permute-done.5.refs_6_), channel_id=1, source_target_pairs={{0,8},{8,0},{16,24},{24,16},{32,40},{40,32},{48,56},{56,48},{64,72... | collective-permute-start | bytes 417800 | tf_op jit(solution)/shard_map/ppermute | solution.py:108
  50.4 6.1 %collective-permute-start.20 = (bf16[2,32,1536]{2,1,0:T(8,128)(2,1)S(1)}, bf16[2,32,1536]{2,1,0:T(8,128)(2,1)S(1)}, u32[]{:S(2)}, u32[]{:S(2)}) collective-permute-start(bf16[2,32,1536]{2,1,0:T(8,128)(2,1)S(1)} %get-tuple-element.59), channel_id=1, source_target_pairs={{0,7},{1,0},{2,1},{3,2},{4,3},{5,4},{6,5},{7,6},{8,15},{9,8},{10,9... | collective-permute-start | bytes 589832 | tf_op jit(solution)/shard_map/ppermute | solution.py:98
  50.6 7.6 %collective-permute-start.17 = (bf16[2,32,1536]{2,1,0:T(8,128)(2,1)S(1)}, bf16[2,32,1536]{2,1,0:T(8,128)(2,1)S(1)}, u32[]{:S(2)}, u32[]{:S(2)}) collective-permute-start(bf16[2,32,1536]{2,1,0:T(8,128)(2,1)S(1)} %get-tuple-element.56), channel_id=1, source_target_pairs={{0,1},{1,2},{2,3},{3,4},{4,5},{5,6},{6,7},{7,0},{8,9},{9,10},{10,1... | collective-permute-start | bytes 589832 | tf_op jit(solution)/shard_map/ppermute | solution.py:98
  52.0 8.7 %collective-permute-start.14 = (bf16[2,32,1536]{2,1,0:T(8,128)(2,1)S(1)}, bf16[2,32,1536]{2,1,0:T(8,128)(2,1)S(1)}, u32[]{:S(2)}, u32[]{:S(2)}) collective-permute-start(bf16[2,32,1536]{2,1,0:T(8,128)(2,1)S(1)} %get-tuple-element.51), channel_id=1, source_target_pairs={{0,7},{1,0},{2,1},{3,2},{4,3},{5,4},{6,5},{7,6},{8,15},{9,8},{10,9... | collective-permute-start | bytes 589832 | tf_op jit(solution)/shard_map/ppermute | solution.py:98
  53.4 9.1 %collective-permute-start.10 = (bf16[2,32,1536]{2,1,0:T(8,128)(2,1)S(1)}, bf16[2,32,1536]{2,1,0:T(8,128)(2,1)S(1)}, u32[]{:S(2)}, u32[]{:S(2)}) collective-permute-start(bf16[2,32,1536]{2,1,0:T(8,128)(2,1)S(1)} %get-tuple-element.47), channel_id=1, source_target_pairs={{0,1},{1,2},{2,3},{3,4},{4,5},{5,6},{6,7},{7,0},{8,9},{9,10},{10,1... | collective-permute-start | bytes 589832 | tf_op jit(solution)/shard_map/ppermute | solution.py:98
  56.6 8.4 %collective-permute-start.21 = (bf16[2,32,1536]{2,1,0:T(8,128)(2,1)S(1)}, bf16[2,32,1536]{2,1,0:T(8,128)(2,1)S(1)}, u32[]{:S(2)}, u32[]{:S(2)}) collective-permute-start(bf16[2,32,1536]{2,1,0:T(8,128)(2,1)S(1)} %add_convert_fusion.2), channel_id=1, source_target_pairs={{0,7},{1,0},{2,1},{3,2},{4,3},{5,4},{6,5},{7,6},{8,15},{9,8},{10,9... | collective-permute-start | bytes 589832 | tf_op jit(solution)/shard_map/ppermute | solution.py:98
  58.3 7.7 %collective-permute-start.18 = (bf16[2,32,1536]{2,1,0:T(8,128)(2,1)S(1)}, bf16[2,32,1536]{2,1,0:T(8,128)(2,1)S(1)}, u32[]{:S(2)}, u32[]{:S(2)}) collective-permute-start(bf16[2,32,1536]{2,1,0:T(8,128)(2,1)S(1)} %add_convert_fusion.4), channel_id=1, source_target_pairs={{0,1},{1,2},{2,3},{3,4},{4,5},{5,6},{6,7},{7,0},{8,9},{9,10},{10,1... | collective-permute-start | bytes 589832 | tf_op jit(solution)/shard_map/ppermute | solution.py:98
  60.8 8.4 %collective-permute-start.15 = (bf16[2,32,1536]{2,1,0:T(8,128)(2,1)S(1)}, bf16[2,32,1536]{2,1,0:T(8,128)(2,1)S(1)}, u32[]{:S(2)}, u32[]{:S(2)}) collective-permute-start(bf16[2,32,1536]{2,1,0:T(8,128)(2,1)S(1)} %add_convert_fusion.6), channel_id=1, source_target_pairs={{0,7},{1,0},{2,1},{3,2},{4,3},{5,4},{6,5},{7,6},{8,15},{9,8},{10,9... | collective-permute-start | bytes 589832 | tf_op jit(solution)/shard_map/ppermute | solution.py:98
  62.5 7.6 %collective-permute-start.11 = (bf16[2,32,1536]{2,1,0:T(8,128)(2,1)S(1)}, bf16[2,32,1536]{2,1,0:T(8,128)(2,1)S(1)}, u32[]{:S(2)}, u32[]{:S(2)}) collective-permute-start(bf16[2,32,1536]{2,1,0:T(8,128)(2,1)S(1)} %add_convert_fusion.9), channel_id=1, source_target_pairs={{0,1},{1,2},{2,3},{3,4},{4,5},{5,6},{6,7},{7,0},{8,9},{9,10},{10,1... | collective-permute-start | bytes 589832 | tf_op jit(solution)/shard_map/ppermute | solution.py:98
  65.0 8.4 %collective-permute-start.22 = (bf16[2,32,1536]{2,1,0:T(8,128)(2,1)S(1)}, bf16[2,32,1536]{2,1,0:T(8,128)(2,1)S(1)}, u32[]{:S(2)}, u32[]{:S(2)}) collective-permute-start(bf16[2,32,1536]{2,1,0:T(8,128)(2,1)S(1)} %add_convert_fusion.1), channel_id=1, source_target_pairs={{0,7},{1,0},{2,1},{3,2},{4,3},{5,4},{6,5},{7,6},{8,15},{9,8},{10,9... | collective-permute-start | bytes 589832 | tf_op jit(solution)/shard_map/ppermute | solution.py:98
  66.0 13.0 %collective-permute-start.19 = (bf16[2,32,1536]{2,1,0:T(8,128)(2,1)S(1)}, bf16[2,32,1536]{2,1,0:T(8,128)(2,1)S(1)}, u32[]{:S(2)}, u32[]{:S(2)}) collective-permute-start(bf16[2,32,1536]{2,1,0:T(8,128)(2,1)S(1)} %add_convert_fusion.3), channel_id=1, source_target_pairs={{0,1},{1,2},{2,3},{3,4},{4,5},{5,6},{6,7},{7,0},{8,9},{9,10},{10,1... | collective-permute-start | bytes 589832 | tf_op jit(solution)/shard_map/ppermute | solution.py:98
  69.2 9.7 %collective-permute-start.16 = (bf16[2,32,1536]{2,1,0:T(8,128)(2,1)S(1)}, bf16[2,32,1536]{2,1,0:T(8,128)(2,1)S(1)}, u32[]{:S(2)}, u32[]{:S(2)}) collective-permute-start(bf16[2,32,1536]{2,1,0:T(8,128)(2,1)S(1)} %add_convert_fusion.5), channel_id=1, source_target_pairs={{0,7},{1,0},{2,1},{3,2},{4,3},{5,4},{6,5},{7,6},{8,15},{9,8},{10,9... | collective-permute-start | bytes 589832 | tf_op jit(solution)/shard_map/ppermute | solution.py:98
  70.2 7.3 %collective-permute-start.12 = (bf16[2,32,1536]{2,1,0:T(8,128)(2,1)S(1)}, bf16[2,32,1536]{2,1,0:T(8,128)(2,1)S(1)}, u32[]{:S(2)}, u32[]{:S(2)}) collective-permute-start(bf16[2,32,1536]{2,1,0:T(8,128)(2,1)S(1)} %add_convert_fusion.8), channel_id=1, source_target_pairs={{0,1},{1,2},{2,3},{3,4},{4,5},{5,6},{6,7},{7,0},{8,9},{9,10},{10,1... | collective-permute-start | bytes 589832 | tf_op jit(solution)/shard_map/ppermute | solution.py:98
  73.4 8.4 %collective-permute-start.23 = (bf16[2,32,1536]{2,1,0:T(8,128)(2,1)S(1)}, bf16[2,32,1536]{2,1,0:T(8,128)(2,1)S(1)}, u32[]{:S(2)}, u32[]{:S(2)}) collective-permute-start(bf16[2,32,1536]{2,1,0:T(8,128)(2,1)S(1)} %add_convert_fusion), channel_id=1, source_target_pairs={{0,7},{1,0},{2,1},{3,2},{4,3},{5,4},{6,5},{7,6},{8,15},{9,8},{10,9... | collective-permute-start | bytes 589832 | tf_op jit(solution)/shard_map/ppermute | solution.py:98
  77.5 5.8 %collective-permute-start.13 = (bf16[2,32,1536]{2,1,0:T(8,128)(2,1)S(1)}, bf16[2,32,1536]{2,1,0:T(8,128)(2,1)S(1)}, u32[]{:S(2)}, u32[]{:S(2)}) collective-permute-start(bf16[2,32,1536]{2,1,0:T(8,128)(2,1)S(1)} %add_convert_fusion.7), channel_id=1, source_target_pairs={{0,1},{1,2},{2,3},{3,4},{4,5},{5,6},{6,7},{7,0},{8,9},{9,10},{10,1... | collective-permute-start | bytes 589832 | tf_op jit(solution)/shard_map/ppermute | solution.py:98
  83.6 10.1 %collective-permute-start.26 = (bf16[4,32,768]{2,1,0:T(8,128)(2,1)S(1)}, bf16[4,32,768]{2,1,0:T(8,128)(2,1)S(1)}, u32[]{:S(2)}, u32[]{:S(2)}) collective-permute-start(bf16[4,32,768]{2,1,0:T(8,128)(2,1)S(1)} %hidden.1.refs_0_), channel_id=1, source_target_pairs={{0,2},{1,3},{2,4},{3,5},{4,6},{5,7},{6,0},{7,1},{8,10},{9,11},{10,... | collective-permute-start | bytes 589832 | tf_op jit(solution)/shard_map/ppermute | solution.py:98
  84.4 9.3 %collective-permute-start.27 = (bf16[4,32,768]{2,1,0:T(8,128)(2,1)S(1)}, bf16[4,32,768]{2,1,0:T(8,128)(2,1)S(1)}, u32[]{:S(2)}, u32[]{:S(2)}) collective-permute-start(bf16[4,32,768]{2,1,0:T(8,128)(2,1)S(1)} %hidden.1.refs_0_), channel_id=1, source_target_pairs={{0,6},{1,7},{2,0},{3,1},{4,2},{5,3},{6,4},{7,5},{8,14},{9,15},{10,... | collective-permute-start | bytes 589832 | tf_op jit(solution)/shard_map/ppermute | solution.py:98
  87.3 11.2 %collective-permute-start.24 = (bf16[4,32,768]{2,1,0:T(8,128)(2,1)S(1)}, bf16[4,32,768]{2,1,0:T(8,128)(2,1)S(1)}, u32[]{:S(2)}, u32[]{:S(2)}) collective-permute-start(bf16[4,32,768]{2,1,0:T(8,128)(2,1)S(1)} %hidden.1.refs_0_), channel_id=1, source_target_pairs={{0,1},{1,2},{2,3},{3,4},{4,5},{5,6},{6,7},{7,0},{8,9},{9,10},{10,1... | collective-permute-start | bytes 589832 | tf_op jit(solution)/shard_map/ppermute | solution.py:98
  87.7 17.1 %collective-permute-start.25 = (bf16[4,32,768]{2,1,0:T(8,128)(2,1)S(1)}, bf16[4,32,768]{2,1,0:T(8,128)(2,1)S(1)}, u32[]{:S(2)}, u32[]{:S(2)}) collective-permute-start(bf16[4,32,768]{2,1,0:T(8,128)(2,1)S(1)} %hidden.1.refs_0_), channel_id=1, source_target_pairs={{0,7},{1,0},{2,1},{3,2},{4,3},{5,4},{6,5},{7,6},{8,15},{9,8},{10,9... | collective-permute-start | bytes 589832 | tf_op jit(solution)/shard_map/ppermute | solution.py:98
  93.7 12.4 %collective-permute-start.28 = (bf16[4,32,768]{2,1,0:T(8,128)(2,1)S(1)}, bf16[4,32,768]{2,1,0:T(8,128)(2,1)S(1)}, u32[]{:S(2)}, u32[]{:S(2)}) collective-permute-start(bf16[4,32,768]{2,1,0:T(8,128)(2,1)S(1)} %collective-permute-done.26.refs_3_), channel_id=1, source_target_pairs={{0,1},{1,2},{2,3},{3,4},{4,5},{5,6},{6,7},{7,0},{8,9},{9,10},{10,1... | collective-permute-start | bytes 589832 | tf_op jit(solution)/shard_map/ppermute | solution.py:98
  93.7 12.4 %collective-permute-start.29 = (bf16[4,32,768]{2,1,0:T(8,128)(2,1)S(1)}, bf16[4,32,768]{2,1,0:T(8,128)(2,1)S(1)}, u32[]{:S(2)}, u32[]{:S(2)}) collective-permute-start(bf16[4,32,768]{2,1,0:T(8,128)(2,1)S(1)} %collective-permute-done.27.refs_4_), channel_id=1, source_target_pairs={{0,7},{1,0},{2,1},{3,2},{4,3},{5,4},{6,5},{7,6},{8,15},{9,8},{10,9... | collective-permute-start | bytes 589832 | tf_op jit(solution)/shard_map/ppermute | solution.py:98
  96.8 9.3 %collective-permute-start.30 = (bf16[2,32,768]{2,1,0:T(8,128)(2,1)S(1)}, bf16[2,32,768]{2,1,0:T(8,128)(2,1)S(1)}, u32[]{:S(2)}, u32[]{:S(2)}) collective-permute-start(bf16[2,32,768]{2,1,0:T(8,128)(2,1)S(1)} %slice.8), channel_id=1, source_target_pairs={{0,2},{1,3},{2,4},{3,5},{4,6},{5,7},{6,0},{7,1},{8,10},{9,11},{10,... | collective-permute-start | bytes 294920 | tf_op jit(solution)/shard_map/ppermute | solution.py:98
  98.5 7.7 %collective-permute-start.31 = (bf16[2,32,768]{2,1,0:T(8,128)(2,1)S(1)}, bf16[2,32,768]{2,1,0:T(8,128)(2,1)S(1)}, u32[]{:S(2)}, u32[]{:S(2)}) collective-permute-start(bf16[2,32,768]{2,1,0:T(8,128)(2,1)S(1)} %slice.9), channel_id=1, source_target_pairs={{0,6},{1,7},{2,0},{3,1},{4,2},{5,3},{6,4},{7,5},{8,14},{9,15},{10,... | collective-permute-start | bytes 294920 | tf_op jit(solution)/shard_map/ppermute | solution.py:98
  109.2 6.9 %collective-permute-start.32 = (bf16[4,128,512]{2,1,0:T(8,128)(2,1)S(1)}, bf16[4,128,512]{2,1,0:T(8,128)(2,1)S(1)}, u32[]{:S(2)}, u32[]{:S(2)}) collective-permute-start(bf16[4,128,512]{2,1,0:T(8,128)(2,1)S(1)} %get-tuple-element.66), channel_id=1, source_target_pairs={{0,8},{8,0},{16,24},{24,16},{32,40},{40,32},{48,56},{56,48},{64,72... | collective-permute-start | bytes 1572872 | tf_op jit(solution)/shard_map/ppermute | solution.py:108
  115.9 4.2 %collective-permute-start.33 = (bf16[4,128,512]{2,1,0:T(8,128)(2,1)S(1)}, bf16[4,128,512]{2,1,0:T(8,128)(2,1)S(1)}, u32[]{:S(2)}, u32[]{:S(2)}) collective-permute-start(bf16[4,128,512]{2,1,0:T(8,128)(2,1)S(1)} %get-tuple-element.67), channel_id=1, source_target_pairs={{0,8},{8,0},{16,24},{24,16},{32,40},{40,32},{48,56},{56,48},{64,72... | collective-permute-start | bytes 1572872 | tf_op jit(solution)/shard_map/ppermute | solution.py:108
  116.2 11.6 %collective-permute-start.36 = (bf16[256,512]{1,0:T(8,128)(2,1)S(1)}, bf16[256,512]{1,0:T(8,128)(2,1)S(1)}, u32[]{:S(2)}, u32[]{:S(2)}) collective-permute-start(bf16[256,512]{1,0:T(8,128)(2,1)S(1)} %get-tuple-element.70), channel_id=1, source_target_pairs={{0,16},{8,120},{16,32},{24,8},{32,48},{40,24},{48,64},{56,40},{64,... | collective-permute-start | bytes 786440 | tf_op jit(solution)/shard_map/ppermute | solution.py:104
  118.5 13.4 %copy-start = (s32[2]{0:T(128)S(1)}, s32[2]{0:T(128)}, u32[]{:S(2)}) copy-start(s32[2]{0:T(128)} %lengths.1) | copy-start | bytes 28
  118.5 9.3 %collective-permute-start.37 = (bf16[128,512]{1,0:T(8,128)(2,1)S(1)}, bf16[128,512]{1,0:T(8,128)(2,1)S(1)}, u32[]{:S(2)}, u32[]{:S(2)}) collective-permute-start(bf16[128,512]{1,0:T(8,128)(2,1)S(1)} %get-tuple-element.71), channel_id=1, source_target_pairs={{0,32},{8,104},{16,48},{24,120},{32,64},{40,8},{48,80},{56,24},{64... | collective-permute-start | bytes 393224 | tf_op jit(solution)/shard_map/ppermute | solution.py:104
  120.2 15.7 %collective-permute-start.34 = (bf16[128,512]{1,0:T(8,128)(2,1)S(1)}, bf16[128,512]{1,0:T(8,128)(2,1)S(1)}, u32[]{:S(2)}, u32[]{:S(2)}) collective-permute-start(bf16[128,512]{1,0:T(8,128)(2,1)S(1)} %get-tuple-element.68), channel_id=1, source_target_pairs={{0,16},{8,120},{16,32},{24,8},{32,48},{40,24},{48,64},{56,40},{64,... | collective-permute-start | bytes 393224 | tf_op jit(solution)/shard_map/ppermute | solution.py:104
  120.5 15.5 %collective-permute-start.35 = (bf16[128,512]{1,0:T(8,128)(2,1)S(1)}, bf16[128,512]{1,0:T(8,128)(2,1)S(1)}, u32[]{:S(2)}, u32[]{:S(2)}) collective-permute-start(bf16[128,512]{1,0:T(8,128)(2,1)S(1)} %get-tuple-element.69), channel_id=1, source_target_pairs={{0,24},{8,112},{16,40},{24,0},{32,56},{40,16},{48,72},{56,32},{64,... | collective-permute-start | bytes 393224 | tf_op jit(solution)/shard_map/ppermute | solution.py:104
  127.9 8.1 %collective-permute-start.38 = (bf16[128,512]{1,0:T(8,128)(2,1)S(1)}, bf16[128,512]{1,0:T(8,128)(2,1)S(1)}, u32[]{:S(2)}, u32[]{:S(2)}) collective-permute-start(bf16[128,512]{1,0:T(8,128)(2,1)S(1)} %get-tuple-element.72), channel_id=1, source_target_pairs={{0,32},{8,104},{16,48},{24,120},{32,64},{40,8},{48,80},{56,24},{64... | collective-permute-start | bytes 393224 | tf_op jit(solution)/shard_map/ppermute | solution.py:104
  128.9 8.6 %collective-permute-start.39 = (bf16[128,512]{1,0:T(8,128)(2,1)S(1)}, bf16[128,512]{1,0:T(8,128)(2,1)S(1)}, u32[]{:S(2)}, u32[]{:S(2)}) collective-permute-start(bf16[128,512]{1,0:T(8,128)(2,1)S(1)} %get-tuple-element.73), channel_id=1, source_target_pairs={{0,40},{8,96},{16,56},{24,112},{32,72},{40,0},{48,88},{56,16},{64,... | collective-permute-start | bytes 393224 | tf_op jit(solution)/shard_map/ppermute | solution.py:104
